TPU v7x, 32 devices: a whole 2x2x4 slice. The times are simulated.
32 devices in a mesh: fsdp: 8 (over z, x), ctx: 2 (over y), tp: 2 (over core).
Axes of the slice: x: 2, y: 2, z: 4, core: 2. Of those that a mesh axis runs over, the one named last changes fastest.
Arguments:
- tokens: bfloat16 [8, 1024, 2048], P('fsdp', 'ctx'), may hold values from -6 to 6
- segment_ids: int32 [8, 1024], P('fsdp'), may hold values from 0 to 3, never falling along the last dimension, each value on 1 to 512 neighbouring positions
- norm_gain: bfloat16 [2048], P('fsdp'), may hold values from 0.5 to 1.5
- query_weight: bfloat16 [2048, 2048], P('fsdp', 'tp'), may hold values from -0.125 to 0.125
- key_matrix: bfloat16 [2048, 1024], P('fsdp', 'tp'), may hold values from -0.125 to 0.125
- value_matrix: bfloat16 [2048, 1024], P('fsdp', 'tp'), may hold values from -0.125 to 0.125
- output_weight: bfloat16 [2048, 2048], P('fsdp', 'tp'), may hold values from -1.5 to 1.5
- query_gain: bfloat16 [128], P('fsdp'), may hold values from 0.7 to 6
- key_gain: bfloat16 [128], P('fsdp'), may hold values from 0.7 to 6
- mlp_gain: bfloat16 [2048], P('fsdp'), may hold values from 0.5 to 1.5
- gate_weight: bfloat16 [2048, 6144], P('fsdp', 'tp'), may hold values from -0.125 to 0.125
- up_weight: bfloat16 [2048, 6144], P('fsdp', 'tp'), may hold values from -0.125 to 0.125
- down_weight: bfloat16 [2048, 6144], P('fsdp', 'tp'), may hold values from -0.078125 to 0.078125
- cotangent: bfloat16 [8, 1024, 2048], P('fsdp', 'ctx'), may hold values from -6 to 6
Outputs:
- layer_out: bfloat16 [8, 1024, 2048], P('fsdp', 'ctx')
- token_grad: bfloat16 [8, 1024, 2048], P('fsdp', 'ctx')
- norm_gain_grad: float32 [2048], P('fsdp')
- query_weight_grad: float32 [2048, 2048], P('fsdp', 'tp')
- key_weight_grad: float32 [2048, 1024], P('fsdp', 'tp')
- value_weight_grad: float32 [2048, 1024], P('fsdp', 'tp')
- output_weight_grad: float32 [2048, 2048], P('fsdp', 'tp')
- query_gain_grad: float32 [128], P('fsdp')
- key_gain_grad: float32 [128], P('fsdp')
- mlp_gain_grad: float32 [2048], P('fsdp')
- gate_weight_grad: float32 [2048, 6144], P('fsdp', 'tp')
- up_weight_grad: float32 [2048, 6144], P('fsdp', 'tp')
- down_weight_grad: float32 [2048, 6144], P('fsdp', 'tp')
Inputs may be any that keep to these rules, and one draw needn't show every extreme that they name: `segment_ids`: segment numbers never fall along a sequence; each document has 1 to 512 tokens and one document of each sequence has exactly 512.
All inputs are finite; a program needn't handle non-finite values.
Results may differ from a plain program's by a relative error of at most 0.02.
The roundings to bfloat16 on the way count: a program that leaves them out, or rounds other values in their place, can miss the bound.
Values may be sent and summed in bfloat16 or wider, within the bound.
A program may use at most 256 MiB of HBM per device.

v0:
```python
import functools
import math

import jax
import jax.numpy as jnp
from jax import lax
from jax.experimental import pallas as pl
from jax.experimental.pallas import tpu as pltpu
from jax.sharding import PartitionSpec as P


HEAD = 128
EPS = 1e-06
THETA = 1000000.0
MASKED = -1e30
MOST_DOC = 512
MESH = pl.DeviceIdType.MESH
F32 = jnp.float32
BF16 = jnp.bfloat16


def mm(left, right, left_dim, right_dim):
    return lax.dot_general(
        left, right, (((left_dim,), (right_dim,)), ((), ())), preferred_element_type=F32
    )


def swap_core(value):
    return lax.ppermute(value, "tp", [(0, 1), (1, 0)])


def swap_ctx(value):
    return lax.ppermute(value, "ctx", [(0, 1), (1, 0)])


def swap_x(value):
    count = lax.axis_size("fsdp")
    return lax.ppermute(value, "fsdp", [(i, i ^ 1) for i in range(count)])


def lines():
    count = lax.axis_size("fsdp")
    return [[i for i in range(count) if i % 2 == parity] for parity in (0, 1)]


def gather_line(value):
    return lax.all_gather(value, "fsdp", axis=0, tiled=True, axis_index_groups=lines())


def scatter_line(value):
    return lax.psum_scatter(
        value, "fsdp", scatter_dimension=0, tiled=True, axis_index_groups=lines()
    )


def flip_if(flag, value, axis):
    return jnp.where(flag, jnp.flip(value, axis), value)


def neighbours():
    mine = lax.axis_index("fsdp")
    return (
        {"fsdp": mine + 1 - 2 * lax.rem(mine, 2)},
        {"ctx": 1 - lax.axis_index("ctx")},
        {"tp": 1 - lax.axis_index("tp")},
    )


def greet(peers):
    barrier = pltpu.get_barrier_semaphore()
    for peer in peers:
        pl.semaphore_signal(barrier, inc=1, device_id=peer, device_id_type=MESH)
    pl.semaphore_wait(barrier, len(peers))


def remote_params(number, limit=None):
    return pltpu.CompilerParams(
        collective_id=number, has_side_effects=True, vmem_limit_bytes=limit
    )


def gather8_kernel(rows, own_ref, out_ref, send_sem, recv_sem, local_sem):
    x_peer, y_peer, c_peer = neighbours()
    greet((x_peer, y_peer, c_peer))

    def slot(away_t, half, outer, inner):
        return out_ref.at[pl.ds((away_t * 8 + half * 4 + outer * 2 + inner) * rows, rows)]

    number = iter(range(14))

    def send(source, target, peer):
        index = next(number)
        copy = pltpu.make_async_remote_copy(
            src_ref=source,
            dst_ref=target,
            send_sem=send_sem.at[index],
            recv_sem=recv_sem.at[index],
            device_id=peer,
            device_id_type=MESH,
        )
        copy.start()
        return copy

    first, second = own_ref.at[pl.ds(0, rows)], own_ref.at[pl.ds(rows, rows)]
    x1 = send(first, slot(0, 0, 0, 1), x_peer)
    y1 = send(second, slot(0, 1, 0, 1), y_peer)
    x2 = send(second, slot(0, 1, 1, 0), x_peer)
    y2 = send(first, slot(0, 0, 1, 0), y_peer)
    rest = [send(first, slot(1, 0, 0, 0), c_peer), send(second, slot(1, 1, 0, 0), c_peer)]
    kept = [
        pltpu.make_async_copy(first, slot(0, 0, 0, 0), local_sem.at[0]),
        pltpu.make_async_copy(second, slot(0, 1, 0, 0), local_sem.at[1]),
    ]
    for copy in kept:
        copy.start()
    x1.wait_recv()
    y3 = send(slot(0, 0, 0, 1), slot(0, 0, 1, 1), y_peer)
    y1.wait_recv()
    x3 = send(slot(0, 1, 0, 1), slot(0, 1, 1, 1), x_peer)
    rest.append(send(slot(0, 0, 0, 1), slot(1, 0, 0, 1), c_peer))
    rest.append(send(slot(0, 1, 0, 1), slot(1, 1, 0, 1), c_peer))
    x2.wait_recv()
    rest.append(send(slot(0, 1, 1, 0), slot(1, 1, 1, 0), c_peer))
    y2.wait_recv()
    rest.append(send(slot(0, 0, 1, 0), slot(1, 0, 1, 0), c_peer))
    y3.wait_recv()
    rest.append(send(slot(0, 0, 1, 1), slot(1, 0, 1, 1), c_peer))
    x3.wait_recv()
    rest.append(send(slot(0, 1, 1, 1), slot(1, 1, 1, 1), c_peer))
    for copy in (x1, y1, x2, y2, y3, x3):
        copy.wait_send()
    for copy in rest:
        copy.wait()
    for copy in kept:
        copy.wait()


def gather8(own):
    rows, width = own.shape[0] // 2, own.shape[1]
    return pl.pallas_call(
        functools.partial(gather8_kernel, rows),
        out_shape=jax.ShapeDtypeStruct((16 * rows, width), own.dtype),
        in_specs=[pl.BlockSpec(memory_space=pltpu.VMEM)],
        out_specs=pl.BlockSpec(memory_space=pl.ANY),
        scratch_shapes=[
            pltpu.SemaphoreType.DMA((14,)),
            pltpu.SemaphoreType.DMA((14,)),
            pltpu.SemaphoreType.DMA((2,)),
        ],
        compiler_params=remote_params(1),
        name="gather8",
    )(own)


def reduce8_kernel(
    rows,
    near_ref,
    far_ref,
    out_ref,
    near,
    core_in,
    link_in,
    link_out,
    send_sem,
    recv_sem,
    local_sem,
):
    x_peer, y_peer, c_peer = neighbours()
    greet((x_peer, y_peer, c_peer))
    order = [(h, o, i) for o, i in ((1, 1), (1, 0), (0, 1), (0, 0)) for h in (0, 1)]
    core_copies, local_copies = {}, {}
    for number, (half, outer, inner) in enumerate(order):
        place = pl.ds((half * 4 + outer * 2 + inner) * rows, rows)
        core_copies[half, outer, inner] = pltpu.make_async_remote_copy(
            src_ref=far_ref.at[place],
            dst_ref=core_in.at[place],
            send_sem=send_sem.at[number],
            recv_sem=recv_sem.at[number],
            device_id=c_peer,
            device_id_type=MESH,
        )
        local_copies[half, outer, inner] = pltpu.make_async_copy(
            near_ref.at[place], near.at[place], local_sem.at[number]
        )
    for block in order:
        core_copies[block].start()
        local_copies[block].start()

    def partial_sum(block):
        half, outer, inner = block
        place = pl.ds((half * 4 + outer * 2 + inner) * rows, rows)
        core_copies[block].wait_recv()
        local_copies[block].wait()
        return near[place, :] + core_in[place, :].astype(F32)

    def link(index, value, peer):
        link_out[index] = value.astype(BF16)
        copy = pltpu.make_async_remote_copy(
            src_ref=link_out.at[index],
            dst_ref=link_in.at[index],
            send_sem=send_sem.at[8 + index],
            recv_sem=recv_sem.at[8 + index],
            device_id=peer,
            device_id_type=MESH,
        )
        copy.start()
        return copy

    y11 = link(0, partial_sum((0, 1, 1)), y_peer)
    x11 = link(1, partial_sum((1, 1, 1)), x_peer)
    y10 = link(2, partial_sum((0, 1, 0)), y_peer)
    x10 = link(3, partial_sum((1, 1, 0)), x_peer)
    first01, second01 = partial_sum((0, 0, 1)), partial_sum((1, 0, 1))
    y11.wait_recv()
    x01 = link(4, first01 + link_in[0].astype(F32), x_peer)
    x11.wait_recv()
    y01 = link(5, second01 + link_in[1].astype(F32), y_peer)
    first = partial_sum((0, 0, 0))
    second = partial_sum((1, 0, 0))
    y10.wait_recv()
    out_ref[pl.ds(0, rows), :] = first + link_in[2].astype(F32)
    x10.wait_recv()
    out_ref[pl.ds(rows, rows), :] = second + link_in[3].astype(F32)
    x01.wait_recv()
    out_ref[pl.ds(0, rows), :] += link_in[4].astype(F32)
    y01.wait_recv()
    out_ref[pl.ds(rows, rows), :] += link_in[5].astype(F32)
    for copy in (y11, x11, y10, x10, x01, y01):
        copy.wait_send()
    for copy in core_copies.values():
        copy.wait_send()


def reduce8(near, far):
    rows, width = near.shape[0] // 8, near.shape[1]
    return pl.pallas_call(
        functools.partial(reduce8_kernel, rows),
        out_shape=jax.ShapeDtypeStruct((2 * rows, width), F32),
        in_specs=[pl.BlockSpec(memory_space=pl.ANY), pl.BlockSpec(memory_space=pl.ANY)],
        out_specs=pl.BlockSpec(memory_space=pltpu.VMEM),
        scratch_shapes=[
            pltpu.VMEM(near.shape, F32),
            pltpu.VMEM(near.shape, BF16),
            pltpu.VMEM((6, rows, width), BF16),
            pltpu.VMEM((6, rows, width), BF16),
            pltpu.SemaphoreType.DMA((14,)),
            pltpu.SemaphoreType.DMA((14,)),
            pltpu.SemaphoreType.DMA((8,)),
        ],
        compiler_params=remote_params(2, 48 * 1024 * 1024),
        name="reduce8",
    )(near, far)


def shard_kernel(plan, outs, *refs):
    ins, out_refs = refs[: len(plan)], refs[len(plan) : len(plan) + outs]
    stage = refs[len(plan) + outs : 2 * len(plan) + outs]
    send_sem, recv_sem, load_sem, store_sem = refs[2 * len(plan) + outs :]
    x_peer, _, _ = neighbours()
    odd = lax.rem(lax.axis_index("fsdp"), 2)
    column = 2 * lax.axis_index("ctx") + odd
    other = 2 * lax.axis_index("ctx") + 1 - odd
    greet((x_peer,))
    remote, loads, stores = [], [], []
    for number, (which, start, size, cut) in enumerate(plan):
        target = out_refs[which].at[odd, :, pl.ds(start, size)]

        def source(index, ref=ins[number], size=size, cut=cut):
            if not cut:
                return ref
            return ref.at[:, pl.ds(pl.multiple_of(index * size, HEAD), size)]

        remote.append(
            pltpu.make_async_remote_copy(
                src_ref=source(other),
                dst_ref=target,
                send_sem=send_sem.at[number],
                recv_sem=recv_sem.at[number],
                device_id=x_peer,
                device_id_type=MESH,
            )
        )
        loads.append(pltpu.make_async_copy(source(column), stage[number], load_sem.at[number]))
        stores.append(pltpu.make_async_copy(stage[number], target, store_sem.at[number]))
    for copy in remote:
        copy.start()
    for copy in loads:
        copy.start()
    for load, store in zip(loads, stores):
        load.wait()
        store.start()
    for copy in stores:
        copy.wait()
    for copy in remote:
        copy.wait()


def shards(groups, number):
    plan, arrays, shapes = [], [], []
    for which, group in enumerate(groups):
        start = 0
        for array, cut in group:
            size = array.shape[1] // 4 if cut else array.shape[1]
            plan.append((which, start, size, cut))
            arrays.append(array)
            start += size
        shapes.append((2, group[0][0].shape[0], start))
    hbm = pl.BlockSpec(memory_space=pl.ANY)
    pairs = pl.pallas_call(
        functools.partial(shard_kernel, tuple(plan), len(groups)),
        out_shape=[jax.ShapeDtypeStruct(shape, BF16) for shape in shapes],
        in_specs=[hbm] * len(arrays),
        out_specs=[hbm] * len(groups),
        scratch_shapes=[
            pltpu.VMEM((array.shape[0], size), BF16)
            for array, (_, _, size, _) in zip(arrays, plan)
        ]
        + [pltpu.SemaphoreType.DMA((len(plan),))] * 4,
        compiler_params=remote_params(number),
        name="shards",
    )(*arrays)
    return [pair.reshape(2 * pair.shape[1], pair.shape[2]) for pair in pairs]


def total_kernel(stages, part_ref, out_ref, inbox, outbox, send_sem, recv_sem):
    peers = []
    for axis, bit in stages:
        mine = lax.axis_index(axis)
        peers.append({axis: mine + bit * (1 - 2 * lax.rem(mine // bit, 2))})
    greet(peers)
    value = part_ref[...]
    copies = []
    for index, peer in enumerate(peers):
        outbox[index] = value
        copy = pltpu.make_async_remote_copy(
            src_ref=outbox.at[index],
            dst_ref=inbox.at[index],
            send_sem=send_sem.at[index],
            recv_sem=recv_sem.at[index],
            device_id=peer,
            device_id_type=MESH,
        )
        copy.start()
        copies.append(copy)
        copy.wait_recv()
        value = value + inbox[index]
    out_ref[...] = value
    for copy in copies:
        copy.wait_send()


def total(part):
    stages = [("tp", 1), ("ctx", 1)]
    bit = 1
    while bit < lax.axis_size("fsdp"):
        stages.append(("fsdp", bit))
        bit *= 2
    return pl.pallas_call(
        functools.partial(total_kernel, tuple(stages)),
        out_shape=jax.ShapeDtypeStruct(part.shape, F32),
        in_specs=[pl.BlockSpec(memory_space=pltpu.VMEM)],
        out_specs=pl.BlockSpec(memory_space=pltpu.VMEM),
        scratch_shapes=[
            pltpu.VMEM((len(stages),) + part.shape, F32),
            pltpu.VMEM((len(stages),) + part.shape, F32),
            pltpu.SemaphoreType.DMA((len(stages),)),
            pltpu.SemaphoreType.DMA((len(stages),)),
        ],
        compiler_params=remote_params(5),
        name="total",
    )(part)


def after(value, *others):
    return lax.optimization_barrier((value,) + others)[0]


def reduce4_links(total_rows, *others):
    rows = total_rows.shape[0] // 8
    first, second = total_rows[: 4 * rows], total_rows[4 * rows :]
    came_first = swap_ctx(first[2 * rows :].astype(BF16))
    came_second = swap_x(second[2 * rows :].astype(BF16))
    first = first[: 2 * rows] + after(came_first, *others).astype(F32)
    second = second[: 2 * rows] + after(came_second, *others).astype(F32)
    came_first = swap_x(first[rows:].astype(BF16))
    came_second = swap_ctx(second[rows:].astype(BF16))
    first = first[:rows] + came_first.astype(F32)
    second = second[:rows] + came_second.astype(F32)
    return jnp.concatenate([first, second])


def rope_tables(positions):
    freqs = THETA ** (-(jnp.arange(HEAD // 2, dtype=F32) * 2.0) / HEAD)
    angle = positions[:, None] * freqs[None, :]
    cosine = jnp.concatenate([jnp.cos(angle), jnp.cos(angle)], axis=-1)
    sine = jnp.concatenate([-jnp.sin(angle), jnp.sin(angle)], axis=-1)
    return cosine, sine


def norm_back(grad, scaled, inverse, gain):
    weighted = grad * gain
    return inverse * (weighted - scaled * jnp.mean(weighted * scaled, axis=-1, keepdims=True))


def inv_rms(value):
    return lax.rsqrt(jnp.mean(value * value, axis=-1, keepdims=True) + EPS)


def block_row(meta_ref, seq, index, rows):
    away_c = lax.rem(meta_ref[0] + index // 4, 2)
    away_t = lax.rem(meta_ref[1] + (index // 2) % 2, 2)
    if index % 2 == 0:
        inner = away_c * 2 + seq
    else:
        inner = seq * 2 + away_c + 4
    return pl.multiple_of((away_t * 8 + inner) * rows, rows)


def scaled_of(raw):
    inverse = lax.rsqrt(jnp.mean(raw * raw, axis=-1, keepdims=True) + EPS)
    return raw * inverse, inverse


def load_heads(meta_ref, qkv_ref, cos_ref, sin_ref, gain_ref, q_scr, k_scr, v_scr, heads):
    seq = pl.program_id(0)
    rows = q_scr.shape[1] // 8
    for index in range(8):
        start = block_row(meta_ref, seq, index, rows)
        here = slice(index * rows, (index + 1) * rows)
        cosine, sine = cos_ref[here, :], sin_ref[here, :]
        for head in range(heads + 1):
            raw = qkv_ref[pl.ds(start, rows), head * HEAD : (head + 1) * HEAD]
            scaled, _ = scaled_of(raw)
            which = 0 if head < heads else 1
            value = scaled * gain_ref[which : which + 1, :]
            turned = value * cosine + pltpu.roll(value, HEAD // 2, 1) * sine
            if head < heads:
                q_scr[head, here, :] = turned.astype(BF16)
            else:
                k_scr[here, :] = turned.astype(BF16)
        v_scr[here, :] = qkv_ref[
            pl.ds(start, rows), (heads + 1) * HEAD : (heads + 2) * HEAD
        ].astype(BF16)


def key_span(index, tile):
    low = max(0, (index * tile - (MOST_DOC - 1)) // tile) * tile
    return low, (index + 1) * tile


def allowed_mask(segc_ref, segr_ref, index, tile):
    low, high = key_span(index, tile)
    shape = (tile, high - low)
    rows = lax.broadcasted_iota(jnp.int32, shape, 0) + index * tile
    cols = lax.broadcasted_iota(jnp.int32, shape, 1) + low
    same = segc_ref[0, index * tile : (index + 1) * tile, :] == segr_ref[0, :, low:high]
    return same & (cols <= rows)


def probs_of(query, keys, allowed, scale):
    scores = jnp.where(allowed, mm(query, keys, 1, 1) * scale, MASKED)
    weights = jnp.exp(scores - jnp.max(scores, axis=-1, keepdims=True))
    return weights * (1.0 / jnp.sum(weights, axis=-1, keepdims=True))


def attend_kernel(
    heads, tile, meta_ref, qkv_ref, segc_ref, segr_ref, cos_ref, sin_ref, gain_ref, out_ref, q_scr, k_scr, v_scr
):
    seq = pl.program_id(0)
    length = k_scr.shape[0]
    rows = length // 8
    scale = 1.0 / math.sqrt(HEAD)
    load_heads(meta_ref, qkv_ref, cos_ref, sin_ref, gain_ref, q_scr, k_scr, v_scr, heads)
    for index in range(length // tile):
        low, high = key_span(index, tile)
        allowed = allowed_mask(segc_ref, segr_ref, index, tile)
        for head in range(heads):
            query = q_scr[head, index * tile : (index + 1) * tile, :]
            probs = probs_of(query, k_scr[low:high, :], allowed, scale)
            mixed = mm(probs.astype(BF16), v_scr[low:high, :], 1, 0).astype(BF16)
            for piece in range(tile // rows):
                start = block_row(meta_ref, seq, index * (tile // rows) + piece, rows)
                out_ref[pl.ds(start, rows), head * HEAD : (head + 1) * HEAD] = mixed[
                    piece * rows : (piece + 1) * rows
                ]


def attend_back_kernel(
    heads,
    tile,
    meta_ref,
    qkv_ref,
    grad_ref,
    segc_ref,
    segr_ref,
    cos_ref,
    sin_ref,
    gain_ref,
    out_ref,
    gain_out_ref,
    q_scr,
    k_scr,
    v_scr,
    g_scr,
    dk_scr,
    dv_scr,
):
    seq = pl.program_id(0)
    length = k_scr.shape[0]
    rows = length // 8
    scale = 1.0 / math.sqrt(HEAD)
    load_heads(meta_ref, qkv_ref, cos_ref, sin_ref, gain_ref, q_scr, k_scr, v_scr, heads)
    for index in range(8):
        start = block_row(meta_ref, seq, index, rows)
        g_scr[index * rows : (index + 1) * rows, :] = grad_ref[pl.ds(start, rows), :]
    dk_scr[...] = jnp.zeros_like(dk_scr)
    dv_scr[...] = jnp.zeros_like(dv_scr)

    @pl.when(seq == 0)
    def _():
        gain_out_ref[...] = jnp.zeros_like(gain_out_ref)

    def finish(grad, index, head, which):
        here = slice(index * rows, (index + 1) * rows)
        start = block_row(meta_ref, seq, index, rows)
        grad = grad * cos_ref[here, :] - pltpu.roll(grad, HEAD // 2, 1) * sin_ref[here, :]
        raw = qkv_ref[pl.ds(start, rows), head * HEAD : (head + 1) * HEAD]
        scaled, inverse = scaled_of(raw)
        gain_out_ref[which : which + 1, :] += jnp.sum(grad * scaled, axis=0, keepdims=True)
        out = norm_back(grad, scaled, inverse, gain_ref[which : which + 1, :])
        out_ref[pl.ds(start, rows), head * HEAD : (head + 1) * HEAD] = out.astype(BF16)

    per = tile // rows
    for index in range(length // tile):
        low, high = key_span(index, tile)
        mine = slice(index * tile, (index + 1) * tile)
        allowed = allowed_mask(segc_ref, segr_ref, index, tile)
        for head in range(heads):
            query = q_scr[head, mine, :]
            keys = k_scr[low:high, :]
            probs = probs_of(query, keys, allowed, scale)
            grad = g_scr[mine, head * HEAD : (head + 1) * HEAD]
            grad_probs = mm(grad, v_scr[low:high, :], 1, 1)
            delta = jnp.sum(probs * grad_probs, axis=-1, keepdims=True)
            grad_scores = (probs * (grad_probs - delta)).astype(BF16)
            dv_scr[low:high, :] += mm(probs.astype(BF16), grad, 0, 0)
            dk_scr[low:high, :] += mm(grad_scores, query, 0, 0) * scale
            grad_query = mm(grad_scores, keys, 1, 0) * scale
            for piece in range(per):
                finish(
                    grad_query[piece * rows : (piece + 1) * rows], index * per + piece, head, 0
                )
    for index in range(8):
        here = slice(index * rows, (index + 1) * rows)
        start = block_row(meta_ref, seq, index, rows)
        finish(dk_scr[here, :], index, heads, 1)
        out_ref[pl.ds(start, rows), (heads + 1) * HEAD : (heads + 2) * HEAD] = dv_scr[
            here, :
        ].astype(BF16)


def whole(shape):
    return pl.BlockSpec(shape, lambda seq, meta: (0,) * len(shape))


def seg_specs(length):
    return [
        pl.BlockSpec((1, length, 1), lambda seq, meta: (seq, 0, 0)),
        pl.BlockSpec((1, 1, length), lambda seq, meta: (seq, 0, 0)),
    ]


def attend(meta, qkv, seg_cols, seg_rows, cosine, sine, gains):
    length = cosine.shape[0]
    tile = length // 4
    heads = qkv.shape[1] // HEAD - 2
    pairs = 2 * heads * length * length // 2
    return pl.pallas_call(
        functools.partial(attend_kernel, heads, tile),
        out_shape=jax.ShapeDtypeStruct((qkv.shape[0], heads * HEAD), BF16),
        grid_spec=pltpu.PrefetchScalarGridSpec(
            num_scalar_prefetch=1,
            grid=(2,),
            in_specs=[whole(qkv.shape)]
            + seg_specs(length)
            + [whole(cosine.shape), whole(sine.shape), whole(gains.shape)],
            out_specs=whole((qkv.shape[0], heads * HEAD)),
            scratch_shapes=[
                pltpu.VMEM((heads, length, HEAD), BF16),
                pltpu.VMEM((length, HEAD), BF16),
                pltpu.VMEM((length, HEAD), BF16),
            ],
        ),
        cost_estimate=pl.CostEstimate(
            flops=4 * pairs * HEAD, bytes_accessed=qkv.size * 4 + qkv.size, transcendentals=pairs
        ),
        name="attend",
    )(meta, qkv, seg_cols, seg_rows, cosine, sine, gains)


def attend_back(meta, qkv, grad, seg_cols, seg_rows, cosine, sine, gains):
    length = cosine.shape[0]
    tile = length // 4
    heads = qkv.shape[1] // HEAD - 2
    pairs = 2 * heads * length * length // 2
    return pl.pallas_call(
        functools.partial(attend_back_kernel, heads, tile),
        out_shape=(
            jax.ShapeDtypeStruct(qkv.shape, BF16),
            jax.ShapeDtypeStruct(gains.shape, F32),
        ),
        grid_spec=pltpu.PrefetchScalarGridSpec(
            num_scalar_prefetch=1,
            grid=(2,),
            in_specs=[whole(qkv.shape), whole(grad.shape)]
            + seg_specs(length)
            + [whole(cosine.shape), whole(sine.shape), whole(gains.shape)],
            out_specs=(whole(qkv.shape), whole(gains.shape)),
            scratch_shapes=[
                pltpu.VMEM((heads, length, HEAD), BF16),
                pltpu.VMEM((length, HEAD), BF16),
                pltpu.VMEM((length, HEAD), BF16),
                pltpu.VMEM((length, heads * HEAD), BF16),
                pltpu.VMEM((length, HEAD), F32),
                pltpu.VMEM((length, HEAD), F32),
            ],
        ),
        cost_estimate=pl.CostEstimate(
            flops=10 * pairs * HEAD, bytes_accessed=qkv.size * 8, transcendentals=pairs
        ),
        name="attend_back",
    )(meta, qkv, grad, seg_cols, seg_rows, cosine, sine, gains)


def body(
    tokens,
    segment_ids,
    norm_gain,
    query_weight,
    key_matrix,
    value_matrix,
    output_weight,
    query_gain,
    key_gain,
    mlp_gain,
    gate_weight,
    up_weight,
    down_weight,
    cotangent,
):
    local, width = tokens.shape[1], tokens.shape[2]
    length = 2 * local
    quarter = local // 2
    count = lax.axis_size("fsdp")
    block = width // count
    mine = lax.axis_index("fsdp")
    odd = mine % 2
    place = lax.axis_index("ctx")
    core = lax.axis_index("tp")

    small = query_gain.shape[0]
    lanes = jnp.arange(HEAD)[None, :]

    def pad_rows(vector):
        return jnp.concatenate([vector, jnp.zeros((block - small,), BF16)])

    gains = jnp.where(
        lanes == 0,
        norm_gain[:, None],
        jnp.where(
            lanes == 1,
            mlp_gain[:, None],
            jnp.where(
                lanes == 2, pad_rows(query_gain)[:, None], pad_rows(key_gain)[:, None]
            ),
        ),
    )
    (first_pair,) = shards(
        [
            [
                (query_weight, True),
                (key_matrix, True),
                (value_matrix, True),
                (output_weight, True),
                (gains, False),
            ]
        ],
        3,
    )
    first = gather_line(first_pair)
    gate_up_pair, down_pair = shards(
        [
            [(after(gate_weight, first_pair), True), (up_weight, True)],
            [(down_weight, True)],
        ],
        4,
    )
    gate_up_w = gather_line(gate_up_pair)
    down_w = gather_line(down_pair)

    def own_quarter(value):
        return lax.dynamic_slice_in_dim(value.reshape(local, width), core * quarter, quarter, 0)

    own_tok, own_cot = own_quarter(tokens), own_quarter(cotangent)
    tok = gather8(after(own_tok, gate_up_pair))
    segments = jnp.concatenate([segment_ids, swap_x(segment_ids)])
    seg_cols, seg_rows = segments[:, :, None], segments[:, None, :]
    cosine, sine = rope_tables(jnp.arange(length).astype(F32))
    meta = jnp.stack([place, core]).astype(jnp.int32)

    heads_q = query_weight.shape[1] // 4 // HEAD
    cols = (heads_q + 2) * HEAD
    qkv_w = first[:, :cols]
    out_w = first[:, cols : cols + heads_q * HEAD]
    gain_cols = first[:, cols + heads_q * HEAD :].astype(F32)
    in_gain, mid_gain = gain_cols[:, 0][None], gain_cols[:, 1][None]
    head_gains = gain_cols.reshape(count, block, HEAD)[:, :small, 2:4].reshape(HEAD, 2).T

    in_f = tok.astype(F32)
    inverse_all = inv_rms(in_f)
    cot = gather8(after(own_cot, inverse_all))
    x_all = (in_f * inverse_all * in_gain).astype(BF16)
    qkv = mm(x_all, qkv_w, 1, 0)
    attended = attend(meta, qkv, seg_cols, seg_rows, cosine, sine, head_gains)
    half = 4 * quarter
    middle = own_tok.astype(F32) + reduce8(
        mm(attended[:half], out_w, 1, 1), mm(attended[half:], out_w, 1, 1).astype(BF16)
    )
    inverse_mid = inv_rms(middle)
    scaled_mid = middle * inverse_mid
    y_all = gather8((scaled_mid * mid_gain).astype(BF16))

    ff = gate_up_w.shape[1] // 2
    gate_up = mm(y_all, gate_up_w, 1, 0)
    gate, up_value = gate_up[:, :ff], gate_up[:, ff:]
    sig = jax.nn.sigmoid(gate)
    active = gate * sig
    hidden = (active * up_value).astype(BF16)
    down_grad = mm(cot, hidden, 0, 0).astype(BF16)

    def finish_rows(own):
        pair = jnp.stack([own, swap_core(own)])
        return flip_if(core == 1, pair, 0).reshape(tokens.shape)

    grad_hidden = mm(after(cot, down_grad), down_w, 1, 0)
    grad_up = (grad_hidden * active).astype(BF16)
    grad_gate = (grad_hidden * up_value * (sig * (1.0 + gate * (1.0 - sig)))).astype(BF16)
    grad_gate_up = jnp.concatenate([grad_gate, grad_up], axis=1)
    gate_up_grad = mm(y_all, grad_gate_up, 0, 0).astype(BF16)
    mid_near = mm(grad_gate_up[:half], gate_up_w, 1, 1)
    mid_far = mm(grad_gate_up[half:], gate_up_w, 1, 1).astype(BF16)
    mid_grad = reduce8(mid_near, after(mid_far, gate_up_grad))

    mlp_gain_part = jnp.sum(mid_grad * scaled_mid, axis=0)
    grad_middle = own_cot.astype(F32) + norm_back(mid_grad, scaled_mid, inverse_mid, mid_gain)
    grad_attn = gather8(grad_middle.astype(BF16))
    out_grad = mm(grad_attn, attended, 0, 0).astype(BF16)
    grad_att = mm(grad_attn, out_w, 1, 0).astype(BF16)
    mlp_hidden = after(hidden, grad_attn)
    mlp_far = mm(mlp_hidden[half:], down_w, 1, 1).astype(BF16)
    mlp_came = swap_core(mlp_far)
    mlp_rows = mm(mlp_hidden[:half], down_w, 1, 1) + mlp_came.astype(F32)
    raw_grads, head_gain_parts = attend_back(
        meta, qkv, after(grad_att, mlp_rows), seg_cols, seg_rows, cosine, sine, head_gains
    )
    first_grad = mm(x_all, raw_grads, 0, 0).astype(BF16)
    mlp = reduce4_links(mlp_rows, raw_grads)
    layer_out = finish_rows((middle + mlp).astype(BF16))
    in_near = mm(raw_grads[:half], qkv_w, 1, 1)
    in_far = mm(raw_grads[half:], qkv_w, 1, 1).astype(BF16)
    in_grad = reduce8(in_near, after(in_far, first_grad))

    def owners(grad, sizes, *others):
        rows = scatter_line(grad)
        rows = after(rows, *others).reshape(2, block, grad.shape[1])
        kept = lax.dynamic_index_in_dim(rows, odd, 0, keepdims=False)
        sent = lax.dynamic_index_in_dim(rows, 1 - odd, 0, keepdims=False)
        came = swap_x(sent)
        pair = flip_if(odd == 1, jnp.stack([kept, came]), 0)
        far = swap_ctx(pair)
        four = flip_if(place == 1, jnp.stack([pair, far]), 0)
        four = four.reshape(4, block, grad.shape[1])
        shares, start = [], 0
        for size in sizes:
            piece = four[:, :, start : start + size]
            shares.append(jnp.moveaxis(piece, 0, 1).reshape(block, 4 * size).astype(F32))
            start += size
        return shares

    (down_share,) = owners(down_grad, (ff,), grad_attn)
    gate_share, up_share = owners(gate_up_grad, (ff, ff), raw_grads)
    (out_share,) = owners(out_grad, (out_grad.shape[1],), raw_grads)
    query_share, key_share, value_share = owners(first_grad, (heads_q * HEAD, HEAD, HEAD))

    own_in = own_tok.astype(F32)
    inverse_in = inv_rms(own_in)
    scaled_in = own_in * inverse_in
    norm_gain_part = jnp.sum(in_grad * scaled_in, axis=0)
    token_grad = finish_rows(
        (grad_middle + norm_back(in_grad, scaled_in, inverse_in, in_gain)).astype(BF16)
    )

    parts = jnp.concatenate([norm_gain_part, mlp_gain_part, head_gain_parts.reshape(-1)])
    sums = total(parts.reshape(-1, HEAD)).reshape(-1)
    norm_gain_grad = lax.dynamic_slice_in_dim(sums, mine * block, block, 0)
    mlp_gain_grad = lax.dynamic_slice_in_dim(sums, width + mine * block, block, 0)
    query_gain_grad = lax.dynamic_slice_in_dim(sums, 2 * width + mine * small, small, 0)
    key_gain_grad = lax.dynamic_slice_in_dim(sums, 2 * width + HEAD + mine * small, small, 0)
    return (
        layer_out,
        token_grad,
        norm_gain_grad,
        query_share,
        key_share,
        value_share,
        out_share,
        query_gain_grad,
        key_gain_grad,
        mlp_gain_grad,
        gate_share,
        up_share,
        down_share,
    )


def solution(mesh):
    in_specs = (
        P("fsdp", "ctx", None),
        P("fsdp", None),
        P("fsdp"),
        P("fsdp", "tp"),
        P("fsdp", "tp"),
        P("fsdp", "tp"),
        P("fsdp", "tp"),
        P("fsdp"),
        P("fsdp"),
        P("fsdp"),
        P("fsdp", "tp"),
        P("fsdp", "tp"),
        P("fsdp", "tp"),
        P("fsdp", "ctx", None),
    )
    out_specs = (
        P("fsdp", "ctx", None),
        P("fsdp", "ctx", None),
        P("fsdp"),
        P("fsdp", "tp"),
        P("fsdp", "tp"),
        P("fsdp", "tp"),
        P("fsdp", "tp"),
        P("fsdp"),
        P("fsdp"),
        P("fsdp"),
        P("fsdp", "tp"),
        P("fsdp", "tp"),
        P("fsdp", "tp"),
    )

    return jax.shard_map(body, mesh=mesh, in_specs=in_specs, out_specs=out_specs, check_vma=False)
```

profile of v0, /device:TPU:0, one launch (start us, length us, event | category | flops | bytes accessed | tf_op | source)
XLA Modules:
  0.0 797.4 jit_solution(16390878738483083271)
XLA Ops:
  10.1 14.0 %shards.2 = bf16[2,256,896]{2,1,0:T(8,128)(2,1)} custom-call(bf16[256,1024]{1,0:T(8,128)(2,1)} %refs_0_.1, bf16[256,512]{1,0:T(8,128)(2,1)} %refs_1_.2, bf16[256,512]{1,0:T(8,128)(2,1)} %refs_2_.2, bf16[256,1024]{1,0:T(8,128)(2,1)} %refs_3_.1, bf16[256,128]{1,0:T(8,128)(2,1)} %select_select_fusion.refs_4_), custom_call_target="tpu_custom_call" | custom-call | tf_op jit(solution)/shard_map/shards/pallas_call | solution.py:309
  26.4 27.6 %shards.3 = (bf16[2,256,1536]{2,1,0:T(8,128)(2,1)}, bf16[2,256,768]{2,1,0:T(8,128)(2,1)}) custom-call(bf16[256,3072]{1,0:T(8,128)(2,1)} %refs_0_.2, bf16[256,3072]{1,0:T(8,128)(2,1)} %refs_1_.3, bf16[256,3072]{1,0:T(8,128)(2,1)} %refs_2_.3), custom_call_target="tpu_custom_call" | custom-call | tf_op jit(solution)/shard_map/shards/pallas_call | solution.py:309
  57.4 40.8 %gather8.4 = bf16[2048,2048]{1,0:T(8,128)(2,1)} custom-call(bf16[256,2048]{1,0:T(8,128)(2,1)} %get-tuple-element.31.own_ref), custom_call_target="tpu_custom_call" | custom-call | tf_op jit(solution)/shard_map/gather8/pallas_call | solution.py:140
  108.4 41.0 %gather8.6 = bf16[2048,2048]{1,0:T(8,128)(2,1)} custom-call(bf16[256,2048]{1,0:T(8,128)(2,1)} %dynamic-slice_bitcast_fusion.own_ref), custom_call_target="tpu_custom_call" | custom-call | tf_op jit(solution)/shard_map/gather8/pallas_call | solution.py:140
  153.6 10.5 %fusion.13.qkv_ref = f32[2048,512]{1,0:T(8,128)} fusion(bf16[2048,2048]{1,0:T(8,128)(2,1)} %gather8.4, f32[2048]{0:T(1024)S(1)} %bitcast.154, f32[2048]{0:T(1024)S(1)} %add_rsqrt_fusion, bf16[2048,896]{0,1:T(8,128)(2,1)} %all-gather.4.cloned.1.call-done), kind=kOutput, calls=%fused_computation.38 | convolution fusion | flops 4311744512 | bytes 14696448 | tf_op jit(solution)/shard_map/dot_general | solution.py:23
  164.1 16.6 %attend.1 = bf16[2048,256]{1,0:T(8,128)(2,1)} custom-call(s32[2]{0:T(128)} %pad_add_fusion.1.meta_ref, f32[2048,512]{1,0:T(8,128)} %fusion.13.qkv_ref, s32[2,1024,1]{2,1,0:T(8,128)} %copy.38.segc_ref, s32[2,1,1024]{2,1,0:T(1,128)} %broadcast_in_dim.76.segr_ref, f32[1024,128]{1,0:T(8,128)} %get-tuple-element.88.cos_ref, ...), custom_call_target="tpu_custom_call" | custom-call | flops 1073741824 | bytes 5242880 | tf_op jit(solution)/shard_map/attend/pallas_call | solution.py:578
  180.8 6.0 fusion.36.near_ref
  191.4 40.1 %reduce8.3 = f32[256,2048]{1,0:T(8,128)S(1)} custom-call(f32[1024,2048]{1,0:T(8,128)} %fusion.36.near_ref, bf16[1024,2048]{1,0:T(8,128)(2,1)} %convolution_convert_fusion.3.far_ref), custom_call_target="tpu_custom_call" | custom-call | tf_op jit(solution)/shard_map/reduce8/pallas_call | solution.py:236
  234.3 40.5 %gather8.5 = bf16[2048,2048]{1,0:T(8,128)(2,1)} custom-call(bf16[256,2048]{1,0:T(8,128)(2,1)} %multiply_convert_fusion.3.own_ref), custom_call_target="tpu_custom_call" | custom-call | tf_op jit(solution)/shard_map/gather8/pallas_call | solution.py:140
  274.8 17.9 %fusion.51 = f32[2048,1536]{0,1:T(8,128)S(1)} fusion(bf16[2048,2048]{1,0:T(8,128)(2,1)} %gather8.5, bf16[2048,1536]{1,0:T(8,128)(2,1)} %all-gather.6.cloned.1.call-done), kind=kOutput, calls=%fused_computation.139 | convolution fusion | flops 12884901888 | bytes 27262976 | tf_op jit(solution)/shard_map/dot_general | solution.py:23
  299.0 10.4 %convolution_convert_fusion.5 = bf16[2048,768]{1,0:T(8,128)(2,1)} fusion(bf16[2048,2048]{1,0:T(8,128)(2,1)} %gather8.6, bf16[2048,768]{0,1:T(8,128)(2,1)S(1)} %multiply_convert_fusion.2), kind=kOutput, calls=%fused_computation.22 | convolution fusion | flops 6444023808 | bytes 14680064 | tf_op jit(solution)/shard_map/dot_general | solution.py:23
  309.4 15.3 %multiply_convert_fusion = (bf16[2048,768]{0,1:T(8,128)(2,1)S(1)}, bf16[2048,768]{0,1:T(8,128)(2,1)S(1)}) fusion(f32[2048,1536]{0,1:T(8,128)} %copy-done.7, bf16[2048,2048]{1,0:T(8,128)(2,1)} %gather8.6, bf16[2048,768]{1,0:T(8,128)(2,1)} %all-gather.8.cloned.1.call-done), kind=kOutput, calls=%fused_computation.12 | convolution fusion | flops 6462898176 | bytes 30408704 | tf_op jit(solution)/shard_map/dot_general | solution.py:23
  327.4 17.5 %convolution_convert_fusion = bf16[2048,1536]{1,0:T(8,128)(2,1)} fusion(bf16[2048,2048]{1,0:T(8,128)(2,1)} %gather8.5, bf16[2048,768]{0,1:T(8,128)(2,1)S(1)} %get-tuple-element.53, bf16[2048,768]{0,1:T(8,128)(2,1)S(1)} %get-tuple-element.54), kind=kOutput, calls=%fused_computation.11 | convolution fusion | flops 12900630528 | bytes 20971520 | tf_op jit(solution)/shard_map/dot_general | solution.py:23
  344.9 11.8 %convolution_convert_fusion.1.far_ref = bf16[1024,2048]{1,0:T(8,128)(2,1)} fusion(bf16[2048,1536]{1,0:T(8,128)(2,1)} %all-gather.6.cloned.1.call-done, bf16[2048,768]{0,1:T(8,128)(2,1)} %copy-done.37, bf16[2048,768]{0,1:T(8,128)(2,1)} %copy-done.35), kind=kOutput, calls=%fused_computation.18 | convolution fusion | flops 6450839552 | bytes 16777216 | tf_op jit(solution)/shard_map/dot_general | solution.py:23
  356.7 11.0 %fusion.5.near_ref = f32[1024,2048]{1,0:T(8,128)} fusion(bf16[2048,1536]{1,0:T(8,128)(2,1)} %all-gather.6.cloned.1.call-done, bf16[2048,768]{0,1:T(8,128)(2,1)S(1)} %copy-done.38, bf16[2048,768]{0,1:T(8,128)(2,1)S(1)} %copy-done.36), kind=kOutput, calls=%fused_computation.24 | convolution fusion | flops 6448742400 | bytes 20971520 | tf_op jit(solution)/shard_map/dot_general | solution.py:23
  367.7 40.1 %reduce8.4 = f32[256,2048]{1,0:T(8,128)S(1)} custom-call(f32[1024,2048]{1,0:T(8,128)} %fusion.5.near_ref, bf16[1024,2048]{1,0:T(8,128)(2,1)} %convolution_convert_fusion.1.far_ref), custom_call_target="tpu_custom_call" | custom-call | tf_op jit(solution)/shard_map/reduce8/pallas_call | solution.py:236
  411.0 40.4 %gather8.7 = bf16[2048,2048]{1,0:T(8,128)(2,1)} custom-call(bf16[256,2048]{1,0:T(8,128)(2,1)} %fusion.45.own_ref), custom_call_target="tpu_custom_call" | custom-call | tf_op jit(solution)/shard_map/gather8/pallas_call | solution.py:140
  451.4 6.9 convolution_convert_fusion.7
  458.3 7.9 convolution_convert_fusion.4
  466.7 7.1 convolution_convert_fusion.8.grad_ref
  473.8 8.4 %fusion.50 = (bf16[1024,2048]{1,0:T(8,128)(2,1)}, f32[1024,2048]{1,0:T(8,128)}) fusion(bf16[1024,2048]{1,0:T(8,128)(2,1)} %collective-permute-done.1, bf16[2048,768]{1,0:T(8,128)(2,1)S(1)} %copy-done.33, bf16[2048,768]{0,1:T(8,128)(2,1)S(1)} %copy-done.14), kind=kOutput, calls=%fused_computation.138 | convolution fusion | flops 3227516928 | bytes 21495808 | tf_op jit(solution)/shard_map/dot_general | solution.py:23
  482.3 28.1 %attend_back.1 = (bf16[2048,512]{1,0:T(8,128)(2,1)}, f32[2,128]{1,0:T(2,128)}) custom-call(s32[2]{0:T(128)} %pad_add_fusion.1.meta_ref, f32[2048,512]{1,0:T(8,128)} %fusion.13.qkv_ref, bf16[2048,256]{1,0:T(8,128)(2,1)} %convolution_convert_fusion.8.grad_ref, s32[2,1024,1]{2,1,0:T(8,128)} %copy.38.segc_ref, s32[2,1,1024]{2,1,0:T(1,128)} %broadcast_in_dim.76.segr_ref, ...), custom_call_target="tpu_custom_call" | custom-call | flops 2684354560 | bytes 8388608 | tf_op jit(solution)/shard_map/attend_back/pallas_call | solution.py:606
  510.4 10.5 %convolution_convert_fusion.6 = bf16[2048,512]{1,0:T(8,128)(2,1)} fusion(bf16[2048,512]{1,0:T(8,128)(2,1)} %get-tuple-element.37, bf16[2048,2048]{1,0:T(8,128)(2,1)} %gather8.4, f32[2048]{0:T(1024)S(1)} %bitcast.155, f32[2048]{0:T(1024)S(1)} %copy-done.28), kind=kOutput, calls=%fused_computation.32 | convolution fusion | flops 4312793088 | bytes 12599296 | tf_op jit(solution)/shard_map/dot_general | solution.py:23
  529.7 6.9 fusion.24.near_ref
  540.8 47.0 %reduce8.5 = f32[256,2048]{1,0:T(8,128)S(1)} custom-call(f32[1024,2048]{1,0:T(8,128)} %fusion.24.near_ref, bf16[1024,2048]{1,0:T(8,128)(2,1)} %convolution_convert_fusion.2.far_ref), custom_call_target="tpu_custom_call" | custom-call | tf_op jit(solution)/shard_map/reduce8/pallas_call | solution.py:236
  591.0 19.6 %total.1 = f32[34,128]{1,0:T(8,128)} custom-call(f32[34,128]{1,0:T(8,128)} %maximum_bitcast_fusion.part_ref), custom_call_target="tpu_custom_call" | custom-call | tf_op jit(solution)/shard_map/total/pallas_call | solution.py:358
  638.2 7.0 collective-permute-done.14
  651.9 12.7 %collective-permute-done.15 = bf16[2,256,768]{2,1,0:T(8,128)(2,1)S(1)} collective-permute-done((bf16[2,256,768]{2,1,0:T(8,128)(2,1)S(1)}, bf16[2,256,768]{2,1,0:T(8,128)(2,1)S(1)}, u32[]{:S(2)}, u32[]{:S(2)}) %collective-permute-start.15) | collective-permute-done | bytes 786464 | tf_op jit(solution)/shard_map/ppermute | solution.py:33
  665.2 41.2 %reduce-scatter.9.cloned.1.call-done = bf16[512,1536]{1,0:T(8,128)(2,1)} async-done(((bf16[2048,1536]{1,0:T(8,128)(2,1)}), bf16[512,1536]{1,0:T(8,128)(2,1)}) %reduce-scatter.9.cloned.1.call-update) | async-done | bytes 1572880 | tf_op jit(solution)/shard_map/reduce_scatter | solution.py:51
  714.7 18.3 %collective-permute-done.8 = bf16[256,512]{1,0:T(8,128)(2,1)S(1)} collective-permute-done((bf16[256,512]{1,0:T(8,128)(2,1)S(1)}, bf16[256,512]{1,0:T(8,128)(2,1)S(1)}, u32[]{:S(2)}, u32[]{:S(2)}) %collective-permute-start.8) | collective-permute-done | bytes 262176 | tf_op jit(solution)/shard_map/ppermute | solution.py:38
  735.8 12.2 %collective-permute-done.9 = bf16[2,256,512]{2,1,0:T(8,128)(2,1)S(1)} collective-permute-done((bf16[2,256,512]{2,1,0:T(8,128)(2,1)S(1)}, bf16[2,256,512]{2,1,0:T(8,128)(2,1)S(1)}, u32[]{:S(2)}, u32[]{:S(2)}) %collective-permute-start.9) | collective-permute-done | bytes 524320 | tf_op jit(solution)/shard_map/ppermute | solution.py:33
  752.9 26.9 %collective-permute-done.13 = bf16[2,256,1536]{2,1,0:T(8,128)(2,1)S(1)} collective-permute-done((bf16[2,256,1536]{2,1,0:T(8,128)(2,1)S(1)}, bf16[2,256,1536]{2,1,0:T(8,128)(2,1)S(1)}, u32[]{:S(2)}, u32[]{:S(2)}) %collective-permute-start.13) | collective-permute-done | bytes 1572896 | tf_op jit(solution)/shard_map/ppermute | solution.py:33
  (217 shorter events, 119.7 us)
Async XLA Ops:
  7.2 144.2 %all-gather.4.cloned.1.call-start = ((), (), s32[]{:S(2)}) async-start(), calls=%async_computation.4 | async-start | bytes 4587520 | tf_op jit(solution)/shard_map/all_gather | solution.py:47
  26.3 29.4 %copy-start.17 = (bf16[1,512,2048]{2,1,0:T(8,128)(2,1)S(1)}, bf16[1,512,2048]{2,1,0:T(8,128)(2,1)}, u32[]{:S(2)}) copy-start(bf16[1,512,2048]{2,1,0:T(8,128)(2,1)} %param.14) | copy-start | bytes 6291460
  26.3 248.5 %all-gather.6.cloned.1.call-start = ((), (), s32[]{:S(2)}) async-start(), calls=%async_computation.5 | async-start | bytes 7864320 | tf_op jit(solution)/shard_map/all_gather | solution.py:47
  54.0 255.4 %all-gather.8.cloned.1.call-start = ((), (), s32[]{:S(2)}) async-start(), calls=%async_computation.6 | async-start | bytes 3932160 | tf_op jit(solution)/shard_map/all_gather | solution.py:47
  54.1 95.4 %collective-permute-start = (s32[1,1024]{1,0:T(1,128)S(1)}, s32[1,1024]{1,0:T(1,128)S(1)}, u32[]{:S(2)}, u32[]{:S(2)}) collective-permute-start(s32[1,1024]{1,0:T(1,128)S(1)} %copy-done.31), channel_id=1, source_target_pairs={{0,4},{4,0},{8,12},{12,8},{16,20},{20,16},{24,28},{28,24},{1,5},{5... | collective-permute-start | bytes 12296 | tf_op jit(solution)/shard_map/ppermute | solution.py:38
  55.6 466.7 %reduce-scatter.7.cloned.1.call-start = ((), (), s32[]{:S(2)}) async-start(), calls=%async_computation.8 | async-start | bytes 1310720 | tf_op jit(solution)/shard_map/reduce_scatter | solution.py:51
  103.5 50.1 %copy-start.27 = (f32[2048]{0:T(1024)}, f32[2048]{0:T(1024)S(1)}, u32[]{:S(2)}) copy-start(f32[2048]{0:T(1024)S(1)} %add_rsqrt_fusion) | copy-start | bytes 24580
  191.4 40.1 %copy-start.5 = (bf16[256,2048]{1,0:T(8,128)(2,1)S(1)}, bf16[256,2048]{1,0:T(8,128)(2,1)}, u32[]{:S(2)}) copy-start(bf16[256,2048]{1,0:T(8,128)(2,1)} %get-tuple-element.31.own_ref) | copy-start | bytes 3145732
  231.8 177.2 %copy-start.21 = (f32[256]{0:T(256)}, f32[256]{0:T(256)S(1)}, u32[]{:S(2)}) copy-start(f32[256]{0:T(256)S(1)} %add_rsqrt_fusion.2) | copy-start | bytes 3076
  367.7 40.1 %copy-start.3 = (f32[256,2048]{1,0:T(8,128)S(1)}, f32[256,2048]{1,0:T(8,128)}, u32[]{:S(2)}) copy-start(f32[256,2048]{1,0:T(8,128)} %copy-done.2) | copy-start | bytes 6291460
  458.3 174.1 %reduce-scatter.11.cloned.1.call-start = ((), (), s32[]{:S(2)}) async-start(), calls=%async_computation.10 | async-start | bytes 3932160 | tf_op jit(solution)/shard_map/reduce_scatter | solution.py:51
  466.2 7.6 collective-permute-start.1
  466.6 198.5 %reduce-scatter.5.cloned.1.call-start = ((), (), s32[]{:S(2)}) async-start(), calls=%async_computation.7 | async-start | bytes 2621440 | tf_op jit(solution)/shard_map/reduce_scatter | solution.py:51
  482.3 28.2 %copy-start.28 = (f32[2048]{0:T(1024)S(1)}, f32[2048]{0:T(1024)}, u32[]{:S(2)}) copy-start(f32[2048]{0:T(1024)} %copy-done.27) | copy-start | bytes 24580
  521.0 185.4 %reduce-scatter.9.cloned.1.call-start = ((), (), s32[]{:S(2)}) async-start(), calls=%async_computation.9 | async-start | bytes 7864320 | tf_op jit(solution)/shard_map/reduce_scatter | solution.py:51
  523.5 88.5 %collective-permute-start.10 = (bf16[256,256]{1,0:T(8,128)(2,1)S(1)}, bf16[256,256]{1,0:T(8,128)(2,1)S(1)}, u32[]{:S(2)}, u32[]{:S(2)}) collective-permute-start(bf16[256,256]{1,0:T(8,128)(2,1)S(1)} %get-tuple-element.74), channel_id=1, source_target_pairs={{0,4},{4,0},{8,12},{12,8},{16,20},{20,16},{24,28},{28,24},{1,5},{5... | collective-permute-start | bytes 393224 | tf_op jit(solution)/shard_map/ppermute | solution.py:38
  527.6 84.4 %collective-permute-start.4 = (bf16[256,2048]{1,0:T(8,128)(2,1)}, bf16[256,2048]{1,0:T(8,128)(2,1)}, u32[]{:S(2)}, u32[]{:S(2)}) collective-permute-start(bf16[256,2048]{1,0:T(8,128)(2,1)} %get-tuple-element.58), channel_id=1, source_target_pairs={{0,4},{4,0},{8,12},{12,8},{16,20},{20,16},{24,28},{28,24},{1,5},{5... | collective-permute-start | bytes 3145736 | tf_op jit(solution)/shard_map/ppermute | solution.py:38
  528.7 83.4 %collective-permute-start.2 = (bf16[256,2048]{1,0:T(8,128)(2,1)}, bf16[256,2048]{1,0:T(8,128)(2,1)}, u32[]{:S(2)}, u32[]{:S(2)}) collective-permute-start(bf16[256,2048]{1,0:T(8,128)(2,1)} %get-tuple-element.57), channel_id=1, source_target_pairs={{0,2},{2,0},{1,3},{3,1},{4,6},{6,4},{5,7},{7,5},{8,10},{10,8},{9,1... | collective-permute-start | bytes 3145736 | tf_op jit(solution)/shard_map/ppermute | solution.py:33
  540.8 48.3 %copy-start.6 = (bf16[256,2048]{1,0:T(8,128)(2,1)S(1)}, bf16[256,2048]{1,0:T(8,128)(2,1)}, u32[]{:S(2)}) copy-start(bf16[256,2048]{1,0:T(8,128)(2,1)} %get-tuple-element.31.own_ref) | copy-start | bytes 3145732
  540.8 48.3 %copy-start.25 = (f32[256]{0:T(256)S(1)}, f32[256]{0:T(256)}, u32[]{:S(2)}) copy-start(f32[256]{0:T(256)} %add_rsqrt_fusion.1) | copy-start | bytes 3076
  615.7 9.3 %collective-permute-start.3 = (bf16[128,2048]{1,0:T(8,128)(2,1)S(1)}, bf16[128,2048]{1,0:T(8,128)(2,1)S(1)}, u32[]{:S(2)}, u32[]{:S(2)}) collective-permute-start(bf16[128,2048]{1,0:T(8,128)(2,1)S(1)} %slice.216), channel_id=1, source_target_pairs={{0,4},{4,0},{8,12},{12,8},{16,20},{20,16},{24,28},{28,24},{1,5},{5... | collective-permute-start | bytes 1572872 | tf_op jit(solution)/shard_map/ppermute | solution.py:38
  617.2 6.9 collective-permute-start.11
  620.1 9.6 %collective-permute-start.5 = (bf16[128,2048]{1,0:T(8,128)(2,1)S(1)}, bf16[128,2048]{1,0:T(8,128)(2,1)S(1)}, u32[]{:S(2)}, u32[]{:S(2)}) collective-permute-start(bf16[128,2048]{1,0:T(8,128)(2,1)S(1)} %slice.215), channel_id=1, source_target_pairs={{0,2},{2,0},{1,3},{3,1},{4,6},{6,4},{5,7},{7,5},{8,10},{10,8},{9,1... | collective-permute-start | bytes 1572872 | tf_op jit(solution)/shard_map/ppermute | solution.py:33
  632.4 14.1 %collective-permute-start.7 = (bf16[256,2048]{1,0:T(8,128)(2,1)}, bf16[256,2048]{1,0:T(8,128)(2,1)S(1)}, u32[]{:S(2)}, u32[]{:S(2)}) collective-permute-start(bf16[256,2048]{1,0:T(8,128)(2,1)} %get-tuple-element.61), channel_id=1, source_target_pairs={{0,1},{1,0},{2,3},{3,2},{4,5},{5,4},{6,7},{7,6},{8,9},{9,8},{10,11... | collective-permute-start | bytes 3145736 | tf_op jit(solution)/shard_map/ppermute | solution.py:29
  633.6 11.6 %collective-permute-start.14 = (bf16[256,768]{1,0:T(8,128)(2,1)S(1)}, bf16[256,768]{1,0:T(8,128)(2,1)S(1)}, u32[]{:S(2)}, u32[]{:S(2)}) collective-permute-start(bf16[256,768]{1,0:T(8,128)(2,1)S(1)} %get-tuple-element.70), channel_id=1, source_target_pairs={{0,4},{4,0},{8,12},{12,8},{16,20},{20,16},{24,28},{28,24},{1,5},{5... | collective-permute-start | bytes 1179656 | tf_op jit(solution)/shard_map/ppermute | solution.py:38
  637.9 12.0 %collective-permute-start.6 = (bf16[256,2048]{1,0:T(8,128)(2,1)S(1)}, bf16[256,2048]{1,0:T(8,128)(2,1)S(1)}, u32[]{:S(2)}, u32[]{:S(2)}) collective-permute-start(bf16[256,2048]{1,0:T(8,128)(2,1)S(1)} %copy-done.12), channel_id=1, source_target_pairs={{0,1},{1,0},{2,3},{3,2},{4,5},{5,4},{6,7},{7,6},{8,9},{9,8},{10,11... | collective-permute-start | bytes 3145736 | tf_op jit(solution)/shard_map/ppermute | solution.py:29
  645.4 19.3 %collective-permute-start.15 = (bf16[2,256,768]{2,1,0:T(8,128)(2,1)S(1)}, bf16[2,256,768]{2,1,0:T(8,128)(2,1)S(1)}, u32[]{:S(2)}, u32[]{:S(2)}) collective-permute-start(bf16[2,256,768]{2,1,0:T(8,128)(2,1)S(1)} %reverse_select_fusion.6), channel_id=1, source_target_pairs={{0,2},{2,0},{1,3},{3,1},{4,6},{6,4},{5,7},{7,5},{8,10},{10,8},{9,1... | collective-permute-start | bytes 2359304 | tf_op jit(solution)/shard_map/ppermute | solution.py:33
  665.1 44.1 %copy-start.16 = (bf16[512,512]{1,0:T(8,128)(2,1)S(1)}, bf16[512,512]{1,0:T(8,128)(2,1)}, u32[]{:S(2)}) copy-start(bf16[512,512]{1,0:T(8,128)(2,1)} %reduce-scatter.5.cloned.1.call-done) | copy-start | bytes 1572868
  707.8 26.5 %collective-permute-start.12 = (bf16[256,1536]{1,0:T(8,128)(2,1)S(1)}, bf16[256,1536]{1,0:T(8,128)(2,1)S(1)}, u32[]{:S(2)}, u32[]{:S(2)}) collective-permute-start(bf16[256,1536]{1,0:T(8,128)(2,1)S(1)} %get-tuple-element.64), channel_id=1, source_target_pairs={{0,4},{4,0},{8,12},{12,8},{16,20},{20,16},{24,28},{28,24},{1,5},{5... | collective-permute-start | bytes 2359304 | tf_op jit(solution)/shard_map/ppermute | solution.py:38
  709.2 23.7 %collective-permute-start.8 = (bf16[256,512]{1,0:T(8,128)(2,1)S(1)}, bf16[256,512]{1,0:T(8,128)(2,1)S(1)}, u32[]{:S(2)}, u32[]{:S(2)}) collective-permute-start(bf16[256,512]{1,0:T(8,128)(2,1)S(1)} %get-tuple-element.72), channel_id=1, source_target_pairs={{0,4},{4,0},{8,12},{12,8},{16,20},{20,16},{24,28},{28,24},{1,5},{5... | collective-permute-start | bytes 786440 | tf_op jit(solution)/shard_map/ppermute | solution.py:38
  733.1 14.9 %collective-permute-start.9 = (bf16[2,256,512]{2,1,0:T(8,128)(2,1)S(1)}, bf16[2,256,512]{2,1,0:T(8,128)(2,1)S(1)}, u32[]{:S(2)}, u32[]{:S(2)}) collective-permute-start(bf16[2,256,512]{2,1,0:T(8,128)(2,1)S(1)} %reverse_select_fusion.8), channel_id=1, source_target_pairs={{0,2},{2,0},{1,3},{3,1},{4,6},{6,4},{5,7},{7,5},{8,10},{10,8},{9,1... | collective-permute-start | bytes 1572872 | tf_op jit(solution)/shard_map/ppermute | solution.py:33
  734.8 45.1 %collective-permute-start.13 = (bf16[2,256,1536]{2,1,0:T(8,128)(2,1)S(1)}, bf16[2,256,1536]{2,1,0:T(8,128)(2,1)S(1)}, u32[]{:S(2)}, u32[]{:S(2)}) collective-permute-start(bf16[2,256,1536]{2,1,0:T(8,128)(2,1)S(1)} %reverse_select_fusion.4), channel_id=1, source_target_pairs={{0,2},{2,0},{1,3},{3,1},{4,6},{6,4},{5,7},{7,5},{8,10},{10,8},{9,1... | collective-permute-start | bytes 4718600 | tf_op jit(solution)/shard_map/ppermute | solution.py:33
  (30 other events, 206.3 us)
Sparse Core Ops, SparseCore 0:
  26.4 73.5 all-gather.3
  101.6 113.8 all-gather.5
  217.1 61.6 all-gather.7
  458.4 27.6 reduce-scatter.6
  488.3 58.9 reduce-scatter.10
  550.0 43.5 reduce-scatter.4
  595.8 110.5 reduce-scatter.8
where the time goes:
time: 806 us; the launch traced here: 797 us
  Pallas kernels  396 us (49%)
  matrix products  157 us (19%)
  waiting for transfers between devices  127 us (16%)
  local copies, waits for them, and re-layouts  46.4 us (6%)
  other arithmetic  40.3 us (5%)
  starting transfers between devices  15.6 us (2%)
  between operations  15.4 us (2%)
    pallas_call x4, Pallas kernels, gather8(): pl.pallas_call(functools.partial(gather8_kernel, rows), out_shape=jax.Sha...  163 us
    dot_general x16, matrix products, mm(): lax.dot_general(left, right, (((left_dim,), (right_dim,)), ((), ())), pre...  157 us
    pallas_call x3, Pallas kernels, reduce8(): pl.pallas_call(functools.partial(reduce8_kernel, rows), out_shape=jax.Sha...  127 us
    ppermute x6, waiting for transfers between devices, swap_ctx(): return lax.ppermute(value, 'ctx', [(0, 1), (1, 0)])  59.8 us
    pallas_call x2, Pallas kernels, shards(): pl.pallas_call(functools.partial(shard_kernel, tuple(plan), len(groups)),...  41.6 us
    reduce_scatter x4, waiting for transfers between devices, scatter_line(): lax.psum_scatter(value, 'fsdp', scatter_dimension=0, tiled=True, axis_ind...  41.2 us
    pallas_call x1, Pallas kernels, attend_back(): pl.pallas_call(functools.partial(attend_back_kernel, heads, tile), out_sh...  28.1 us
    unnamed x91, local copies, waits for them, and re-layouts  26.8 us
  transfers between devices with their start and end apart: 23, of which 8 were waited for; matrix products, arithmetic and copies ran while one was open for 19% of the time, Pallas kernels for 38%

commit v1 on v0

--- a/solution.py
+++ b/solution.py
@@ -371,6 +371,40 @@
     )(part)
 
 
+def join_kernel(sizes, spot_ref, kept_ref, x_ref, y_ref, both_ref, *out_refs):
+    place, odd = spot_ref[0], spot_ref[1]
+    parts = (
+        (kept_ref, 2 * place + odd),
+        (x_ref, 2 * place + 1 - odd),
+        (y_ref, 2 - 2 * place + odd),
+        (both_ref, 3 - 2 * place - odd),
+    )
+    for part, column in parts:
+        start = 0
+        for size, out_ref in zip(sizes, out_refs):
+            target = pl.ds(pl.multiple_of(column * size, HEAD), size)
+            out_ref[:, target] = part[:, start : start + size].astype(F32)
+            start += size
+
+
+def join_columns(spot, parts, sizes):
+    rows = parts[0].shape[0]
+    tile = min(rows, 64)
+    return pl.pallas_call(
+        functools.partial(join_kernel, sizes),
+        out_shape=[jax.ShapeDtypeStruct((rows, 4 * size), F32) for size in sizes],
+        grid_spec=pltpu.PrefetchScalarGridSpec(
+            num_scalar_prefetch=1,
+            grid=(rows // tile,),
+            in_specs=[
+                pl.BlockSpec((tile, part.shape[1]), lambda i, spot: (i, 0)) for part in parts
+            ],
+            out_specs=[pl.BlockSpec((tile, 4 * size), lambda i, spot: (i, 0)) for size in sizes],
+        ),
+        name="join",
+    )(spot, *parts)
+
+
 def after(value, *others):
     return lax.optimization_barrier((value,) + others)[0]
 
@@ -717,18 +751,37 @@
     head_gains = gain_cols.reshape(count, block, HEAD)[:, :small, 2:4].reshape(HEAD, 2).T
 
     in_f = tok.astype(F32)
-    inverse_all = inv_rms(in_f)
-    cot = gather8(after(own_cot, inverse_all))
-    x_all = (in_f * inverse_all * in_gain).astype(BF16)
+    cot_from = after(own_cot, tok)
+    cot_x, cot_y = swap_x(cot_from), swap_ctx(cot_from)
+    x_all = (in_f * inv_rms(in_f) * in_gain).astype(BF16)
     qkv = mm(x_all, qkv_w, 1, 0)
     attended = attend(meta, qkv, seg_cols, seg_rows, cosine, sine, head_gains)
     half = 4 * quarter
-    middle = own_tok.astype(F32) + reduce8(
-        mm(attended[:half], out_w, 1, 1), mm(attended[half:], out_w, 1, 1).astype(BF16)
-    )
+    cot_x, cot_y = after(cot_x, attended), after(cot_y, attended)
+    eighth = quarter // 2
+    cot_first, cot_second = swap_ctx(cot_x[:eighth]), swap_x(cot_y[eighth:])
+    out_far = mm(attended[half:], out_w, 1, 1).astype(BF16)
+    out_near = mm(attended[:half], out_w, 1, 1)
+    cot_first = after(cot_first, out_near, out_far)
+    cot_second = after(cot_second, out_near, out_far)
+    cot_side = jnp.concatenate(
+        [
+            cot_from[:eighth],
+            cot_x[:eighth],
+            cot_y[:eighth],
+            cot_first,
+            cot_from[eighth:],
+            cot_y[eighth:],
+            cot_x[eighth:],
+            cot_second,
+        ]
+    )
+    cot_far = swap_core(cot_side)
+    middle = own_tok.astype(F32) + reduce8(out_near, out_far)
     inverse_mid = inv_rms(middle)
     scaled_mid = middle * inverse_mid
     y_all = gather8((scaled_mid * mid_gain).astype(BF16))
+    cot = jnp.concatenate([cot_side, after(cot_far, y_all)])
 
     ff = gate_up_w.shape[1] // 2
     gate_up = mm(y_all, gate_up_w, 1, 0)
@@ -763,34 +816,29 @@
     raw_grads, head_gain_parts = attend_back(
         meta, qkv, after(grad_att, mlp_rows), seg_cols, seg_rows, cosine, sine, head_gains
     )
-    first_grad = mm(x_all, raw_grads, 0, 0).astype(BF16)
+    first_grad = jnp.concatenate([mm(x_all, raw_grads, 0, 0).astype(BF16), out_grad], axis=1)
     mlp = reduce4_links(mlp_rows, raw_grads)
     layer_out = finish_rows((middle + mlp).astype(BF16))
     in_near = mm(raw_grads[:half], qkv_w, 1, 1)
     in_far = mm(raw_grads[half:], qkv_w, 1, 1).astype(BF16)
     in_grad = reduce8(in_near, after(in_far, first_grad))
 
+    spot = jnp.stack([place, odd]).astype(jnp.int32)
+
     def owners(grad, sizes, *others):
         rows = scatter_line(grad)
-        rows = after(rows, *others).reshape(2, block, grad.shape[1])
-        kept = lax.dynamic_index_in_dim(rows, odd, 0, keepdims=False)
-        sent = lax.dynamic_index_in_dim(rows, 1 - odd, 0, keepdims=False)
-        came = swap_x(sent)
-        pair = flip_if(odd == 1, jnp.stack([kept, came]), 0)
-        far = swap_ctx(pair)
-        four = flip_if(place == 1, jnp.stack([pair, far]), 0)
-        four = four.reshape(4, block, grad.shape[1])
-        shares, start = [], 0
-        for size in sizes:
-            piece = four[:, :, start : start + size]
-            shares.append(jnp.moveaxis(piece, 0, 1).reshape(block, 4 * size).astype(F32))
-            start += size
-        return shares
-
-    (down_share,) = owners(down_grad, (ff,), grad_attn)
-    gate_share, up_share = owners(gate_up_grad, (ff, ff), raw_grads)
-    (out_share,) = owners(out_grad, (out_grad.shape[1],), raw_grads)
-    query_share, key_share, value_share = owners(first_grad, (heads_q * HEAD, HEAD, HEAD))
+        rows = after(rows, *others)
+        kept = lax.dynamic_slice_in_dim(rows, odd * block, block, 0)
+        sent = lax.dynamic_slice_in_dim(rows, (1 - odd) * block, block, 0)
+        by_x, by_y = swap_x(sent), swap_ctx(kept)
+        by_both = swap_ctx(by_x)
+        return join_columns(spot, (kept, by_x, by_y, by_both), sizes)
+
+    (down_share,) = owners(down_grad, (ff,))
+    gate_share, up_share = owners(gate_up_grad, (ff, ff))
+    query_share, key_share, value_share, out_share = owners(
+        first_grad, (heads_q * HEAD, HEAD, HEAD, heads_q * HEAD)
+    )
 
     own_in = own_tok.astype(F32)
     inverse_in = inv_rms(own_in)

time: 806 us -> 728 us (0.903)
  Pallas kernels: 396 us -> 363 us
  waiting for transfers between devices: 127 us -> 99.8 us
  matrix products: 157 us -> 145 us
    reduce_scatter x4 -> x3, waiting for transfers between devices: 41.2 us -> 0.02 us  [scatter_line(): lax.psum_scatter(value, 'fsdp', scatter_dimension=0, tiled=True, axis_ind...]
    pallas_call x4 -> x3, Pallas kernels: 163 us -> 122 us  [gather8(): pl.pallas_call(functools.partial(gather8_kernel, rows), out_shape=jax.Sha...]
    ppermute x7 -> x8, waiting for transfers between devices: 25.3 us -> 57.9 us  [swap_x(): return lax.ppermute(value, 'fsdp', [(i, i ^ 1) for i in range(count)])]
    ppermute x6 -> x10, waiting for transfers between devices: 59.8 us -> 41.8 us  [swap_ctx(): return lax.ppermute(value, 'ctx', [(0, 1), (1, 0)])]
    pallas_call x0 -> x3, Pallas kernels: none -> 15.1 us  [join_columns(): pl.pallas_call(functools.partial(join_kernel, sizes), out_shape=[jax.Shap...]
    dot_general x16, matrix products: 157 us -> 145 us  [mm(): lax.dot_general(left, right, (((left_dim,), (right_dim,)), ((), ())), pre...]
    unnamed x91 -> x83, local copies, waits for them, and re-layouts: 26.8 us -> 19.2 us
  transfers between devices with their start and end apart: 23 -> 28, of which waited for: 8 -> 9; matrix products, arithmetic and copies ran while one was open for 19% -> 28% of each run, Pallas kernels for 38% -> 48%
where the time goes in v1:
time: 728 us; the launch traced here: 719 us
  Pallas kernels  363 us (50%)
  matrix products  145 us (20%)
  waiting for transfers between devices  99.8 us (14%)
  local copies, waits for them, and re-layouts  42.8 us (6%)
  other arithmetic  33.9 us (5%)
  starting transfers between devices  19.4 us (3%)
  between operations  15.2 us (2%)
    dot_general x16, matrix products, mm(): lax.dot_general(left, right, (((left_dim,), (right_dim,)), ((), ())), pre...  145 us
    pallas_call x3, Pallas kernels, gather8(): pl.pallas_call(functools.partial(gather8_kernel, rows), out_shape=jax.Sha...  122 us
    pallas_call x3, Pallas kernels, reduce8(): pl.pallas_call(functools.partial(reduce8_kernel, rows), out_shape=jax.Sha...  121 us
    ppermute x8, waiting for transfers between devices, swap_x(): return lax.ppermute(value, 'fsdp', [(i, i ^ 1) for i in range(count)])  57.9 us
    ppermute x10, waiting for transfers between devices, swap_ctx(): return lax.ppermute(value, 'ctx', [(0, 1), (1, 0)])  41.8 us
    pallas_call x2, Pallas kernels, shards(): pl.pallas_call(functools.partial(shard_kernel, tuple(plan), len(groups)),...  41.6 us
    pallas_call x1, Pallas kernels, attend_back(): pl.pallas_call(functools.partial(attend_back_kernel, heads, tile), out_sh...  28.3 us
    unnamed x83, local copies, waits for them, and re-layouts  19.2 us
  transfers between devices with their start and end apart: 28, of which 9 were waited for; matrix products, arithmetic and copies ran while one was open for 28% of the time, Pallas kernels for 48%

profile of v1, /device:TPU:0, one launch (start us, length us, event | category | flops | bytes accessed | tf_op | source)
XLA Modules:
  0.0 719.0 jit_solution(16651261685861543752)
XLA Ops:
  10.1 14.0 %shards.2 = bf16[2,256,896]{2,1,0:T(8,128)(2,1)} custom-call(bf16[256,1024]{1,0:T(8,128)(2,1)} %refs_0_.1, bf16[256,512]{1,0:T(8,128)(2,1)} %refs_1_.2, bf16[256,512]{1,0:T(8,128)(2,1)} %refs_2_.2, bf16[256,1024]{1,0:T(8,128)(2,1)} %refs_3_.1, bf16[256,128]{1,0:T(8,128)(2,1)} %select_select_fusion.refs_4_), custom_call_target="tpu_custom_call" | custom-call | tf_op jit(solution)/shard_map/shards/pallas_call | solution.py:309
  26.4 27.6 %shards.3 = (bf16[2,256,1536]{2,1,0:T(8,128)(2,1)}, bf16[2,256,768]{2,1,0:T(8,128)(2,1)}) custom-call(bf16[256,3072]{1,0:T(8,128)(2,1)} %refs_0_.2, bf16[256,3072]{1,0:T(8,128)(2,1)} %refs_1_.3, bf16[256,3072]{1,0:T(8,128)(2,1)} %refs_2_.3), custom_call_target="tpu_custom_call" | custom-call | tf_op jit(solution)/shard_map/shards/pallas_call | solution.py:309
  55.8 40.9 %gather8.3 = bf16[2048,2048]{1,0:T(8,128)(2,1)} custom-call(bf16[256,2048]{1,0:T(8,128)(2,1)} %get-tuple-element.40.own_ref), custom_call_target="tpu_custom_call" | custom-call | tf_op jit(solution)/shard_map/gather8/pallas_call | solution.py:140
  109.6 12.9 %collective-permute-done = s32[1,1024]{1,0:T(1,128)S(1)} collective-permute-done((s32[1,1024]{1,0:T(1,128)S(1)}, s32[1,1024]{1,0:T(1,128)S(1)}, u32[]{:S(2)}, u32[]{:S(2)}) %collective-permute-start) | collective-permute-done | bytes 4128 | tf_op jit(solution)/shard_map/ppermute | solution.py:38
  126.6 10.6 %fusion.13.qkv_ref = f32[2048,512]{1,0:T(8,128)} fusion(bf16[2048,2048]{1,0:T(8,128)(2,1)} %gather8.3, f32[2048]{0:T(1024)S(1)} %bitcast.66, f32[2048]{0:T(1024)S(1)} %add_rsqrt_fusion, bf16[2048,896]{0,1:T(8,128)(2,1)} %all-gather.4.cloned.1.call-done), kind=kOutput, calls=%fused_computation.37 | convolution fusion | flops 4311744512 | bytes 14696448 | tf_op jit(solution)/shard_map/dot_general | solution.py:23
  137.2 16.3 %attend.1 = bf16[2048,256]{1,0:T(8,128)(2,1)} custom-call(s32[2]{0:T(128)} %pad_add_fusion.1.meta_ref, f32[2048,512]{1,0:T(8,128)} %fusion.13.qkv_ref, s32[2,1024,1]{2,1,0:T(8,128)} %copy.33.segc_ref, s32[2,1,1024]{2,1,0:T(1,128)} %broadcast_in_dim.76.segr_ref, f32[1024,128]{1,0:T(8,128)} %get-tuple-element.110.cos_ref, ...), custom_call_target="tpu_custom_call" | custom-call | flops 1073741824 | bytes 5242880 | tf_op jit(solution)/shard_map/attend/pallas_call | solution.py:612
  159.9 5.8 fusion.36.near_ref
  165.7 39.5 %reduce8.3 = f32[256,2048]{1,0:T(8,128)S(1)} custom-call(f32[1024,2048]{1,0:T(8,128)} %fusion.36.near_ref, bf16[1024,2048]{1,0:T(8,128)(2,1)} %convolution_convert_fusion.3.far_ref), custom_call_target="tpu_custom_call" | custom-call | tf_op jit(solution)/shard_map/reduce8/pallas_call | solution.py:236
  211.3 13.6 %collective-permute-done.4 = bf16[128,2048]{1,0:T(8,128)(2,1)S(1)} collective-permute-done((bf16[128,2048]{1,0:T(8,128)(2,1)S(1)}, bf16[128,2048]{1,0:T(8,128)(2,1)S(1)}, u32[]{:S(2)}, u32[]{:S(2)}) %collective-permute-start.4) | collective-permute-done | bytes 524320 | tf_op jit(solution)/shard_map/ppermute | solution.py:38
  230.4 41.0 %gather8.4 = bf16[2048,2048]{1,0:T(8,128)(2,1)} custom-call(bf16[256,2048]{1,0:T(8,128)(2,1)} %multiply_convert_fusion.3.own_ref), custom_call_target="tpu_custom_call" | custom-call | tf_op jit(solution)/shard_map/gather8/pallas_call | solution.py:140
  271.5 18.1 %fusion.51 = f32[2048,1536]{0,1:T(8,128)S(1)} fusion(bf16[2048,2048]{1,0:T(8,128)(2,1)} %gather8.4, bf16[2048,1536]{1,0:T(8,128)(2,1)} %all-gather.6.cloned.1.call-done), kind=kOutput, calls=%fused_computation.131 | convolution fusion | flops 12884901888 | bytes 27262976 | tf_op jit(solution)/shard_map/dot_general | solution.py:23
  294.2 6.0 constant_dynamic-update-slice_fusion.4
  300.2 10.4 %convolution_convert_fusion.5 = bf16[2048,768]{1,0:T(8,128)(2,1)} fusion(bf16[2048,2048]{1,0:T(8,128)(2,1)} %constant_dynamic-update-slice_fusion.4, bf16[2048,768]{0,1:T(8,128)(2,1)S(1)} %multiply_convert_fusion.2), kind=kOutput, calls=%fused_computation.21 | convolution fusion | flops 6444023808 | bytes 14680064 | tf_op jit(solution)/shard_map/dot_general | solution.py:23
  310.7 15.3 %multiply_convert_fusion = (bf16[2048,768]{0,1:T(8,128)(2,1)S(1)}, bf16[2048,768]{0,1:T(8,128)(2,1)S(1)}) fusion(f32[2048,1536]{0,1:T(8,128)} %copy-done.5, bf16[2048,2048]{1,0:T(8,128)(2,1)} %constant_dynamic-update-slice_fusion.4, bf16[2048,768]{1,0:T(8,128)(2,1)} %all-gather.8.cloned.1.call-done), kind=kOutput, calls=%fused_computation.12 | convolution fusion | flops 6462898176 | bytes 30408704 | tf_op jit(solution)/shard_map/dot_general | solution.py:23
  327.7 17.4 %convolution_convert_fusion = bf16[2048,1536]{1,0:T(8,128)(2,1)} fusion(bf16[2048,2048]{1,0:T(8,128)(2,1)} %gather8.4, bf16[2048,768]{0,1:T(8,128)(2,1)S(1)} %get-tuple-element.71, bf16[2048,768]{0,1:T(8,128)(2,1)S(1)} %get-tuple-element.72), kind=kOutput, calls=%fused_computation.11 | convolution fusion | flops 12900630528 | bytes 20971520 | tf_op jit(solution)/shard_map/dot_general | solution.py:23
  345.1 11.1 %convolution_convert_fusion.1.far_ref = bf16[1024,2048]{1,0:T(8,128)(2,1)} fusion(bf16[2048,1536]{1,0:T(8,128)(2,1)} %all-gather.6.cloned.1.call-done, bf16[2048,768]{0,1:T(8,128)(2,1)} %copy-done.31, bf16[2048,768]{0,1:T(8,128)(2,1)S(1)} %get-tuple-element.71), kind=kOutput, calls=%fused_computation.17 | convolution fusion | flops 6450839552 | bytes 16777216 | tf_op jit(solution)/shard_map/dot_general | solution.py:23
  356.2 11.2 %fusion.5.near_ref = f32[1024,2048]{1,0:T(8,128)} fusion(bf16[2048,1536]{1,0:T(8,128)(2,1)} %all-gather.6.cloned.1.call-done, bf16[2048,768]{0,1:T(8,128)(2,1)S(1)} %copy-done.32, bf16[2048,768]{0,1:T(8,128)(2,1)S(1)} %get-tuple-element.71), kind=kOutput, calls=%fused_computation.23 | convolution fusion | flops 6448742400 | bytes 20971520 | tf_op jit(solution)/shard_map/dot_general | solution.py:23
  367.5 40.1 %reduce8.4 = f32[256,2048]{1,0:T(8,128)S(1)} custom-call(f32[1024,2048]{1,0:T(8,128)} %fusion.5.near_ref, bf16[1024,2048]{1,0:T(8,128)(2,1)} %convolution_convert_fusion.1.far_ref), custom_call_target="tpu_custom_call" | custom-call | tf_op jit(solution)/shard_map/reduce8/pallas_call | solution.py:236
  410.8 40.5 %gather8.5 = bf16[2048,2048]{1,0:T(8,128)(2,1)} custom-call(bf16[256,2048]{1,0:T(8,128)(2,1)} %fusion.45.own_ref), custom_call_target="tpu_custom_call" | custom-call | tf_op jit(solution)/shard_map/gather8/pallas_call | solution.py:140
  451.3 6.0 convolution_convert_fusion.4
  465.3 6.6 fusion.50
  471.8 28.3 %attend_back.1 = (bf16[2048,512]{1,0:T(8,128)(2,1)}, f32[2,128]{1,0:T(2,128)}) custom-call(s32[2]{0:T(128)} %pad_add_fusion.1.meta_ref, f32[2048,512]{1,0:T(8,128)} %fusion.13.qkv_ref, bf16[2048,256]{1,0:T(8,128)(2,1)} %convolution_convert_fusion.8.grad_ref, s32[2,1024,1]{2,1,0:T(8,128)} %copy.33.segc_ref, s32[2,1,1024]{2,1,0:T(1,128)} %broadcast_in_dim.76.segr_ref, ...), custom_call_target="tpu_custom_call" | custom-call | flops 2684354560 | bytes 8388608 | tf_op jit(solution)/shard_map/attend_back/pallas_call | solution.py:640
  500.2 9.2 %convolution_convert_fusion.6 = bf16[2048,512]{1,0:T(8,128)(2,1)S(1)} fusion(bf16[2048,512]{1,0:T(8,128)(2,1)} %get-tuple-element.52, bf16[2048,2048]{1,0:T(8,128)(2,1)} %gather8.3, f32[2048]{0:T(1024)S(1)} %bitcast.67, f32[2048]{0:T(1024)S(1)} %copy-done.26), kind=kOutput, calls=%fused_computation.31 | convolution fusion | flops 4312793088 | bytes 12599296 | tf_op jit(solution)/shard_map/dot_general | solution.py:23
  515.4 7.0 fusion.24.near_ref
  522.4 16.3 %collective-permute-done.9 = bf16[256,2048]{1,0:T(8,128)(2,1)S(1)} collective-permute-done((bf16[256,2048]{1,0:T(8,128)(2,1)S(1)}, bf16[256,2048]{1,0:T(8,128)(2,1)S(1)}, u32[]{:S(2)}, u32[]{:S(2)}) %collective-permute-start.9) | collective-permute-done | bytes 1048608 | tf_op jit(solution)/shard_map/ppermute | solution.py:38
  545.8 41.7 %reduce8.5 = f32[256,2048]{1,0:T(8,128)S(1)} custom-call(f32[1024,2048]{1,0:T(8,128)} %fusion.24.near_ref, bf16[1024,2048]{1,0:T(8,128)(2,1)} %convolution_convert_fusion.2.far_ref), custom_call_target="tpu_custom_call" | custom-call | tf_op jit(solution)/shard_map/reduce8/pallas_call | solution.py:236
  589.9 11.0 %collective-permute-done.10 = bf16[128,2048]{1,0:T(8,128)(2,1)S(1)} collective-permute-done((bf16[128,2048]{1,0:T(8,128)(2,1)S(1)}, bf16[128,2048]{1,0:T(8,128)(2,1)S(1)}, u32[]{:S(2)}, u32[]{:S(2)}) %collective-permute-start.10) | collective-permute-done | bytes 524320 | tf_op jit(solution)/shard_map/ppermute | solution.py:33
  607.8 17.7 %total.1 = f32[34,128]{1,0:T(8,128)} custom-call(f32[34,128]{1,0:T(8,128)} %maximum_bitcast_fusion.part_ref), custom_call_target="tpu_custom_call" | custom-call | tf_op jit(solution)/shard_map/total/pallas_call | solution.py:358
  642.4 11.2 %collective-permute-done.16.x_ref = bf16[256,1536]{1,0:T(8,128)(2,1)} collective-permute-done((bf16[256,1536]{1,0:T(8,128)(2,1)}, bf16[256,1536]{1,0:T(8,128)(2,1)}, u32[]{:S(2)}, u32[]{:S(2)}) %collective-permute-start.16) | collective-permute-done | bytes 786464 | tf_op jit(solution)/shard_map/ppermute | solution.py:38
  668.5 22.2 %collective-permute-done.14.y_ref = bf16[256,768]{1,0:T(8,128)(2,1)S(1)} collective-permute-done((bf16[256,768]{1,0:T(8,128)(2,1)}, bf16[256,768]{1,0:T(8,128)(2,1)S(1)}, u32[]{:S(2)}, u32[]{:S(2)}) %collective-permute-start.14) | collective-permute-done | bytes 393248 | tf_op jit(solution)/shard_map/ppermute | solution.py:33
  690.7 8.0 %collective-permute-done.15.both_ref = bf16[256,768]{1,0:T(8,128)(2,1)S(1)} collective-permute-done((bf16[256,768]{1,0:T(8,128)(2,1)}, bf16[256,768]{1,0:T(8,128)(2,1)S(1)}, u32[]{:S(2)}, u32[]{:S(2)}) %collective-permute-start.15) | collective-permute-done | bytes 393248 | tf_op jit(solution)/shard_map/ppermute | solution.py:33
  705.9 5.8 join.4
  (197 shorter events, 120.4 us)
Async XLA Ops:
  7.2 117.2 %all-gather.4.cloned.1.call-start = ((), (), s32[]{:S(2)}) async-start(), calls=%async_computation.3 | async-start | bytes 4587520 | tf_op jit(solution)/shard_map/all_gather | solution.py:47
  26.3 245.2 %all-gather.6.cloned.1.call-start = ((), (), s32[]{:S(2)}) async-start(), calls=%async_computation.4 | async-start | bytes 7864320 | tf_op jit(solution)/shard_map/all_gather | solution.py:47
  54.0 256.8 %all-gather.8.cloned.1.call-start = ((), (), s32[]{:S(2)}) async-start(), calls=%async_computation.5 | async-start | bytes 3932160 | tf_op jit(solution)/shard_map/all_gather | solution.py:47
  55.8 41.0 %copy-start.9 = (bf16[1,512,2048]{2,1,0:T(8,128)(2,1)S(1)}, bf16[1,512,2048]{2,1,0:T(8,128)(2,1)}, u32[]{:S(2)}) copy-start(bf16[1,512,2048]{2,1,0:T(8,128)(2,1)} %param.27) | copy-start | bytes 6291460
  55.8 43.1 %copy-start.28 = (s32[1,1024]{1,0:T(1,128)S(1)}, s32[1,1024]{1,0:T(1,128)}, u32[]{:S(2)}) copy-start(s32[1,1024]{1,0:T(1,128)} %param.15) | copy-start | bytes 12292
  96.9 56.6 %collective-permute-start.1 = (bf16[256,2048]{1,0:T(8,128)(2,1)S(1)}, bf16[256,2048]{1,0:T(8,128)(2,1)S(1)}, u32[]{:S(2)}, u32[]{:S(2)}) collective-permute-start(bf16[256,2048]{1,0:T(8,128)(2,1)S(1)} %dynamic-slice_bitcast_fusion), channel_id=1, source_target_pairs={{0,4},{4,0},{8,12},{12,8},{16,20},{20,16},{24,28},{28,24},{1,5},{5... | collective-permute-start | bytes 3145736 | tf_op jit(solution)/shard_map/ppermute | solution.py:38
  98.4 107.2 %collective-permute-start.2 = (bf16[256,2048]{1,0:T(8,128)(2,1)S(1)}, bf16[256,2048]{1,0:T(8,128)(2,1)S(1)}, u32[]{:S(2)}, u32[]{:S(2)}) collective-permute-start(bf16[256,2048]{1,0:T(8,128)(2,1)S(1)} %dynamic-slice_bitcast_fusion), channel_id=1, source_target_pairs={{0,2},{2,0},{1,3},{3,1},{4,6},{6,4},{5,7},{7,5},{8,10},{10,8},{9,1... | collective-permute-start | bytes 3145736 | tf_op jit(solution)/shard_map/ppermute | solution.py:33
  98.9 23.5 %collective-permute-start = (s32[1,1024]{1,0:T(1,128)S(1)}, s32[1,1024]{1,0:T(1,128)S(1)}, u32[]{:S(2)}, u32[]{:S(2)}) collective-permute-start(s32[1,1024]{1,0:T(1,128)S(1)} %copy-done.28), channel_id=1, source_target_pairs={{0,4},{4,0},{8,12},{12,8},{16,20},{20,16},{24,28},{28,24},{1,5},{5... | collective-permute-start | bytes 12296 | tf_op jit(solution)/shard_map/ppermute | solution.py:38
  99.7 503.6 %reduce-scatter.8.cloned.1.call-start = ((), (), s32[]{:S(2)}) async-start(), calls=%async_computation.8 | async-start | bytes 3932160 | tf_op jit(solution)/shard_map/reduce_scatter | solution.py:51
  154.4 52.2 %collective-permute-start.3 = (bf16[128,2048]{1,0:T(8,128)(2,1)S(1)}, bf16[128,2048]{1,0:T(8,128)(2,1)S(1)}, u32[]{:S(2)}, u32[]{:S(2)}) collective-permute-start(bf16[128,2048]{1,0:T(8,128)(2,1)S(1)} %get-tuple-element.88), channel_id=1, source_target_pairs={{0,2},{2,0},{1,3},{3,1},{4,6},{6,4},{5,7},{7,5},{8,10},{10,8},{9,1... | collective-permute-start | bytes 1572872 | tf_op jit(solution)/shard_map/ppermute | solution.py:33
  210.2 14.7 %collective-permute-start.4 = (bf16[128,2048]{1,0:T(8,128)(2,1)S(1)}, bf16[128,2048]{1,0:T(8,128)(2,1)S(1)}, u32[]{:S(2)}, u32[]{:S(2)}) collective-permute-start(bf16[128,2048]{1,0:T(8,128)(2,1)S(1)} %get-tuple-element.84), channel_id=1, source_target_pairs={{0,4},{4,0},{8,12},{12,8},{16,20},{20,16},{24,28},{28,24},{1,5},{5... | collective-permute-start | bytes 1572872 | tf_op jit(solution)/shard_map/ppermute | solution.py:38
  229.2 65.0 %collective-permute-start.5 = (bf16[1024,2048]{1,0:T(8,128)(2,1)}, bf16[1024,2048]{1,0:T(8,128)(2,1)}, u32[]{:S(2)}, u32[]{:S(2)}) collective-permute-start(bf16[1024,2048]{1,0:T(8,128)(2,1)} %get-tuple-element.95), channel_id=1, source_target_pairs={{0,1},{1,0},{2,3},{3,2},{4,5},{5,4},{6,7},{7,6},{8,9},{9,8},{10,11... | collective-permute-start | bytes 12582920 | tf_op jit(solution)/shard_map/ppermute | solution.py:29
  310.7 319.5 %reduce-scatter.6.cloned.1.call-start = ((), (), s32[]{:S(2)}) async-start(), calls=%async_computation.7 | async-start | bytes 7864320 | tf_op jit(solution)/shard_map/reduce_scatter | solution.py:51
  345.1 291.2 %reduce-scatter.4.cloned.1.call-start = ((), (), s32[]{:S(2)}) async-start(), calls=%async_computation.6 | async-start | bytes 3932160 | tf_op jit(solution)/shard_map/reduce_scatter | solution.py:51
  367.5 40.1 %copy-start.1 = (f32[256,2048]{1,0:T(8,128)S(1)}, f32[256,2048]{1,0:T(8,128)}, u32[]{:S(2)}) copy-start(f32[256,2048]{1,0:T(8,128)} %copy-done) | copy-start | bytes 6291460
  457.3 7.8 %collective-permute-start.6 = (bf16[1024,2048]{1,0:T(8,128)(2,1)S(1)}, bf16[1024,2048]{1,0:T(8,128)(2,1)S(1)}, u32[]{:S(2)}, u32[]{:S(2)}) collective-permute-start(bf16[1024,2048]{1,0:T(8,128)(2,1)S(1)} %convolution_convert_fusion.4), channel_id=1, source_target_pairs={{0,1},{1,0},{2,3},{3,2},{4,5},{5,4},{6,7},{7,6},{8,9},{9,8},{10,11... | collective-permute-start | bytes 12582920 | tf_op jit(solution)/shard_map/ppermute | solution.py:29
  513.3 25.5 %collective-permute-start.9 = (bf16[256,2048]{1,0:T(8,128)(2,1)S(1)}, bf16[256,2048]{1,0:T(8,128)(2,1)S(1)}, u32[]{:S(2)}, u32[]{:S(2)}) collective-permute-start(bf16[256,2048]{1,0:T(8,128)(2,1)S(1)} %get-tuple-element.76), channel_id=1, source_target_pairs={{0,4},{4,0},{8,12},{12,8},{16,20},{20,16},{24,28},{28,24},{1,5},{5... | collective-permute-start | bytes 3145736 | tf_op jit(solution)/shard_map/ppermute | solution.py:38
  514.2 25.0 %collective-permute-start.7 = (bf16[256,2048]{1,0:T(8,128)(2,1)S(1)}, bf16[256,2048]{1,0:T(8,128)(2,1)S(1)}, u32[]{:S(2)}, u32[]{:S(2)}) collective-permute-start(bf16[256,2048]{1,0:T(8,128)(2,1)S(1)} %get-tuple-element.75), channel_id=1, source_target_pairs={{0,2},{2,0},{1,3},{3,1},{4,6},{6,4},{5,7},{7,5},{8,10},{10,8},{9,1... | collective-permute-start | bytes 3145736 | tf_op jit(solution)/shard_map/ppermute | solution.py:33
  540.3 49.5 %collective-permute-start.8 = (bf16[128,2048]{1,0:T(8,128)(2,1)S(1)}, bf16[128,2048]{1,0:T(8,128)(2,1)S(1)}, u32[]{:S(2)}, u32[]{:S(2)}) collective-permute-start(bf16[128,2048]{1,0:T(8,128)(2,1)S(1)} %slice.224), channel_id=1, source_target_pairs={{0,4},{4,0},{8,12},{12,8},{16,20},{20,16},{24,28},{28,24},{1,5},{5... | collective-permute-start | bytes 1572872 | tf_op jit(solution)/shard_map/ppermute | solution.py:38
  545.8 41.8 %copy-start.4 = (bf16[256,2048]{1,0:T(8,128)(2,1)S(1)}, bf16[256,2048]{1,0:T(8,128)(2,1)}, u32[]{:S(2)}) copy-start(bf16[256,2048]{1,0:T(8,128)(2,1)} %get-tuple-element.40.own_ref) | copy-start | bytes 3145732
  588.6 12.3 %collective-permute-start.10 = (bf16[128,2048]{1,0:T(8,128)(2,1)S(1)}, bf16[128,2048]{1,0:T(8,128)(2,1)S(1)}, u32[]{:S(2)}, u32[]{:S(2)}) collective-permute-start(bf16[128,2048]{1,0:T(8,128)(2,1)S(1)} %slice.223), channel_id=1, source_target_pairs={{0,2},{2,0},{1,3},{3,1},{4,6},{6,4},{5,7},{7,5},{8,10},{10,8},{9,1... | collective-permute-start | bytes 1572872 | tf_op jit(solution)/shard_map/ppermute | solution.py:33
  603.4 30.2 %collective-permute-start.12 = (bf16[256,2048]{1,0:T(8,128)(2,1)}, bf16[256,2048]{1,0:T(8,128)(2,1)S(1)}, u32[]{:S(2)}, u32[]{:S(2)}) collective-permute-start(bf16[256,2048]{1,0:T(8,128)(2,1)} %get-tuple-element.77), channel_id=1, source_target_pairs={{0,1},{1,0},{2,3},{3,2},{4,5},{5,4},{6,7},{7,6},{8,9},{9,8},{10,11... | collective-permute-start | bytes 3145736 | tf_op jit(solution)/shard_map/ppermute | solution.py:29
  604.5 24.7 %collective-permute-start.19 = (bf16[256,768]{1,0:T(8,128)(2,1)S(1)}, bf16[256,768]{1,0:T(8,128)(2,1)}, u32[]{:S(2)}, u32[]{:S(2)}) collective-permute-start(bf16[256,768]{1,0:T(8,128)(2,1)S(1)} %get-tuple-element.91), channel_id=1, source_target_pairs={{0,4},{4,0},{8,12},{12,8},{16,20},{20,16},{24,28},{28,24},{1,5},{5... | collective-permute-start | bytes 1179656 | tf_op jit(solution)/shard_map/ppermute | solution.py:38
  628.1 13.2 %collective-permute-start.11 = (bf16[256,2048]{1,0:T(8,128)(2,1)S(1)}, bf16[256,2048]{1,0:T(8,128)(2,1)}, u32[]{:S(2)}, u32[]{:S(2)}) collective-permute-start(bf16[256,2048]{1,0:T(8,128)(2,1)S(1)} %get-tuple-element.78), channel_id=1, source_target_pairs={{0,1},{1,0},{2,3},{3,2},{4,5},{5,4},{6,7},{7,6},{8,9},{9,8},{10,11... | collective-permute-start | bytes 3145736 | tf_op jit(solution)/shard_map/ppermute | solution.py:29
  628.1 27.9 %collective-permute-start.20 = (bf16[256,768]{1,0:T(8,128)(2,1)S(1)}, bf16[256,768]{1,0:T(8,128)(2,1)}, u32[]{:S(2)}, u32[]{:S(2)}) collective-permute-start(bf16[256,768]{1,0:T(8,128)(2,1)S(1)} %get-tuple-element.92.kept_ref), channel_id=1, source_target_pairs={{0,2},{2,0},{1,3},{3,1},{4,6},{6,4},{5,7},{7,5},{8,10},{10,8},{9,1... | collective-permute-start | bytes 1179656 | tf_op jit(solution)/shard_map/ppermute | solution.py:33
  629.2 34.6 %collective-permute-start.21 = (bf16[256,768]{1,0:T(8,128)(2,1)}, bf16[256,768]{1,0:T(8,128)(2,1)}, u32[]{:S(2)}, u32[]{:S(2)}) collective-permute-start(bf16[256,768]{1,0:T(8,128)(2,1)} %collective-permute-done.19.x_ref), channel_id=1, source_target_pairs={{0,2},{2,0},{1,3},{3,1},{4,6},{6,4},{5,7},{7,5},{8,10},{10,8},{9,1... | collective-permute-start | bytes 1179656 | tf_op jit(solution)/shard_map/ppermute | solution.py:33
  632.8 20.7 %collective-permute-start.16 = (bf16[256,1536]{1,0:T(8,128)(2,1)}, bf16[256,1536]{1,0:T(8,128)(2,1)}, u32[]{:S(2)}, u32[]{:S(2)}) collective-permute-start(bf16[256,1536]{1,0:T(8,128)(2,1)} %get-tuple-element.79), channel_id=1, source_target_pairs={{0,4},{4,0},{8,12},{12,8},{16,20},{20,16},{24,28},{28,24},{1,5},{5... | collective-permute-start | bytes 2359304 | tf_op jit(solution)/shard_map/ppermute | solution.py:38
  638.2 22.7 %collective-permute-start.13 = (bf16[256,768]{1,0:T(8,128)(2,1)S(1)}, bf16[256,768]{1,0:T(8,128)(2,1)}, u32[]{:S(2)}, u32[]{:S(2)}) collective-permute-start(bf16[256,768]{1,0:T(8,128)(2,1)S(1)} %get-tuple-element.93), channel_id=1, source_target_pairs={{0,4},{4,0},{8,12},{12,8},{16,20},{20,16},{24,28},{28,24},{1,5},{5... | collective-permute-start | bytes 1179656 | tf_op jit(solution)/shard_map/ppermute | solution.py:38
  641.3 62.7 %collective-permute-start.17 = (bf16[256,1536]{1,0:T(8,128)(2,1)}, bf16[256,1536]{1,0:T(8,128)(2,1)S(1)}, u32[]{:S(2)}, u32[]{:S(2)}) collective-permute-start(bf16[256,1536]{1,0:T(8,128)(2,1)} %get-tuple-element.80.kept_ref), channel_id=1, source_target_pairs={{0,2},{2,0},{1,3},{3,1},{4,6},{6,4},{5,7},{7,5},{8,10},{10,8},{9,1... | collective-permute-start | bytes 2359304 | tf_op jit(solution)/shard_map/ppermute | solution.py:33
  653.6 50.5 %collective-permute-start.18 = (bf16[256,1536]{1,0:T(8,128)(2,1)}, bf16[256,1536]{1,0:T(8,128)(2,1)S(1)}, u32[]{:S(2)}, u32[]{:S(2)}) collective-permute-start(bf16[256,1536]{1,0:T(8,128)(2,1)} %collective-permute-done.16.x_ref), channel_id=1, source_target_pairs={{0,2},{2,0},{1,3},{3,1},{4,6},{6,4},{5,7},{7,5},{8,10},{10,8},{9,1... | collective-permute-start | bytes 2359304 | tf_op jit(solution)/shard_map/ppermute | solution.py:33
  656.1 34.6 %collective-permute-start.14 = (bf16[256,768]{1,0:T(8,128)(2,1)}, bf16[256,768]{1,0:T(8,128)(2,1)S(1)}, u32[]{:S(2)}, u32[]{:S(2)}) collective-permute-start(bf16[256,768]{1,0:T(8,128)(2,1)} %get-tuple-element.94.kept_ref), channel_id=1, source_target_pairs={{0,2},{2,0},{1,3},{3,1},{4,6},{6,4},{5,7},{7,5},{8,10},{10,8},{9,1... | collective-permute-start | bytes 1179656 | tf_op jit(solution)/shard_map/ppermute | solution.py:33
  661.0 37.7 %collective-permute-start.15 = (bf16[256,768]{1,0:T(8,128)(2,1)}, bf16[256,768]{1,0:T(8,128)(2,1)S(1)}, u32[]{:S(2)}, u32[]{:S(2)}) collective-permute-start(bf16[256,768]{1,0:T(8,128)(2,1)} %collective-permute-done.13.x_ref), channel_id=1, source_target_pairs={{0,2},{2,0},{1,3},{3,1},{4,6},{6,4},{5,7},{7,5},{8,10},{10,8},{9,1... | collective-permute-start | bytes 1179656 | tf_op jit(solution)/shard_map/ppermute | solution.py:33
  (31 other events, 378.4 us)
Sparse Core Ops, SparseCore 0:
  26.4 73.5 all-gather.3
  101.6 113.8 all-gather.5
  217.1 61.6 all-gather.7
  310.8 60.7 reduce-scatter.7
  373.7 110.7 reduce-scatter.5
  511.4 60.8 reduce-scatter.3

commit v2 on v1

--- a/solution.py
+++ b/solution.py
@@ -79,12 +79,53 @@
     )
 
 
-def gather8_kernel(rows, own_ref, out_ref, send_sem, recv_sem, local_sem):
+def gather8_kernel(rows, spread, *refs):
+    if spread:
+        own_ref, kept_ref, x_ref, y_ref, first_ref, second_ref, out_ref, also_ref = refs[:8]
+        send_sem, recv_sem, local_sem, stage, also_send, also_recv, also_in, also_out = refs[8:]
+    else:
+        own_ref, out_ref, send_sem, recv_sem, local_sem = refs
     x_peer, y_peer, c_peer = neighbours()
+
+    def start_of(away_t, half, outer, inner):
+        return pl.ds((away_t * 8 + half * 4 + outer * 2 + inner) * rows, rows)
+
+    def slot(*block):
+        return out_ref.at[start_of(*block)]
+
+    also_loads, also_remote, also_stores = [], [], []
+    if spread:
+        top, low = pl.ds(0, rows), pl.ds(rows, rows)
+        pieces = [
+            ((0, 0, 0), kept_ref.at[top]),
+            ((0, 0, 1), x_ref.at[top]),
+            ((0, 1, 0), y_ref.at[top]),
+            ((0, 1, 1), first_ref),
+            ((1, 0, 0), kept_ref.at[low]),
+            ((1, 0, 1), y_ref.at[low]),
+            ((1, 1, 0), x_ref.at[low]),
+            ((1, 1, 1), second_ref),
+        ]
+        for index, (block, source) in enumerate(pieces):
+            also_loads.append(pltpu.make_async_copy(source, stage.at[index], also_in.at[index]))
+            also_stores.append(
+                pltpu.make_async_copy(
+                    stage.at[index], also_ref.at[start_of(0, *block)], also_out.at[index]
+                )
+            )
+            also_remote.append(
+                pltpu.make_async_remote_copy(
+                    src_ref=source,
+                    dst_ref=also_ref.at[start_of(1, *block)],
+                    send_sem=also_send.at[index],
+                    recv_sem=also_recv.at[index],
+                    device_id=c_peer,
+                    device_id_type=MESH,
+                )
+            )
+        for copy in also_loads:
+            copy.start()
     greet((x_peer, y_peer, c_peer))
-
-    def slot(away_t, half, outer, inner):
-        return out_ref.at[pl.ds((away_t * 8 + half * 4 + outer * 2 + inner) * rows, rows)]
 
     number = iter(range(14))
 
@@ -113,6 +154,11 @@
     ]
     for copy in kept:
         copy.start()
+    for copy in also_remote:
+        copy.start()
+    for load, store in zip(also_loads, also_stores):
+        load.wait()
+        store.start()
     x1.wait_recv()
     y3 = send(slot(0, 0, 0, 1), slot(0, 0, 1, 1), y_peer)
     y1.wait_recv()
@@ -129,27 +175,31 @@
     rest.append(send(slot(0, 1, 1, 1), slot(1, 1, 1, 1), c_peer))
     for copy in (x1, y1, x2, y2, y3, x3):
         copy.wait_send()
-    for copy in rest:
+    for copy in rest + also_remote + kept + also_stores:
         copy.wait()
-    for copy in kept:
-        copy.wait()
-
-
-def gather8(own):
+
+
+def gather8(own, also=()):
     rows, width = own.shape[0] // 2, own.shape[1]
-    return pl.pallas_call(
-        functools.partial(gather8_kernel, rows),
-        out_shape=jax.ShapeDtypeStruct((16 * rows, width), own.dtype),
-        in_specs=[pl.BlockSpec(memory_space=pltpu.VMEM)],
-        out_specs=pl.BlockSpec(memory_space=pl.ANY),
-        scratch_shapes=[
-            pltpu.SemaphoreType.DMA((14,)),
-            pltpu.SemaphoreType.DMA((14,)),
-            pltpu.SemaphoreType.DMA((2,)),
-        ],
-        compiler_params=remote_params(1),
-        name="gather8",
-    )(own)
+    hbm = pl.BlockSpec(memory_space=pl.ANY)
+    whole_shape = jax.ShapeDtypeStruct((16 * rows, width), own.dtype)
+    sems = [
+        pltpu.SemaphoreType.DMA((14,)),
+        pltpu.SemaphoreType.DMA((14,)),
+        pltpu.SemaphoreType.DMA((2,)),
+    ]
+    if also:
+        sems += [pltpu.VMEM((8, rows, width), own.dtype)] + [pltpu.SemaphoreType.DMA((8,))] * 4
+    outs = pl.pallas_call(
+        functools.partial(gather8_kernel, rows, bool(also)),
+        out_shape=[whole_shape] * (2 if also else 1),
+        in_specs=[pl.BlockSpec(memory_space=pltpu.VMEM)] + [hbm] * len(also),
+        out_specs=[hbm] * (2 if also else 1),
+        scratch_shapes=sems,
+        compiler_params=remote_params(6 if also else 1),
+        name="gather8_also" if also else "gather8",
+    )(own, *also)
+    return outs if also else outs[0]
 
 
 def reduce8_kernel(
@@ -263,7 +313,9 @@
     greet((x_peer,))
     remote, loads, stores = [], [], []
     for number, (which, start, size, cut) in enumerate(plan):
-        target = out_refs[which].at[odd, :, pl.ds(start, size)]
+        rows = ins[number].shape[0]
+        place = pl.ds(pl.multiple_of(odd * rows, rows), rows)
+        target = out_refs[which].at[place, pl.ds(start, size)]
 
         def source(index, ref=ins[number], size=size, cut=cut):
             if not cut:
@@ -304,9 +356,9 @@
             plan.append((which, start, size, cut))
             arrays.append(array)
             start += size
-        shapes.append((2, group[0][0].shape[0], start))
+        shapes.append((2 * group[0][0].shape[0], start))
     hbm = pl.BlockSpec(memory_space=pl.ANY)
-    pairs = pl.pallas_call(
+    return pl.pallas_call(
         functools.partial(shard_kernel, tuple(plan), len(groups)),
         out_shape=[jax.ShapeDtypeStruct(shape, BF16) for shape in shapes],
         in_specs=[hbm] * len(arrays),
@@ -319,7 +371,6 @@
         compiler_params=remote_params(number),
         name="shards",
     )(*arrays)
-    return [pair.reshape(2 * pair.shape[1], pair.shape[2]) for pair in pairs]
 
 
 def total_kernel(stages, part_ref, out_ref, inbox, outbox, send_sem, recv_sem):
@@ -418,9 +469,7 @@
     second = second[: 2 * rows] + after(came_second, *others).astype(F32)
     came_first = swap_x(first[rows:].astype(BF16))
     came_second = swap_ctx(second[rows:].astype(BF16))
-    first = first[:rows] + came_first.astype(F32)
-    second = second[:rows] + came_second.astype(F32)
-    return jnp.concatenate([first, second])
+    return first[:rows], second[:rows], came_first, came_second
 
 
 def rope_tables(positions):
@@ -709,6 +758,7 @@
             ),
         ),
     )
+    far_segments = swap_x(segment_ids)
     (first_pair,) = shards(
         [
             [
@@ -737,7 +787,7 @@
 
     own_tok, own_cot = own_quarter(tokens), own_quarter(cotangent)
     tok = gather8(after(own_tok, gate_up_pair))
-    segments = jnp.concatenate([segment_ids, swap_x(segment_ids)])
+    segments = jnp.concatenate([segment_ids, far_segments])
     seg_cols, seg_rows = segments[:, :, None], segments[:, None, :]
     cosine, sine = rope_tables(jnp.arange(length).astype(F32))
     meta = jnp.stack([place, core]).astype(jnp.int32)
@@ -762,26 +812,12 @@
     cot_first, cot_second = swap_ctx(cot_x[:eighth]), swap_x(cot_y[eighth:])
     out_far = mm(attended[half:], out_w, 1, 1).astype(BF16)
     out_near = mm(attended[:half], out_w, 1, 1)
-    cot_first = after(cot_first, out_near, out_far)
-    cot_second = after(cot_second, out_near, out_far)
-    cot_side = jnp.concatenate(
-        [
-            cot_from[:eighth],
-            cot_x[:eighth],
-            cot_y[:eighth],
-            cot_first,
-            cot_from[eighth:],
-            cot_y[eighth:],
-            cot_x[eighth:],
-            cot_second,
-        ]
-    )
-    cot_far = swap_core(cot_side)
     middle = own_tok.astype(F32) + reduce8(out_near, out_far)
     inverse_mid = inv_rms(middle)
     scaled_mid = middle * inverse_mid
-    y_all = gather8((scaled_mid * mid_gain).astype(BF16))
-    cot = jnp.concatenate([cot_side, after(cot_far, y_all)])
+    y_own = (scaled_mid * mid_gain).astype(BF16)
+    cot_first, cot_second = after(cot_first, y_own), after(cot_second, y_own)
+    y_all, cot = gather8(y_own, (cot_from, cot_x, cot_y, cot_first, cot_second))
 
     ff = gate_up_w.shape[1] // 2
     gate_up = mm(y_all, gate_up_w, 1, 0)
@@ -817,11 +853,14 @@
         meta, qkv, after(grad_att, mlp_rows), seg_cols, seg_rows, cosine, sine, head_gains
     )
     first_grad = jnp.concatenate([mm(x_all, raw_grads, 0, 0).astype(BF16), out_grad], axis=1)
-    mlp = reduce4_links(mlp_rows, raw_grads)
-    layer_out = finish_rows((middle + mlp).astype(BF16))
+    mlp_first, mlp_second, mlp_came1, mlp_came2 = reduce4_links(mlp_rows, raw_grads)
     in_near = mm(raw_grads[:half], qkv_w, 1, 1)
     in_far = mm(raw_grads[half:], qkv_w, 1, 1).astype(BF16)
     in_grad = reduce8(in_near, after(in_far, first_grad))
+
+    mlp_first = mlp_first + after(mlp_came1, in_grad).astype(F32)
+    mlp_second = mlp_second + after(mlp_came2, in_grad).astype(F32)
+    layer_out = finish_rows((middle + jnp.concatenate([mlp_first, mlp_second])).astype(BF16))
 
     spot = jnp.stack([place, odd]).astype(jnp.int32)
 

time: 728 us -> 702 us (0.964)
  waiting for transfers between devices: 99.8 us -> 88.1 us
  local copies, waits for them, and re-layouts: 42.8 us -> 31.7 us
    ppermute x8, waiting for transfers between devices: 57.9 us -> 30.3 us  [swap_x(): return lax.ppermute(value, 'fsdp', [(i, i ^ 1) for i in range(count)])]
    ppermute x10, waiting for transfers between devices: 41.8 us -> 57.6 us  [swap_ctx(): return lax.ppermute(value, 'ctx', [(0, 1), (1, 0)])]
    unnamed x83 -> x80, local copies, waits for them, and re-layouts: 19.2 us -> 16.3 us
  transfers between devices with their start and end apart: 28 -> 27, of which waited for: 9 -> 9; matrix products, arithmetic and copies ran while one was open for 28% -> 27% of each run, Pallas kernels for 48% -> 49%
where the time goes in v2:
time: 702 us; the launch traced here: 693 us
  Pallas kernels  363 us (52%)
  matrix products  143 us (20%)
  waiting for transfers between devices  88.1 us (13%)
  other arithmetic  33.6 us (5%)
  local copies, waits for them, and re-layouts  31.7 us (5%)
  starting transfers between devices  18.8 us (3%)
  between operations  15.2 us (2%)
    dot_general x16, matrix products, mm(): lax.dot_general(left, right, (((left_dim,), (right_dim,)), ((), ())), pre...  143 us
    pallas_call x3, Pallas kernels, gather8(): pl.pallas_call(functools.partial(gather8_kernel, rows, bool(also)), out_s...  122 us
    pallas_call x3, Pallas kernels, reduce8(): pl.pallas_call(functools.partial(reduce8_kernel, rows), out_shape=jax.Sha...  122 us
    ppermute x10, waiting for transfers between devices, swap_ctx(): return lax.ppermute(value, 'ctx', [(0, 1), (1, 0)])  57.6 us
    pallas_call x2, Pallas kernels, shards(): pl.pallas_call(functools.partial(shard_kernel, tuple(plan), len(groups)),...  41.6 us
    ppermute x8, waiting for transfers between devices, swap_x(): return lax.ppermute(value, 'fsdp', [(i, i ^ 1) for i in range(count)])  30.3 us
    pallas_call x1, Pallas kernels, attend_back(): pl.pallas_call(functools.partial(attend_back_kernel, heads, tile), out_sh...  28.3 us
    pallas_call x1, Pallas kernels, total(): pl.pallas_call(functools.partial(total_kernel, tuple(stages)), out_shape=...  17.5 us
  transfers between devices with their start and end apart: 27, of which 9 were waited for; matrix products, arithmetic and copies ran while one was open for 27% of the time, Pallas kernels for 49%

profile of v2, /device:TPU:0, one launch (start us, length us, event | category | flops | bytes accessed | tf_op | source)
XLA Modules:
  0.0 693.3 jit_solution(15288458204493791172)
XLA Ops:
  10.1 14.0 %shards.2 = bf16[512,896]{1,0:T(8,128)(2,1)} custom-call(bf16[256,1024]{1,0:T(8,128)(2,1)} %refs_0_.1, bf16[256,512]{1,0:T(8,128)(2,1)} %refs_1_.2, bf16[256,512]{1,0:T(8,128)(2,1)} %refs_2_.2, bf16[256,1024]{1,0:T(8,128)(2,1)} %refs_3_.1, bf16[256,128]{1,0:T(8,128)(2,1)} %select_select_fusion.refs_4_), custom_call_target="tpu_custom_call" | custom-call | tf_op jit(solution)/shard_map/shards/pallas_call | solution.py:361
  24.1 27.6 %shards.3 = (bf16[512,1536]{1,0:T(8,128)(2,1)}, bf16[512,768]{1,0:T(8,128)(2,1)}) custom-call(bf16[256,3072]{1,0:T(8,128)(2,1)} %refs_0_.2, bf16[256,3072]{1,0:T(8,128)(2,1)} %refs_1_.3, bf16[256,3072]{1,0:T(8,128)(2,1)} %refs_2_.3), custom_call_target="tpu_custom_call" | custom-call | tf_op jit(solution)/shard_map/shards/pallas_call | solution.py:361
  53.6 40.9 %gather8.2 = bf16[2048,2048]{1,0:T(8,128)(2,1)} custom-call(bf16[256,2048]{1,0:T(8,128)(2,1)} %get-tuple-element.43.refs_0_), custom_call_target="tpu_custom_call" | custom-call | tf_op jit(solution)/shard_map/gather8/pallas_call | solution.py:193
  97.6 5.1 fusion
  106.5 13.8 %collective-permute-done = s32[1,1024]{1,0:T(1,128)S(1)} collective-permute-done((s32[1,1024]{1,0:T(1,128)S(1)}, s32[1,1024]{1,0:T(1,128)S(1)}, u32[]{:S(2)}, u32[]{:S(2)}) %collective-permute-start) | collective-permute-done | bytes 4128 | tf_op jit(solution)/shard_map/ppermute | solution.py:38
  125.0 10.6 %fusion.13.qkv_ref = f32[2048,512]{1,0:T(8,128)} fusion(bf16[2048,2048]{1,0:T(8,128)(2,1)} %gather8.2, f32[2048]{0:T(1024)S(1)} %get-tuple-element.74, f32[2048]{0:T(1024)S(1)} %add_rsqrt_fusion, bf16[2048,896]{1,0:T(8,128)(2,1)} %all-gather.4.cloned.1.call-done), kind=kOutput, calls=%fused_computation.37 | convolution fusion | flops 4311744512 | bytes 14696448 | tf_op jit(solution)/shard_map/dot_general | solution.py:23
  135.5 16.3 %attend.1 = bf16[2048,256]{1,0:T(8,128)(2,1)} custom-call(s32[2]{0:T(128)} %pad_add_fusion.1.meta_ref, f32[2048,512]{1,0:T(8,128)} %fusion.13.qkv_ref, s32[2,1024,1]{2,1,0:T(8,128)} %copy.33.segc_ref, s32[2,1,1024]{2,1,0:T(1,128)} %broadcast_in_dim.76.segr_ref, f32[1024,128]{1,0:T(8,128)} %get-tuple-element.106.cos_ref, ...), custom_call_target="tpu_custom_call" | custom-call | flops 1073741824 | bytes 5242880 | tf_op jit(solution)/shard_map/attend/pallas_call | solution.py:661
  151.8 5.1 convolution_convert_fusion.3.far_ref
  157.0 5.8 fusion.36.near_ref
  162.8 40.1 %reduce8.3 = f32[256,2048]{1,0:T(8,128)S(1)} custom-call(f32[1024,2048]{1,0:T(8,128)} %fusion.36.near_ref, bf16[1024,2048]{1,0:T(8,128)(2,1)} %convolution_convert_fusion.3.far_ref), custom_call_target="tpu_custom_call" | custom-call | tf_op jit(solution)/shard_map/reduce8/pallas_call | solution.py:286
  205.9 11.4 %collective-permute-done.3.refs_4_ = bf16[128,2048]{1,0:T(8,128)(2,1)S(1)} collective-permute-done((bf16[128,2048]{1,0:T(8,128)(2,1)S(1)}, bf16[128,2048]{1,0:T(8,128)(2,1)S(1)}, u32[]{:S(2)}, u32[]{:S(2)}) %collective-permute-start.3) | collective-permute-done | bytes 524320 | tf_op jit(solution)/shard_map/ppermute | solution.py:33
  219.1 40.6 %gather8_also.1 = (bf16[2048,2048]{1,0:T(8,128)(2,1)}, bf16[2048,2048]{1,0:T(8,128)(2,1)}) custom-call(bf16[256,2048]{1,0:T(8,128)(2,1)} %multiply_convert_fusion.3.refs_0_, bf16[256,2048]{1,0:T(8,128)(2,1)} %copy-done.12, bf16[256,2048]{1,0:T(8,128)(2,1)} %copy-done.15, bf16[256,2048]{1,0:T(8,128)(2,1)} %copy-done.16, bf16[128,2048]{1,0:T(8,128)(2,1)} %copy-done.22, ...), custom_call_target="tpu_custom_call" | custom-call | tf_op jit(solution)/shard_map/gather8_also/pallas_call | solution.py:193
  259.7 18.2 %fusion.50 = f32[2048,1536]{0,1:T(8,128)S(1)} fusion(bf16[2048,2048]{1,0:T(8,128)(2,1)} %get-tuple-element.49, bf16[2048,1536]{1,0:T(8,128)(2,1)} %all-gather.6.cloned.1.call-done), kind=kOutput, calls=%fused_computation.115 | convolution fusion | flops 12884901888 | bytes 27262976 | tf_op jit(solution)/shard_map/dot_general | solution.py:23
  286.9 8.2 %convolution_convert_fusion.5 = bf16[2048,768]{1,0:T(8,128)(2,1)} fusion(bf16[2048,2048]{1,0:T(8,128)(2,1)S(1)} %copy-done.33, bf16[2048,768]{0,1:T(8,128)(2,1)S(1)} %multiply_convert_fusion.2), kind=kOutput, calls=%fused_computation.21 | convolution fusion | flops 6444023808 | bytes 14680064 | tf_op jit(solution)/shard_map/dot_general | solution.py:23
  295.2 15.3 %multiply_convert_fusion = (bf16[2048,768]{0,1:T(8,128)(2,1)S(1)}, bf16[2048,768]{0,1:T(8,128)(2,1)S(1)}) fusion(f32[2048,1536]{0,1:T(8,128)} %copy-done.5, bf16[2048,2048]{1,0:T(8,128)(2,1)} %get-tuple-element.51, bf16[2048,768]{1,0:T(8,128)(2,1)} %all-gather.8.cloned.1.call-done), kind=kOutput, calls=%fused_computation.12 | convolution fusion | flops 6462898176 | bytes 30408704 | tf_op jit(solution)/shard_map/dot_general | solution.py:23
  312.2 17.4 %convolution_convert_fusion = bf16[2048,1536]{1,0:T(8,128)(2,1)} fusion(bf16[2048,2048]{1,0:T(8,128)(2,1)} %get-tuple-element.49, bf16[2048,768]{0,1:T(8,128)(2,1)S(1)} %get-tuple-element.79, bf16[2048,768]{0,1:T(8,128)(2,1)S(1)} %get-tuple-element.80), kind=kOutput, calls=%fused_computation.11 | convolution fusion | flops 12900630528 | bytes 20971520 | tf_op jit(solution)/shard_map/dot_general | solution.py:23
  329.6 11.1 %convolution_convert_fusion.1.far_ref = bf16[1024,2048]{1,0:T(8,128)(2,1)} fusion(bf16[2048,1536]{1,0:T(8,128)(2,1)} %all-gather.6.cloned.1.call-done, bf16[2048,768]{0,1:T(8,128)(2,1)} %copy-done.36, bf16[2048,768]{0,1:T(8,128)(2,1)S(1)} %get-tuple-element.79), kind=kOutput, calls=%fused_computation.17 | convolution fusion | flops 6450839552 | bytes 16777216 | tf_op jit(solution)/shard_map/dot_general | solution.py:23
  340.7 11.2 %fusion.5.near_ref = f32[1024,2048]{1,0:T(8,128)} fusion(bf16[2048,1536]{1,0:T(8,128)(2,1)} %all-gather.6.cloned.1.call-done, bf16[2048,768]{0,1:T(8,128)(2,1)S(1)} %copy-done.37, bf16[2048,768]{0,1:T(8,128)(2,1)S(1)} %get-tuple-element.79), kind=kOutput, calls=%fused_computation.23 | convolution fusion | flops 6448742400 | bytes 20971520 | tf_op jit(solution)/shard_map/dot_general | solution.py:23
  351.9 40.1 %reduce8.4 = f32[256,2048]{1,0:T(8,128)S(1)} custom-call(f32[1024,2048]{1,0:T(8,128)} %fusion.5.near_ref, bf16[1024,2048]{1,0:T(8,128)(2,1)} %convolution_convert_fusion.1.far_ref), custom_call_target="tpu_custom_call" | custom-call | tf_op jit(solution)/shard_map/reduce8/pallas_call | solution.py:286
  395.2 40.5 %gather8.3 = bf16[2048,2048]{1,0:T(8,128)(2,1)} custom-call(bf16[256,2048]{1,0:T(8,128)(2,1)} %fusion.45.refs_0_), custom_call_target="tpu_custom_call" | custom-call | tf_op jit(solution)/shard_map/gather8/pallas_call | solution.py:193
  435.7 6.0 convolution_convert_fusion.4
  449.7 6.5 fusion.49
  456.2 28.3 %attend_back.1 = (bf16[2048,512]{1,0:T(8,128)(2,1)}, f32[2,128]{1,0:T(2,128)}) custom-call(s32[2]{0:T(128)} %pad_add_fusion.1.meta_ref, f32[2048,512]{1,0:T(8,128)} %fusion.13.qkv_ref, bf16[2048,256]{1,0:T(8,128)(2,1)} %convolution_convert_fusion.8.grad_ref, s32[2,1024,1]{2,1,0:T(8,128)} %copy.33.segc_ref, s32[2,1,1024]{2,1,0:T(1,128)} %broadcast_in_dim.76.segr_ref, ...), custom_call_target="tpu_custom_call" | custom-call | flops 2684354560 | bytes 8388608 | tf_op jit(solution)/shard_map/attend_back/pallas_call | solution.py:689
  484.6 9.2 %convolution_convert_fusion.6 = bf16[2048,512]{1,0:T(8,128)(2,1)S(1)} fusion(bf16[2048,512]{1,0:T(8,128)(2,1)} %get-tuple-element.56, bf16[2048,2048]{1,0:T(8,128)(2,1)} %gather8.2, f32[2048]{0:T(1024)S(1)} %copy-done.28, f32[2048]{0:T(1024)S(1)} %copy-done.30), kind=kOutput, calls=%fused_computation.31 | convolution fusion | flops 4312793088 | bytes 12599296 | tf_op jit(solution)/shard_map/dot_general | solution.py:23
  499.6 7.0 %fusion.24.near_ref = f32[1024,2048]{1,0:T(8,128)} fusion(bf16[2048,896]{1,0:T(8,128)(2,1)S(1)} %copy-done.17, bf16[2048,512]{1,0:T(8,128)(2,1)} %get-tuple-element.56), kind=kOutput, calls=%fused_computation.57 | convolution fusion | flops 2147483648 | bytes 11534336 | tf_op jit(solution)/shard_map/dot_general | solution.py:23
  506.7 16.3 %collective-permute-done.6 = bf16[256,2048]{1,0:T(8,128)(2,1)S(1)} collective-permute-done((bf16[256,2048]{1,0:T(8,128)(2,1)S(1)}, bf16[256,2048]{1,0:T(8,128)(2,1)S(1)}, u32[]{:S(2)}, u32[]{:S(2)}) %collective-permute-start.6) | collective-permute-done | bytes 1048608 | tf_op jit(solution)/shard_map/ppermute | solution.py:33
  531.2 41.7 %reduce8.5 = f32[256,2048]{1,0:T(8,128)S(1)} custom-call(f32[1024,2048]{1,0:T(8,128)} %fusion.24.near_ref, bf16[1024,2048]{1,0:T(8,128)(2,1)} %convolution_convert_fusion.2.far_ref), custom_call_target="tpu_custom_call" | custom-call | tf_op jit(solution)/shard_map/reduce8/pallas_call | solution.py:286
  582.3 17.5 %total.1 = f32[34,128]{1,0:T(8,128)} custom-call(f32[34,128]{1,0:T(8,128)} %maximum_bitcast_fusion.part_ref), custom_call_target="tpu_custom_call" | custom-call | tf_op jit(solution)/shard_map/total/pallas_call | solution.py:409
  616.9 11.0 %collective-permute-done.15.x_ref = bf16[256,1536]{1,0:T(8,128)(2,1)} collective-permute-done((bf16[256,1536]{1,0:T(8,128)(2,1)}, bf16[256,1536]{1,0:T(8,128)(2,1)}, u32[]{:S(2)}, u32[]{:S(2)}) %collective-permute-start.15) | collective-permute-done | bytes 786464 | tf_op jit(solution)/shard_map/ppermute | solution.py:38
  643.0 22.0 %collective-permute-done.13.y_ref = bf16[256,768]{1,0:T(8,128)(2,1)S(1)} collective-permute-done((bf16[256,768]{1,0:T(8,128)(2,1)}, bf16[256,768]{1,0:T(8,128)(2,1)S(1)}, u32[]{:S(2)}, u32[]{:S(2)}) %collective-permute-start.13) | collective-permute-done | bytes 393248 | tf_op jit(solution)/shard_map/ppermute | solution.py:33
  665.0 8.0 %collective-permute-done.14.both_ref = bf16[256,768]{1,0:T(8,128)(2,1)S(1)} collective-permute-done((bf16[256,768]{1,0:T(8,128)(2,1)}, bf16[256,768]{1,0:T(8,128)(2,1)S(1)}, u32[]{:S(2)}, u32[]{:S(2)}) %collective-permute-start.14) | collective-permute-done | bytes 393248 | tf_op jit(solution)/shard_map/ppermute | solution.py:33
  680.2 5.8 join.4
  (191 shorter events, 105.7 us)
Async XLA Ops:
  7.2 115.0 %all-gather.4.cloned.1.call-start = ((), (), s32[]{:S(2)}) async-start(), calls=%async_computation.3 | async-start | bytes 4587520 | tf_op jit(solution)/shard_map/all_gather | solution.py:47
  24.1 235.6 %all-gather.6.cloned.1.call-start = ((), (), s32[]{:S(2)}) async-start(), calls=%async_computation.4 | async-start | bytes 7864320 | tf_op jit(solution)/shard_map/all_gather | solution.py:47
  51.8 243.5 %all-gather.8.cloned.1.call-start = ((), (), s32[]{:S(2)}) async-start(), calls=%async_computation.5 | async-start | bytes 3932160 | tf_op jit(solution)/shard_map/all_gather | solution.py:47
  53.6 41.0 %copy-start.9 = (bf16[1,512,2048]{2,1,0:T(8,128)(2,1)S(1)}, bf16[1,512,2048]{2,1,0:T(8,128)(2,1)}, u32[]{:S(2)}) copy-start(bf16[1,512,2048]{2,1,0:T(8,128)(2,1)} %param.27) | copy-start | bytes 6291460
  53.6 43.2 %copy-start.32 = (s32[1,1024]{1,0:T(1,128)S(1)}, s32[1,1024]{1,0:T(1,128)}, u32[]{:S(2)}) copy-start(s32[1,1024]{1,0:T(1,128)} %param.15) | copy-start | bytes 12292
  94.7 57.1 %collective-permute-start.1 = (bf16[256,2048]{1,0:T(8,128)(2,1)S(1)}, bf16[256,2048]{1,0:T(8,128)(2,1)S(1)}, u32[]{:S(2)}, u32[]{:S(2)}) collective-permute-start(bf16[256,2048]{1,0:T(8,128)(2,1)S(1)} %dynamic-slice_bitcast_fusion.refs_1_), channel_id=1, source_target_pairs={{0,4},{4,0},{8,12},{12,8},{16,20},{20,16},{24,28},{28,24},{1,5},{5... | collective-permute-start | bytes 3145736 | tf_op jit(solution)/shard_map/ppermute | solution.py:38
  96.2 107.0 %collective-permute-start.2 = (bf16[256,2048]{1,0:T(8,128)(2,1)S(1)}, bf16[256,2048]{1,0:T(8,128)(2,1)S(1)}, u32[]{:S(2)}, u32[]{:S(2)}) collective-permute-start(bf16[256,2048]{1,0:T(8,128)(2,1)S(1)} %dynamic-slice_bitcast_fusion.refs_1_), channel_id=1, source_target_pairs={{0,2},{2,0},{1,3},{3,1},{4,6},{6,4},{5,7},{7,5},{8,10},{10,8},{9,1... | collective-permute-start | bytes 3145736 | tf_op jit(solution)/shard_map/ppermute | solution.py:33
  96.7 23.5 %collective-permute-start = (s32[1,1024]{1,0:T(1,128)S(1)}, s32[1,1024]{1,0:T(1,128)S(1)}, u32[]{:S(2)}, u32[]{:S(2)}) collective-permute-start(s32[1,1024]{1,0:T(1,128)S(1)} %copy-done.32), channel_id=1, source_target_pairs={{0,4},{4,0},{8,12},{12,8},{16,20},{20,16},{24,28},{28,24},{1,5},{5... | collective-permute-start | bytes 12296 | tf_op jit(solution)/shard_map/ppermute | solution.py:38
  97.5 480.7 %reduce-scatter.8.cloned.1.call-start = ((), (), s32[]{:S(2)}) async-start(), calls=%async_computation.8 | async-start | bytes 3932160 | tf_op jit(solution)/shard_map/reduce_scatter | solution.py:51
  151.8 51.4 %copy-start.15 = (bf16[256,2048]{1,0:T(8,128)(2,1)}, bf16[256,2048]{1,0:T(8,128)(2,1)S(1)}, u32[]{:S(2)}) copy-start(bf16[256,2048]{1,0:T(8,128)(2,1)S(1)} %collective-permute-done.1.refs_2_) | copy-start | bytes 3145732
  203.3 14.0 %collective-permute-start.3 = (bf16[128,2048]{1,0:T(8,128)(2,1)S(1)}, bf16[128,2048]{1,0:T(8,128)(2,1)S(1)}, u32[]{:S(2)}, u32[]{:S(2)}) collective-permute-start(bf16[128,2048]{1,0:T(8,128)(2,1)S(1)} %slice.96), channel_id=1, source_target_pairs={{0,2},{2,0},{1,3},{3,1},{4,6},{6,4},{5,7},{7,5},{8,10},{10,8},{9,1... | collective-permute-start | bytes 1572872 | tf_op jit(solution)/shard_map/ppermute | solution.py:33
  203.9 14.3 %collective-permute-start.4 = (bf16[128,2048]{1,0:T(8,128)(2,1)S(1)}, bf16[128,2048]{1,0:T(8,128)(2,1)S(1)}, u32[]{:S(2)}, u32[]{:S(2)}) collective-permute-start(bf16[128,2048]{1,0:T(8,128)(2,1)S(1)} %slice.97), channel_id=1, source_target_pairs={{0,4},{4,0},{8,12},{12,8},{16,20},{20,16},{24,28},{28,24},{1,5},{5... | collective-permute-start | bytes 1572872 | tf_op jit(solution)/shard_map/ppermute | solution.py:38
  295.2 309.3 %reduce-scatter.6.cloned.1.call-start = ((), (), s32[]{:S(2)}) async-start(), calls=%async_computation.7 | async-start | bytes 7864320 | tf_op jit(solution)/shard_map/reduce_scatter | solution.py:51
  329.6 281.7 %reduce-scatter.4.cloned.1.call-start = ((), (), s32[]{:S(2)}) async-start(), calls=%async_computation.6 | async-start | bytes 3932160 | tf_op jit(solution)/shard_map/reduce_scatter | solution.py:51
  351.9 40.1 %copy-start.1 = (f32[256,2048]{1,0:T(8,128)S(1)}, f32[256,2048]{1,0:T(8,128)}, u32[]{:S(2)}) copy-start(f32[256,2048]{1,0:T(8,128)} %copy-done) | copy-start | bytes 6291460
  441.7 7.7 %collective-permute-start.5 = (bf16[1024,2048]{1,0:T(8,128)(2,1)S(1)}, bf16[1024,2048]{1,0:T(8,128)(2,1)S(1)}, u32[]{:S(2)}, u32[]{:S(2)}) collective-permute-start(bf16[1024,2048]{1,0:T(8,128)(2,1)S(1)} %convolution_convert_fusion.4), channel_id=1, source_target_pairs={{0,1},{1,0},{2,3},{3,2},{4,5},{5,4},{6,7},{7,6},{8,9},{9,8},{10,11... | collective-permute-start | bytes 12582920 | tf_op jit(solution)/shard_map/ppermute | solution.py:29
  497.5 25.4 %collective-permute-start.6 = (bf16[256,2048]{1,0:T(8,128)(2,1)S(1)}, bf16[256,2048]{1,0:T(8,128)(2,1)S(1)}, u32[]{:S(2)}, u32[]{:S(2)}) collective-permute-start(bf16[256,2048]{1,0:T(8,128)(2,1)S(1)} %get-tuple-element.83), channel_id=1, source_target_pairs={{0,2},{2,0},{1,3},{3,1},{4,6},{6,4},{5,7},{7,5},{8,10},{10,8},{9,1... | collective-permute-start | bytes 3145736 | tf_op jit(solution)/shard_map/ppermute | solution.py:33
  498.7 25.0 %collective-permute-start.8 = (bf16[256,2048]{1,0:T(8,128)(2,1)S(1)}, bf16[256,2048]{1,0:T(8,128)(2,1)S(1)}, u32[]{:S(2)}, u32[]{:S(2)}) collective-permute-start(bf16[256,2048]{1,0:T(8,128)(2,1)S(1)} %get-tuple-element.84), channel_id=1, source_target_pairs={{0,4},{4,0},{8,12},{12,8},{16,20},{20,16},{24,28},{28,24},{1,5},{5... | collective-permute-start | bytes 3145736 | tf_op jit(solution)/shard_map/ppermute | solution.py:38
  524.7 49.2 %collective-permute-start.9 = (bf16[128,2048]{1,0:T(8,128)(2,1)S(1)}, bf16[128,2048]{1,0:T(8,128)(2,1)S(1)}, u32[]{:S(2)}, u32[]{:S(2)}) collective-permute-start(bf16[128,2048]{1,0:T(8,128)(2,1)S(1)} %slice.195), channel_id=1, source_target_pairs={{0,2},{2,0},{1,3},{3,1},{4,6},{6,4},{5,7},{7,5},{8,10},{10,8},{9,1... | collective-permute-start | bytes 1572872 | tf_op jit(solution)/shard_map/ppermute | solution.py:33
  525.8 48.1 %collective-permute-start.7 = (bf16[128,2048]{1,0:T(8,128)(2,1)S(1)}, bf16[128,2048]{1,0:T(8,128)(2,1)S(1)}, u32[]{:S(2)}, u32[]{:S(2)}) collective-permute-start(bf16[128,2048]{1,0:T(8,128)(2,1)S(1)} %slice.196), channel_id=1, source_target_pairs={{0,4},{4,0},{8,12},{12,8},{16,20},{20,16},{24,28},{28,24},{1,5},{5... | collective-permute-start | bytes 1572872 | tf_op jit(solution)/shard_map/ppermute | solution.py:38
  531.2 41.7 %copy-start.4 = (bf16[256,2048]{1,0:T(8,128)(2,1)S(1)}, bf16[256,2048]{1,0:T(8,128)(2,1)}, u32[]{:S(2)}) copy-start(bf16[256,2048]{1,0:T(8,128)(2,1)} %get-tuple-element.43.refs_0_) | copy-start | bytes 3145732
  578.2 30.4 %collective-permute-start.10 = (bf16[256,2048]{1,0:T(8,128)(2,1)}, bf16[256,2048]{1,0:T(8,128)(2,1)S(1)}, u32[]{:S(2)}, u32[]{:S(2)}) collective-permute-start(bf16[256,2048]{1,0:T(8,128)(2,1)} %get-tuple-element.86), channel_id=1, source_target_pairs={{0,1},{1,0},{2,3},{3,2},{4,5},{5,4},{6,7},{7,6},{8,9},{9,8},{10,11... | collective-permute-start | bytes 3145736 | tf_op jit(solution)/shard_map/ppermute | solution.py:29
  579.4 24.4 %collective-permute-start.18 = (bf16[256,768]{1,0:T(8,128)(2,1)S(1)}, bf16[256,768]{1,0:T(8,128)(2,1)}, u32[]{:S(2)}, u32[]{:S(2)}) collective-permute-start(bf16[256,768]{1,0:T(8,128)(2,1)S(1)} %get-tuple-element.89), channel_id=1, source_target_pairs={{0,4},{4,0},{8,12},{12,8},{16,20},{20,16},{24,28},{28,24},{1,5},{5... | collective-permute-start | bytes 1179656 | tf_op jit(solution)/shard_map/ppermute | solution.py:38
  602.5 13.2 %collective-permute-start.11 = (bf16[256,2048]{1,0:T(8,128)(2,1)S(1)}, bf16[256,2048]{1,0:T(8,128)(2,1)}, u32[]{:S(2)}, u32[]{:S(2)}) collective-permute-start(bf16[256,2048]{1,0:T(8,128)(2,1)S(1)} %get-tuple-element.85), channel_id=1, source_target_pairs={{0,1},{1,0},{2,3},{3,2},{4,5},{5,4},{6,7},{7,6},{8,9},{9,8},{10,11... | collective-permute-start | bytes 3145736 | tf_op jit(solution)/shard_map/ppermute | solution.py:29
  602.5 28.1 %collective-permute-start.19 = (bf16[256,768]{1,0:T(8,128)(2,1)S(1)}, bf16[256,768]{1,0:T(8,128)(2,1)}, u32[]{:S(2)}, u32[]{:S(2)}) collective-permute-start(bf16[256,768]{1,0:T(8,128)(2,1)S(1)} %get-tuple-element.90.kept_ref), channel_id=1, source_target_pairs={{0,2},{2,0},{1,3},{3,1},{4,6},{6,4},{5,7},{7,5},{8,10},{10,8},{9,1... | collective-permute-start | bytes 1179656 | tf_op jit(solution)/shard_map/ppermute | solution.py:33
  603.8 34.6 %collective-permute-start.20 = (bf16[256,768]{1,0:T(8,128)(2,1)}, bf16[256,768]{1,0:T(8,128)(2,1)}, u32[]{:S(2)}, u32[]{:S(2)}) collective-permute-start(bf16[256,768]{1,0:T(8,128)(2,1)} %collective-permute-done.18.x_ref), channel_id=1, source_target_pairs={{0,2},{2,0},{1,3},{3,1},{4,6},{6,4},{5,7},{7,5},{8,10},{10,8},{9,1... | collective-permute-start | bytes 1179656 | tf_op jit(solution)/shard_map/ppermute | solution.py:33
  607.2 20.7 %collective-permute-start.15 = (bf16[256,1536]{1,0:T(8,128)(2,1)}, bf16[256,1536]{1,0:T(8,128)(2,1)}, u32[]{:S(2)}, u32[]{:S(2)}) collective-permute-start(bf16[256,1536]{1,0:T(8,128)(2,1)} %get-tuple-element.87), channel_id=1, source_target_pairs={{0,4},{4,0},{8,12},{12,8},{16,20},{20,16},{24,28},{28,24},{1,5},{5... | collective-permute-start | bytes 2359304 | tf_op jit(solution)/shard_map/ppermute | solution.py:38
  613.2 22.1 %collective-permute-start.12 = (bf16[256,768]{1,0:T(8,128)(2,1)S(1)}, bf16[256,768]{1,0:T(8,128)(2,1)}, u32[]{:S(2)}, u32[]{:S(2)}) collective-permute-start(bf16[256,768]{1,0:T(8,128)(2,1)S(1)} %get-tuple-element.91), channel_id=1, source_target_pairs={{0,4},{4,0},{8,12},{12,8},{16,20},{20,16},{24,28},{28,24},{1,5},{5... | collective-permute-start | bytes 1179656 | tf_op jit(solution)/shard_map/ppermute | solution.py:38
  615.7 62.7 %collective-permute-start.16 = (bf16[256,1536]{1,0:T(8,128)(2,1)}, bf16[256,1536]{1,0:T(8,128)(2,1)S(1)}, u32[]{:S(2)}, u32[]{:S(2)}) collective-permute-start(bf16[256,1536]{1,0:T(8,128)(2,1)} %get-tuple-element.88.kept_ref), channel_id=1, source_target_pairs={{0,2},{2,0},{1,3},{3,1},{4,6},{6,4},{5,7},{7,5},{8,10},{10,8},{9,1... | collective-permute-start | bytes 2359304 | tf_op jit(solution)/shard_map/ppermute | solution.py:33
  627.9 50.5 %collective-permute-start.17 = (bf16[256,1536]{1,0:T(8,128)(2,1)}, bf16[256,1536]{1,0:T(8,128)(2,1)S(1)}, u32[]{:S(2)}, u32[]{:S(2)}) collective-permute-start(bf16[256,1536]{1,0:T(8,128)(2,1)} %collective-permute-done.15.x_ref), channel_id=1, source_target_pairs={{0,2},{2,0},{1,3},{3,1},{4,6},{6,4},{5,7},{7,5},{8,10},{10,8},{9,1... | collective-permute-start | bytes 2359304 | tf_op jit(solution)/shard_map/ppermute | solution.py:33
  630.6 34.4 %collective-permute-start.13 = (bf16[256,768]{1,0:T(8,128)(2,1)}, bf16[256,768]{1,0:T(8,128)(2,1)S(1)}, u32[]{:S(2)}, u32[]{:S(2)}) collective-permute-start(bf16[256,768]{1,0:T(8,128)(2,1)} %get-tuple-element.92.kept_ref), channel_id=1, source_target_pairs={{0,2},{2,0},{1,3},{3,1},{4,6},{6,4},{5,7},{7,5},{8,10},{10,8},{9,1... | collective-permute-start | bytes 1179656 | tf_op jit(solution)/shard_map/ppermute | solution.py:33
  635.3 37.7 %collective-permute-start.14 = (bf16[256,768]{1,0:T(8,128)(2,1)}, bf16[256,768]{1,0:T(8,128)(2,1)S(1)}, u32[]{:S(2)}, u32[]{:S(2)}) collective-permute-start(bf16[256,768]{1,0:T(8,128)(2,1)} %collective-permute-done.12.x_ref), channel_id=1, source_target_pairs={{0,2},{2,0},{1,3},{3,1},{4,6},{6,4},{5,7},{7,5},{8,10},{10,8},{9,1... | collective-permute-start | bytes 1179656 | tf_op jit(solution)/shard_map/ppermute | solution.py:33
  (35 other events, 365.4 us)
Sparse Core Ops, SparseCore 0:
  24.2 73.5 all-gather.3
  99.4 113.8 all-gather.5
  214.9 61.6 all-gather.7
  295.3 60.7 reduce-scatter.7
  358.3 110.6 reduce-scatter.5
  495.8 60.8 reduce-scatter.3

commit v3 on v2

--- a/solution.py
+++ b/solution.py
@@ -179,6 +179,165 @@
         copy.wait()
 
 
+def gather8_product_kernel(
+    rows,
+    own_ref,
+    acts_ref,
+    weight_ref,
+    out_ref,
+    kept_ref,
+    to_y_ref,
+    to_x_ref,
+    send_sem,
+    recv_sem,
+    local_sem,
+    acts,
+    weight,
+    far,
+    core_in,
+    core_send,
+    core_recv,
+    load_sem,
+):
+    x_peer, y_peer, c_peer = neighbours()
+    width = weight.shape[0]
+    wide = 2 * rows
+    loads = [
+        pltpu.make_async_copy(weight_ref, weight, load_sem.at[0]),
+        pltpu.make_async_copy(acts_ref, acts, load_sem.at[1]),
+    ]
+    for copy in loads:
+        copy.start()
+    greet((x_peer, y_peer, c_peer))
+
+    def slot(away_t, half, outer, inner):
+        return out_ref.at[pl.ds((away_t * 8 + half * 4 + outer * 2 + inner) * rows, rows)]
+
+    number = iter(range(14))
+
+    def send(source, target, peer):
+        index = next(number)
+        copy = pltpu.make_async_remote_copy(
+            src_ref=source,
+            dst_ref=target,
+            send_sem=send_sem.at[index],
+            recv_sem=recv_sem.at[index],
+            device_id=peer,
+            device_id_type=MESH,
+        )
+        copy.start()
+        return copy
+
+    core_copies = []
+
+    def far_chunk(index):
+        place = pl.ds(index * wide, wide)
+        source = pl.ds(4 * wide + index * wide, wide)
+
+        def step(cols):
+            far[place, cols] = mm(acts[source, :], weight[cols, :], 1, 1).astype(BF16)
+            return 0
+
+        tiled(width, width // 2, step)
+        copy = pltpu.make_async_remote_copy(
+            src_ref=far.at[place],
+            dst_ref=core_in.at[place],
+            send_sem=core_send.at[index],
+            recv_sem=core_recv.at[index],
+            device_id=c_peer,
+            device_id_type=MESH,
+        )
+        copy.start()
+        core_copies.append(copy)
+
+    def near_chunk(index, target_ref, start):
+        core_copies[index].wait_recv()
+        place = pl.ds(index * wide, wide)
+        target = pl.ds(start, wide)
+
+        def step(cols):
+            value = mm(acts[place, :], weight[cols, :], 1, 1) + core_in[place, cols].astype(F32)
+            target_ref[target, cols] = value.astype(target_ref.dtype)
+            return 0
+
+        tiled(width, width // 2, step)
+
+    first, second = own_ref.at[pl.ds(0, rows)], own_ref.at[pl.ds(rows, rows)]
+    x1 = send(first, slot(0, 0, 0, 1), x_peer)
+    y1 = send(second, slot(0, 1, 0, 1), y_peer)
+    x2 = send(second, slot(0, 1, 1, 0), x_peer)
+    y2 = send(first, slot(0, 0, 1, 0), y_peer)
+    rest = [send(first, slot(1, 0, 0, 0), c_peer), send(second, slot(1, 1, 0, 0), c_peer)]
+    kept = [
+        pltpu.make_async_copy(first, slot(0, 0, 0, 0), local_sem.at[0]),
+        pltpu.make_async_copy(second, slot(0, 1, 0, 0), local_sem.at[1]),
+    ]
+    for copy in kept:
+        copy.start()
+    for copy in loads:
+        copy.wait()
+    for index in range(4):
+        far_chunk(index)
+    x1.wait_recv()
+    y3 = send(slot(0, 0, 0, 1), slot(0, 0, 1, 1), y_peer)
+    y1.wait_recv()
+    x3 = send(slot(0, 1, 0, 1), slot(0, 1, 1, 1), x_peer)
+    rest.append(send(slot(0, 0, 0, 1), slot(1, 0, 0, 1), c_peer))
+    rest.append(send(slot(0, 1, 0, 1), slot(1, 1, 0, 1), c_peer))
+    near_chunk(0, kept_ref, 0)
+    near_chunk(1, to_y_ref, 0)
+    near_chunk(2, kept_ref, wide)
+    near_chunk(3, to_x_ref, 0)
+    x2.wait_recv()
+    rest.append(send(slot(0, 1, 1, 0), slot(1, 1, 1, 0), c_peer))
+    y2.wait_recv()
+    rest.append(send(slot(0, 0, 1, 0), slot(1, 0, 1, 0), c_peer))
+    y3.wait_recv()
+    rest.append(send(slot(0, 0, 1, 1), slot(1, 0, 1, 1), c_peer))
+    x3.wait_recv()
+    rest.append(send(slot(0, 1, 1, 1), slot(1, 1, 1, 1), c_peer))
+    for copy in (x1, y1, x2, y2, y3, x3):
+        copy.wait_send()
+    for copy in core_copies:
+        copy.wait_send()
+    for copy in rest + kept:
+        copy.wait()
+
+
+def gather8_product(own, acts, weight):
+    rows, width = own.shape[0] // 2, own.shape[1]
+    hbm = pl.BlockSpec(memory_space=pl.ANY)
+    vmem = pl.BlockSpec(memory_space=pltpu.VMEM)
+    return pl.pallas_call(
+        functools.partial(gather8_product_kernel, rows),
+        out_shape=[
+            jax.ShapeDtypeStruct((16 * rows, width), own.dtype),
+            jax.ShapeDtypeStruct((4 * rows, width), F32),
+            jax.ShapeDtypeStruct((2 * rows, width), BF16),
+            jax.ShapeDtypeStruct((2 * rows, width), BF16),
+        ],
+        in_specs=[vmem, hbm, hbm],
+        out_specs=[hbm, vmem, vmem, vmem],
+        scratch_shapes=[
+            pltpu.SemaphoreType.DMA((14,)),
+            pltpu.SemaphoreType.DMA((14,)),
+            pltpu.SemaphoreType.DMA((2,)),
+            pltpu.VMEM(acts.shape, BF16),
+            pltpu.VMEM(weight.shape, BF16),
+            pltpu.VMEM((8 * rows, width), BF16),
+            pltpu.VMEM((8 * rows, width), BF16),
+            pltpu.SemaphoreType.DMA((4,)),
+            pltpu.SemaphoreType.DMA((4,)),
+            pltpu.SemaphoreType.DMA((2,)),
+        ],
+        compiler_params=remote_params(9, 48 * 1024 * 1024),
+        cost_estimate=pl.CostEstimate(
+            flops=2 * acts.size * width, bytes_accessed=16 * own.size, transcendentals=0
+        ),
+        name="gather8_product",
+    )(own, acts, weight)
+
+
 def gather8(own, also=()):
     rows, width = own.shape[0] // 2, own.shape[1]
     hbm = pl.BlockSpec(memory_space=pl.ANY)
@@ -302,6 +461,191 @@
     )(near, far)
 
 
+def tiled(count, tile, step):
+    lax.fori_loop(0, count // tile, lambda i, _: step(pl.ds(pl.multiple_of(i * tile, tile), tile)), 0)
+
+
+def product_reduce8_kernel(rows, filler, *refs):
+    if filler:
+        acts_ref, weight_ref, lhs_ref, out_ref, grad_ref, *refs = refs
+    else:
+        acts_ref, weight_ref, out_ref, *refs = refs
+    acts, weight, far, near, core_in, link_in, link_out, send_sem, recv_sem, load_sem, *refs = refs
+    x_peer, y_peer, c_peer = neighbours()
+    width = weight.shape[0]
+    wide = 2 * rows
+    chunks = [(0, 1), (1, 1), (0, 0), (1, 0)]
+
+    def where(chunk):
+        return chunk[0] * 2 * wide + chunk[1] * wide
+
+    load_weight = pltpu.make_async_copy(weight_ref, weight, load_sem.at[8])
+    loads = {}
+    for number, chunk in enumerate(chunks):
+        for side in (1, 0):
+            place = pl.ds(side * 4 * wide + where(chunk), wide)
+            loads[side, chunk] = pltpu.make_async_copy(
+                acts_ref.at[place], acts.at[place], load_sem.at[2 * number + side]
+            )
+    loads[1, chunks[0]].start()
+    load_weight.start()
+    for chunk in chunks:
+        for side in (1, 0):
+            if (side, chunk) != (1, chunks[0]):
+                loads[side, chunk].start()
+    if filler:
+        lhs, grad, grad_sem = refs
+        load_lhs = pltpu.make_async_copy(lhs_ref, lhs, load_sem.at[9])
+        load_lhs.start()
+    greet((x_peer, y_peer, c_peer))
+
+    core_copies = {}
+
+    def product(chunk, side, target):
+        loads[side, chunk].wait()
+        place = pl.ds(where(chunk), wide)
+        source = pl.ds(side * 4 * wide + where(chunk), wide)
+
+        def step(cols):
+            target[place, cols] = mm(acts[source, :], weight[cols, :], 1, 1).astype(target.dtype)
+            return 0
+
+        tiled(width, width // 2, step)
+
+    def send_core(chunk):
+        product(chunk, 1, far)
+        number = chunks.index(chunk)
+        place = pl.ds(where(chunk), wide)
+        core_copies[chunk] = pltpu.make_async_remote_copy(
+            src_ref=far.at[place],
+            dst_ref=core_in.at[place],
+            send_sem=send_sem.at[number],
+            recv_sem=recv_sem.at[number],
+            device_id=c_peer,
+            device_id_type=MESH,
+        )
+        core_copies[chunk].start()
+
+    def partial_sum(half, outer, inner):
+        place = pl.ds(where((half, outer)) + inner * rows, rows)
+        return near[place, :] + core_in[place, :].astype(F32)
+
+    def link(index, value, peer):
+        link_out[index] = value.astype(BF16)
+        copy = pltpu.make_async_remote_copy(
+            src_ref=link_out.at[index],
+            dst_ref=link_in.at[index],
+            send_sem=send_sem.at[4 + index],
+            recv_sem=recv_sem.at[4 + index],
+            device_id=peer,
+            device_id_type=MESH,
+        )
+        copy.start()
+        return copy
+
+    load_weight.wait()
+    send_core((0, 1))
+    product((0, 1), 0, near)
+    core_copies[0, 1].wait_recv()
+    y11 = link(0, partial_sum(0, 1, 1), y_peer)
+    send_core((1, 1))
+    y10 = link(2, partial_sum(0, 1, 0), y_peer)
+    product((1, 1), 0, near)
+    core_copies[1, 1].wait_recv()
+    x11 = link(1, partial_sum(1, 1, 1), x_peer)
+    x10 = link(3, partial_sum(1, 1, 0), x_peer)
+    send_core((0, 0))
+    product((0, 0), 0, near)
+    send_core((1, 0))
+    product((1, 0), 0, near)
+    core_copies[0, 0].wait_recv()
+    core_copies[1, 0].wait_recv()
+    grad_copies = []
+    parts = grad_sem.shape[0] if filler else 0
+
+    def fill(index):
+        size = width // parts
+        cols = pl.ds(index * size, size)
+
+        def step(columns):
+            grad[cols, columns] = mm(lhs[:, cols], acts[:, columns], 0, 0).astype(BF16)
+            return 0
+
+        tiled(acts.shape[1], acts.shape[1] // 3, step)
+        copy = pltpu.make_async_copy(grad.at[cols], grad_ref.at[cols], grad_sem.at[index])
+        copy.start()
+        grad_copies.append(copy)
+
+    if filler:
+        load_lhs.wait()
+    y11.wait_recv()
+    x01 = link(4, partial_sum(0, 0, 1) + link_in[0].astype(F32), x_peer)
+    if filler:
+        fill(0)
+    x11.wait_recv()
+    y01 = link(5, partial_sum(1, 0, 1) + link_in[1].astype(F32), y_peer)
+    for index in range(1, parts):
+        fill(index)
+    y10.wait_recv()
+    out_ref[pl.ds(0, rows), :] = partial_sum(0, 0, 0) + link_in[2].astype(F32)
+    x10.wait_recv()
+    out_ref[pl.ds(rows, rows), :] = partial_sum(1, 0, 0) + link_in[3].astype(F32)
+    x01.wait_recv()
+    out_ref[pl.ds(0, rows), :] += link_in[4].astype(F32)
+    y01.wait_recv()
+    out_ref[pl.ds(rows, rows), :] += link_in[5].astype(F32)
+    for copy in (y11, x11, y10, x10, x01, y01):
+        copy.wait_send()
+    for copy in core_copies.values():
+        copy.wait_send()
+    for copy in grad_copies:
+        copy.wait()
+
+
+def product_reduce8(acts, weight, number, lhs=None):
+    rows, width, depth = acts.shape[0] // 16, weight.shape[0], weight.shape[1]
+    filler = lhs is not None
+    hbm = pl.BlockSpec(memory_space=pl.ANY)
+    parts = 4
+    scratch = [
+        pltpu.VMEM(acts.shape, BF16),
+        pltpu.VMEM(weight.shape, BF16),
+        pltpu.VMEM((8 * rows, width), BF16),
+        pltpu.VMEM((8 * rows, width), F32),
+        pltpu.VMEM((8 * rows, width), BF16),
+        pltpu.VMEM((6, rows, width), BF16),
+        pltpu.VMEM((6, rows, width), BF16),
+        pltpu.SemaphoreType.DMA((10,)),
+        pltpu.SemaphoreType.DMA((10,)),
+        pltpu.SemaphoreType.DMA((10,)),
+    ]
+    out_shape = [jax.ShapeDtypeStruct((2 * rows, width), F32)]
+    out_specs = [pl.BlockSpec(memory_space=pltpu.VMEM)]
+    flops = 2 * acts.shape[0] * width * depth
+    if filler:
+        scratch += [
+            pltpu.VMEM(lhs.shape, BF16),
+            pltpu.VMEM((width, depth), BF16),
+            pltpu.SemaphoreType.DMA((parts,)),
+        ]
+        out_shape.append(jax.ShapeDtypeStruct((width, depth), BF16))
+        out_specs.append(hbm)
+        flops *= 2
+    outs = pl.pallas_call(
+        functools.partial(product_reduce8_kernel, rows, filler),
+        out_shape=out_shape,
+        in_specs=[hbm] * (3 if filler else 2),
+        out_specs=out_specs,
+        scratch_shapes=scratch,
+        compiler_params=remote_params(number, 63 * 1024 * 1024),
+        cost_estimate=pl.CostEstimate(
+            flops=flops, bytes_accessed=4 * (acts.size + weight.size), transcendentals=0
+        ),
+        name="product_reduce8",
+    )(acts, weight, *((lhs,) if filler else ()))
+    return outs if filler else outs[0]
+
+
 def shard_kernel(plan, outs, *refs):
     ins, out_refs = refs[: len(plan)], refs[len(plan) : len(plan) + outs]
     stage = refs[len(plan) + outs : 2 * len(plan) + outs]
@@ -401,11 +745,11 @@
 
 
 def total(part):
-    stages = [("tp", 1), ("ctx", 1)]
-    bit = 1
+    stages, bit = [], 2
     while bit < lax.axis_size("fsdp"):
         stages.append(("fsdp", bit))
         bit *= 2
+    stages += [("tp", 1), ("fsdp", 1), ("ctx", 1)]
     return pl.pallas_call(
         functools.partial(total_kernel, tuple(stages)),
         out_shape=jax.ShapeDtypeStruct(part.shape, F32),
@@ -460,13 +804,11 @@
     return lax.optimization_barrier((value,) + others)[0]
 
 
-def reduce4_links(total_rows, *others):
-    rows = total_rows.shape[0] // 8
-    first, second = total_rows[: 4 * rows], total_rows[4 * rows :]
-    came_first = swap_ctx(first[2 * rows :].astype(BF16))
-    came_second = swap_x(second[2 * rows :].astype(BF16))
-    first = first[: 2 * rows] + after(came_first, *others).astype(F32)
-    second = second[: 2 * rows] + after(came_second, *others).astype(F32)
+def reduce4_links(kept, to_y, to_x, *others):
+    rows = kept.shape[0] // 4
+    came_first, came_second = swap_ctx(to_y), swap_x(to_x)
+    first = kept[: 2 * rows] + after(came_first, *others).astype(F32)
+    second = kept[2 * rows :] + after(came_second, *others).astype(F32)
     came_first = swap_x(first[rows:].astype(BF16))
     came_second = swap_ctx(second[rows:].astype(BF16))
     return first[:rows], second[:rows], came_first, came_second
@@ -835,28 +1177,21 @@
     grad_up = (grad_hidden * active).astype(BF16)
     grad_gate = (grad_hidden * up_value * (sig * (1.0 + gate * (1.0 - sig)))).astype(BF16)
     grad_gate_up = jnp.concatenate([grad_gate, grad_up], axis=1)
-    gate_up_grad = mm(y_all, grad_gate_up, 0, 0).astype(BF16)
-    mid_near = mm(grad_gate_up[:half], gate_up_w, 1, 1)
-    mid_far = mm(grad_gate_up[half:], gate_up_w, 1, 1).astype(BF16)
-    mid_grad = reduce8(mid_near, after(mid_far, gate_up_grad))
+    mid_grad, gate_up_grad = product_reduce8(grad_gate_up, gate_up_w, 7, y_all)
 
     mlp_gain_part = jnp.sum(mid_grad * scaled_mid, axis=0)
     grad_middle = own_cot.astype(F32) + norm_back(mid_grad, scaled_mid, inverse_mid, mid_gain)
-    grad_attn = gather8(grad_middle.astype(BF16))
+    grad_attn, mlp_kept, mlp_to_y, mlp_to_x = gather8_product(
+        grad_middle.astype(BF16), hidden, down_w
+    )
     out_grad = mm(grad_attn, attended, 0, 0).astype(BF16)
     grad_att = mm(grad_attn, out_w, 1, 0).astype(BF16)
-    mlp_hidden = after(hidden, grad_attn)
-    mlp_far = mm(mlp_hidden[half:], down_w, 1, 1).astype(BF16)
-    mlp_came = swap_core(mlp_far)
-    mlp_rows = mm(mlp_hidden[:half], down_w, 1, 1) + mlp_came.astype(F32)
     raw_grads, head_gain_parts = attend_back(
-        meta, qkv, after(grad_att, mlp_rows), seg_cols, seg_rows, cosine, sine, head_gains
+        meta, qkv, grad_att, seg_cols, seg_rows, cosine, sine, head_gains
     )
     first_grad = jnp.concatenate([mm(x_all, raw_grads, 0, 0).astype(BF16), out_grad], axis=1)
-    mlp_first, mlp_second, mlp_came1, mlp_came2 = reduce4_links(mlp_rows, raw_grads)
-    in_near = mm(raw_grads[:half], qkv_w, 1, 1)
-    in_far = mm(raw_grads[half:], qkv_w, 1, 1).astype(BF16)
-    in_grad = reduce8(in_near, after(in_far, first_grad))
+    mlp_first, mlp_second, mlp_came1, mlp_came2 = reduce4_links(mlp_kept, mlp_to_y, mlp_to_x, raw_grads)
+    in_grad = product_reduce8(after(raw_grads, first_grad), qkv_w, 8)
 
     mlp_first = mlp_first + after(mlp_came1, in_grad).astype(F32)
     mlp_second = mlp_second + after(mlp_came2, in_grad).astype(F32)

time: 702 us -> 793 us (1.13)
  waiting for transfers between devices: 88.1 us -> 209 us
  matrix products: 143 us -> 81.7 us
  Pallas kernels: 363 us -> 383 us
  other arithmetic: 33.6 us -> 44.4 us
    pallas_call x0 -> x3, Pallas kernels: none -> 139 us  [the longest x2 97.6 us: product_reduce8(): pl.pallas_call(functools.partial(product_reduce8_kernel, rows, filler), o...]
    reduce_scatter x3, waiting for transfers between devices: 0.02 us -> 114 us  [scatter_line(): lax.psum_scatter(value, 'fsdp', scatter_dimension=0, tiled=True, axis_ind...]
    pallas_call x3 -> x1, Pallas kernels: 122 us -> 40.1 us  [reduce8(): pl.pallas_call(functools.partial(reduce8_kernel, rows), out_shape=jax.Sha...]
    dot_general x16 -> x9, matrix products: 143 us -> 81.7 us  [mm(): lax.dot_general(left, right, (((left_dim,), (right_dim,)), ((), ())), pre...]
    pallas_call x3 -> x2, Pallas kernels: 122 us -> 81.6 us  [gather8(): pl.pallas_call(functools.partial(gather8_kernel, rows, bool(also)), out_s...]
    ppermute x10, waiting for transfers between devices: 57.6 us -> 76.7 us  [swap_ctx(): return lax.ppermute(value, 'ctx', [(0, 1), (1, 0)])]
    ppermute x8, waiting for transfers between devices: 30.3 us -> 17.2 us  [swap_x(): return lax.ppermute(value, 'fsdp', [(i, i ^ 1) for i in range(count)])]
  transfers between devices with their start and end apart: 27 -> 26, of which waited for: 9 -> 10; matrix products, arithmetic and copies ran while one was open for 27% -> 12% of each run, Pallas kernels for 49% -> 31%
where the time goes in v3:
time: 793 us; the launch traced here: 784 us
  Pallas kernels  383 us (48%)
  waiting for transfers between devices  209 us (26%)
  matrix products  81.7 us (10%)
  other arithmetic  44.4 us (6%)
  local copies, waits for them, and re-layouts  30.1 us (4%)
  starting transfers between devices  19.5 us (2%)
  between operations  15.3 us (2%)
    reduce_scatter x3, waiting for transfers between devices, scatter_line(): lax.psum_scatter(value, 'fsdp', scatter_dimension=0, tiled=True, axis_ind...  114 us
    pallas_call x2, Pallas kernels, product_reduce8(): pl.pallas_call(functools.partial(product_reduce8_kernel, rows, filler), o...  97.6 us
    dot_general x9, matrix products, mm(): lax.dot_general(left, right, (((left_dim,), (right_dim,)), ((), ())), pre...  81.7 us
    pallas_call x2, Pallas kernels, gather8(): pl.pallas_call(functools.partial(gather8_kernel, rows, bool(also)), out_s...  81.6 us
    ppermute x10, waiting for transfers between devices, swap_ctx(): return lax.ppermute(value, 'ctx', [(0, 1), (1, 0)])  76.7 us
    pallas_call x2, Pallas kernels, shards(): pl.pallas_call(functools.partial(shard_kernel, tuple(plan), len(groups)),...  41.6 us
    pallas_call x1, Pallas kernels, gather8_product(): pl.pallas_call(functools.partial(gather8_product_kernel, rows), out_shape...  41.3 us
    pallas_call x1, Pallas kernels, reduce8(): pl.pallas_call(functools.partial(reduce8_kernel, rows), out_shape=jax.Sha...  40.1 us
  transfers between devices with their start and end apart: 26, of which 10 were waited for; matrix products, arithmetic and copies ran while one was open for 12% of the time, Pallas kernels for 31%

profile of v3, /device:TPU:0, one launch (start us, length us, event | category | flops | bytes accessed | tf_op | source)
XLA Modules:
  0.0 783.7 jit_solution(3508937789519315537)
XLA Ops:
  10.1 14.0 %shards.2 = bf16[512,896]{1,0:T(8,128)(2,1)} custom-call(bf16[256,1024]{1,0:T(8,128)(2,1)} %refs_0_.1, bf16[256,512]{1,0:T(8,128)(2,1)} %refs_1_.2, bf16[256,512]{1,0:T(8,128)(2,1)} %refs_2_.2, bf16[256,1024]{1,0:T(8,128)(2,1)} %refs_3_.1, bf16[256,128]{1,0:T(8,128)(2,1)} %select_select_fusion.refs_4_), custom_call_target="tpu_custom_call" | custom-call | tf_op jit(solution)/shard_map/shards/pallas_call | solution.py:705
  24.1 27.6 %shards.3 = (bf16[512,1536]{1,0:T(8,128)(2,1)}, bf16[512,768]{1,0:T(8,128)(2,1)}) custom-call(bf16[256,3072]{1,0:T(8,128)(2,1)} %refs_0_.2, bf16[256,3072]{1,0:T(8,128)(2,1)} %refs_1_.3, bf16[256,3072]{1,0:T(8,128)(2,1)} %refs_2_.3), custom_call_target="tpu_custom_call" | custom-call | tf_op jit(solution)/shard_map/shards/pallas_call | solution.py:705
  53.6 40.9 %gather8.1 = bf16[2048,2048]{1,0:T(8,128)(2,1)} custom-call(bf16[256,2048]{1,0:T(8,128)(2,1)} %get-tuple-element.46.refs_0_), custom_call_target="tpu_custom_call" | custom-call | tf_op jit(solution)/shard_map/gather8/pallas_call | solution.py:352
  97.6 5.1 fusion
  106.5 13.7 %collective-permute-done = s32[1,1024]{1,0:T(1,128)S(1)} collective-permute-done((s32[1,1024]{1,0:T(1,128)S(1)}, s32[1,1024]{1,0:T(1,128)S(1)}, u32[]{:S(2)}, u32[]{:S(2)}) %collective-permute-start) | collective-permute-done | bytes 4128 | tf_op jit(solution)/shard_map/ppermute | solution.py:38
  125.0 10.6 %fusion.8.qkv_ref = f32[2048,512]{1,0:T(8,128)} fusion(bf16[2048,2048]{1,0:T(8,128)(2,1)} %gather8.1, f32[2048]{0:T(1024)S(1)} %get-tuple-element.80, f32[2048]{0:T(1024)S(1)} %add_rsqrt_fusion, bf16[2048,896]{1,0:T(8,128)(2,1)} %all-gather.4.cloned.1.call-done), kind=kOutput, calls=%fused_computation.25 | convolution fusion | flops 4311744512 | bytes 14696448 | tf_op jit(solution)/shard_map/dot_general | solution.py:23
  135.5 16.5 %attend.1 = bf16[2048,256]{1,0:T(8,128)(2,1)} custom-call(s32[2]{0:T(128)} %pad_add_fusion.1.meta_ref, f32[2048,512]{1,0:T(8,128)} %fusion.8.qkv_ref, s32[2,1024,1]{2,1,0:T(8,128)} %copy.37.segc_ref, s32[2,1,1024]{2,1,0:T(1,128)} %broadcast_in_dim.76.segr_ref, f32[1024,128]{1,0:T(8,128)} %get-tuple-element.108.cos_ref, ...), custom_call_target="tpu_custom_call" | custom-call | flops 1073741824 | bytes 5242880 | tf_op jit(solution)/shard_map/attend/pallas_call | solution.py:1003
  152.1 5.1 convolution_convert_fusion.far_ref
  157.2 5.8 fusion.20.near_ref
  163.1 40.1 %reduce8.1 = f32[256,2048]{1,0:T(8,128)S(1)} custom-call(f32[1024,2048]{1,0:T(8,128)} %fusion.20.near_ref, bf16[1024,2048]{1,0:T(8,128)(2,1)} %convolution_convert_fusion.far_ref), custom_call_target="tpu_custom_call" | custom-call | tf_op jit(solution)/shard_map/reduce8/pallas_call | solution.py:445
  206.2 11.4 %collective-permute-done.3.refs_4_ = bf16[128,2048]{1,0:T(8,128)(2,1)S(1)} collective-permute-done((bf16[128,2048]{1,0:T(8,128)(2,1)S(1)}, bf16[128,2048]{1,0:T(8,128)(2,1)S(1)}, u32[]{:S(2)}, u32[]{:S(2)}) %collective-permute-start.3) | collective-permute-done | bytes 524320 | tf_op jit(solution)/shard_map/ppermute | solution.py:33
  219.3 40.6 %gather8_also.1 = (bf16[2048,2048]{1,0:T(8,128)(2,1)}, bf16[2048,2048]{1,0:T(8,128)(2,1)}) custom-call(bf16[256,2048]{1,0:T(8,128)(2,1)} %multiply_convert_fusion.3.refs_0_, bf16[256,2048]{1,0:T(8,128)(2,1)} %copy-done.14, bf16[256,2048]{1,0:T(8,128)(2,1)} %copy-done.18, bf16[256,2048]{1,0:T(8,128)(2,1)} %copy-done.19, bf16[128,2048]{1,0:T(8,128)(2,1)} %copy-done.25, ...), custom_call_target="tpu_custom_call" | custom-call | tf_op jit(solution)/shard_map/gather8_also/pallas_call | solution.py:352
  260.0 17.6 %fusion.30 = f32[2048,1536]{1,0:T(8,128)S(1)} fusion(bf16[2048,2048]{1,0:T(8,128)(2,1)} %get-tuple-element.53.refs_2_, bf16[2048,1536]{1,0:T(8,128)(2,1)} %all-gather.6.cloned.1.call-done.refs_1_), kind=kOutput, calls=%fused_computation.90 | convolution fusion | flops 12884901888 | bytes 27262976 | tf_op jit(solution)/shard_map/dot_general | solution.py:23
  279.7 4.3 copy-done.7
  286.6 8.5 %convolution_convert_fusion.1 = bf16[2048,768]{1,0:T(8,128)(2,1)} fusion(bf16[2048,2048]{1,0:T(8,128)(2,1)S(1)} %copy-done.38, bf16[2048,768]{1,0:T(8,128)(2,1)S(1)} %multiply_convert_fusion.2.acts_ref), kind=kOutput, calls=%fused_computation.12 | convolution fusion | flops 6444023808 | bytes 14680064 | tf_op jit(solution)/shard_map/dot_general | solution.py:23
  295.1 14.3 %multiply_convert_fusion.1 = (bf16[2048,768]{1,0:T(8,128)(2,1)S(1)}, bf16[2048,768]{1,0:T(8,128)(2,1)S(1)}) fusion(f32[2048,1536]{1,0:T(8,128)} %copy-done.7, bf16[2048,2048]{1,0:T(8,128)(2,1)} %get-tuple-element.54, bf16[2048,768]{1,0:T(8,128)(2,1)} %all-gather.8.cloned.1.call-done.weight_ref), kind=kOutput, calls=%fused_computation.7 | convolution fusion | flops 6462898176 | bytes 30408704 | tf_op jit(solution)/shard_map/dot_general | solution.py:23
  309.4 3.1 pad_maximum_fusion.refs_0_
  312.6 50.1 %product_reduce8.2 = (f32[256,2048]{1,0:T(8,128)}, bf16[2048,1536]{1,0:T(8,128)(2,1)}) custom-call(bf16[2048,1536]{1,0:T(8,128)(2,1)} %pad_maximum_fusion.refs_0_, bf16[2048,1536]{1,0:T(8,128)(2,1)} %all-gather.6.cloned.1.call-done.refs_1_, bf16[2048,2048]{1,0:T(8,128)(2,1)} %get-tuple-element.53.refs_2_), custom_call_target="tpu_custom_call" | custom-call | flops 25769803776 | bytes 25165824 | tf_op jit(solution)/shard_map/product_reduce8/pallas_call | solution.py:634
  368.1 41.3 %gather8_product.1 = (bf16[2048,2048]{1,0:T(8,128)(2,1)}, f32[512,2048]{1,0:T(8,128)}, bf16[256,2048]{1,0:T(8,128)(2,1)S(1)}, bf16[256,2048]{1,0:T(8,128)(2,1)S(1)}) custom-call(bf16[256,2048]{1,0:T(8,128)(2,1)S(1)} %fusion.27.own_ref, bf16[2048,768]{1,0:T(8,128)(2,1)} %copy-done.17, bf16[2048,768]{1,0:T(8,128)(2,1)} %all-gather.8.cloned.1.call-done.weight_ref), custom_call_target="tpu_custom_call" | custom-call | flops 6442450944 | bytes 8388608 | tf_op jit(solution)/shard_map/gather8_product/pallas_call | solution.py:311
  409.4 6.0 convolution_convert_fusion.3
  415.5 4.5 convolution_convert_fusion.4.grad_ref
  420.0 28.5 %attend_back.1 = (bf16[2048,512]{1,0:T(8,128)(2,1)}, f32[2,128]{1,0:T(2,128)}) custom-call(s32[2]{0:T(128)} %pad_add_fusion.1.meta_ref, f32[2048,512]{1,0:T(8,128)} %fusion.8.qkv_ref, bf16[2048,256]{1,0:T(8,128)(2,1)} %convolution_convert_fusion.4.grad_ref, s32[2,1024,1]{2,1,0:T(8,128)} %copy.37.segc_ref, s32[2,1,1024]{2,1,0:T(1,128)} %broadcast_in_dim.76.segr_ref, ...), custom_call_target="tpu_custom_call" | custom-call | flops 2684354560 | bytes 8388608 | tf_op jit(solution)/shard_map/attend_back/pallas_call | solution.py:1031
  448.6 9.2 %convolution_convert_fusion.2 = bf16[2048,512]{1,0:T(8,128)(2,1)S(1)} fusion(bf16[2048,512]{1,0:T(8,128)(2,1)} %get-tuple-element.62.refs_0_, bf16[2048,2048]{1,0:T(8,128)(2,1)} %gather8.1, f32[2048]{0:T(1024)S(1)} %copy-done.32, f32[2048]{0:T(1024)S(1)} %copy-done.34), kind=kOutput, calls=%fused_computation.19 | convolution fusion | flops 4312793088 | bytes 12599296 | tf_op jit(solution)/shard_map/dot_general | solution.py:23
  466.0 20.3 %collective-permute-done.5 = bf16[256,2048]{1,0:T(8,128)(2,1)S(1)} collective-permute-done((bf16[256,2048]{1,0:T(8,128)(2,1)S(1)}, bf16[256,2048]{1,0:T(8,128)(2,1)S(1)}, u32[]{:S(2)}, u32[]{:S(2)}) %collective-permute-start.5) | collective-permute-done | bytes 1048608 | tf_op jit(solution)/shard_map/ppermute | solution.py:33
  491.9 47.5 %product_reduce8.3 = f32[256,2048]{1,0:T(8,128)} custom-call(bf16[2048,512]{1,0:T(8,128)(2,1)} %get-tuple-element.62.refs_0_, bf16[2048,512]{1,0:T(8,128)(2,1)} %slice.76.refs_1_), custom_call_target="tpu_custom_call" | custom-call | flops 4294967296 | bytes 8388608 | tf_op jit(solution)/shard_map/product_reduce8/pallas_call | solution.py:634
  549.6 21.2 %total.1 = f32[34,128]{1,0:T(8,128)} custom-call(f32[34,128]{1,0:T(8,128)} %maximum_bitcast_fusion.part_ref), custom_call_target="tpu_custom_call" | custom-call | tf_op jit(solution)/shard_map/total/pallas_call | solution.py:753
  576.5 57.8 %reduce-scatter.6.cloned.1.call-done = bf16[512,1536]{1,0:T(8,128)(2,1)} async-done(((bf16[2048,1536]{1,0:T(8,128)(2,1)}), bf16[512,1536]{1,0:T(8,128)(2,1)}) %reduce-scatter.6.cloned.1.call-update) | async-done | bytes 1572880 | tf_op jit(solution)/shard_map/reduce_scatter | solution.py:51
  641.4 56.5 %reduce-scatter.8.cloned.1.call-done = bf16[512,768]{1,0:T(8,128)(2,1)} async-done(((bf16[2048,768]{1,0:T(8,128)(2,1)}), bf16[512,768]{1,0:T(8,128)(2,1)}) %reduce-scatter.8.cloned.1.call-update) | async-done | bytes 786448 | tf_op jit(solution)/shard_map/reduce_scatter | solution.py:51
  713.0 43.8 %collective-permute-done.13.both_ref = bf16[256,768]{1,0:T(8,128)(2,1)S(1)} collective-permute-done((bf16[256,768]{1,0:T(8,128)(2,1)}, bf16[256,768]{1,0:T(8,128)(2,1)S(1)}, u32[]{:S(2)}, u32[]{:S(2)}) %collective-permute-start.13) | collective-permute-done | bytes 393248 | tf_op jit(solution)/shard_map/ppermute | solution.py:33
  757.6 4.6 join.3
  764.2 4.6 join.5
  770.6 5.8 join.4
  (182 shorter events, 87.4 us)
Async XLA Ops:
  7.2 115.0 %all-gather.4.cloned.1.call-start = ((), (), s32[]{:S(2)}) async-start(), calls=%async_computation.3 | async-start | bytes 4587520 | tf_op jit(solution)/shard_map/all_gather | solution.py:47
  24.1 235.9 %all-gather.6.cloned.1.call-start = ((), (), s32[]{:S(2)}) async-start(), calls=%async_computation.4 | async-start | bytes 7864320 | tf_op jit(solution)/shard_map/all_gather | solution.py:47
  51.8 243.4 %all-gather.8.cloned.1.call-start = ((), (), s32[]{:S(2)}) async-start(), calls=%async_computation.5 | async-start | bytes 3932160 | tf_op jit(solution)/shard_map/all_gather | solution.py:47
  53.6 41.0 %copy-start.13 = (bf16[1,512,2048]{2,1,0:T(8,128)(2,1)S(1)}, bf16[1,512,2048]{2,1,0:T(8,128)(2,1)}, u32[]{:S(2)}) copy-start(bf16[1,512,2048]{2,1,0:T(8,128)(2,1)} %param.27) | copy-start | bytes 6291460
  53.6 43.2 %copy-start.36 = (s32[1,1024]{1,0:T(1,128)S(1)}, s32[1,1024]{1,0:T(1,128)}, u32[]{:S(2)}) copy-start(s32[1,1024]{1,0:T(1,128)} %param.15) | copy-start | bytes 12292
  94.7 57.4 %collective-permute-start.1 = (bf16[256,2048]{1,0:T(8,128)(2,1)S(1)}, bf16[256,2048]{1,0:T(8,128)(2,1)S(1)}, u32[]{:S(2)}, u32[]{:S(2)}) collective-permute-start(bf16[256,2048]{1,0:T(8,128)(2,1)S(1)} %dynamic-slice_bitcast_fusion.refs_1_), channel_id=1, source_target_pairs={{0,4},{4,0},{8,12},{12,8},{16,20},{20,16},{24,28},{28,24},{1,5},{5... | collective-permute-start | bytes 3145736 | tf_op jit(solution)/shard_map/ppermute | solution.py:38
  96.2 107.3 %collective-permute-start.2 = (bf16[256,2048]{1,0:T(8,128)(2,1)S(1)}, bf16[256,2048]{1,0:T(8,128)(2,1)S(1)}, u32[]{:S(2)}, u32[]{:S(2)}) collective-permute-start(bf16[256,2048]{1,0:T(8,128)(2,1)S(1)} %dynamic-slice_bitcast_fusion.refs_1_), channel_id=1, source_target_pairs={{0,2},{2,0},{1,3},{3,1},{4,6},{6,4},{5,7},{7,5},{8,10},{10,8},{9,1... | collective-permute-start | bytes 3145736 | tf_op jit(solution)/shard_map/ppermute | solution.py:33
  96.7 23.5 %collective-permute-start = (s32[1,1024]{1,0:T(1,128)S(1)}, s32[1,1024]{1,0:T(1,128)S(1)}, u32[]{:S(2)}, u32[]{:S(2)}) collective-permute-start(s32[1,1024]{1,0:T(1,128)S(1)} %copy-done.36), channel_id=1, source_target_pairs={{0,4},{4,0},{8,12},{12,8},{16,20},{20,16},{24,28},{28,24},{1,5},{5... | collective-permute-start | bytes 12296 | tf_op jit(solution)/shard_map/ppermute | solution.py:38
  97.5 478.9 %reduce-scatter.4.cloned.1.call-start = ((), (), s32[]{:S(2)}) async-start(), calls=%async_computation.6 | async-start | bytes 3932160 | tf_op jit(solution)/shard_map/reduce_scatter | solution.py:51
  152.1 51.5 %copy-start.18 = (bf16[256,2048]{1,0:T(8,128)(2,1)}, bf16[256,2048]{1,0:T(8,128)(2,1)S(1)}, u32[]{:S(2)}) copy-start(bf16[256,2048]{1,0:T(8,128)(2,1)S(1)} %collective-permute-done.1.refs_2_) | copy-start | bytes 3145732
  163.1 40.1 %copy-start.3 = (bf16[256,2048]{1,0:T(8,128)(2,1)S(1)}, bf16[256,2048]{1,0:T(8,128)(2,1)}, u32[]{:S(2)}) copy-start(bf16[256,2048]{1,0:T(8,128)(2,1)} %get-tuple-element.46.refs_0_) | copy-start | bytes 3145732
  203.6 14.0 %collective-permute-start.3 = (bf16[128,2048]{1,0:T(8,128)(2,1)S(1)}, bf16[128,2048]{1,0:T(8,128)(2,1)S(1)}, u32[]{:S(2)}, u32[]{:S(2)}) collective-permute-start(bf16[128,2048]{1,0:T(8,128)(2,1)S(1)} %slice.64), channel_id=1, source_target_pairs={{0,2},{2,0},{1,3},{3,1},{4,6},{6,4},{5,7},{7,5},{8,10},{10,8},{9,1... | collective-permute-start | bytes 1572872 | tf_op jit(solution)/shard_map/ppermute | solution.py:33
  204.2 14.3 %collective-permute-start.4 = (bf16[128,2048]{1,0:T(8,128)(2,1)S(1)}, bf16[128,2048]{1,0:T(8,128)(2,1)S(1)}, u32[]{:S(2)}, u32[]{:S(2)}) collective-permute-start(bf16[128,2048]{1,0:T(8,128)(2,1)S(1)} %slice.65), channel_id=1, source_target_pairs={{0,4},{4,0},{8,12},{12,8},{16,20},{20,16},{24,28},{28,24},{1,5},{5... | collective-permute-start | bytes 1572872 | tf_op jit(solution)/shard_map/ppermute | solution.py:38
  368.1 41.3 %copy-start.10 = (bf16[2048,256]{1,0:T(8,128)(2,1)S(1)}, bf16[2048,256]{1,0:T(8,128)(2,1)}, u32[]{:S(2)}) copy-start(bf16[2048,256]{1,0:T(8,128)(2,1)} %attend.1) | copy-start | bytes 3145732
  420.0 28.5 %copy-start.34 = (f32[2048]{0:T(1024)S(1)}, f32[2048]{0:T(1024)}, u32[]{:S(2)}) copy-start(f32[2048]{0:T(1024)} %copy-done.33) | copy-start | bytes 24580
  459.7 174.6 %reduce-scatter.6.cloned.1.call-start = ((), (), s32[]{:S(2)}) async-start(), calls=%async_computation.7 | async-start | bytes 7864320 | tf_op jit(solution)/shard_map/reduce_scatter | solution.py:51
  460.3 237.7 %reduce-scatter.8.cloned.1.call-start = ((), (), s32[]{:S(2)}) async-start(), calls=%async_computation.8 | async-start | bytes 3932160 | tf_op jit(solution)/shard_map/reduce_scatter | solution.py:51
  460.9 25.5 %collective-permute-start.5 = (bf16[256,2048]{1,0:T(8,128)(2,1)S(1)}, bf16[256,2048]{1,0:T(8,128)(2,1)S(1)}, u32[]{:S(2)}, u32[]{:S(2)}) collective-permute-start(bf16[256,2048]{1,0:T(8,128)(2,1)S(1)} %get-tuple-element.58), channel_id=1, source_target_pairs={{0,2},{2,0},{1,3},{3,1},{4,6},{6,4},{5,7},{7,5},{8,10},{10,8},{9,1... | collective-permute-start | bytes 3145736 | tf_op jit(solution)/shard_map/ppermute | solution.py:33
  461.9 25.2 %collective-permute-start.7 = (bf16[256,2048]{1,0:T(8,128)(2,1)S(1)}, bf16[256,2048]{1,0:T(8,128)(2,1)S(1)}, u32[]{:S(2)}, u32[]{:S(2)}) collective-permute-start(bf16[256,2048]{1,0:T(8,128)(2,1)S(1)} %get-tuple-element.64), channel_id=1, source_target_pairs={{0,4},{4,0},{8,12},{12,8},{16,20},{20,16},{24,28},{28,24},{1,5},{5... | collective-permute-start | bytes 3145736 | tf_op jit(solution)/shard_map/ppermute | solution.py:38
  489.0 53.2 %collective-permute-start.8 = (bf16[128,2048]{1,0:T(8,128)(2,1)}, bf16[128,2048]{1,0:T(8,128)(2,1)S(1)}, u32[]{:S(2)}, u32[]{:S(2)}) collective-permute-start(bf16[128,2048]{1,0:T(8,128)(2,1)} %slice.117), channel_id=1, source_target_pairs={{0,2},{2,0},{1,3},{3,1},{4,6},{6,4},{5,7},{7,5},{8,10},{10,8},{9,1... | collective-permute-start | bytes 1572872 | tf_op jit(solution)/shard_map/ppermute | solution.py:33
  490.8 51.4 %collective-permute-start.6 = (bf16[128,2048]{1,0:T(8,128)(2,1)}, bf16[128,2048]{1,0:T(8,128)(2,1)}, u32[]{:S(2)}, u32[]{:S(2)}) collective-permute-start(bf16[128,2048]{1,0:T(8,128)(2,1)} %slice.118), channel_id=1, source_target_pairs={{0,4},{4,0},{8,12},{12,8},{16,20},{20,16},{24,28},{28,24},{1,5},{5... | collective-permute-start | bytes 1572872 | tf_op jit(solution)/shard_map/ppermute | solution.py:38
  548.1 25.7 %collective-permute-start.9 = (bf16[256,2048]{1,0:T(8,128)(2,1)S(1)}, bf16[256,2048]{1,0:T(8,128)(2,1)S(1)}, u32[]{:S(2)}, u32[]{:S(2)}) collective-permute-start(bf16[256,2048]{1,0:T(8,128)(2,1)S(1)} %get-tuple-element.90), channel_id=1, source_target_pairs={{0,1},{1,0},{2,3},{3,2},{4,5},{5,4},{6,7},{7,6},{8,9},{9,8},{10,11... | collective-permute-start | bytes 3145736 | tf_op jit(solution)/shard_map/ppermute | solution.py:29
  573.5 129.0 %collective-permute-start.10 = (bf16[256,2048]{1,0:T(8,128)(2,1)S(1)}, bf16[256,2048]{1,0:T(8,128)(2,1)}, u32[]{:S(2)}, u32[]{:S(2)}) collective-permute-start(bf16[256,2048]{1,0:T(8,128)(2,1)S(1)} %get-tuple-element.89), channel_id=1, source_target_pairs={{0,1},{1,0},{2,3},{3,2},{4,5},{5,4},{6,7},{7,6},{8,9},{9,8},{10,11... | collective-permute-start | bytes 3145736 | tf_op jit(solution)/shard_map/ppermute | solution.py:29
  637.0 67.0 %collective-permute-start.14 = (bf16[256,1536]{1,0:T(8,128)(2,1)}, bf16[256,1536]{1,0:T(8,128)(2,1)}, u32[]{:S(2)}, u32[]{:S(2)}) collective-permute-start(bf16[256,1536]{1,0:T(8,128)(2,1)} %get-tuple-element.91), channel_id=1, source_target_pairs={{0,4},{4,0},{8,12},{12,8},{16,20},{20,16},{24,28},{28,24},{1,5},{5... | collective-permute-start | bytes 2359304 | tf_op jit(solution)/shard_map/ppermute | solution.py:38
  639.4 66.5 %collective-permute-start.11 = (bf16[256,768]{1,0:T(8,128)(2,1)}, bf16[256,768]{1,0:T(8,128)(2,1)}, u32[]{:S(2)}, u32[]{:S(2)}) collective-permute-start(bf16[256,768]{1,0:T(8,128)(2,1)} %get-tuple-element.95), channel_id=1, source_target_pairs={{0,4},{4,0},{8,12},{12,8},{16,20},{20,16},{24,28},{28,24},{1,5},{5... | collective-permute-start | bytes 1179656 | tf_op jit(solution)/shard_map/ppermute | solution.py:38
  639.9 67.5 %collective-permute-start.12 = (bf16[256,768]{1,0:T(8,128)(2,1)}, bf16[256,768]{1,0:T(8,128)(2,1)}, u32[]{:S(2)}, u32[]{:S(2)}) collective-permute-start(bf16[256,768]{1,0:T(8,128)(2,1)} %get-tuple-element.96.kept_ref), channel_id=1, source_target_pairs={{0,2},{2,0},{1,3},{3,1},{4,6},{6,4},{5,7},{7,5},{8,10},{10,8},{9,1... | collective-permute-start | bytes 1179656 | tf_op jit(solution)/shard_map/ppermute | solution.py:33
  699.2 10.6 %collective-permute-start.17 = (bf16[256,768]{1,0:T(8,128)(2,1)S(1)}, bf16[256,768]{1,0:T(8,128)(2,1)}, u32[]{:S(2)}, u32[]{:S(2)}) collective-permute-start(bf16[256,768]{1,0:T(8,128)(2,1)S(1)} %get-tuple-element.93), channel_id=1, source_target_pairs={{0,4},{4,0},{8,12},{12,8},{16,20},{20,16},{24,28},{28,24},{1,5},{5... | collective-permute-start | bytes 1179656 | tf_op jit(solution)/shard_map/ppermute | solution.py:38
  702.5 66.4 %collective-permute-start.15 = (bf16[256,1536]{1,0:T(8,128)(2,1)}, bf16[256,1536]{1,0:T(8,128)(2,1)S(1)}, u32[]{:S(2)}, u32[]{:S(2)}) collective-permute-start(bf16[256,1536]{1,0:T(8,128)(2,1)} %get-tuple-element.92.kept_ref), channel_id=1, source_target_pairs={{0,2},{2,0},{1,3},{3,1},{4,6},{6,4},{5,7},{7,5},{8,10},{10,8},{9,1... | collective-permute-start | bytes 2359304 | tf_op jit(solution)/shard_map/ppermute | solution.py:33
  703.9 64.9 %collective-permute-start.16 = (bf16[256,1536]{1,0:T(8,128)(2,1)}, bf16[256,1536]{1,0:T(8,128)(2,1)S(1)}, u32[]{:S(2)}, u32[]{:S(2)}) collective-permute-start(bf16[256,1536]{1,0:T(8,128)(2,1)} %collective-permute-done.14.x_ref), channel_id=1, source_target_pairs={{0,2},{2,0},{1,3},{3,1},{4,6},{6,4},{5,7},{7,5},{8,10},{10,8},{9,1... | collective-permute-start | bytes 2359304 | tf_op jit(solution)/shard_map/ppermute | solution.py:33
  705.9 56.2 %collective-permute-start.18 = (bf16[256,768]{1,0:T(8,128)(2,1)S(1)}, bf16[256,768]{1,0:T(8,128)(2,1)S(1)}, u32[]{:S(2)}, u32[]{:S(2)}) collective-permute-start(bf16[256,768]{1,0:T(8,128)(2,1)S(1)} %get-tuple-element.94.kept_ref), channel_id=1, source_target_pairs={{0,2},{2,0},{1,3},{3,1},{4,6},{6,4},{5,7},{7,5},{8,10},{10,8},{9,1... | collective-permute-start | bytes 1179656 | tf_op jit(solution)/shard_map/ppermute | solution.py:33
  707.5 49.3 %collective-permute-start.13 = (bf16[256,768]{1,0:T(8,128)(2,1)}, bf16[256,768]{1,0:T(8,128)(2,1)S(1)}, u32[]{:S(2)}, u32[]{:S(2)}) collective-permute-start(bf16[256,768]{1,0:T(8,128)(2,1)} %collective-permute-done.11.x_ref), channel_id=1, source_target_pairs={{0,2},{2,0},{1,3},{3,1},{4,6},{6,4},{5,7},{7,5},{8,10},{10,8},{9,1... | collective-permute-start | bytes 1179656 | tf_op jit(solution)/shard_map/ppermute | solution.py:33
  709.8 53.7 %collective-permute-start.19 = (bf16[256,768]{1,0:T(8,128)(2,1)}, bf16[256,768]{1,0:T(8,128)(2,1)S(1)}, u32[]{:S(2)}, u32[]{:S(2)}) collective-permute-start(bf16[256,768]{1,0:T(8,128)(2,1)} %collective-permute-done.17.x_ref), channel_id=1, source_target_pairs={{0,2},{2,0},{1,3},{3,1},{4,6},{6,4},{5,7},{7,5},{8,10},{10,8},{9,1... | collective-permute-start | bytes 1179656 | tf_op jit(solution)/shard_map/ppermute | solution.py:33
  (34 other events, 246.5 us)
Sparse Core Ops, SparseCore 0:
  24.2 73.5 all-gather.3
  99.4 113.8 all-gather.5
  214.9 61.6 all-gather.7
  459.8 60.8 reduce-scatter.3
  522.8 111.4 reduce-scatter.5
  637.0 60.9 reduce-scatter.7

commit v4 on v3

--- a/solution.py
+++ b/solution.py
@@ -465,11 +465,12 @@
     lax.fori_loop(0, count // tile, lambda i, _: step(pl.ds(pl.multiple_of(i * tile, tile), tile)), 0)
 
 
-def product_reduce8_kernel(rows, filler, *refs):
+def product_reduce8_kernel(rows, groups, filler, *refs):
+    acts_refs, refs = refs[:groups], refs[groups:]
     if filler:
-        acts_ref, weight_ref, lhs_ref, out_ref, grad_ref, *refs = refs
+        weight_ref, lhs_ref, out_ref, grad_ref, *refs = refs
     else:
-        acts_ref, weight_ref, out_ref, *refs = refs
+        weight_ref, out_ref, *refs = refs
     acts, weight, far, near, core_in, link_in, link_out, send_sem, recv_sem, load_sem, *refs = refs
     x_peer, y_peer, c_peer = neighbours()
     width = weight.shape[0]
@@ -481,18 +482,26 @@
 
     load_weight = pltpu.make_async_copy(weight_ref, weight, load_sem.at[8])
     loads = {}
+    depth = weight.shape[1] // groups
     for number, chunk in enumerate(chunks):
         for side in (1, 0):
             place = pl.ds(side * 4 * wide + where(chunk), wide)
-            loads[side, chunk] = pltpu.make_async_copy(
-                acts_ref.at[place], acts.at[place], load_sem.at[2 * number + side]
-            )
-    loads[1, chunks[0]].start()
+            loads[side, chunk] = [
+                pltpu.make_async_copy(
+                    acts_refs[group].at[place],
+                    acts.at[place, pl.ds(group * depth, depth)],
+                    load_sem.at[10 + (2 * number + side) * groups + group],
+                )
+                for group in range(groups)
+            ]
+    for copy in loads[1, chunks[0]]:
+        copy.start()
     load_weight.start()
     for chunk in chunks:
         for side in (1, 0):
             if (side, chunk) != (1, chunks[0]):
-                loads[side, chunk].start()
+                for copy in loads[side, chunk]:
+                    copy.start()
     if filler:
         lhs, grad, grad_sem = refs
         load_lhs = pltpu.make_async_copy(lhs_ref, lhs, load_sem.at[9])
@@ -502,7 +511,8 @@
     core_copies = {}
 
     def product(chunk, side, target):
-        loads[side, chunk].wait()
+        for copy in loads[side, chunk]:
+            copy.wait()
         place = pl.ds(where(chunk), wide)
         source = pl.ds(side * 4 * wide + where(chunk), wide)
 
@@ -602,8 +612,10 @@
         copy.wait()
 
 
-def product_reduce8(acts, weight, number, lhs=None):
+def product_reduce8(columns, weight, number, lhs=None):
+    acts = jax.ShapeDtypeStruct((columns[0].shape[0], weight.shape[1]), BF16)
     rows, width, depth = acts.shape[0] // 16, weight.shape[0], weight.shape[1]
+    groups = len(columns)
     filler = lhs is not None
     hbm = pl.BlockSpec(memory_space=pl.ANY)
     parts = 4
@@ -617,7 +629,7 @@
         pltpu.VMEM((6, rows, width), BF16),
         pltpu.SemaphoreType.DMA((10,)),
         pltpu.SemaphoreType.DMA((10,)),
-        pltpu.SemaphoreType.DMA((10,)),
+        pltpu.SemaphoreType.DMA((10 + 8 * groups,)),
     ]
     out_shape = [jax.ShapeDtypeStruct((2 * rows, width), F32)]
     out_specs = [pl.BlockSpec(memory_space=pltpu.VMEM)]
@@ -632,9 +644,9 @@
         out_specs.append(hbm)
         flops *= 2
     outs = pl.pallas_call(
-        functools.partial(product_reduce8_kernel, rows, filler),
+        functools.partial(product_reduce8_kernel, rows, groups, filler),
         out_shape=out_shape,
-        in_specs=[hbm] * (3 if filler else 2),
+        in_specs=[hbm] * (groups + (2 if filler else 1)),
         out_specs=out_specs,
         scratch_shapes=scratch,
         compiler_params=remote_params(number, 63 * 1024 * 1024),
@@ -642,7 +654,7 @@
             flops=flops, bytes_accessed=4 * (acts.size + weight.size), transcendentals=0
         ),
         name="product_reduce8",
-    )(acts, weight, *((lhs,) if filler else ()))
+    )(*columns, weight, *((lhs,) if filler else ()))
     return outs if filler else outs[0]
 
 
@@ -1176,8 +1188,7 @@
     grad_hidden = mm(after(cot, down_grad), down_w, 1, 0)
     grad_up = (grad_hidden * active).astype(BF16)
     grad_gate = (grad_hidden * up_value * (sig * (1.0 + gate * (1.0 - sig)))).astype(BF16)
-    grad_gate_up = jnp.concatenate([grad_gate, grad_up], axis=1)
-    mid_grad, gate_up_grad = product_reduce8(grad_gate_up, gate_up_w, 7, y_all)
+    mid_grad, gate_up_grad = product_reduce8((grad_gate, grad_up), gate_up_w, 7, y_all)
 
     mlp_gain_part = jnp.sum(mid_grad * scaled_mid, axis=0)
     grad_middle = own_cot.astype(F32) + norm_back(mid_grad, scaled_mid, inverse_mid, mid_gain)
@@ -1189,13 +1200,16 @@
     raw_grads, head_gain_parts = attend_back(
         meta, qkv, grad_att, seg_cols, seg_rows, cosine, sine, head_gains
     )
-    first_grad = jnp.concatenate([mm(x_all, raw_grads, 0, 0).astype(BF16), out_grad], axis=1)
-    mlp_first, mlp_second, mlp_came1, mlp_came2 = reduce4_links(mlp_kept, mlp_to_y, mlp_to_x, raw_grads)
-    in_grad = product_reduce8(after(raw_grads, first_grad), qkv_w, 8)
-
-    mlp_first = mlp_first + after(mlp_came1, in_grad).astype(F32)
-    mlp_second = mlp_second + after(mlp_came2, in_grad).astype(F32)
-    layer_out = finish_rows((middle + jnp.concatenate([mlp_first, mlp_second])).astype(BF16))
+    mlp_first, mlp_second, mlp_came1, mlp_came2 = reduce4_links(
+        mlp_kept, mlp_to_y, mlp_to_x, raw_grads
+    )
+    first_grad = mm(x_all, raw_grads, 0, 0).astype(BF16)
+    first_grad = jnp.concatenate([first_grad, out_grad], axis=1)
+    mlp_first = mlp_first + after(mlp_came1, first_grad).astype(F32)
+    mlp_second = mlp_second + after(mlp_came2, first_grad).astype(F32)
+    mlp_sum = (middle + jnp.concatenate([mlp_first, mlp_second])).astype(BF16)
+    layer_out = finish_rows(mlp_sum)
+    in_grad = product_reduce8((after(raw_grads, first_grad, mlp_sum),), qkv_w, 8)
 
     spot = jnp.stack([place, odd]).astype(jnp.int32)
 

time: 793 us -> 791 us (level)
    ppermute x10, waiting for transfers between devices: 76.7 us -> 86.3 us  [swap_ctx(): return lax.ppermute(value, 'ctx', [(0, 1), (1, 0)])]
    reduce_scatter x3, waiting for transfers between devices: 114 us -> 106 us  [scatter_line(): lax.psum_scatter(value, 'fsdp', scatter_dimension=0, tiled=True, axis_ind...]
  transfers between devices with their start and end apart: 26 -> 26, of which waited for: 10 -> 12; matrix products, arithmetic and copies ran while one was open for 12% -> 13% of each run, Pallas kernels for 31% -> 31%
where the time goes in v4:
time: 791 us; the launch traced here: 782 us
  Pallas kernels  379 us (48%)
  waiting for transfers between devices  212 us (27%)
  matrix products  83.5 us (11%)
  other arithmetic  42.6 us (5%)
  local copies, waits for them, and re-layouts  30.5 us (4%)
  starting transfers between devices  19.2 us (2%)
  between operations  15.1 us (2%)
    reduce_scatter x3, waiting for transfers between devices, scatter_line(): lax.psum_scatter(value, 'fsdp', scatter_dimension=0, tiled=True, axis_ind...  106 us
    pallas_call x2, Pallas kernels, product_reduce8(): pl.pallas_call(functools.partial(product_reduce8_kernel, rows, groups, fi...  96.7 us
    ppermute x10, waiting for transfers between devices, swap_ctx(): return lax.ppermute(value, 'ctx', [(0, 1), (1, 0)])  86.3 us
    dot_general x9, matrix products, mm(): lax.dot_general(left, right, (((left_dim,), (right_dim,)), ((), ())), pre...  83.5 us
    pallas_call x2, Pallas kernels, gather8(): pl.pallas_call(functools.partial(gather8_kernel, rows, bool(also)), out_s...  81.6 us
    pallas_call x2, Pallas kernels, shards(): pl.pallas_call(functools.partial(shard_kernel, tuple(plan), len(groups)),...  41.6 us
    pallas_call x1, Pallas kernels, gather8_product(): pl.pallas_call(functools.partial(gather8_product_kernel, rows), out_shape...  41.3 us
    pallas_call x1, Pallas kernels, reduce8(): pl.pallas_call(functools.partial(reduce8_kernel, rows), out_shape=jax.Sha...  40.1 us
  transfers between devices with their start and end apart: 26, of which 12 were waited for; matrix products, arithmetic and copies ran while one was open for 13% of the time, Pallas kernels for 31%

profile of v4, /device:TPU:0, one launch (start us, length us, event | category | flops | bytes accessed | tf_op | source)
XLA Modules:
  0.0 781.6 jit_solution(8803981607550037485)
XLA Ops:
  10.1 14.0 %shards.2 = bf16[512,896]{1,0:T(8,128)(2,1)} custom-call(bf16[256,1024]{1,0:T(8,128)(2,1)} %refs_0_.1, bf16[256,512]{1,0:T(8,128)(2,1)} %refs_1_.2, bf16[256,512]{1,0:T(8,128)(2,1)} %refs_2_.2, bf16[256,1024]{1,0:T(8,128)(2,1)} %refs_3_.1, bf16[256,128]{1,0:T(8,128)(2,1)} %select_select_fusion.refs_4_), custom_call_target="tpu_custom_call" | custom-call | tf_op jit(solution)/shard_map/shards/pallas_call | solution.py:717
  24.1 27.6 %shards.3 = (bf16[512,1536]{1,0:T(8,128)(2,1)}, bf16[512,768]{1,0:T(8,128)(2,1)}) custom-call(bf16[256,3072]{1,0:T(8,128)(2,1)} %refs_0_.2, bf16[256,3072]{1,0:T(8,128)(2,1)} %refs_1_.3, bf16[256,3072]{1,0:T(8,128)(2,1)} %refs_2_.3), custom_call_target="tpu_custom_call" | custom-call | tf_op jit(solution)/shard_map/shards/pallas_call | solution.py:717
  53.6 40.9 %gather8.1 = bf16[2048,2048]{1,0:T(8,128)(2,1)} custom-call(bf16[256,2048]{1,0:T(8,128)(2,1)} %get-tuple-element.46.refs_0_), custom_call_target="tpu_custom_call" | custom-call | tf_op jit(solution)/shard_map/gather8/pallas_call | solution.py:352
  97.6 5.1 fusion
  106.5 13.7 %collective-permute-done = s32[1,1024]{1,0:T(1,128)S(1)} collective-permute-done((s32[1,1024]{1,0:T(1,128)S(1)}, s32[1,1024]{1,0:T(1,128)S(1)}, u32[]{:S(2)}, u32[]{:S(2)}) %collective-permute-start) | collective-permute-done | bytes 4128 | tf_op jit(solution)/shard_map/ppermute | solution.py:38
  125.0 10.6 %fusion.8.qkv_ref = f32[2048,512]{1,0:T(8,128)} fusion(bf16[2048,2048]{1,0:T(8,128)(2,1)} %gather8.1, f32[2048]{0:T(1024)S(1)} %get-tuple-element.80, f32[2048]{0:T(1024)S(1)} %add_rsqrt_fusion, bf16[2048,896]{1,0:T(8,128)(2,1)} %all-gather.4.cloned.1.call-done), kind=kOutput, calls=%fused_computation.24 | convolution fusion | flops 4311744512 | bytes 14696448 | tf_op jit(solution)/shard_map/dot_general | solution.py:23
  135.6 16.5 %attend.1 = bf16[2048,256]{1,0:T(8,128)(2,1)} custom-call(s32[2]{0:T(128)} %pad_add_fusion.1.meta_ref, f32[2048,512]{1,0:T(8,128)} %fusion.8.qkv_ref, s32[2,1024,1]{2,1,0:T(8,128)} %copy.33.segc_ref, s32[2,1,1024]{2,1,0:T(1,128)} %broadcast_in_dim.76.segr_ref, f32[1024,128]{1,0:T(8,128)} %get-tuple-element.106.cos_ref, ...), custom_call_target="tpu_custom_call" | custom-call | flops 1073741824 | bytes 5242880 | tf_op jit(solution)/shard_map/attend/pallas_call | solution.py:1015
  152.2 5.1 convolution_convert_fusion.far_ref
  157.3 5.8 fusion.20.near_ref
  163.1 40.1 %reduce8.1 = f32[256,2048]{1,0:T(8,128)S(1)} custom-call(f32[1024,2048]{1,0:T(8,128)} %fusion.20.near_ref, bf16[1024,2048]{1,0:T(8,128)(2,1)} %convolution_convert_fusion.far_ref), custom_call_target="tpu_custom_call" | custom-call | tf_op jit(solution)/shard_map/reduce8/pallas_call | solution.py:445
  206.2 11.4 %collective-permute-done.3.refs_4_ = bf16[128,2048]{1,0:T(8,128)(2,1)S(1)} collective-permute-done((bf16[128,2048]{1,0:T(8,128)(2,1)S(1)}, bf16[128,2048]{1,0:T(8,128)(2,1)S(1)}, u32[]{:S(2)}, u32[]{:S(2)}) %collective-permute-start.3) | collective-permute-done | bytes 524320 | tf_op jit(solution)/shard_map/ppermute | solution.py:33
  219.4 40.7 %gather8_also.1 = (bf16[2048,2048]{1,0:T(8,128)(2,1)}, bf16[2048,2048]{1,0:T(8,128)(2,1)}) custom-call(bf16[256,2048]{1,0:T(8,128)(2,1)} %multiply_convert_fusion.3.refs_0_, bf16[256,2048]{1,0:T(8,128)(2,1)} %copy-done.13, bf16[256,2048]{1,0:T(8,128)(2,1)} %copy-done.15, bf16[256,2048]{1,0:T(8,128)(2,1)} %copy-done.16, bf16[128,2048]{1,0:T(8,128)(2,1)} %copy-done.21, ...), custom_call_target="tpu_custom_call" | custom-call | tf_op jit(solution)/shard_map/gather8_also/pallas_call | solution.py:352
  260.1 17.6 %fusion.30 = f32[2048,1536]{1,0:T(8,128)S(1)} fusion(bf16[2048,2048]{1,0:T(8,128)(2,1)} %get-tuple-element.53.refs_3_, bf16[2048,1536]{1,0:T(8,128)(2,1)} %all-gather.6.cloned.1.call-done.refs_2_), kind=kOutput, calls=%fused_computation.89 | convolution fusion | flops 12884901888 | bytes 27262976 | tf_op jit(solution)/shard_map/dot_general | solution.py:23
  279.8 4.3 copy-done.7
  286.8 8.5 %convolution_convert_fusion.1 = bf16[2048,768]{1,0:T(8,128)(2,1)} fusion(bf16[2048,2048]{1,0:T(8,128)(2,1)S(1)} %copy-done.30, bf16[2048,768]{1,0:T(8,128)(2,1)S(1)} %multiply_convert_fusion.2.acts_ref), kind=kOutput, calls=%fused_computation.11 | convolution fusion | flops 6444023808 | bytes 14680064 | tf_op jit(solution)/shard_map/dot_general | solution.py:23
  295.3 16.0 %multiply_convert_fusion = (bf16[2048,768]{1,0:T(8,128)(2,1)}, bf16[2048,768]{1,0:T(8,128)(2,1)}) fusion(f32[2048,1536]{1,0:T(8,128)} %copy-done.7, bf16[2048,2048]{1,0:T(8,128)(2,1)} %get-tuple-element.54, bf16[2048,768]{1,0:T(8,128)(2,1)} %all-gather.8.cloned.1.call-done.weight_ref), kind=kOutput, calls=%fused_computation.5 | convolution fusion | flops 6462898176 | bytes 30408704 | tf_op jit(solution)/shard_map/dot_general | solution.py:23
  311.3 50.0 %product_reduce8.2 = (f32[256,2048]{1,0:T(8,128)}, bf16[2048,1536]{1,0:T(8,128)(2,1)}) custom-call(bf16[2048,768]{1,0:T(8,128)(2,1)} %get-tuple-element.86.refs_0_, bf16[2048,768]{1,0:T(8,128)(2,1)} %get-tuple-element.85.refs_1_, bf16[2048,1536]{1,0:T(8,128)(2,1)} %all-gather.6.cloned.1.call-done.refs_2_, bf16[2048,2048]{1,0:T(8,128)(2,1)} %get-tuple-element.53.refs_3_), custom_call_target="tpu_custom_call" | custom-call | flops 25769803776 | bytes 25165824 | tf_op jit(solution)/shard_map/product_reduce8/pallas_call | solution.py:646
  366.7 41.3 %gather8_product.1 = (bf16[2048,2048]{1,0:T(8,128)(2,1)}, f32[512,2048]{1,0:T(8,128)}, bf16[256,2048]{1,0:T(8,128)(2,1)S(1)}, bf16[256,2048]{1,0:T(8,128)(2,1)S(1)}) custom-call(bf16[256,2048]{1,0:T(8,128)(2,1)S(1)} %fusion.27.own_ref, bf16[2048,768]{1,0:T(8,128)(2,1)} %copy-done.14, bf16[2048,768]{1,0:T(8,128)(2,1)} %all-gather.8.cloned.1.call-done.weight_ref), custom_call_target="tpu_custom_call" | custom-call | flops 6442450944 | bytes 8388608 | tf_op jit(solution)/shard_map/gather8_product/pallas_call | solution.py:311
  408.1 6.0 convolution_convert_fusion.3
  414.1 4.5 convolution_convert_fusion.4.grad_ref
  418.7 28.3 %attend_back.1 = (bf16[2048,512]{1,0:T(8,128)(2,1)}, f32[2,128]{1,0:T(2,128)}) custom-call(s32[2]{0:T(128)} %pad_add_fusion.1.meta_ref, f32[2048,512]{1,0:T(8,128)} %fusion.8.qkv_ref, bf16[2048,256]{1,0:T(8,128)(2,1)} %convolution_convert_fusion.4.grad_ref, s32[2,1024,1]{2,1,0:T(8,128)} %copy.33.segc_ref, s32[2,1,1024]{2,1,0:T(1,128)} %broadcast_in_dim.76.segr_ref, ...), custom_call_target="tpu_custom_call" | custom-call | flops 2684354560 | bytes 8388608 | tf_op jit(solution)/shard_map/attend_back/pallas_call | solution.py:1043
  447.0 9.2 %convolution_convert_fusion.2 = bf16[2048,512]{1,0:T(8,128)(2,1)S(1)} fusion(bf16[2048,512]{1,0:T(8,128)(2,1)} %get-tuple-element.66.refs_0_, bf16[2048,2048]{1,0:T(8,128)(2,1)} %gather8.1, f32[2048]{0:T(1024)S(1)} %get-tuple-element.80, f32[2048]{0:T(1024)S(1)} %add_rsqrt_fusion), kind=kOutput, calls=%fused_computation.18 | convolution fusion | flops 4312793088 | bytes 12599296 | tf_op jit(solution)/shard_map/dot_general | solution.py:23
  460.9 23.4 %collective-permute-done.5 = bf16[256,2048]{1,0:T(8,128)(2,1)S(1)} collective-permute-done((bf16[256,2048]{1,0:T(8,128)(2,1)S(1)}, bf16[256,2048]{1,0:T(8,128)(2,1)S(1)}, u32[]{:S(2)}, u32[]{:S(2)}) %collective-permute-start.5) | collective-permute-done | bytes 1048608 | tf_op jit(solution)/shard_map/ppermute | solution.py:33
  497.0 6.5 collective-permute-done.8
  506.7 46.7 %product_reduce8.3 = f32[256,2048]{1,0:T(8,128)} custom-call(bf16[2048,512]{1,0:T(8,128)(2,1)} %get-tuple-element.66.refs_0_, bf16[2048,512]{1,0:T(8,128)(2,1)} %slice.76.refs_1_), custom_call_target="tpu_custom_call" | custom-call | flops 4294967296 | bytes 8388608 | tf_op jit(solution)/shard_map/product_reduce8/pallas_call | solution.py:646
  560.7 17.9 %total.1 = f32[34,128]{1,0:T(8,128)} custom-call(f32[34,128]{1,0:T(8,128)} %maximum_bitcast_fusion.part_ref), custom_call_target="tpu_custom_call" | custom-call | tf_op jit(solution)/shard_map/total/pallas_call | solution.py:765
  583.1 49.7 %reduce-scatter.6.cloned.1.call-done = bf16[512,1536]{1,0:T(8,128)(2,1)} async-done(((bf16[2048,1536]{1,0:T(8,128)(2,1)}), bf16[512,1536]{1,0:T(8,128)(2,1)}) %reduce-scatter.6.cloned.1.call-update) | async-done | bytes 1572880 | tf_op jit(solution)/shard_map/reduce_scatter | solution.py:51
  639.9 56.0 %reduce-scatter.8.cloned.1.call-done = bf16[512,768]{1,0:T(8,128)(2,1)} async-done(((bf16[2048,768]{1,0:T(8,128)(2,1)}), bf16[512,768]{1,0:T(8,128)(2,1)}) %reduce-scatter.8.cloned.1.call-update) | async-done | bytes 786448 | tf_op jit(solution)/shard_map/reduce_scatter | solution.py:51
  711.0 43.8 %collective-permute-done.13.both_ref = bf16[256,768]{1,0:T(8,128)(2,1)S(1)} collective-permute-done((bf16[256,768]{1,0:T(8,128)(2,1)}, bf16[256,768]{1,0:T(8,128)(2,1)S(1)}, u32[]{:S(2)}, u32[]{:S(2)}) %collective-permute-start.13) | collective-permute-done | bytes 393248 | tf_op jit(solution)/shard_map/ppermute | solution.py:33
  755.5 4.6 join.3
  762.1 4.6 join.5
  768.5 5.8 join.4
  (166 shorter events, 90.1 us)
Async XLA Ops:
  7.2 115.0 %all-gather.4.cloned.1.call-start = ((), (), s32[]{:S(2)}) async-start(), calls=%async_computation.3 | async-start | bytes 4587520 | tf_op jit(solution)/shard_map/all_gather | solution.py:47
  24.1 27.7 %copy-start.23 = (bf16[1,512,2048]{2,1,0:T(8,128)(2,1)S(1)}, bf16[1,512,2048]{2,1,0:T(8,128)(2,1)}, u32[]{:S(2)}) copy-start(bf16[1,512,2048]{2,1,0:T(8,128)(2,1)} %param.14) | copy-start | bytes 6291460
  24.1 236.0 %all-gather.6.cloned.1.call-start = ((), (), s32[]{:S(2)}) async-start(), calls=%async_computation.4 | async-start | bytes 7864320 | tf_op jit(solution)/shard_map/all_gather | solution.py:47
  51.8 243.5 %all-gather.8.cloned.1.call-start = ((), (), s32[]{:S(2)}) async-start(), calls=%async_computation.5 | async-start | bytes 3932160 | tf_op jit(solution)/shard_map/all_gather | solution.py:47
  53.6 41.0 %copy-start.12 = (bf16[1,512,2048]{2,1,0:T(8,128)(2,1)S(1)}, bf16[1,512,2048]{2,1,0:T(8,128)(2,1)}, u32[]{:S(2)}) copy-start(bf16[1,512,2048]{2,1,0:T(8,128)(2,1)} %param.27) | copy-start | bytes 6291460
  94.7 57.5 %collective-permute-start.1 = (bf16[256,2048]{1,0:T(8,128)(2,1)S(1)}, bf16[256,2048]{1,0:T(8,128)(2,1)S(1)}, u32[]{:S(2)}, u32[]{:S(2)}) collective-permute-start(bf16[256,2048]{1,0:T(8,128)(2,1)S(1)} %dynamic-slice_bitcast_fusion.refs_1_), channel_id=1, source_target_pairs={{0,4},{4,0},{8,12},{12,8},{16,20},{20,16},{24,28},{28,24},{1,5},{5... | collective-permute-start | bytes 3145736 | tf_op jit(solution)/shard_map/ppermute | solution.py:38
  96.2 107.4 %collective-permute-start.2 = (bf16[256,2048]{1,0:T(8,128)(2,1)S(1)}, bf16[256,2048]{1,0:T(8,128)(2,1)S(1)}, u32[]{:S(2)}, u32[]{:S(2)}) collective-permute-start(bf16[256,2048]{1,0:T(8,128)(2,1)S(1)} %dynamic-slice_bitcast_fusion.refs_1_), channel_id=1, source_target_pairs={{0,2},{2,0},{1,3},{3,1},{4,6},{6,4},{5,7},{7,5},{8,10},{10,8},{9,1... | collective-permute-start | bytes 3145736 | tf_op jit(solution)/shard_map/ppermute | solution.py:33
  96.7 23.5 %collective-permute-start = (s32[1,1024]{1,0:T(1,128)S(1)}, s32[1,1024]{1,0:T(1,128)S(1)}, u32[]{:S(2)}, u32[]{:S(2)}) collective-permute-start(s32[1,1024]{1,0:T(1,128)S(1)} %copy-done.28), channel_id=1, source_target_pairs={{0,4},{4,0},{8,12},{12,8},{16,20},{20,16},{24,28},{28,24},{1,5},{5... | collective-permute-start | bytes 12296 | tf_op jit(solution)/shard_map/ppermute | solution.py:38
  97.5 485.6 %reduce-scatter.4.cloned.1.call-start = ((), (), s32[]{:S(2)}) async-start(), calls=%async_computation.6 | async-start | bytes 3932160 | tf_op jit(solution)/shard_map/reduce_scatter | solution.py:51
  152.1 51.5 %copy-start.15 = (bf16[256,2048]{1,0:T(8,128)(2,1)}, bf16[256,2048]{1,0:T(8,128)(2,1)S(1)}, u32[]{:S(2)}) copy-start(bf16[256,2048]{1,0:T(8,128)(2,1)S(1)} %collective-permute-done.1.refs_2_) | copy-start | bytes 3145732
  163.1 40.1 %copy-start.4 = (bf16[256,2048]{1,0:T(8,128)(2,1)S(1)}, bf16[256,2048]{1,0:T(8,128)(2,1)}, u32[]{:S(2)}) copy-start(bf16[256,2048]{1,0:T(8,128)(2,1)} %get-tuple-element.46.refs_0_) | copy-start | bytes 3145732
  203.7 14.0 %collective-permute-start.3 = (bf16[128,2048]{1,0:T(8,128)(2,1)S(1)}, bf16[128,2048]{1,0:T(8,128)(2,1)S(1)}, u32[]{:S(2)}, u32[]{:S(2)}) collective-permute-start(bf16[128,2048]{1,0:T(8,128)(2,1)S(1)} %slice.64), channel_id=1, source_target_pairs={{0,2},{2,0},{1,3},{3,1},{4,6},{6,4},{5,7},{7,5},{8,10},{10,8},{9,1... | collective-permute-start | bytes 1572872 | tf_op jit(solution)/shard_map/ppermute | solution.py:33
  204.3 14.3 %collective-permute-start.4 = (bf16[128,2048]{1,0:T(8,128)(2,1)S(1)}, bf16[128,2048]{1,0:T(8,128)(2,1)S(1)}, u32[]{:S(2)}, u32[]{:S(2)}) collective-permute-start(bf16[128,2048]{1,0:T(8,128)(2,1)S(1)} %slice.65), channel_id=1, source_target_pairs={{0,4},{4,0},{8,12},{12,8},{16,20},{20,16},{24,28},{28,24},{1,5},{5... | collective-permute-start | bytes 1572872 | tf_op jit(solution)/shard_map/ppermute | solution.py:38
  366.7 41.3 %copy-start.9 = (bf16[2048,256]{1,0:T(8,128)(2,1)S(1)}, bf16[2048,256]{1,0:T(8,128)(2,1)}, u32[]{:S(2)}) copy-start(bf16[2048,256]{1,0:T(8,128)(2,1)} %attend.1) | copy-start | bytes 3145732
  458.1 174.7 %reduce-scatter.6.cloned.1.call-start = ((), (), s32[]{:S(2)}) async-start(), calls=%async_computation.7 | async-start | bytes 7864320 | tf_op jit(solution)/shard_map/reduce_scatter | solution.py:51
  458.7 237.2 %reduce-scatter.8.cloned.1.call-start = ((), (), s32[]{:S(2)}) async-start(), calls=%async_computation.8 | async-start | bytes 3932160 | tf_op jit(solution)/shard_map/reduce_scatter | solution.py:51
  458.8 25.5 %collective-permute-start.5 = (bf16[256,2048]{1,0:T(8,128)(2,1)S(1)}, bf16[256,2048]{1,0:T(8,128)(2,1)S(1)}, u32[]{:S(2)}, u32[]{:S(2)}) collective-permute-start(bf16[256,2048]{1,0:T(8,128)(2,1)S(1)} %get-tuple-element.58), channel_id=1, source_target_pairs={{0,2},{2,0},{1,3},{3,1},{4,6},{6,4},{5,7},{7,5},{8,10},{10,8},{9,1... | collective-permute-start | bytes 3145736 | tf_op jit(solution)/shard_map/ppermute | solution.py:33
  459.8 25.3 %collective-permute-start.7 = (bf16[256,2048]{1,0:T(8,128)(2,1)S(1)}, bf16[256,2048]{1,0:T(8,128)(2,1)}, u32[]{:S(2)}, u32[]{:S(2)}) collective-permute-start(bf16[256,2048]{1,0:T(8,128)(2,1)S(1)} %get-tuple-element.63), channel_id=1, source_target_pairs={{0,4},{4,0},{8,12},{12,8},{16,20},{20,16},{24,28},{28,24},{1,5},{5... | collective-permute-start | bytes 3145736 | tf_op jit(solution)/shard_map/ppermute | solution.py:38
  490.4 13.2 %collective-permute-start.8 = (bf16[128,2048]{1,0:T(8,128)(2,1)}, bf16[128,2048]{1,0:T(8,128)(2,1)S(1)}, u32[]{:S(2)}, u32[]{:S(2)}) collective-permute-start(bf16[128,2048]{1,0:T(8,128)(2,1)} %slice.117), channel_id=1, source_target_pairs={{0,2},{2,0},{1,3},{3,1},{4,6},{6,4},{5,7},{7,5},{8,10},{10,8},{9,1... | collective-permute-start | bytes 1572872 | tf_op jit(solution)/shard_map/ppermute | solution.py:33
  492.2 13.0 %collective-permute-start.6 = (bf16[128,2048]{1,0:T(8,128)(2,1)}, bf16[128,2048]{1,0:T(8,128)(2,1)S(1)}, u32[]{:S(2)}, u32[]{:S(2)}) collective-permute-start(bf16[128,2048]{1,0:T(8,128)(2,1)} %slice.118), channel_id=1, source_target_pairs={{0,4},{4,0},{8,12},{12,8},{16,20},{20,16},{24,28},{28,24},{1,5},{5... | collective-permute-start | bytes 1572872 | tf_op jit(solution)/shard_map/ppermute | solution.py:38
  493.8 11.4 %copy-start.11 = (f32[256,2048]{1,0:T(8,128)S(1)}, f32[256,2048]{1,0:T(8,128)}, u32[]{:S(2)}) copy-start(f32[256,2048]{1,0:T(8,128)} %copy-done.10) | copy-start | bytes 6291460
  506.7 74.7 %collective-permute-start.9 = (bf16[256,2048]{1,0:T(8,128)(2,1)}, bf16[256,2048]{1,0:T(8,128)(2,1)}, u32[]{:S(2)}, u32[]{:S(2)}) collective-permute-start(bf16[256,2048]{1,0:T(8,128)(2,1)} %fusion.17), channel_id=1, source_target_pairs={{0,1},{1,0},{2,3},{3,2},{4,5},{5,4},{6,7},{7,6},{8,9},{9,8},{10,11... | collective-permute-start | bytes 3145736 | tf_op jit(solution)/shard_map/ppermute | solution.py:29
  560.0 140.4 %collective-permute-start.10 = (bf16[256,2048]{1,0:T(8,128)(2,1)S(1)}, bf16[256,2048]{1,0:T(8,128)(2,1)}, u32[]{:S(2)}, u32[]{:S(2)}) collective-permute-start(bf16[256,2048]{1,0:T(8,128)(2,1)S(1)} %fusion.14), channel_id=1, source_target_pairs={{0,1},{1,0},{2,3},{3,2},{4,5},{5,4},{6,7},{7,6},{8,9},{9,8},{10,11... | collective-permute-start | bytes 3145736 | tf_op jit(solution)/shard_map/ppermute | solution.py:29
  635.5 66.4 %collective-permute-start.14 = (bf16[256,1536]{1,0:T(8,128)(2,1)}, bf16[256,1536]{1,0:T(8,128)(2,1)}, u32[]{:S(2)}, u32[]{:S(2)}) collective-permute-start(bf16[256,1536]{1,0:T(8,128)(2,1)} %get-tuple-element.89), channel_id=1, source_target_pairs={{0,4},{4,0},{8,12},{12,8},{16,20},{20,16},{24,28},{28,24},{1,5},{5... | collective-permute-start | bytes 2359304 | tf_op jit(solution)/shard_map/ppermute | solution.py:38
  637.9 66.0 %collective-permute-start.11 = (bf16[256,768]{1,0:T(8,128)(2,1)}, bf16[256,768]{1,0:T(8,128)(2,1)}, u32[]{:S(2)}, u32[]{:S(2)}) collective-permute-start(bf16[256,768]{1,0:T(8,128)(2,1)} %get-tuple-element.93), channel_id=1, source_target_pairs={{0,4},{4,0},{8,12},{12,8},{16,20},{20,16},{24,28},{28,24},{1,5},{5... | collective-permute-start | bytes 1179656 | tf_op jit(solution)/shard_map/ppermute | solution.py:38
  638.4 67.0 %collective-permute-start.12 = (bf16[256,768]{1,0:T(8,128)(2,1)}, bf16[256,768]{1,0:T(8,128)(2,1)}, u32[]{:S(2)}, u32[]{:S(2)}) collective-permute-start(bf16[256,768]{1,0:T(8,128)(2,1)} %get-tuple-element.94.kept_ref), channel_id=1, source_target_pairs={{0,2},{2,0},{1,3},{3,1},{4,6},{6,4},{5,7},{7,5},{8,10},{10,8},{9,1... | collective-permute-start | bytes 1179656 | tf_op jit(solution)/shard_map/ppermute | solution.py:33
  697.1 10.6 %collective-permute-start.17 = (bf16[256,768]{1,0:T(8,128)(2,1)S(1)}, bf16[256,768]{1,0:T(8,128)(2,1)}, u32[]{:S(2)}, u32[]{:S(2)}) collective-permute-start(bf16[256,768]{1,0:T(8,128)(2,1)S(1)} %get-tuple-element.91), channel_id=1, source_target_pairs={{0,4},{4,0},{8,12},{12,8},{16,20},{20,16},{24,28},{28,24},{1,5},{5... | collective-permute-start | bytes 1179656 | tf_op jit(solution)/shard_map/ppermute | solution.py:38
  700.4 66.4 %collective-permute-start.15 = (bf16[256,1536]{1,0:T(8,128)(2,1)}, bf16[256,1536]{1,0:T(8,128)(2,1)S(1)}, u32[]{:S(2)}, u32[]{:S(2)}) collective-permute-start(bf16[256,1536]{1,0:T(8,128)(2,1)} %get-tuple-element.90.kept_ref), channel_id=1, source_target_pairs={{0,2},{2,0},{1,3},{3,1},{4,6},{6,4},{5,7},{7,5},{8,10},{10,8},{9,1... | collective-permute-start | bytes 2359304 | tf_op jit(solution)/shard_map/ppermute | solution.py:33
  701.9 64.9 %collective-permute-start.16 = (bf16[256,1536]{1,0:T(8,128)(2,1)}, bf16[256,1536]{1,0:T(8,128)(2,1)S(1)}, u32[]{:S(2)}, u32[]{:S(2)}) collective-permute-start(bf16[256,1536]{1,0:T(8,128)(2,1)} %collective-permute-done.14.x_ref), channel_id=1, source_target_pairs={{0,2},{2,0},{1,3},{3,1},{4,6},{6,4},{5,7},{7,5},{8,10},{10,8},{9,1... | collective-permute-start | bytes 2359304 | tf_op jit(solution)/shard_map/ppermute | solution.py:33
  703.9 56.2 %collective-permute-start.18 = (bf16[256,768]{1,0:T(8,128)(2,1)S(1)}, bf16[256,768]{1,0:T(8,128)(2,1)S(1)}, u32[]{:S(2)}, u32[]{:S(2)}) collective-permute-start(bf16[256,768]{1,0:T(8,128)(2,1)S(1)} %get-tuple-element.92.kept_ref), channel_id=1, source_target_pairs={{0,2},{2,0},{1,3},{3,1},{4,6},{6,4},{5,7},{7,5},{8,10},{10,8},{9,1... | collective-permute-start | bytes 1179656 | tf_op jit(solution)/shard_map/ppermute | solution.py:33
  705.4 49.3 %collective-permute-start.13 = (bf16[256,768]{1,0:T(8,128)(2,1)}, bf16[256,768]{1,0:T(8,128)(2,1)S(1)}, u32[]{:S(2)}, u32[]{:S(2)}) collective-permute-start(bf16[256,768]{1,0:T(8,128)(2,1)} %collective-permute-done.11.x_ref), channel_id=1, source_target_pairs={{0,2},{2,0},{1,3},{3,1},{4,6},{6,4},{5,7},{7,5},{8,10},{10,8},{9,1... | collective-permute-start | bytes 1179656 | tf_op jit(solution)/shard_map/ppermute | solution.py:33
  707.7 53.7 %collective-permute-start.19 = (bf16[256,768]{1,0:T(8,128)(2,1)}, bf16[256,768]{1,0:T(8,128)(2,1)S(1)}, u32[]{:S(2)}, u32[]{:S(2)}) collective-permute-start(bf16[256,768]{1,0:T(8,128)(2,1)} %collective-permute-done.17.x_ref), channel_id=1, source_target_pairs={{0,2},{2,0},{1,3},{3,1},{4,6},{6,4},{5,7},{7,5},{8,10},{10,8},{9,1... | collective-permute-start | bytes 1179656 | tf_op jit(solution)/shard_map/ppermute | solution.py:33
  (26 other events, 92.4 us)
Sparse Core Ops, SparseCore 0:
  24.2 73.5 all-gather.3
  99.4 113.8 all-gather.5
  214.9 61.6 all-gather.7
  458.2 60.8 reduce-scatter.3
  521.3 111.4 reduce-scatter.5
  634.9 60.8 reduce-scatter.7

commit v5 on v4

--- a/solution.py
+++ b/solution.py
@@ -480,7 +480,15 @@
     def where(chunk):
         return chunk[0] * 2 * wide + chunk[1] * wide
 
-    load_weight = pltpu.make_async_copy(weight_ref, weight, load_sem.at[8])
+    half = width // 2
+    load_weights = [
+        pltpu.make_async_copy(
+            weight_ref.at[pl.ds(part * half, half), pl.ds(0, weight.shape[1])],
+            weight.at[pl.ds(part * half, half)],
+            load_sem.at[part],
+        )
+        for part in (0, 1)
+    ]
     loads = {}
     depth = weight.shape[1] // groups
     for number, chunk in enumerate(chunks):
@@ -490,146 +498,142 @@
                 pltpu.make_async_copy(
                     acts_refs[group].at[place],
                     acts.at[place, pl.ds(group * depth, depth)],
-                    load_sem.at[10 + (2 * number + side) * groups + group],
+                    load_sem.at[3 + (2 * number + side) * groups + group],
                 )
                 for group in range(groups)
             ]
-    for copy in loads[1, chunks[0]]:
-        copy.start()
-    load_weight.start()
-    for chunk in chunks:
-        for side in (1, 0):
-            if (side, chunk) != (1, chunks[0]):
-                for copy in loads[side, chunk]:
-                    copy.start()
+    started = [loads[1, chunks[0]], [load_weights[0]], loads[1, chunks[1]], loads[0, chunks[0]]]
+    started += [loads[0, chunks[1]], [load_weights[1]]]
+    started += [loads[side, chunk] for chunk in chunks[2:] for side in (1, 0)]
+    for group in started:
+        for copy in group:
+            copy.start()
     if filler:
         lhs, grad, grad_sem = refs
-        load_lhs = pltpu.make_async_copy(lhs_ref, lhs, load_sem.at[9])
+        load_lhs = pltpu.make_async_copy(lhs_ref, lhs, load_sem.at[2])
         load_lhs.start()
     greet((x_peer, y_peer, c_peer))
 
-    core_copies = {}
-
-    def product(chunk, side, target):
-        for copy in loads[side, chunk]:
-            copy.wait()
+    core_copies, link_copies = {}, {}
+
+    def product(chunk, side, part, target):
         place = pl.ds(where(chunk), wide)
         source = pl.ds(side * 4 * wide + where(chunk), wide)
 
-        def step(cols):
+        def step(index, _):
+            cols = pl.ds(pl.multiple_of(part * half + index * (half // 2), half // 2), half // 2)
             target[place, cols] = mm(acts[source, :], weight[cols, :], 1, 1).astype(target.dtype)
             return 0
 
-        tiled(width, width // 2, step)
-
-    def send_core(chunk):
-        product(chunk, 1, far)
-        number = chunks.index(chunk)
-        place = pl.ds(where(chunk), wide)
-        core_copies[chunk] = pltpu.make_async_remote_copy(
-            src_ref=far.at[place],
-            dst_ref=core_in.at[place],
+        lax.fori_loop(0, 2, step, 0)
+
+    def remote(copies, key, number, source, target, peer):
+        copies[key] = pltpu.make_async_remote_copy(
+            src_ref=source,
+            dst_ref=target,
             send_sem=send_sem.at[number],
             recv_sem=recv_sem.at[number],
-            device_id=c_peer,
-            device_id_type=MESH,
-        )
-        core_copies[chunk].start()
-
-    def partial_sum(half, outer, inner):
-        place = pl.ds(where((half, outer)) + inner * rows, rows)
-        return near[place, :] + core_in[place, :].astype(F32)
-
-    def link(index, value, peer):
-        link_out[index] = value.astype(BF16)
-        copy = pltpu.make_async_remote_copy(
-            src_ref=link_out.at[index],
-            dst_ref=link_in.at[index],
-            send_sem=send_sem.at[4 + index],
-            recv_sem=recv_sem.at[4 + index],
             device_id=peer,
             device_id_type=MESH,
         )
-        copy.start()
-        return copy
-
-    load_weight.wait()
-    send_core((0, 1))
-    product((0, 1), 0, near)
-    core_copies[0, 1].wait_recv()
-    y11 = link(0, partial_sum(0, 1, 1), y_peer)
-    send_core((1, 1))
-    y10 = link(2, partial_sum(0, 1, 0), y_peer)
-    product((1, 1), 0, near)
-    core_copies[1, 1].wait_recv()
-    x11 = link(1, partial_sum(1, 1, 1), x_peer)
-    x10 = link(3, partial_sum(1, 1, 0), x_peer)
-    send_core((0, 0))
-    product((0, 0), 0, near)
-    send_core((1, 0))
-    product((1, 0), 0, near)
-    core_copies[0, 0].wait_recv()
-    core_copies[1, 0].wait_recv()
-    grad_copies = []
-    parts = grad_sem.shape[0] if filler else 0
-
-    def fill(index):
-        size = width // parts
-        cols = pl.ds(index * size, size)
-
-        def step(columns):
-            grad[cols, columns] = mm(lhs[:, cols], acts[:, columns], 0, 0).astype(BF16)
-            return 0
-
-        tiled(acts.shape[1], acts.shape[1] // 3, step)
-        copy = pltpu.make_async_copy(grad.at[cols], grad_ref.at[cols], grad_sem.at[index])
-        copy.start()
-        grad_copies.append(copy)
-
+        copies[key].start()
+
+    def send_core(chunk, part):
+        product(chunk, 1, part, far)
+        here = (pl.ds(where(chunk), wide), pl.ds(part * half, half))
+        number = 2 * chunks.index(chunk) + part
+        remote(core_copies, (chunk, part), number, far.at[here], core_in.at[here], c_peer)
+
+    def partial_sum(chunk, start, size, part):
+        here = (pl.ds(where(chunk) + start, size), pl.ds(part * half, half))
+        return near[here] + core_in[here].astype(F32)
+
+    def link(hop, side, part, value, peer):
+        size = value.shape[0]
+        start = (side * 3 + hop * 2) * rows
+        here = (pl.ds(start, size), pl.ds(part * half, half))
+        link_out[here] = value.astype(BF16)
+        number = 8 + hop * 4 + side * 2 + part
+        remote(link_copies, (hop, side, part), number, link_out.at[here], link_in.at[here], peer)
+
+    def came(hop, side, start, part):
+        return link_in[
+            pl.ds((side * 3 + hop * 2) * rows + start, rows), pl.ds(part * half, half)
+        ].astype(F32)
+
+    for chunk in chunks[:2]:
+        for copy in loads[1, chunk]:
+            copy.wait()
+    for part in (0, 1):
+        load_weights[part].wait()
+        send_core((0, 1), part)
+        send_core((1, 1), part)
+        for side, peer in ((0, y_peer), (1, x_peer)):
+            if part == 0:
+                for copy in loads[0, (side, 1)]:
+                    copy.wait()
+            product((side, 1), 0, part, near)
+            core_copies[(side, 1), part].wait_recv()
+            link(0, side, part, partial_sum((side, 1), 0, wide, part), peer)
+    for chunk in chunks[2:]:
+        for side in (1, 0):
+            for copy in loads[side, chunk]:
+                copy.wait()
+    for part in (0, 1):
+        for chunk in chunks[2:]:
+            send_core(chunk, part)
+        for chunk in chunks[2:]:
+            product(chunk, 0, part, near)
+        for side, peer in ((0, x_peer), (1, y_peer)):
+            core_copies[(side, 0), part].wait_recv()
+            link_copies[0, side, part].wait_recv()
+            link(1, side, part, partial_sum((side, 0), rows, rows, part) + came(0, side, rows, part), peer)
     if filler:
         load_lhs.wait()
-    y11.wait_recv()
-    x01 = link(4, partial_sum(0, 0, 1) + link_in[0].astype(F32), x_peer)
+        size = width // 4
+
+        def fill(index, _):
+            cols = pl.ds(pl.multiple_of(index * size, size), size)
+
+            def step(columns):
+                grad[cols, columns] = mm(lhs[:, cols], acts[:, columns], 0, 0).astype(BF16)
+                return 0
+
+            tiled(acts.shape[1], acts.shape[1] // 3, step)
+            return 0
+
+        lax.fori_loop(0, 4, fill, 0)
+        grad_copy = pltpu.make_async_copy(grad, grad_ref, grad_sem.at[0])
+        grad_copy.start()
+    for side in (0, 1):
+        for part in (0, 1):
+            place = (pl.ds(side * rows, rows), pl.ds(part * half, half))
+            kept = partial_sum((side, 0), 0, rows, part) + came(0, side, 0, part)
+            link_copies[1, side, part].wait_recv()
+            out_ref[place] = kept + came(1, side, 0, part)
+    for copy in list(link_copies.values()) + list(core_copies.values()):
+        copy.wait_send()
     if filler:
-        fill(0)
-    x11.wait_recv()
-    y01 = link(5, partial_sum(1, 0, 1) + link_in[1].astype(F32), y_peer)
-    for index in range(1, parts):
-        fill(index)
-    y10.wait_recv()
-    out_ref[pl.ds(0, rows), :] = partial_sum(0, 0, 0) + link_in[2].astype(F32)
-    x10.wait_recv()
-    out_ref[pl.ds(rows, rows), :] = partial_sum(1, 0, 0) + link_in[3].astype(F32)
-    x01.wait_recv()
-    out_ref[pl.ds(0, rows), :] += link_in[4].astype(F32)
-    y01.wait_recv()
-    out_ref[pl.ds(rows, rows), :] += link_in[5].astype(F32)
-    for copy in (y11, x11, y10, x10, x01, y01):
-        copy.wait_send()
-    for copy in core_copies.values():
-        copy.wait_send()
-    for copy in grad_copies:
-        copy.wait()
+        grad_copy.wait()
 
 
 def product_reduce8(columns, weight, number, lhs=None):
-    acts = jax.ShapeDtypeStruct((columns[0].shape[0], weight.shape[1]), BF16)
-    rows, width, depth = acts.shape[0] // 16, weight.shape[0], weight.shape[1]
-    groups = len(columns)
+    depth, groups = sum(column.shape[1] for column in columns), len(columns)
+    acts = jax.ShapeDtypeStruct((columns[0].shape[0], depth), BF16)
+    rows, width = acts.shape[0] // 16, weight.shape[0]
     filler = lhs is not None
     hbm = pl.BlockSpec(memory_space=pl.ANY)
-    parts = 4
     scratch = [
         pltpu.VMEM(acts.shape, BF16),
-        pltpu.VMEM(weight.shape, BF16),
+        pltpu.VMEM((width, depth), BF16),
         pltpu.VMEM((8 * rows, width), BF16),
         pltpu.VMEM((8 * rows, width), F32),
         pltpu.VMEM((8 * rows, width), BF16),
-        pltpu.VMEM((6, rows, width), BF16),
-        pltpu.VMEM((6, rows, width), BF16),
-        pltpu.SemaphoreType.DMA((10,)),
-        pltpu.SemaphoreType.DMA((10,)),
-        pltpu.SemaphoreType.DMA((10 + 8 * groups,)),
+        pltpu.VMEM((6 * rows, width), BF16),
+        pltpu.VMEM((6 * rows, width), BF16),
+        pltpu.SemaphoreType.DMA((16,)),
+        pltpu.SemaphoreType.DMA((16,)),
+        pltpu.SemaphoreType.DMA((3 + 8 * groups,)),
     ]
     out_shape = [jax.ShapeDtypeStruct((2 * rows, width), F32)]
     out_specs = [pl.BlockSpec(memory_space=pltpu.VMEM)]
@@ -638,7 +642,7 @@
         scratch += [
             pltpu.VMEM(lhs.shape, BF16),
             pltpu.VMEM((width, depth), BF16),
-            pltpu.SemaphoreType.DMA((parts,)),
+            pltpu.SemaphoreType.DMA((1,)),
         ]
         out_shape.append(jax.ShapeDtypeStruct((width, depth), BF16))
         out_specs.append(hbm)
@@ -651,7 +655,7 @@
         scratch_shapes=scratch,
         compiler_params=remote_params(number, 63 * 1024 * 1024),
         cost_estimate=pl.CostEstimate(
-            flops=flops, bytes_accessed=4 * (acts.size + weight.size), transcendentals=0
+            flops=flops, bytes_accessed=4 * depth * (acts.shape[0] + width), transcendentals=0
         ),
         name="product_reduce8",
     )(*columns, weight, *((lhs,) if filler else ()))
@@ -1209,7 +1213,7 @@
     mlp_second = mlp_second + after(mlp_came2, first_grad).astype(F32)
     mlp_sum = (middle + jnp.concatenate([mlp_first, mlp_second])).astype(BF16)
     layer_out = finish_rows(mlp_sum)
-    in_grad = product_reduce8((after(raw_grads, first_grad, mlp_sum),), qkv_w, 8)
+    in_grad = product_reduce8((after(raw_grads, first_grad, mlp_sum),), first, 8)
 
     spot = jnp.stack([place, odd]).astype(jnp.int32)
 

time: 791 us -> 793 us (level)
  transfers between devices with their start and end apart: 26 -> 26, of which waited for: 12 -> 12; matrix products, arithmetic and copies ran while one was open for 13% -> 12% of each run, Pallas kernels for 31% -> 30%
where the time goes in v5:
time: 793 us; the launch traced here: 784 us
  Pallas kernels  380 us (48%)
  waiting for transfers between devices  215 us (27%)
  matrix products  83.5 us (11%)
  other arithmetic  45.2 us (6%)
  local copies, waits for them, and re-layouts  26 us (3%)
  starting transfers between devices  19.2 us (2%)
  between operations  15.1 us (2%)
    reduce_scatter x3, waiting for transfers between devices, scatter_line(): lax.psum_scatter(value, 'fsdp', scatter_dimension=0, tiled=True, axis_ind...  106 us
    pallas_call x2, Pallas kernels, product_reduce8(): pl.pallas_call(functools.partial(product_reduce8_kernel, rows, groups, fi...  95.4 us
    ppermute x10, waiting for transfers between devices, swap_ctx(): return lax.ppermute(value, 'ctx', [(0, 1), (1, 0)])  89.5 us
    dot_general x9, matrix products, mm(): lax.dot_general(left, right, (((left_dim,), (right_dim,)), ((), ())), pre...  83.5 us
    pallas_call x2, Pallas kernels, gather8(): pl.pallas_call(functools.partial(gather8_kernel, rows, bool(also)), out_s...  81.6 us
    pallas_call x2, Pallas kernels, shards(): pl.pallas_call(functools.partial(shard_kernel, tuple(plan), len(groups)),...  41.6 us
    pallas_call x1, Pallas kernels, gather8_product(): pl.pallas_call(functools.partial(gather8_product_kernel, rows), out_shape...  41.3 us
    pallas_call x1, Pallas kernels, reduce8(): pl.pallas_call(functools.partial(reduce8_kernel, rows), out_shape=jax.Sha...  40.1 us
  transfers between devices with their start and end apart: 26, of which 12 were waited for; matrix products, arithmetic and copies ran while one was open for 12% of the time, Pallas kernels for 30%

profile of v5, /device:TPU:0, one launch (start us, length us, event | category | flops | bytes accessed | tf_op | source)
XLA Modules:
  0.0 783.9 jit_solution(15125981040223785324)
XLA Ops:
  10.1 14.0 %shards.2 = bf16[512,896]{1,0:T(8,128)(2,1)} custom-call(bf16[256,1024]{1,0:T(8,128)(2,1)} %refs_0_.1, bf16[256,512]{1,0:T(8,128)(2,1)} %refs_1_.2, bf16[256,512]{1,0:T(8,128)(2,1)} %refs_2_.2, bf16[256,1024]{1,0:T(8,128)(2,1)} %refs_3_.1, bf16[256,128]{1,0:T(8,128)(2,1)} %select_select_fusion.refs_4_), custom_call_target="tpu_custom_call" | custom-call | tf_op jit(solution)/shard_map/shards/pallas_call | solution.py:721
  24.1 27.6 %shards.3 = (bf16[512,1536]{1,0:T(8,128)(2,1)}, bf16[512,768]{1,0:T(8,128)(2,1)}) custom-call(bf16[256,3072]{1,0:T(8,128)(2,1)} %refs_0_.2, bf16[256,3072]{1,0:T(8,128)(2,1)} %refs_1_.3, bf16[256,3072]{1,0:T(8,128)(2,1)} %refs_2_.3), custom_call_target="tpu_custom_call" | custom-call | tf_op jit(solution)/shard_map/shards/pallas_call | solution.py:721
  53.6 40.9 %gather8.1 = bf16[2048,2048]{1,0:T(8,128)(2,1)} custom-call(bf16[256,2048]{1,0:T(8,128)(2,1)} %get-tuple-element.46.refs_0_), custom_call_target="tpu_custom_call" | custom-call | tf_op jit(solution)/shard_map/gather8/pallas_call | solution.py:352
  97.6 5.1 fusion
  106.5 13.7 %collective-permute-done = s32[1,1024]{1,0:T(1,128)S(1)} collective-permute-done((s32[1,1024]{1,0:T(1,128)S(1)}, s32[1,1024]{1,0:T(1,128)S(1)}, u32[]{:S(2)}, u32[]{:S(2)}) %collective-permute-start) | collective-permute-done | bytes 4128 | tf_op jit(solution)/shard_map/ppermute | solution.py:38
  125.0 10.6 %fusion.8.qkv_ref = f32[2048,512]{1,0:T(8,128)} fusion(bf16[2048,2048]{1,0:T(8,128)(2,1)} %gather8.1, f32[2048]{0:T(1024)S(1)} %get-tuple-element.80, f32[2048]{0:T(1024)S(1)} %add_rsqrt_fusion, bf16[2048,896]{1,0:T(8,128)(2,1)} %all-gather.4.cloned.1.call-done.refs_1_), kind=kOutput, calls=%fused_computation.24 | convolution fusion | flops 4311744512 | bytes 14696448 | tf_op jit(solution)/shard_map/dot_general | solution.py:23
  135.6 16.5 %attend.1 = bf16[2048,256]{1,0:T(8,128)(2,1)} custom-call(s32[2]{0:T(128)} %pad_add_fusion.1.meta_ref, f32[2048,512]{1,0:T(8,128)} %fusion.8.qkv_ref, s32[2,1024,1]{2,1,0:T(8,128)} %copy.33.segc_ref, s32[2,1,1024]{2,1,0:T(1,128)} %broadcast_in_dim.76.segr_ref, f32[1024,128]{1,0:T(8,128)} %get-tuple-element.106.cos_ref, ...), custom_call_target="tpu_custom_call" | custom-call | flops 1073741824 | bytes 5242880 | tf_op jit(solution)/shard_map/attend/pallas_call | solution.py:1019
  152.1 5.1 convolution_convert_fusion.far_ref
  157.3 5.8 fusion.21.near_ref
  163.1 40.1 %reduce8.1 = f32[256,2048]{1,0:T(8,128)S(1)} custom-call(f32[1024,2048]{1,0:T(8,128)} %fusion.21.near_ref, bf16[1024,2048]{1,0:T(8,128)(2,1)} %convolution_convert_fusion.far_ref), custom_call_target="tpu_custom_call" | custom-call | tf_op jit(solution)/shard_map/reduce8/pallas_call | solution.py:445
  206.2 11.4 %collective-permute-done.3.refs_4_ = bf16[128,2048]{1,0:T(8,128)(2,1)S(1)} collective-permute-done((bf16[128,2048]{1,0:T(8,128)(2,1)S(1)}, bf16[128,2048]{1,0:T(8,128)(2,1)S(1)}, u32[]{:S(2)}, u32[]{:S(2)}) %collective-permute-start.3) | collective-permute-done | bytes 524320 | tf_op jit(solution)/shard_map/ppermute | solution.py:33
  219.4 40.7 %gather8_also.1 = (bf16[2048,2048]{1,0:T(8,128)(2,1)}, bf16[2048,2048]{1,0:T(8,128)(2,1)}) custom-call(bf16[256,2048]{1,0:T(8,128)(2,1)} %multiply_convert_fusion.3.refs_0_, bf16[256,2048]{1,0:T(8,128)(2,1)} %copy-done.13, bf16[256,2048]{1,0:T(8,128)(2,1)} %copy-done.15, bf16[256,2048]{1,0:T(8,128)(2,1)} %copy-done.16, bf16[128,2048]{1,0:T(8,128)(2,1)} %copy-done.21, ...), custom_call_target="tpu_custom_call" | custom-call | tf_op jit(solution)/shard_map/gather8_also/pallas_call | solution.py:352
  260.1 17.6 %fusion.30 = f32[2048,1536]{1,0:T(8,128)S(1)} fusion(bf16[2048,2048]{1,0:T(8,128)(2,1)} %get-tuple-element.53.refs_3_, bf16[2048,1536]{1,0:T(8,128)(2,1)} %all-gather.6.cloned.1.call-done.refs_2_), kind=kOutput, calls=%fused_computation.89 | convolution fusion | flops 12884901888 | bytes 27262976 | tf_op jit(solution)/shard_map/dot_general | solution.py:23
  279.8 4.3 copy-done.7
  286.8 8.5 %convolution_convert_fusion.1 = bf16[2048,768]{1,0:T(8,128)(2,1)} fusion(bf16[2048,2048]{1,0:T(8,128)(2,1)S(1)} %copy-done.30, bf16[2048,768]{1,0:T(8,128)(2,1)S(1)} %multiply_convert_fusion.2.acts_ref), kind=kOutput, calls=%fused_computation.11 | convolution fusion | flops 6444023808 | bytes 14680064 | tf_op jit(solution)/shard_map/dot_general | solution.py:23
  295.3 16.0 %multiply_convert_fusion = (bf16[2048,768]{1,0:T(8,128)(2,1)}, bf16[2048,768]{1,0:T(8,128)(2,1)}) fusion(f32[2048,1536]{1,0:T(8,128)} %copy-done.7, bf16[2048,2048]{1,0:T(8,128)(2,1)} %get-tuple-element.54, bf16[2048,768]{1,0:T(8,128)(2,1)} %all-gather.8.cloned.1.call-done.weight_ref), kind=kOutput, calls=%fused_computation.5 | convolution fusion | flops 6462898176 | bytes 30408704 | tf_op jit(solution)/shard_map/dot_general | solution.py:23
  311.3 52.7 %product_reduce8.2 = (f32[256,2048]{1,0:T(8,128)}, bf16[2048,1536]{1,0:T(8,128)(2,1)}) custom-call(bf16[2048,768]{1,0:T(8,128)(2,1)} %get-tuple-element.86.refs_0_, bf16[2048,768]{1,0:T(8,128)(2,1)} %get-tuple-element.85.refs_1_, bf16[2048,1536]{1,0:T(8,128)(2,1)} %all-gather.6.cloned.1.call-done.refs_2_, bf16[2048,2048]{1,0:T(8,128)(2,1)} %get-tuple-element.53.refs_3_), custom_call_target="tpu_custom_call" | custom-call | flops 25769803776 | bytes 25165824 | tf_op jit(solution)/shard_map/product_reduce8/pallas_call | solution.py:650
  369.4 41.3 %gather8_product.1 = (bf16[2048,2048]{1,0:T(8,128)(2,1)}, f32[512,2048]{1,0:T(8,128)}, bf16[256,2048]{1,0:T(8,128)(2,1)S(1)}, bf16[256,2048]{1,0:T(8,128)(2,1)S(1)}) custom-call(bf16[256,2048]{1,0:T(8,128)(2,1)S(1)} %fusion.27.own_ref, bf16[2048,768]{1,0:T(8,128)(2,1)} %copy-done.14, bf16[2048,768]{1,0:T(8,128)(2,1)} %all-gather.8.cloned.1.call-done.weight_ref), custom_call_target="tpu_custom_call" | custom-call | flops 6442450944 | bytes 8388608 | tf_op jit(solution)/shard_map/gather8_product/pallas_call | solution.py:311
  410.7 6.0 convolution_convert_fusion.3
  416.8 4.5 convolution_convert_fusion.4.grad_ref
  421.3 28.2 %attend_back.1 = (bf16[2048,512]{1,0:T(8,128)(2,1)}, f32[2,128]{1,0:T(2,128)}) custom-call(s32[2]{0:T(128)} %pad_add_fusion.1.meta_ref, f32[2048,512]{1,0:T(8,128)} %fusion.8.qkv_ref, bf16[2048,256]{1,0:T(8,128)(2,1)} %convolution_convert_fusion.4.grad_ref, s32[2,1024,1]{2,1,0:T(8,128)} %copy.33.segc_ref, s32[2,1,1024]{2,1,0:T(1,128)} %broadcast_in_dim.76.segr_ref, ...), custom_call_target="tpu_custom_call" | custom-call | flops 2684354560 | bytes 8388608 | tf_op jit(solution)/shard_map/attend_back/pallas_call | solution.py:1047
  449.5 9.2 %convolution_convert_fusion.2 = bf16[2048,512]{1,0:T(8,128)(2,1)S(1)} fusion(bf16[2048,512]{1,0:T(8,128)(2,1)} %get-tuple-element.66.refs_0_, bf16[2048,2048]{1,0:T(8,128)(2,1)} %gather8.1, f32[2048]{0:T(1024)S(1)} %get-tuple-element.80, f32[2048]{0:T(1024)S(1)} %add_rsqrt_fusion), kind=kOutput, calls=%fused_computation.18 | convolution fusion | flops 4312793088 | bytes 12599296 | tf_op jit(solution)/shard_map/dot_general | solution.py:23
  463.4 23.4 %collective-permute-done.5 = bf16[256,2048]{1,0:T(8,128)(2,1)S(1)} collective-permute-done((bf16[256,2048]{1,0:T(8,128)(2,1)S(1)}, bf16[256,2048]{1,0:T(8,128)(2,1)S(1)}, u32[]{:S(2)}, u32[]{:S(2)}) %collective-permute-start.5) | collective-permute-done | bytes 1048608 | tf_op jit(solution)/shard_map/ppermute | solution.py:33
  495.2 9.8 %collective-permute-done.8 = bf16[128,2048]{1,0:T(8,128)(2,1)S(1)} collective-permute-done((bf16[128,2048]{1,0:T(8,128)(2,1)}, bf16[128,2048]{1,0:T(8,128)(2,1)S(1)}, u32[]{:S(2)}, u32[]{:S(2)}) %collective-permute-start.8) | collective-permute-done | bytes 524320 | tf_op jit(solution)/shard_map/ppermute | solution.py:33
  510.5 42.7 %product_reduce8.3 = f32[256,2048]{1,0:T(8,128)} custom-call(bf16[2048,512]{1,0:T(8,128)(2,1)} %get-tuple-element.66.refs_0_, bf16[2048,896]{1,0:T(8,128)(2,1)} %all-gather.4.cloned.1.call-done.refs_1_), custom_call_target="tpu_custom_call" | custom-call | flops 4294967296 | bytes 8388608 | tf_op jit(solution)/shard_map/product_reduce8/pallas_call | solution.py:650
  560.5 20.5 %total.1 = f32[34,128]{1,0:T(8,128)} custom-call(f32[34,128]{1,0:T(8,128)} %maximum_bitcast_fusion.part_ref), custom_call_target="tpu_custom_call" | custom-call | tf_op jit(solution)/shard_map/total/pallas_call | solution.py:769
  585.5 49.6 %reduce-scatter.6.cloned.1.call-done = bf16[512,1536]{1,0:T(8,128)(2,1)} async-done(((bf16[2048,1536]{1,0:T(8,128)(2,1)}), bf16[512,1536]{1,0:T(8,128)(2,1)}) %reduce-scatter.6.cloned.1.call-update) | async-done | bytes 1572880 | tf_op jit(solution)/shard_map/reduce_scatter | solution.py:51
  642.2 56.0 %reduce-scatter.8.cloned.1.call-done = bf16[512,768]{1,0:T(8,128)(2,1)} async-done(((bf16[2048,768]{1,0:T(8,128)(2,1)}), bf16[512,768]{1,0:T(8,128)(2,1)}) %reduce-scatter.8.cloned.1.call-update) | async-done | bytes 786448 | tf_op jit(solution)/shard_map/reduce_scatter | solution.py:51
  713.3 43.7 %collective-permute-done.13.both_ref = bf16[256,768]{1,0:T(8,128)(2,1)S(1)} collective-permute-done((bf16[256,768]{1,0:T(8,128)(2,1)}, bf16[256,768]{1,0:T(8,128)(2,1)S(1)}, u32[]{:S(2)}, u32[]{:S(2)}) %collective-permute-start.13) | collective-permute-done | bytes 393248 | tf_op jit(solution)/shard_map/ppermute | solution.py:33
  757.8 4.6 join.3
  764.4 4.6 join.5
  770.8 5.8 join.4
  (165 shorter events, 88.1 us)
Async XLA Ops:
  7.2 115.0 %all-gather.4.cloned.1.call-start = ((), (), s32[]{:S(2)}) async-start(), calls=%async_computation.3 | async-start | bytes 4587520 | tf_op jit(solution)/shard_map/all_gather | solution.py:47
  24.1 27.7 %copy-start.23 = (bf16[1,512,2048]{2,1,0:T(8,128)(2,1)S(1)}, bf16[1,512,2048]{2,1,0:T(8,128)(2,1)}, u32[]{:S(2)}) copy-start(bf16[1,512,2048]{2,1,0:T(8,128)(2,1)} %param.14) | copy-start | bytes 6291460
  24.1 236.0 %all-gather.6.cloned.1.call-start = ((), (), s32[]{:S(2)}) async-start(), calls=%async_computation.4 | async-start | bytes 7864320 | tf_op jit(solution)/shard_map/all_gather | solution.py:47
  51.8 243.5 %all-gather.8.cloned.1.call-start = ((), (), s32[]{:S(2)}) async-start(), calls=%async_computation.5 | async-start | bytes 3932160 | tf_op jit(solution)/shard_map/all_gather | solution.py:47
  53.6 41.0 %copy-start.12 = (bf16[1,512,2048]{2,1,0:T(8,128)(2,1)S(1)}, bf16[1,512,2048]{2,1,0:T(8,128)(2,1)}, u32[]{:S(2)}) copy-start(bf16[1,512,2048]{2,1,0:T(8,128)(2,1)} %param.27) | copy-start | bytes 6291460
  53.6 43.2 %copy-start.28 = (s32[1,1024]{1,0:T(1,128)S(1)}, s32[1,1024]{1,0:T(1,128)}, u32[]{:S(2)}) copy-start(s32[1,1024]{1,0:T(1,128)} %param.15) | copy-start | bytes 12292
  94.7 57.5 %collective-permute-start.1 = (bf16[256,2048]{1,0:T(8,128)(2,1)S(1)}, bf16[256,2048]{1,0:T(8,128)(2,1)S(1)}, u32[]{:S(2)}, u32[]{:S(2)}) collective-permute-start(bf16[256,2048]{1,0:T(8,128)(2,1)S(1)} %dynamic-slice_bitcast_fusion.refs_1_), channel_id=1, source_target_pairs={{0,4},{4,0},{8,12},{12,8},{16,20},{20,16},{24,28},{28,24},{1,5},{5... | collective-permute-start | bytes 3145736 | tf_op jit(solution)/shard_map/ppermute | solution.py:38
  96.2 107.4 %collective-permute-start.2 = (bf16[256,2048]{1,0:T(8,128)(2,1)S(1)}, bf16[256,2048]{1,0:T(8,128)(2,1)S(1)}, u32[]{:S(2)}, u32[]{:S(2)}) collective-permute-start(bf16[256,2048]{1,0:T(8,128)(2,1)S(1)} %dynamic-slice_bitcast_fusion.refs_1_), channel_id=1, source_target_pairs={{0,2},{2,0},{1,3},{3,1},{4,6},{6,4},{5,7},{7,5},{8,10},{10,8},{9,1... | collective-permute-start | bytes 3145736 | tf_op jit(solution)/shard_map/ppermute | solution.py:33
  96.7 23.5 %collective-permute-start = (s32[1,1024]{1,0:T(1,128)S(1)}, s32[1,1024]{1,0:T(1,128)S(1)}, u32[]{:S(2)}, u32[]{:S(2)}) collective-permute-start(s32[1,1024]{1,0:T(1,128)S(1)} %copy-done.28), channel_id=1, source_target_pairs={{0,4},{4,0},{8,12},{12,8},{16,20},{20,16},{24,28},{28,24},{1,5},{5... | collective-permute-start | bytes 12296 | tf_op jit(solution)/shard_map/ppermute | solution.py:38
  97.5 487.9 %reduce-scatter.4.cloned.1.call-start = ((), (), s32[]{:S(2)}) async-start(), calls=%async_computation.6 | async-start | bytes 3932160 | tf_op jit(solution)/shard_map/reduce_scatter | solution.py:51
  152.1 51.5 %copy-start.15 = (bf16[256,2048]{1,0:T(8,128)(2,1)}, bf16[256,2048]{1,0:T(8,128)(2,1)S(1)}, u32[]{:S(2)}) copy-start(bf16[256,2048]{1,0:T(8,128)(2,1)S(1)} %collective-permute-done.1.refs_2_) | copy-start | bytes 3145732
  163.1 40.1 %copy-start.4 = (bf16[256,2048]{1,0:T(8,128)(2,1)S(1)}, bf16[256,2048]{1,0:T(8,128)(2,1)}, u32[]{:S(2)}) copy-start(bf16[256,2048]{1,0:T(8,128)(2,1)} %get-tuple-element.46.refs_0_) | copy-start | bytes 3145732
  203.6 14.0 %collective-permute-start.3 = (bf16[128,2048]{1,0:T(8,128)(2,1)S(1)}, bf16[128,2048]{1,0:T(8,128)(2,1)S(1)}, u32[]{:S(2)}, u32[]{:S(2)}) collective-permute-start(bf16[128,2048]{1,0:T(8,128)(2,1)S(1)} %slice.64), channel_id=1, source_target_pairs={{0,2},{2,0},{1,3},{3,1},{4,6},{6,4},{5,7},{7,5},{8,10},{10,8},{9,1... | collective-permute-start | bytes 1572872 | tf_op jit(solution)/shard_map/ppermute | solution.py:33
  204.3 14.3 %collective-permute-start.4 = (bf16[128,2048]{1,0:T(8,128)(2,1)S(1)}, bf16[128,2048]{1,0:T(8,128)(2,1)S(1)}, u32[]{:S(2)}, u32[]{:S(2)}) collective-permute-start(bf16[128,2048]{1,0:T(8,128)(2,1)S(1)} %slice.65), channel_id=1, source_target_pairs={{0,4},{4,0},{8,12},{12,8},{16,20},{20,16},{24,28},{28,24},{1,5},{5... | collective-permute-start | bytes 1572872 | tf_op jit(solution)/shard_map/ppermute | solution.py:38
  369.4 41.3 %copy-start.9 = (bf16[2048,256]{1,0:T(8,128)(2,1)S(1)}, bf16[2048,256]{1,0:T(8,128)(2,1)}, u32[]{:S(2)}) copy-start(bf16[2048,256]{1,0:T(8,128)(2,1)} %attend.1) | copy-start | bytes 3145732
  460.6 174.5 %reduce-scatter.6.cloned.1.call-start = ((), (), s32[]{:S(2)}) async-start(), calls=%async_computation.7 | async-start | bytes 7864320 | tf_op jit(solution)/shard_map/reduce_scatter | solution.py:51
  461.2 237.0 %reduce-scatter.8.cloned.1.call-start = ((), (), s32[]{:S(2)}) async-start(), calls=%async_computation.8 | async-start | bytes 3932160 | tf_op jit(solution)/shard_map/reduce_scatter | solution.py:51
  461.2 25.5 %collective-permute-start.5 = (bf16[256,2048]{1,0:T(8,128)(2,1)S(1)}, bf16[256,2048]{1,0:T(8,128)(2,1)S(1)}, u32[]{:S(2)}, u32[]{:S(2)}) collective-permute-start(bf16[256,2048]{1,0:T(8,128)(2,1)S(1)} %get-tuple-element.58), channel_id=1, source_target_pairs={{0,2},{2,0},{1,3},{3,1},{4,6},{6,4},{5,7},{7,5},{8,10},{10,8},{9,1... | collective-permute-start | bytes 3145736 | tf_op jit(solution)/shard_map/ppermute | solution.py:33
  462.4 25.2 %collective-permute-start.7 = (bf16[256,2048]{1,0:T(8,128)(2,1)S(1)}, bf16[256,2048]{1,0:T(8,128)(2,1)}, u32[]{:S(2)}, u32[]{:S(2)}) collective-permute-start(bf16[256,2048]{1,0:T(8,128)(2,1)S(1)} %get-tuple-element.63), channel_id=1, source_target_pairs={{0,4},{4,0},{8,12},{12,8},{16,20},{20,16},{24,28},{28,24},{1,5},{5... | collective-permute-start | bytes 3145736 | tf_op jit(solution)/shard_map/ppermute | solution.py:38
  491.7 13.2 %collective-permute-start.8 = (bf16[128,2048]{1,0:T(8,128)(2,1)}, bf16[128,2048]{1,0:T(8,128)(2,1)S(1)}, u32[]{:S(2)}, u32[]{:S(2)}) collective-permute-start(bf16[128,2048]{1,0:T(8,128)(2,1)} %slice.117), channel_id=1, source_target_pairs={{0,2},{2,0},{1,3},{3,1},{4,6},{6,4},{5,7},{7,5},{8,10},{10,8},{9,1... | collective-permute-start | bytes 1572872 | tf_op jit(solution)/shard_map/ppermute | solution.py:33
  493.5 13.0 %collective-permute-start.6 = (bf16[128,2048]{1,0:T(8,128)(2,1)}, bf16[128,2048]{1,0:T(8,128)(2,1)S(1)}, u32[]{:S(2)}, u32[]{:S(2)}) collective-permute-start(bf16[128,2048]{1,0:T(8,128)(2,1)} %slice.118), channel_id=1, source_target_pairs={{0,4},{4,0},{8,12},{12,8},{16,20},{20,16},{24,28},{28,24},{1,5},{5... | collective-permute-start | bytes 1572872 | tf_op jit(solution)/shard_map/ppermute | solution.py:38
  510.5 73.2 %collective-permute-start.9 = (bf16[256,2048]{1,0:T(8,128)(2,1)}, bf16[256,2048]{1,0:T(8,128)(2,1)}, u32[]{:S(2)}, u32[]{:S(2)}) collective-permute-start(bf16[256,2048]{1,0:T(8,128)(2,1)} %fusion.18), channel_id=1, source_target_pairs={{0,1},{1,0},{2,3},{3,2},{4,5},{5,4},{6,7},{7,6},{8,9},{9,8},{10,11... | collective-permute-start | bytes 3145736 | tf_op jit(solution)/shard_map/ppermute | solution.py:29
  559.8 142.9 %collective-permute-start.10 = (bf16[256,2048]{1,0:T(8,128)(2,1)S(1)}, bf16[256,2048]{1,0:T(8,128)(2,1)}, u32[]{:S(2)}, u32[]{:S(2)}) collective-permute-start(bf16[256,2048]{1,0:T(8,128)(2,1)S(1)} %fusion.14), channel_id=1, source_target_pairs={{0,1},{1,0},{2,3},{3,2},{4,5},{5,4},{6,7},{7,6},{8,9},{9,8},{10,11... | collective-permute-start | bytes 3145736 | tf_op jit(solution)/shard_map/ppermute | solution.py:29
  637.8 66.4 %collective-permute-start.14 = (bf16[256,1536]{1,0:T(8,128)(2,1)}, bf16[256,1536]{1,0:T(8,128)(2,1)}, u32[]{:S(2)}, u32[]{:S(2)}) collective-permute-start(bf16[256,1536]{1,0:T(8,128)(2,1)} %get-tuple-element.89), channel_id=1, source_target_pairs={{0,4},{4,0},{8,12},{12,8},{16,20},{20,16},{24,28},{28,24},{1,5},{5... | collective-permute-start | bytes 2359304 | tf_op jit(solution)/shard_map/ppermute | solution.py:38
  640.2 66.0 %collective-permute-start.11 = (bf16[256,768]{1,0:T(8,128)(2,1)}, bf16[256,768]{1,0:T(8,128)(2,1)}, u32[]{:S(2)}, u32[]{:S(2)}) collective-permute-start(bf16[256,768]{1,0:T(8,128)(2,1)} %get-tuple-element.93), channel_id=1, source_target_pairs={{0,4},{4,0},{8,12},{12,8},{16,20},{20,16},{24,28},{28,24},{1,5},{5... | collective-permute-start | bytes 1179656 | tf_op jit(solution)/shard_map/ppermute | solution.py:38
  640.7 67.0 %collective-permute-start.12 = (bf16[256,768]{1,0:T(8,128)(2,1)}, bf16[256,768]{1,0:T(8,128)(2,1)}, u32[]{:S(2)}, u32[]{:S(2)}) collective-permute-start(bf16[256,768]{1,0:T(8,128)(2,1)} %get-tuple-element.94.kept_ref), channel_id=1, source_target_pairs={{0,2},{2,0},{1,3},{3,1},{4,6},{6,4},{5,7},{7,5},{8,10},{10,8},{9,1... | collective-permute-start | bytes 1179656 | tf_op jit(solution)/shard_map/ppermute | solution.py:33
  699.3 10.6 %collective-permute-start.17 = (bf16[256,768]{1,0:T(8,128)(2,1)S(1)}, bf16[256,768]{1,0:T(8,128)(2,1)}, u32[]{:S(2)}, u32[]{:S(2)}) collective-permute-start(bf16[256,768]{1,0:T(8,128)(2,1)S(1)} %get-tuple-element.91), channel_id=1, source_target_pairs={{0,4},{4,0},{8,12},{12,8},{16,20},{20,16},{24,28},{28,24},{1,5},{5... | collective-permute-start | bytes 1179656 | tf_op jit(solution)/shard_map/ppermute | solution.py:38
  702.7 66.3 %collective-permute-start.15 = (bf16[256,1536]{1,0:T(8,128)(2,1)}, bf16[256,1536]{1,0:T(8,128)(2,1)S(1)}, u32[]{:S(2)}, u32[]{:S(2)}) collective-permute-start(bf16[256,1536]{1,0:T(8,128)(2,1)} %get-tuple-element.90.kept_ref), channel_id=1, source_target_pairs={{0,2},{2,0},{1,3},{3,1},{4,6},{6,4},{5,7},{7,5},{8,10},{10,8},{9,1... | collective-permute-start | bytes 2359304 | tf_op jit(solution)/shard_map/ppermute | solution.py:33
  704.2 64.9 %collective-permute-start.16 = (bf16[256,1536]{1,0:T(8,128)(2,1)}, bf16[256,1536]{1,0:T(8,128)(2,1)S(1)}, u32[]{:S(2)}, u32[]{:S(2)}) collective-permute-start(bf16[256,1536]{1,0:T(8,128)(2,1)} %collective-permute-done.14.x_ref), channel_id=1, source_target_pairs={{0,2},{2,0},{1,3},{3,1},{4,6},{6,4},{5,7},{7,5},{8,10},{10,8},{9,1... | collective-permute-start | bytes 2359304 | tf_op jit(solution)/shard_map/ppermute | solution.py:33
  706.1 56.2 %collective-permute-start.18 = (bf16[256,768]{1,0:T(8,128)(2,1)S(1)}, bf16[256,768]{1,0:T(8,128)(2,1)S(1)}, u32[]{:S(2)}, u32[]{:S(2)}) collective-permute-start(bf16[256,768]{1,0:T(8,128)(2,1)S(1)} %get-tuple-element.92.kept_ref), channel_id=1, source_target_pairs={{0,2},{2,0},{1,3},{3,1},{4,6},{6,4},{5,7},{7,5},{8,10},{10,8},{9,1... | collective-permute-start | bytes 1179656 | tf_op jit(solution)/shard_map/ppermute | solution.py:33
  707.7 49.3 %collective-permute-start.13 = (bf16[256,768]{1,0:T(8,128)(2,1)}, bf16[256,768]{1,0:T(8,128)(2,1)S(1)}, u32[]{:S(2)}, u32[]{:S(2)}) collective-permute-start(bf16[256,768]{1,0:T(8,128)(2,1)} %collective-permute-done.11.x_ref), channel_id=1, source_target_pairs={{0,2},{2,0},{1,3},{3,1},{4,6},{6,4},{5,7},{7,5},{8,10},{10,8},{9,1... | collective-permute-start | bytes 1179656 | tf_op jit(solution)/shard_map/ppermute | solution.py:33
  710.0 53.7 %collective-permute-start.19 = (bf16[256,768]{1,0:T(8,128)(2,1)}, bf16[256,768]{1,0:T(8,128)(2,1)S(1)}, u32[]{:S(2)}, u32[]{:S(2)}) collective-permute-start(bf16[256,768]{1,0:T(8,128)(2,1)} %collective-permute-done.17.x_ref), channel_id=1, source_target_pairs={{0,2},{2,0},{1,3},{3,1},{4,6},{6,4},{5,7},{7,5},{8,10},{10,8},{9,1... | collective-permute-start | bytes 1179656 | tf_op jit(solution)/shard_map/ppermute | solution.py:33
  (26 other events, 114.6 us)
Sparse Core Ops, SparseCore 0:
  24.2 73.5 all-gather.3
  99.4 113.8 all-gather.5
  214.9 61.6 all-gather.7
  460.7 60.6 reduce-scatter.3
  523.6 111.4 reduce-scatter.5
  637.2 60.8 reduce-scatter.7

commit v6 on v5

--- a/solution.py
+++ b/solution.py
@@ -520,12 +520,8 @@
         place = pl.ds(where(chunk), wide)
         source = pl.ds(side * 4 * wide + where(chunk), wide)
 
-        def step(index, _):
-            cols = pl.ds(pl.multiple_of(part * half + index * (half // 2), half // 2), half // 2)
-            target[place, cols] = mm(acts[source, :], weight[cols, :], 1, 1).astype(target.dtype)
-            return 0
-
-        lax.fori_loop(0, 2, step, 0)
+        cols = pl.ds(part * half, half)
+        target[place, cols] = mm(acts[source, :], weight[cols, :], 1, 1).astype(target.dtype)
 
     def remote(copies, key, number, source, target, peer):
         copies[key] = pltpu.make_async_remote_copy(
@@ -765,7 +761,7 @@
     while bit < lax.axis_size("fsdp"):
         stages.append(("fsdp", bit))
         bit *= 2
-    stages += [("tp", 1), ("fsdp", 1), ("ctx", 1)]
+    stages += [("tp", 1), ("fsdp", 1)]
     return pl.pallas_call(
         functools.partial(total_kernel, tuple(stages)),
         out_shape=jax.ShapeDtypeStruct(part.shape, F32),
@@ -1236,12 +1232,13 @@
     inverse_in = inv_rms(own_in)
     scaled_in = own_in * inverse_in
     norm_gain_part = jnp.sum(in_grad * scaled_in, axis=0)
-    token_grad = finish_rows(
-        (grad_middle + norm_back(in_grad, scaled_in, inverse_in, in_gain)).astype(BF16)
-    )
+    own_token_grad = (grad_middle + norm_back(in_grad, scaled_in, inverse_in, in_gain)).astype(BF16)
+    token_grad = finish_rows(own_token_grad)
 
     parts = jnp.concatenate([norm_gain_part, mlp_gain_part, head_gain_parts.reshape(-1)])
-    sums = total(parts.reshape(-1, HEAD)).reshape(-1)
+    parts = parts.reshape(-1, HEAD)
+    far_parts = swap_ctx(parts)
+    sums = total(parts + after(far_parts, token_grad)).reshape(-1)
     norm_gain_grad = lax.dynamic_slice_in_dim(sums, mine * block, block, 0)
     mlp_gain_grad = lax.dynamic_slice_in_dim(sums, width + mine * block, block, 0)
     query_gain_grad = lax.dynamic_slice_in_dim(sums, 2 * width + mine * small, small, 0)

time: 793 us -> 696 us (0.88)
  waiting for transfers between devices: 215 us -> 123 us
    reduce_scatter x3, waiting for transfers between devices: 106 us -> 13.5 us  [scatter_line(): lax.psum_scatter(value, 'fsdp', scatter_dimension=0, tiled=True, axis_ind...]
    ppermute x10 -> x11, waiting for transfers between devices: 89.5 us -> 91.6 us  [swap_ctx(): return lax.ppermute(value, 'ctx', [(0, 1), (1, 0)])]
  transfers between devices with their start and end apart: 26 -> 27, of which waited for: 12 -> 12; matrix products, arithmetic and copies ran while one was open for 12% -> 18% of each run, Pallas kernels for 30% -> 44%
where the time goes in v6:
time: 696 us; the launch traced here: 687 us
  Pallas kernels  375 us (54%)
  waiting for transfers between devices  123 us (18%)
  matrix products  85.8 us (12%)
  other arithmetic  40.9 us (6%)
  local copies, waits for them, and re-layouts  26.4 us (4%)
  starting transfers between devices  20.2 us (3%)
  between operations  15 us (2%)
    pallas_call x2, Pallas kernels, product_reduce8(): pl.pallas_call(functools.partial(product_reduce8_kernel, rows, groups, fi...  93.1 us
    ppermute x11, waiting for transfers between devices, swap_ctx(): return lax.ppermute(value, 'ctx', [(0, 1), (1, 0)])  91.6 us
    dot_general x9, matrix products, mm(): lax.dot_general(left, right, (((left_dim,), (right_dim,)), ((), ())), pre...  85.8 us
    pallas_call x2, Pallas kernels, gather8(): pl.pallas_call(functools.partial(gather8_kernel, rows, bool(also)), out_s...  81.5 us
    pallas_call x2, Pallas kernels, shards(): pl.pallas_call(functools.partial(shard_kernel, tuple(plan), len(groups)),...  41.6 us
    pallas_call x1, Pallas kernels, gather8_product(): pl.pallas_call(functools.partial(gather8_product_kernel, rows), out_shape...  41.2 us
    pallas_call x1, Pallas kernels, reduce8(): pl.pallas_call(functools.partial(reduce8_kernel, rows), out_shape=jax.Sha...  40.1 us
    pallas_call x1, Pallas kernels, attend_back(): pl.pallas_call(functools.partial(attend_back_kernel, heads, tile), out_sh...  28.7 us
  transfers between devices with their start and end apart: 27, of which 12 were waited for; matrix products, arithmetic and copies ran while one was open for 18% of the time, Pallas kernels for 44%

profile of v6, /device:TPU:0, one launch (start us, length us, event | category | flops | bytes accessed | tf_op | source)
XLA Modules:
  0.0 686.6 jit_solution(7651310329360135982)
XLA Ops:
  10.1 14.0 %shards.2 = bf16[512,896]{1,0:T(8,128)(2,1)} custom-call(bf16[256,1024]{1,0:T(8,128)(2,1)} %refs_0_.1, bf16[256,512]{1,0:T(8,128)(2,1)} %refs_1_.2, bf16[256,512]{1,0:T(8,128)(2,1)} %refs_2_.2, bf16[256,1024]{1,0:T(8,128)(2,1)} %refs_3_.1, bf16[256,128]{1,0:T(8,128)(2,1)} %select_select_fusion.refs_4_), custom_call_target="tpu_custom_call" | custom-call | tf_op jit(solution)/shard_map/shards/pallas_call | solution.py:717
  24.1 27.6 %shards.3 = (bf16[512,1536]{1,0:T(8,128)(2,1)}, bf16[512,768]{1,0:T(8,128)(2,1)}) custom-call(bf16[256,3072]{1,0:T(8,128)(2,1)} %refs_0_.2, bf16[256,3072]{1,0:T(8,128)(2,1)} %refs_1_.3, bf16[256,3072]{1,0:T(8,128)(2,1)} %refs_2_.3), custom_call_target="tpu_custom_call" | custom-call | tf_op jit(solution)/shard_map/shards/pallas_call | solution.py:717
  53.6 40.9 %gather8.1 = bf16[2048,2048]{1,0:T(8,128)(2,1)} custom-call(bf16[256,2048]{1,0:T(8,128)(2,1)} %get-tuple-element.47.refs_0_), custom_call_target="tpu_custom_call" | custom-call | tf_op jit(solution)/shard_map/gather8/pallas_call | solution.py:352
  97.6 5.1 fusion
  106.5 13.8 %collective-permute-done = s32[1,1024]{1,0:T(1,128)S(1)} collective-permute-done((s32[1,1024]{1,0:T(1,128)S(1)}, s32[1,1024]{1,0:T(1,128)S(1)}, u32[]{:S(2)}, u32[]{:S(2)}) %collective-permute-start) | collective-permute-done | bytes 4128 | tf_op jit(solution)/shard_map/ppermute | solution.py:38
  125.0 10.6 %fusion.8.qkv_ref = f32[2048,512]{1,0:T(8,128)} fusion(bf16[2048,2048]{1,0:T(8,128)(2,1)} %gather8.1, f32[2048]{0:T(1024)S(1)} %get-tuple-element.82, f32[2048]{0:T(1024)S(1)} %add_rsqrt_fusion, bf16[2048,896]{1,0:T(8,128)(2,1)} %all-gather.4.cloned.1.call-done.refs_1_), kind=kOutput, calls=%fused_computation.24 | convolution fusion | flops 4311744512 | bytes 14696448 | tf_op jit(solution)/shard_map/dot_general | solution.py:23
  135.5 16.2 %attend.1 = bf16[2048,256]{1,0:T(8,128)(2,1)} custom-call(s32[2]{0:T(128)} %pad_add_fusion.1.meta_ref, f32[2048,512]{1,0:T(8,128)} %fusion.8.qkv_ref, s32[2,1024,1]{2,1,0:T(8,128)} %copy.33.segc_ref, s32[2,1,1024]{2,1,0:T(1,128)} %broadcast_in_dim.76.segr_ref, f32[1024,128]{1,0:T(8,128)} %get-tuple-element.108.cos_ref, ...), custom_call_target="tpu_custom_call" | custom-call | flops 1073741824 | bytes 5242880 | tf_op jit(solution)/shard_map/attend/pallas_call | solution.py:1015
  151.8 5.1 convolution_convert_fusion.far_ref
  156.9 5.8 fusion.21.near_ref
  162.7 40.1 %reduce8.1 = f32[256,2048]{1,0:T(8,128)S(1)} custom-call(f32[1024,2048]{1,0:T(8,128)} %fusion.21.near_ref, bf16[1024,2048]{1,0:T(8,128)(2,1)} %convolution_convert_fusion.far_ref), custom_call_target="tpu_custom_call" | custom-call | tf_op jit(solution)/shard_map/reduce8/pallas_call | solution.py:445
  205.9 11.4 %collective-permute-done.3.refs_4_ = bf16[128,2048]{1,0:T(8,128)(2,1)S(1)} collective-permute-done((bf16[128,2048]{1,0:T(8,128)(2,1)S(1)}, bf16[128,2048]{1,0:T(8,128)(2,1)S(1)}, u32[]{:S(2)}, u32[]{:S(2)}) %collective-permute-start.3) | collective-permute-done | bytes 524320 | tf_op jit(solution)/shard_map/ppermute | solution.py:33
  219.0 40.6 %gather8_also.1 = (bf16[2048,2048]{1,0:T(8,128)(2,1)}, bf16[2048,2048]{1,0:T(8,128)(2,1)}) custom-call(bf16[256,2048]{1,0:T(8,128)(2,1)} %multiply_convert_fusion.3.refs_0_, bf16[256,2048]{1,0:T(8,128)(2,1)} %copy-done.12, bf16[256,2048]{1,0:T(8,128)(2,1)} %copy-done.16, bf16[256,2048]{1,0:T(8,128)(2,1)} %copy-done.17, bf16[128,2048]{1,0:T(8,128)(2,1)} %copy-done.22, ...), custom_call_target="tpu_custom_call" | custom-call | tf_op jit(solution)/shard_map/gather8_also/pallas_call | solution.py:352
  259.7 17.6 %fusion.31 = f32[2048,1536]{1,0:T(8,128)S(1)} fusion(bf16[2048,2048]{1,0:T(8,128)(2,1)} %get-tuple-element.54.refs_3_, bf16[2048,1536]{1,0:T(8,128)(2,1)} %all-gather.6.cloned.1.call-done.refs_2_), kind=kOutput, calls=%fused_computation.90 | convolution fusion | flops 12884901888 | bytes 27262976 | tf_op jit(solution)/shard_map/dot_general | solution.py:23
  279.4 4.3 copy-done.7
  286.4 8.5 %convolution_convert_fusion.1 = bf16[2048,768]{1,0:T(8,128)(2,1)} fusion(bf16[2048,2048]{1,0:T(8,128)(2,1)S(1)} %copy-done.37, bf16[2048,768]{1,0:T(8,128)(2,1)S(1)} %multiply_convert_fusion.2.acts_ref), kind=kOutput, calls=%fused_computation.11 | convolution fusion | flops 6444023808 | bytes 14680064 | tf_op jit(solution)/shard_map/dot_general | solution.py:23
  294.9 16.4 %multiply_convert_fusion = (bf16[2048,768]{1,0:T(8,128)(2,1)}, bf16[2048,768]{1,0:T(8,128)(2,1)}) fusion(f32[2048,1536]{1,0:T(8,128)} %copy-done.7, bf16[2048,2048]{1,0:T(8,128)(2,1)} %get-tuple-element.55, bf16[2048,768]{1,0:T(8,128)(2,1)} %all-gather.8.cloned.1.call-done.weight_ref), kind=kOutput, calls=%fused_computation.5 | convolution fusion | flops 6462898176 | bytes 30408704 | tf_op jit(solution)/shard_map/dot_general | solution.py:23
  311.3 51.7 %product_reduce8.2 = (f32[256,2048]{1,0:T(8,128)}, bf16[2048,1536]{1,0:T(8,128)(2,1)}) custom-call(bf16[2048,768]{1,0:T(8,128)(2,1)} %get-tuple-element.88.refs_0_, bf16[2048,768]{1,0:T(8,128)(2,1)} %get-tuple-element.87.refs_1_, bf16[2048,1536]{1,0:T(8,128)(2,1)} %all-gather.6.cloned.1.call-done.refs_2_, bf16[2048,2048]{1,0:T(8,128)(2,1)} %get-tuple-element.54.refs_3_), custom_call_target="tpu_custom_call" | custom-call | flops 25769803776 | bytes 25165824 | tf_op jit(solution)/shard_map/product_reduce8/pallas_call | solution.py:646
  367.7 41.2 %gather8_product.1 = (bf16[2048,2048]{1,0:T(8,128)(2,1)}, f32[512,2048]{1,0:T(8,128)}, bf16[256,2048]{1,0:T(8,128)(2,1)S(1)}, bf16[256,2048]{1,0:T(8,128)(2,1)S(1)}) custom-call(bf16[256,2048]{1,0:T(8,128)(2,1)S(1)} %fusion.28.own_ref, bf16[2048,768]{1,0:T(8,128)(2,1)} %copy-done.15, bf16[2048,768]{1,0:T(8,128)(2,1)} %all-gather.8.cloned.1.call-done.weight_ref), custom_call_target="tpu_custom_call" | custom-call | flops 6442450944 | bytes 8388608 | tf_op jit(solution)/shard_map/gather8_product/pallas_call | solution.py:311
  409.0 7.0 %convolution_convert_fusion.4.grad_ref = bf16[2048,256]{1,0:T(8,128)(2,1)} fusion(bf16[2048,2048]{1,0:T(8,128)(2,1)} %get-tuple-element.60, bf16[2048,896]{1,0:T(8,128)(2,1)} %all-gather.4.cloned.1.call-done.refs_1_), kind=kOutput, calls=%fused_computation.23 | convolution fusion | flops 2148007936 | bytes 10485760 | tf_op jit(solution)/shard_map/dot_general | solution.py:23
  416.0 28.7 %attend_back.1 = (bf16[2048,512]{1,0:T(8,128)(2,1)}, f32[2,128]{1,0:T(2,128)}) custom-call(s32[2]{0:T(128)} %pad_add_fusion.1.meta_ref, f32[2048,512]{1,0:T(8,128)} %fusion.8.qkv_ref, bf16[2048,256]{1,0:T(8,128)(2,1)} %convolution_convert_fusion.4.grad_ref, s32[2,1024,1]{2,1,0:T(8,128)} %copy.33.segc_ref, s32[2,1,1024]{2,1,0:T(1,128)} %broadcast_in_dim.76.segr_ref, ...), custom_call_target="tpu_custom_call" | custom-call | flops 2684354560 | bytes 8388608 | tf_op jit(solution)/shard_map/attend_back/pallas_call | solution.py:1043
  444.8 6.0 convolution_convert_fusion.3
  450.9 8.7 %convolution_convert_fusion.2 = bf16[2048,512]{1,0:T(8,128)(2,1)S(1)} fusion(bf16[2048,512]{1,0:T(8,128)(2,1)S(1)} %copy-done.38, bf16[2048,2048]{1,0:T(8,128)(2,1)} %gather8.1, f32[2048]{0:T(1024)S(1)} %copy-done.31, f32[2048]{0:T(1024)S(1)} %copy-done.33), kind=kOutput, calls=%fused_computation.18 | convolution fusion | flops 4312793088 | bytes 12599296 | tf_op jit(solution)/shard_map/dot_general | solution.py:23
  463.8 23.4 %collective-permute-done.5 = bf16[256,2048]{1,0:T(8,128)(2,1)S(1)} collective-permute-done((bf16[256,2048]{1,0:T(8,128)(2,1)S(1)}, bf16[256,2048]{1,0:T(8,128)(2,1)S(1)}, u32[]{:S(2)}, u32[]{:S(2)}) %collective-permute-start.5) | collective-permute-done | bytes 1048608 | tf_op jit(solution)/shard_map/ppermute | solution.py:33
  493.5 10.9 %collective-permute-done.8 = bf16[128,2048]{1,0:T(8,128)(2,1)S(1)} collective-permute-done((bf16[128,2048]{1,0:T(8,128)(2,1)S(1)}, bf16[128,2048]{1,0:T(8,128)(2,1)S(1)}, u32[]{:S(2)}, u32[]{:S(2)}) %collective-permute-start.8) | collective-permute-done | bytes 524320 | tf_op jit(solution)/shard_map/ppermute | solution.py:33
  506.7 41.4 %product_reduce8.3 = f32[256,2048]{1,0:T(8,128)} custom-call(bf16[2048,512]{1,0:T(8,128)(2,1)} %get-tuple-element.67.refs_0_, bf16[2048,896]{1,0:T(8,128)(2,1)} %all-gather.4.cloned.1.call-done.refs_1_), custom_call_target="tpu_custom_call" | custom-call | flops 4294967296 | bytes 8388608 | tf_op jit(solution)/shard_map/product_reduce8/pallas_call | solution.py:646
  550.9 3.8 fusion.14
  566.2 17.7 %total.1 = f32[34,128]{1,0:T(8,128)} custom-call(f32[34,128]{1,0:T(8,128)} %fusion.26.part_ref), custom_call_target="tpu_custom_call" | custom-call | tf_op jit(solution)/shard_map/total/pallas_call | solution.py:765
  587.8 13.4 %reduce-scatter.8.cloned.1.call-done = bf16[512,768]{1,0:T(8,128)(2,1)} async-done(((bf16[2048,768]{1,0:T(8,128)(2,1)}), bf16[512,768]{1,0:T(8,128)(2,1)}) %reduce-scatter.8.cloned.1.call-update) | async-done | bytes 786448 | tf_op jit(solution)/shard_map/reduce_scatter | solution.py:51
  616.2 44.7 %collective-permute-done.14.both_ref = bf16[256,768]{1,0:T(8,128)(2,1)S(1)} collective-permute-done((bf16[256,768]{1,0:T(8,128)(2,1)S(1)}, bf16[256,768]{1,0:T(8,128)(2,1)S(1)}, u32[]{:S(2)}, u32[]{:S(2)}) %collective-permute-start.14) | collective-permute-done | bytes 393248 | tf_op jit(solution)/shard_map/ppermute | solution.py:33
  661.7 4.6 join.3
  668.3 4.6 join.5
  673.8 5.8 join.4
  (182 shorter events, 79.9 us)
Async XLA Ops:
  7.2 115.0 %all-gather.4.cloned.1.call-start = ((), (), s32[]{:S(2)}) async-start(), calls=%async_computation.3 | async-start | bytes 4587520 | tf_op jit(solution)/shard_map/all_gather | solution.py:47
  24.1 235.6 %all-gather.6.cloned.1.call-start = ((), (), s32[]{:S(2)}) async-start(), calls=%async_computation.4 | async-start | bytes 7864320 | tf_op jit(solution)/shard_map/all_gather | solution.py:47
  51.8 243.1 %all-gather.8.cloned.1.call-start = ((), (), s32[]{:S(2)}) async-start(), calls=%async_computation.5 | async-start | bytes 3932160 | tf_op jit(solution)/shard_map/all_gather | solution.py:47
  53.6 41.0 %copy-start.10 = (bf16[1,512,2048]{2,1,0:T(8,128)(2,1)S(1)}, bf16[1,512,2048]{2,1,0:T(8,128)(2,1)}, u32[]{:S(2)}) copy-start(bf16[1,512,2048]{2,1,0:T(8,128)(2,1)} %param.27) | copy-start | bytes 6291460
  53.6 43.2 %copy-start.36 = (s32[1,1024]{1,0:T(1,128)S(1)}, s32[1,1024]{1,0:T(1,128)}, u32[]{:S(2)}) copy-start(s32[1,1024]{1,0:T(1,128)} %param.15) | copy-start | bytes 12292
  94.7 57.1 %collective-permute-start.1 = (bf16[256,2048]{1,0:T(8,128)(2,1)S(1)}, bf16[256,2048]{1,0:T(8,128)(2,1)S(1)}, u32[]{:S(2)}, u32[]{:S(2)}) collective-permute-start(bf16[256,2048]{1,0:T(8,128)(2,1)S(1)} %dynamic-slice_bitcast_fusion.refs_1_), channel_id=1, source_target_pairs={{0,4},{4,0},{8,12},{12,8},{16,20},{20,16},{24,28},{28,24},{1,5},{5... | collective-permute-start | bytes 3145736 | tf_op jit(solution)/shard_map/ppermute | solution.py:38
  96.2 107.0 %collective-permute-start.2 = (bf16[256,2048]{1,0:T(8,128)(2,1)S(1)}, bf16[256,2048]{1,0:T(8,128)(2,1)S(1)}, u32[]{:S(2)}, u32[]{:S(2)}) collective-permute-start(bf16[256,2048]{1,0:T(8,128)(2,1)S(1)} %dynamic-slice_bitcast_fusion.refs_1_), channel_id=1, source_target_pairs={{0,2},{2,0},{1,3},{3,1},{4,6},{6,4},{5,7},{7,5},{8,10},{10,8},{9,1... | collective-permute-start | bytes 3145736 | tf_op jit(solution)/shard_map/ppermute | solution.py:33
  96.7 23.5 %collective-permute-start = (s32[1,1024]{1,0:T(1,128)S(1)}, s32[1,1024]{1,0:T(1,128)S(1)}, u32[]{:S(2)}, u32[]{:S(2)}) collective-permute-start(s32[1,1024]{1,0:T(1,128)S(1)} %copy-done.36), channel_id=1, source_target_pairs={{0,4},{4,0},{8,12},{12,8},{16,20},{20,16},{24,28},{28,24},{1,5},{5... | collective-permute-start | bytes 12296 | tf_op jit(solution)/shard_map/ppermute | solution.py:38
  97.5 462.7 %reduce-scatter.6.cloned.1.call-start = ((), (), s32[]{:S(2)}) async-start(), calls=%async_computation.7 | async-start | bytes 7864320 | tf_op jit(solution)/shard_map/reduce_scatter | solution.py:51
  151.8 51.4 %copy-start.16 = (bf16[256,2048]{1,0:T(8,128)(2,1)}, bf16[256,2048]{1,0:T(8,128)(2,1)S(1)}, u32[]{:S(2)}) copy-start(bf16[256,2048]{1,0:T(8,128)(2,1)S(1)} %collective-permute-done.1.refs_2_) | copy-start | bytes 3145732
  203.3 14.0 %collective-permute-start.3 = (bf16[128,2048]{1,0:T(8,128)(2,1)S(1)}, bf16[128,2048]{1,0:T(8,128)(2,1)S(1)}, u32[]{:S(2)}, u32[]{:S(2)}) collective-permute-start(bf16[128,2048]{1,0:T(8,128)(2,1)S(1)} %slice.64), channel_id=1, source_target_pairs={{0,2},{2,0},{1,3},{3,1},{4,6},{6,4},{5,7},{7,5},{8,10},{10,8},{9,1... | collective-permute-start | bytes 1572872 | tf_op jit(solution)/shard_map/ppermute | solution.py:33
  203.9 14.3 %collective-permute-start.4 = (bf16[128,2048]{1,0:T(8,128)(2,1)S(1)}, bf16[128,2048]{1,0:T(8,128)(2,1)S(1)}, u32[]{:S(2)}, u32[]{:S(2)}) collective-permute-start(bf16[128,2048]{1,0:T(8,128)(2,1)S(1)} %slice.65), channel_id=1, source_target_pairs={{0,4},{4,0},{8,12},{12,8},{16,20},{20,16},{24,28},{28,24},{1,5},{5... | collective-permute-start | bytes 1572872 | tf_op jit(solution)/shard_map/ppermute | solution.py:38
  363.0 220.9 %reduce-scatter.4.cloned.1.call-start = ((), (), s32[]{:S(2)}) async-start(), calls=%async_computation.6 | async-start | bytes 3932160 | tf_op jit(solution)/shard_map/reduce_scatter | solution.py:51
  461.5 139.8 %reduce-scatter.8.cloned.1.call-start = ((), (), s32[]{:S(2)}) async-start(), calls=%async_computation.8 | async-start | bytes 3932160 | tf_op jit(solution)/shard_map/reduce_scatter | solution.py:51
  461.7 25.5 %collective-permute-start.5 = (bf16[256,2048]{1,0:T(8,128)(2,1)S(1)}, bf16[256,2048]{1,0:T(8,128)(2,1)S(1)}, u32[]{:S(2)}, u32[]{:S(2)}) collective-permute-start(bf16[256,2048]{1,0:T(8,128)(2,1)S(1)} %get-tuple-element.59), channel_id=1, source_target_pairs={{0,2},{2,0},{1,3},{3,1},{4,6},{6,4},{5,7},{7,5},{8,10},{10,8},{9,1... | collective-permute-start | bytes 3145736 | tf_op jit(solution)/shard_map/ppermute | solution.py:33
  462.8 25.3 %collective-permute-start.7 = (bf16[256,2048]{1,0:T(8,128)(2,1)S(1)}, bf16[256,2048]{1,0:T(8,128)(2,1)}, u32[]{:S(2)}, u32[]{:S(2)}) collective-permute-start(bf16[256,2048]{1,0:T(8,128)(2,1)S(1)} %get-tuple-element.64), channel_id=1, source_target_pairs={{0,4},{4,0},{8,12},{12,8},{16,20},{20,16},{24,28},{28,24},{1,5},{5... | collective-permute-start | bytes 3145736 | tf_op jit(solution)/shard_map/ppermute | solution.py:38
  491.3 13.1 %collective-permute-start.8 = (bf16[128,2048]{1,0:T(8,128)(2,1)S(1)}, bf16[128,2048]{1,0:T(8,128)(2,1)S(1)}, u32[]{:S(2)}, u32[]{:S(2)}) collective-permute-start(bf16[128,2048]{1,0:T(8,128)(2,1)S(1)} %slice.117), channel_id=1, source_target_pairs={{0,2},{2,0},{1,3},{3,1},{4,6},{6,4},{5,7},{7,5},{8,10},{10,8},{9,1... | collective-permute-start | bytes 1572872 | tf_op jit(solution)/shard_map/ppermute | solution.py:33
  492.4 12.8 %collective-permute-start.6 = (bf16[128,2048]{1,0:T(8,128)(2,1)S(1)}, bf16[128,2048]{1,0:T(8,128)(2,1)S(1)}, u32[]{:S(2)}, u32[]{:S(2)}) collective-permute-start(bf16[128,2048]{1,0:T(8,128)(2,1)S(1)} %slice.118), channel_id=1, source_target_pairs={{0,4},{4,0},{8,12},{12,8},{16,20},{20,16},{24,28},{28,24},{1,5},{5... | collective-permute-start | bytes 1572872 | tf_op jit(solution)/shard_map/ppermute | solution.py:38
  554.8 2.7 collective-permute-start.10
  555.8 50.8 %collective-permute-start.9 = (bf16[256,2048]{1,0:T(8,128)(2,1)S(1)}, bf16[256,2048]{1,0:T(8,128)(2,1)}, u32[]{:S(2)}, u32[]{:S(2)}) collective-permute-start(bf16[256,2048]{1,0:T(8,128)(2,1)S(1)} %copy-done.13), channel_id=1, source_target_pairs={{0,1},{1,0},{2,3},{3,2},{4,5},{5,4},{6,7},{7,6},{8,9},{9,8},{10,11... | collective-permute-start | bytes 3145736 | tf_op jit(solution)/shard_map/ppermute | solution.py:29
  556.0 9.6 %collective-permute-start.11 = (f32[34,128]{1,0:T(8,128)S(1)}, f32[34,128]{1,0:T(8,128)S(1)}, u32[]{:S(2)}, u32[]{:S(2)}) collective-permute-start(f32[34,128]{1,0:T(8,128)S(1)} %maximum_bitcast_fusion), channel_id=1, source_target_pairs={{0,2},{2,0},{1,3},{3,1},{4,6},{6,4},{5,7},{7,5},{8,10},{10,8},{9,1... | collective-permute-start | bytes 52232 | tf_op jit(solution)/shard_map/ppermute | solution.py:33
  562.9 45.2 %collective-permute-start.15 = (bf16[256,1536]{1,0:T(8,128)(2,1)}, bf16[256,1536]{1,0:T(8,128)(2,1)}, u32[]{:S(2)}, u32[]{:S(2)}) collective-permute-start(bf16[256,1536]{1,0:T(8,128)(2,1)} %get-tuple-element.91), channel_id=1, source_target_pairs={{0,4},{4,0},{8,12},{12,8},{16,20},{20,16},{24,28},{28,24},{1,5},{5... | collective-permute-start | bytes 2359304 | tf_op jit(solution)/shard_map/ppermute | solution.py:38
  585.9 24.1 %collective-permute-start.12 = (bf16[256,768]{1,0:T(8,128)(2,1)}, bf16[256,768]{1,0:T(8,128)(2,1)S(1)}, u32[]{:S(2)}, u32[]{:S(2)}) collective-permute-start(bf16[256,768]{1,0:T(8,128)(2,1)} %get-tuple-element.95), channel_id=1, source_target_pairs={{0,4},{4,0},{8,12},{12,8},{16,20},{20,16},{24,28},{28,24},{1,5},{5... | collective-permute-start | bytes 1179656 | tf_op jit(solution)/shard_map/ppermute | solution.py:38
  586.8 24.8 %collective-permute-start.13 = (bf16[256,768]{1,0:T(8,128)(2,1)S(1)}, bf16[256,768]{1,0:T(8,128)(2,1)}, u32[]{:S(2)}, u32[]{:S(2)}) collective-permute-start(bf16[256,768]{1,0:T(8,128)(2,1)S(1)} %get-tuple-element.96.kept_ref), channel_id=1, source_target_pairs={{0,2},{2,0},{1,3},{3,1},{4,6},{6,4},{5,7},{7,5},{8,10},{10,8},{9,1... | collective-permute-start | bytes 1179656 | tf_op jit(solution)/shard_map/ppermute | solution.py:33
  602.5 10.5 %collective-permute-start.18 = (bf16[256,768]{1,0:T(8,128)(2,1)S(1)}, bf16[256,768]{1,0:T(8,128)(2,1)S(1)}, u32[]{:S(2)}, u32[]{:S(2)}) collective-permute-start(bf16[256,768]{1,0:T(8,128)(2,1)S(1)} %get-tuple-element.93), channel_id=1, source_target_pairs={{0,4},{4,0},{8,12},{12,8},{16,20},{20,16},{24,28},{28,24},{1,5},{5... | collective-permute-start | bytes 1179656 | tf_op jit(solution)/shard_map/ppermute | solution.py:38
  606.6 66.3 %collective-permute-start.16 = (bf16[256,1536]{1,0:T(8,128)(2,1)}, bf16[256,1536]{1,0:T(8,128)(2,1)S(1)}, u32[]{:S(2)}, u32[]{:S(2)}) collective-permute-start(bf16[256,1536]{1,0:T(8,128)(2,1)} %get-tuple-element.92.kept_ref), channel_id=1, source_target_pairs={{0,2},{2,0},{1,3},{3,1},{4,6},{6,4},{5,7},{7,5},{8,10},{10,8},{9,1... | collective-permute-start | bytes 2359304 | tf_op jit(solution)/shard_map/ppermute | solution.py:33
  608.0 64.9 %collective-permute-start.17 = (bf16[256,1536]{1,0:T(8,128)(2,1)}, bf16[256,1536]{1,0:T(8,128)(2,1)}, u32[]{:S(2)}, u32[]{:S(2)}) collective-permute-start(bf16[256,1536]{1,0:T(8,128)(2,1)} %collective-permute-done.15.x_ref), channel_id=1, source_target_pairs={{0,2},{2,0},{1,3},{3,1},{4,6},{6,4},{5,7},{7,5},{8,10},{10,8},{9,1... | collective-permute-start | bytes 2359304 | tf_op jit(solution)/shard_map/ppermute | solution.py:33
  610.0 50.9 %copy-start.28 = (bf16[256,768]{1,0:T(8,128)(2,1)}, bf16[256,768]{1,0:T(8,128)(2,1)S(1)}, u32[]{:S(2)}) copy-start(bf16[256,768]{1,0:T(8,128)(2,1)S(1)} %collective-permute-done.12.x_ref) | copy-start | bytes 1179652
  610.0 56.2 %collective-permute-start.19 = (bf16[256,768]{1,0:T(8,128)(2,1)S(1)}, bf16[256,768]{1,0:T(8,128)(2,1)S(1)}, u32[]{:S(2)}, u32[]{:S(2)}) collective-permute-start(bf16[256,768]{1,0:T(8,128)(2,1)S(1)} %get-tuple-element.94.kept_ref), channel_id=1, source_target_pairs={{0,2},{2,0},{1,3},{3,1},{4,6},{6,4},{5,7},{7,5},{8,10},{10,8},{9,1... | collective-permute-start | bytes 1179656 | tf_op jit(solution)/shard_map/ppermute | solution.py:33
  611.6 49.3 %collective-permute-start.14 = (bf16[256,768]{1,0:T(8,128)(2,1)S(1)}, bf16[256,768]{1,0:T(8,128)(2,1)S(1)}, u32[]{:S(2)}, u32[]{:S(2)}) collective-permute-start(bf16[256,768]{1,0:T(8,128)(2,1)S(1)} %collective-permute-done.12.x_ref), channel_id=1, source_target_pairs={{0,2},{2,0},{1,3},{3,1},{4,6},{6,4},{5,7},{7,5},{8,10},{10,8},{9,1... | collective-permute-start | bytes 1179656 | tf_op jit(solution)/shard_map/ppermute | solution.py:33
  613.0 54.5 %copy-start.25 = (bf16[256,768]{1,0:T(8,128)(2,1)}, bf16[256,768]{1,0:T(8,128)(2,1)S(1)}, u32[]{:S(2)}) copy-start(bf16[256,768]{1,0:T(8,128)(2,1)S(1)} %collective-permute-done.18.x_ref) | copy-start | bytes 1179652
  613.0 54.5 %collective-permute-start.20 = (bf16[256,768]{1,0:T(8,128)(2,1)S(1)}, bf16[256,768]{1,0:T(8,128)(2,1)S(1)}, u32[]{:S(2)}, u32[]{:S(2)}) collective-permute-start(bf16[256,768]{1,0:T(8,128)(2,1)S(1)} %collective-permute-done.18.x_ref), channel_id=1, source_target_pairs={{0,2},{2,0},{1,3},{3,1},{4,6},{6,4},{5,7},{7,5},{8,10},{10,8},{9,1... | collective-permute-start | bytes 1179656 | tf_op jit(solution)/shard_map/ppermute | solution.py:33
  (34 other events, 291.8 us)
Sparse Core Ops, SparseCore 0:
  24.2 73.5 all-gather.3
  99.4 113.8 all-gather.5
  214.9 61.6 all-gather.7
  363.2 111.1 reduce-scatter.5
  477.1 60.9 reduce-scatter.3
  540.2 61.0 reduce-scatter.7

commit v7 on v6

--- a/solution.py
+++ b/solution.py
@@ -51,10 +51,6 @@
     return lax.psum_scatter(
         value, "fsdp", scatter_dimension=0, tiled=True, axis_index_groups=lines()
     )
-
-
-def flip_if(flag, value, axis):
-    return jnp.where(flag, jnp.flip(value, axis), value)
 
 
 def neighbours():
@@ -575,6 +571,19 @@
         for side in (1, 0):
             for copy in loads[side, chunk]:
                 copy.wait()
+    if filler:
+        size = width // 4
+
+        def fill(index, _):
+            cols = pl.ds(pl.multiple_of(index * size, size), size)
+
+            def step(columns):
+                grad[cols, columns] = mm(lhs[:, cols], acts[:, columns], 0, 0).astype(BF16)
+                return 0
+
+            tiled(acts.shape[1], acts.shape[1] // 3, step)
+            return 0
+
     for part in (0, 1):
         for chunk in chunks[2:]:
             send_core(chunk, part)
@@ -584,21 +593,11 @@
             core_copies[(side, 0), part].wait_recv()
             link_copies[0, side, part].wait_recv()
             link(1, side, part, partial_sum((side, 0), rows, rows, part) + came(0, side, rows, part), peer)
+        if filler and part == 0:
+            load_lhs.wait()
+            lax.fori_loop(0, 1, fill, 0)
     if filler:
-        load_lhs.wait()
-        size = width // 4
-
-        def fill(index, _):
-            cols = pl.ds(pl.multiple_of(index * size, size), size)
-
-            def step(columns):
-                grad[cols, columns] = mm(lhs[:, cols], acts[:, columns], 0, 0).astype(BF16)
-                return 0
-
-            tiled(acts.shape[1], acts.shape[1] // 3, step)
-            return 0
-
-        lax.fori_loop(0, 4, fill, 0)
+        lax.fori_loop(1, 4, fill, 0)
         grad_copy = pltpu.make_async_copy(grad, grad_ref, grad_sem.at[0])
         grad_copy.start()
     for side in (0, 1):
@@ -778,6 +777,31 @@
     )(part)
 
 
+def stack_kernel(spot_ref, own_ref, other_ref, out_ref):
+    @pl.when(pl.program_id(0) == 0)
+    def _():
+        out_ref[...] = own_ref[...]
+
+    @pl.when(pl.program_id(0) == 1)
+    def _():
+        out_ref[...] = other_ref[...]
+
+
+def stack_rows(spot, own, other):
+    block = pl.BlockSpec(own.shape, lambda i, spot: (0, 0))
+    return pl.pallas_call(
+        stack_kernel,
+        out_shape=jax.ShapeDtypeStruct((2 * own.shape[0], own.shape[1]), own.dtype),
+        grid_spec=pltpu.PrefetchScalarGridSpec(
+            num_scalar_prefetch=1,
+            grid=(2,),
+            in_specs=[block, block],
+            out_specs=pl.BlockSpec(own.shape, lambda i, spot: (lax.rem(spot[1] + i, 2), 0)),
+        ),
+        name="stack",
+    )(spot, own, other)
+
+
 def join_kernel(sizes, spot_ref, kept_ref, x_ref, y_ref, both_ref, *out_refs):
     place, odd = spot_ref[0], spot_ref[1]
     parts = (
@@ -1182,8 +1206,7 @@
     down_grad = mm(cot, hidden, 0, 0).astype(BF16)
 
     def finish_rows(own):
-        pair = jnp.stack([own, swap_core(own)])
-        return flip_if(core == 1, pair, 0).reshape(tokens.shape)
+        return stack_rows(meta, own, swap_core(own)).reshape(tokens.shape)
 
     grad_hidden = mm(after(cot, down_grad), down_w, 1, 0)
     grad_up = (grad_hidden * active).astype(BF16)

time: 696 us -> 697 us (level)
  waiting for transfers between devices: 123 us -> 130 us
    reduce_scatter x3, waiting for transfers between devices: 13.5 us -> 33.8 us  [scatter_line(): lax.psum_scatter(value, 'fsdp', scatter_dimension=0, tiled=True, axis_ind...]
    ppermute x11, waiting for transfers between devices: 91.6 us -> 78.9 us  [swap_ctx(): return lax.ppermute(value, 'ctx', [(0, 1), (1, 0)])]
    pallas_call x0 -> x2, Pallas kernels: none -> 7.25 us  [stack_rows(): pl.pallas_call(stack_kernel, out_shape=jax.ShapeDtypeStruct((2 * own.shap...]
  transfers between devices with their start and end apart: 27 -> 27, of which waited for: 12 -> 11; matrix products, arithmetic and copies ran while one was open for 18% -> 17% of each run, Pallas kernels for 44% -> 45%
where the time goes in v7:
time: 697 us; the launch traced here: 688 us
  Pallas kernels  374 us (54%)
  waiting for transfers between devices  130 us (19%)
  matrix products  85.7 us (12%)
  other arithmetic  36.5 us (5%)
  local copies, waits for them, and re-layouts  26.4 us (4%)
  starting transfers between devices  19.3 us (3%)
  between operations  14.9 us (2%)
    pallas_call x2, Pallas kernels, product_reduce8(): pl.pallas_call(functools.partial(product_reduce8_kernel, rows, groups, fi...  90.3 us
    dot_general x9, matrix products, mm(): lax.dot_general(left, right, (((left_dim,), (right_dim,)), ((), ())), pre...  85.7 us
    pallas_call x2, Pallas kernels, gather8(): pl.pallas_call(functools.partial(gather8_kernel, rows, bool(also)), out_s...  81.5 us
    ppermute x11, waiting for transfers between devices, swap_ctx(): return lax.ppermute(value, 'ctx', [(0, 1), (1, 0)])  78.9 us
    pallas_call x2, Pallas kernels, shards(): pl.pallas_call(functools.partial(shard_kernel, tuple(plan), len(groups)),...  41.6 us
    pallas_call x1, Pallas kernels, gather8_product(): pl.pallas_call(functools.partial(gather8_product_kernel, rows), out_shape...  41.2 us
    pallas_call x1, Pallas kernels, reduce8(): pl.pallas_call(functools.partial(reduce8_kernel, rows), out_shape=jax.Sha...  40.1 us
    reduce_scatter x3, waiting for transfers between devices, scatter_line(): lax.psum_scatter(value, 'fsdp', scatter_dimension=0, tiled=True, axis_ind...  33.8 us
  transfers between devices with their start and end apart: 27, of which 11 were waited for; matrix products, arithmetic and copies ran while one was open for 17% of the time, Pallas kernels for 45%

profile of v7, /device:TPU:0, one launch (start us, length us, event | category | flops | bytes accessed | tf_op | source)
XLA Modules:
  0.0 687.6 jit_solution(10236112989904589176)
XLA Ops:
  10.1 14.0 %shards.2 = bf16[512,896]{1,0:T(8,128)(2,1)} custom-call(bf16[256,1024]{1,0:T(8,128)(2,1)} %refs_0_.1, bf16[256,512]{1,0:T(8,128)(2,1)} %refs_1_.2, bf16[256,512]{1,0:T(8,128)(2,1)} %refs_2_.2, bf16[256,1024]{1,0:T(8,128)(2,1)} %refs_3_.1, bf16[256,128]{1,0:T(8,128)(2,1)} %select_select_fusion.refs_4_), custom_call_target="tpu_custom_call" | custom-call | tf_op jit(solution)/shard_map/shards/pallas_call | solution.py:716
  24.1 27.6 %shards.3 = (bf16[512,1536]{1,0:T(8,128)(2,1)}, bf16[512,768]{1,0:T(8,128)(2,1)}) custom-call(bf16[256,3072]{1,0:T(8,128)(2,1)} %refs_0_.2, bf16[256,3072]{1,0:T(8,128)(2,1)} %refs_1_.3, bf16[256,3072]{1,0:T(8,128)(2,1)} %refs_2_.3), custom_call_target="tpu_custom_call" | custom-call | tf_op jit(solution)/shard_map/shards/pallas_call | solution.py:716
  53.6 40.9 %gather8.1 = bf16[2048,2048]{1,0:T(8,128)(2,1)} custom-call(bf16[256,2048]{1,0:T(8,128)(2,1)} %get-tuple-element.47.refs_0_), custom_call_target="tpu_custom_call" | custom-call | tf_op jit(solution)/shard_map/gather8/pallas_call | solution.py:348
  97.6 5.1 fusion
  106.6 13.7 %collective-permute-done = s32[1,1024]{1,0:T(1,128)S(1)} collective-permute-done((s32[1,1024]{1,0:T(1,128)S(1)}, s32[1,1024]{1,0:T(1,128)S(1)}, u32[]{:S(2)}, u32[]{:S(2)}) %collective-permute-start) | collective-permute-done | bytes 4128 | tf_op jit(solution)/shard_map/ppermute | solution.py:38
  125.0 10.6 %fusion.8.qkv_ref = f32[2048,512]{1,0:T(8,128)} fusion(bf16[2048,2048]{1,0:T(8,128)(2,1)} %gather8.1, f32[2048]{0:T(1024)S(1)} %get-tuple-element.82, f32[2048]{0:T(1024)S(1)} %add_rsqrt_fusion, bf16[2048,896]{1,0:T(8,128)(2,1)} %all-gather.4.cloned.1.call-done.refs_1_), kind=kOutput, calls=%fused_computation.22 | convolution fusion | flops 4311744512 | bytes 14696448 | tf_op jit(solution)/shard_map/dot_general | solution.py:23
  135.6 16.2 %attend.1 = bf16[2048,256]{1,0:T(8,128)(2,1)} custom-call(s32[2]{0:T(128)} %pad_add_fusion.1.meta_ref.spot_ref, f32[2048,512]{1,0:T(8,128)} %fusion.8.qkv_ref, s32[2,1024,1]{2,1,0:T(8,128)} %copy.33.segc_ref, s32[2,1,1024]{2,1,0:T(1,128)} %broadcast_in_dim.76.segr_ref, f32[1024,128]{1,0:T(8,128)} %get-tuple-element.108.cos_ref, ...), custom_call_target="tpu_custom_call" | custom-call | flops 1073741824 | bytes 5242880 | tf_op jit(solution)/shard_map/attend/pallas_call | solution.py:1039
  151.8 5.1 convolution_convert_fusion.far_ref
  156.9 5.8 fusion.21.near_ref
  162.8 40.1 %reduce8.1 = f32[256,2048]{1,0:T(8,128)S(1)} custom-call(f32[1024,2048]{1,0:T(8,128)} %fusion.21.near_ref, bf16[1024,2048]{1,0:T(8,128)(2,1)} %convolution_convert_fusion.far_ref), custom_call_target="tpu_custom_call" | custom-call | tf_op jit(solution)/shard_map/reduce8/pallas_call | solution.py:441
  205.9 11.4 %collective-permute-done.3.refs_4_ = bf16[128,2048]{1,0:T(8,128)(2,1)S(1)} collective-permute-done((bf16[128,2048]{1,0:T(8,128)(2,1)S(1)}, bf16[128,2048]{1,0:T(8,128)(2,1)S(1)}, u32[]{:S(2)}, u32[]{:S(2)}) %collective-permute-start.3) | collective-permute-done | bytes 524320 | tf_op jit(solution)/shard_map/ppermute | solution.py:33
  219.1 40.6 %gather8_also.1 = (bf16[2048,2048]{1,0:T(8,128)(2,1)}, bf16[2048,2048]{1,0:T(8,128)(2,1)}) custom-call(bf16[256,2048]{1,0:T(8,128)(2,1)} %multiply_convert_fusion.3.refs_0_, bf16[256,2048]{1,0:T(8,128)(2,1)} %copy-done.15, bf16[256,2048]{1,0:T(8,128)(2,1)} %copy-done.18, bf16[256,2048]{1,0:T(8,128)(2,1)} %copy-done.19, bf16[128,2048]{1,0:T(8,128)(2,1)} %copy-done.24, ...), custom_call_target="tpu_custom_call" | custom-call | tf_op jit(solution)/shard_map/gather8_also/pallas_call | solution.py:348
  259.7 17.6 %fusion.31 = f32[2048,1536]{1,0:T(8,128)S(1)} fusion(bf16[2048,2048]{1,0:T(8,128)(2,1)} %get-tuple-element.54.refs_3_, bf16[2048,1536]{1,0:T(8,128)(2,1)} %all-gather.6.cloned.1.call-done.refs_2_), kind=kOutput, calls=%fused_computation.86 | convolution fusion | flops 12884901888 | bytes 27262976 | tf_op jit(solution)/shard_map/dot_general | solution.py:23
  279.4 4.3 copy-done.7
  286.4 8.5 %convolution_convert_fusion.1 = bf16[2048,768]{1,0:T(8,128)(2,1)} fusion(bf16[2048,2048]{1,0:T(8,128)(2,1)S(1)} %copy-done.34, bf16[2048,768]{1,0:T(8,128)(2,1)S(1)} %multiply_convert_fusion.2.acts_ref), kind=kOutput, calls=%fused_computation.11 | convolution fusion | flops 6444023808 | bytes 14680064 | tf_op jit(solution)/shard_map/dot_general | solution.py:23
  294.9 16.4 %multiply_convert_fusion = (bf16[2048,768]{1,0:T(8,128)(2,1)}, bf16[2048,768]{1,0:T(8,128)(2,1)}) fusion(f32[2048,1536]{1,0:T(8,128)} %copy-done.7, bf16[2048,2048]{1,0:T(8,128)(2,1)} %get-tuple-element.55, bf16[2048,768]{1,0:T(8,128)(2,1)} %all-gather.8.cloned.1.call-done.weight_ref), kind=kOutput, calls=%fused_computation.5 | convolution fusion | flops 6462898176 | bytes 30408704 | tf_op jit(solution)/shard_map/dot_general | solution.py:23
  311.3 47.9 %product_reduce8.2 = (f32[256,2048]{1,0:T(8,128)}, bf16[2048,1536]{1,0:T(8,128)(2,1)}) custom-call(bf16[2048,768]{1,0:T(8,128)(2,1)} %get-tuple-element.88.refs_0_, bf16[2048,768]{1,0:T(8,128)(2,1)} %get-tuple-element.87.refs_1_, bf16[2048,1536]{1,0:T(8,128)(2,1)} %all-gather.6.cloned.1.call-done.refs_2_, bf16[2048,2048]{1,0:T(8,128)(2,1)} %get-tuple-element.54.refs_3_), custom_call_target="tpu_custom_call" | custom-call | flops 25769803776 | bytes 25165824 | tf_op jit(solution)/shard_map/product_reduce8/pallas_call | solution.py:645
  363.9 41.2 %gather8_product.1 = (bf16[2048,2048]{1,0:T(8,128)(2,1)}, f32[512,2048]{1,0:T(8,128)}, bf16[256,2048]{1,0:T(8,128)(2,1)S(1)}, bf16[256,2048]{1,0:T(8,128)(2,1)S(1)}) custom-call(bf16[256,2048]{1,0:T(8,128)(2,1)S(1)} %fusion.28.own_ref, bf16[2048,768]{1,0:T(8,128)(2,1)} %copy-done.17, bf16[2048,768]{1,0:T(8,128)(2,1)} %all-gather.8.cloned.1.call-done.weight_ref), custom_call_target="tpu_custom_call" | custom-call | flops 6442450944 | bytes 8388608 | tf_op jit(solution)/shard_map/gather8_product/pallas_call | solution.py:307
  405.1 7.0 %convolution_convert_fusion.4.grad_ref = bf16[2048,256]{1,0:T(8,128)(2,1)} fusion(bf16[2048,2048]{1,0:T(8,128)(2,1)} %get-tuple-element.60, bf16[2048,896]{1,0:T(8,128)(2,1)} %all-gather.4.cloned.1.call-done.refs_1_), kind=kOutput, calls=%fused_computation.21 | convolution fusion | flops 2148007936 | bytes 10485760 | tf_op jit(solution)/shard_map/dot_general | solution.py:23
  412.1 28.8 %attend_back.1 = (bf16[2048,512]{1,0:T(8,128)(2,1)}, f32[2,128]{1,0:T(2,128)}) custom-call(s32[2]{0:T(128)} %pad_add_fusion.1.meta_ref.spot_ref, f32[2048,512]{1,0:T(8,128)} %fusion.8.qkv_ref, bf16[2048,256]{1,0:T(8,128)(2,1)} %convolution_convert_fusion.4.grad_ref, s32[2,1024,1]{2,1,0:T(8,128)} %copy.33.segc_ref, s32[2,1,1024]{2,1,0:T(1,128)} %broadcast_in_dim.76.segr_ref, ...), custom_call_target="tpu_custom_call" | custom-call | flops 2684354560 | bytes 8388608 | tf_op jit(solution)/shard_map/attend_back/pallas_call | solution.py:1067
  440.9 6.0 convolution_convert_fusion.3
  447.0 8.7 %convolution_convert_fusion.2 = bf16[2048,512]{1,0:T(8,128)(2,1)S(1)} fusion(bf16[2048,512]{1,0:T(8,128)(2,1)S(1)} %copy-done.35, bf16[2048,2048]{1,0:T(8,128)(2,1)} %gather8.1, f32[2048]{0:T(1024)S(1)} %copy-done.28, f32[2048]{0:T(1024)S(1)} %copy-done.30), kind=kOutput, calls=%fused_computation.16 | convolution fusion | flops 4312793088 | bytes 12599296 | tf_op jit(solution)/shard_map/dot_general | solution.py:23
  460.2 23.5 %collective-permute-done.5 = bf16[256,2048]{1,0:T(8,128)(2,1)S(1)} collective-permute-done((bf16[256,2048]{1,0:T(8,128)(2,1)S(1)}, bf16[256,2048]{1,0:T(8,128)(2,1)S(1)}, u32[]{:S(2)}, u32[]{:S(2)}) %collective-permute-start.5) | collective-permute-done | bytes 1048608 | tf_op jit(solution)/shard_map/ppermute | solution.py:33
  491.3 10.5 %collective-permute-done.8 = bf16[128,2048]{1,0:T(8,128)(2,1)S(1)} collective-permute-done((bf16[128,2048]{1,0:T(8,128)(2,1)}, bf16[128,2048]{1,0:T(8,128)(2,1)S(1)}, u32[]{:S(2)}, u32[]{:S(2)}) %collective-permute-start.8) | collective-permute-done | bytes 524320 | tf_op jit(solution)/shard_map/ppermute | solution.py:33
  507.3 42.3 %product_reduce8.3 = f32[256,2048]{1,0:T(8,128)} custom-call(bf16[2048,512]{1,0:T(8,128)(2,1)} %get-tuple-element.67.refs_0_, bf16[2048,896]{1,0:T(8,128)(2,1)} %all-gather.4.cloned.1.call-done.refs_1_), custom_call_target="tpu_custom_call" | custom-call | flops 4294967296 | bytes 8388608 | tf_op jit(solution)/shard_map/product_reduce8/pallas_call | solution.py:645
  552.5 3.8 fusion.14.own_ref
  563.0 33.8 %reduce-scatter.8.cloned.1.call-done = bf16[512,768]{1,0:T(8,128)(2,1)} async-done(((bf16[2048,768]{1,0:T(8,128)(2,1)}), bf16[512,768]{1,0:T(8,128)(2,1)}) %reduce-scatter.8.cloned.1.call-update) | async-done | bytes 786448 | tf_op jit(solution)/shard_map/reduce_scatter | solution.py:51
  613.5 12.6 %total.1 = f32[34,128]{1,0:T(8,128)} custom-call(f32[34,128]{1,0:T(8,128)} %fusion.26.part_ref), custom_call_target="tpu_custom_call" | custom-call | tf_op jit(solution)/shard_map/total/pallas_call | solution.py:764
  632.4 29.0 %collective-permute-done.14.both_ref = bf16[256,768]{1,0:T(8,128)(2,1)} collective-permute-done((bf16[256,768]{1,0:T(8,128)(2,1)}, bf16[256,768]{1,0:T(8,128)(2,1)}, u32[]{:S(2)}, u32[]{:S(2)}) %collective-permute-start.14) | collective-permute-done | bytes 393248 | tf_op jit(solution)/shard_map/ppermute | solution.py:33
  661.4 4.6 join.3
  668.3 4.6 join.5
  674.7 5.8 join.4
  (174 shorter events, 84.8 us)
Async XLA Ops:
  7.2 115.0 %all-gather.4.cloned.1.call-start = ((), (), s32[]{:S(2)}) async-start(), calls=%async_computation.3 | async-start | bytes 4587520 | tf_op jit(solution)/shard_map/all_gather | solution.py:47
  24.1 235.6 %all-gather.6.cloned.1.call-start = ((), (), s32[]{:S(2)}) async-start(), calls=%async_computation.4 | async-start | bytes 7864320 | tf_op jit(solution)/shard_map/all_gather | solution.py:47
  51.8 243.1 %all-gather.8.cloned.1.call-start = ((), (), s32[]{:S(2)}) async-start(), calls=%async_computation.5 | async-start | bytes 3932160 | tf_op jit(solution)/shard_map/all_gather | solution.py:47
  53.6 43.2 %copy-start.33 = (s32[1,1024]{1,0:T(1,128)S(1)}, s32[1,1024]{1,0:T(1,128)}, u32[]{:S(2)}) copy-start(s32[1,1024]{1,0:T(1,128)} %param.15) | copy-start | bytes 12292
  94.7 57.1 %collective-permute-start.1 = (bf16[256,2048]{1,0:T(8,128)(2,1)S(1)}, bf16[256,2048]{1,0:T(8,128)(2,1)S(1)}, u32[]{:S(2)}, u32[]{:S(2)}) collective-permute-start(bf16[256,2048]{1,0:T(8,128)(2,1)S(1)} %dynamic-slice_bitcast_fusion.refs_1_), channel_id=1, source_target_pairs={{0,4},{4,0},{8,12},{12,8},{16,20},{20,16},{24,28},{28,24},{1,5},{5... | collective-permute-start | bytes 3145736 | tf_op jit(solution)/shard_map/ppermute | solution.py:38
  96.2 107.0 %collective-permute-start.2 = (bf16[256,2048]{1,0:T(8,128)(2,1)S(1)}, bf16[256,2048]{1,0:T(8,128)(2,1)S(1)}, u32[]{:S(2)}, u32[]{:S(2)}) collective-permute-start(bf16[256,2048]{1,0:T(8,128)(2,1)S(1)} %dynamic-slice_bitcast_fusion.refs_1_), channel_id=1, source_target_pairs={{0,2},{2,0},{1,3},{3,1},{4,6},{6,4},{5,7},{7,5},{8,10},{10,8},{9,1... | collective-permute-start | bytes 3145736 | tf_op jit(solution)/shard_map/ppermute | solution.py:33
  96.7 23.5 %collective-permute-start = (s32[1,1024]{1,0:T(1,128)S(1)}, s32[1,1024]{1,0:T(1,128)S(1)}, u32[]{:S(2)}, u32[]{:S(2)}) collective-permute-start(s32[1,1024]{1,0:T(1,128)S(1)} %copy-done.33), channel_id=1, source_target_pairs={{0,4},{4,0},{8,12},{12,8},{16,20},{20,16},{24,28},{28,24},{1,5},{5... | collective-permute-start | bytes 12296 | tf_op jit(solution)/shard_map/ppermute | solution.py:38
  97.5 458.8 %reduce-scatter.6.cloned.1.call-start = ((), (), s32[]{:S(2)}) async-start(), calls=%async_computation.7 | async-start | bytes 7864320 | tf_op jit(solution)/shard_map/reduce_scatter | solution.py:51
  151.8 51.5 %copy-start.18 = (bf16[256,2048]{1,0:T(8,128)(2,1)}, bf16[256,2048]{1,0:T(8,128)(2,1)S(1)}, u32[]{:S(2)}) copy-start(bf16[256,2048]{1,0:T(8,128)(2,1)S(1)} %collective-permute-done.1.refs_2_) | copy-start | bytes 3145732
  203.3 13.9 %collective-permute-start.3 = (bf16[128,2048]{1,0:T(8,128)(2,1)S(1)}, bf16[128,2048]{1,0:T(8,128)(2,1)S(1)}, u32[]{:S(2)}, u32[]{:S(2)}) collective-permute-start(bf16[128,2048]{1,0:T(8,128)(2,1)S(1)} %slice.64), channel_id=1, source_target_pairs={{0,2},{2,0},{1,3},{3,1},{4,6},{6,4},{5,7},{7,5},{8,10},{10,8},{9,1... | collective-permute-start | bytes 1572872 | tf_op jit(solution)/shard_map/ppermute | solution.py:33
  203.9 14.3 %collective-permute-start.4 = (bf16[128,2048]{1,0:T(8,128)(2,1)S(1)}, bf16[128,2048]{1,0:T(8,128)(2,1)S(1)}, u32[]{:S(2)}, u32[]{:S(2)}) collective-permute-start(bf16[128,2048]{1,0:T(8,128)(2,1)S(1)} %slice.65), channel_id=1, source_target_pairs={{0,4},{4,0},{8,12},{12,8},{16,20},{20,16},{24,28},{28,24},{1,5},{5... | collective-permute-start | bytes 1572872 | tf_op jit(solution)/shard_map/ppermute | solution.py:38
  359.2 200.9 %reduce-scatter.4.cloned.1.call-start = ((), (), s32[]{:S(2)}) async-start(), calls=%async_computation.6 | async-start | bytes 3932160 | tf_op jit(solution)/shard_map/reduce_scatter | solution.py:51
  457.6 139.2 %reduce-scatter.8.cloned.1.call-start = ((), (), s32[]{:S(2)}) async-start(), calls=%async_computation.8 | async-start | bytes 3932160 | tf_op jit(solution)/shard_map/reduce_scatter | solution.py:51
  458.2 25.5 %collective-permute-start.5 = (bf16[256,2048]{1,0:T(8,128)(2,1)S(1)}, bf16[256,2048]{1,0:T(8,128)(2,1)S(1)}, u32[]{:S(2)}, u32[]{:S(2)}) collective-permute-start(bf16[256,2048]{1,0:T(8,128)(2,1)S(1)} %get-tuple-element.59), channel_id=1, source_target_pairs={{0,2},{2,0},{1,3},{3,1},{4,6},{6,4},{5,7},{7,5},{8,10},{10,8},{9,1... | collective-permute-start | bytes 3145736 | tf_op jit(solution)/shard_map/ppermute | solution.py:33
  459.3 25.2 %collective-permute-start.7 = (bf16[256,2048]{1,0:T(8,128)(2,1)S(1)}, bf16[256,2048]{1,0:T(8,128)(2,1)S(1)}, u32[]{:S(2)}, u32[]{:S(2)}) collective-permute-start(bf16[256,2048]{1,0:T(8,128)(2,1)S(1)} %get-tuple-element.64), channel_id=1, source_target_pairs={{0,4},{4,0},{8,12},{12,8},{16,20},{20,16},{24,28},{28,24},{1,5},{5... | collective-permute-start | bytes 3145736 | tf_op jit(solution)/shard_map/ppermute | solution.py:38
  488.3 13.4 %collective-permute-start.8 = (bf16[128,2048]{1,0:T(8,128)(2,1)}, bf16[128,2048]{1,0:T(8,128)(2,1)S(1)}, u32[]{:S(2)}, u32[]{:S(2)}) collective-permute-start(bf16[128,2048]{1,0:T(8,128)(2,1)} %slice.117), channel_id=1, source_target_pairs={{0,2},{2,0},{1,3},{3,1},{4,6},{6,4},{5,7},{7,5},{8,10},{10,8},{9,1... | collective-permute-start | bytes 1572872 | tf_op jit(solution)/shard_map/ppermute | solution.py:33
  490.2 13.1 %collective-permute-start.6 = (bf16[128,2048]{1,0:T(8,128)(2,1)}, bf16[128,2048]{1,0:T(8,128)(2,1)S(1)}, u32[]{:S(2)}, u32[]{:S(2)}) collective-permute-start(bf16[128,2048]{1,0:T(8,128)(2,1)} %slice.118), channel_id=1, source_target_pairs={{0,4},{4,0},{8,12},{12,8},{16,20},{20,16},{24,28},{28,24},{1,5},{5... | collective-permute-start | bytes 1572872 | tf_op jit(solution)/shard_map/ppermute | solution.py:38
  507.3 93.0 %collective-permute-start.9 = (bf16[256,2048]{1,0:T(8,128)(2,1)}, bf16[256,2048]{1,0:T(8,128)(2,1)}, u32[]{:S(2)}, u32[]{:S(2)}) collective-permute-start(bf16[256,2048]{1,0:T(8,128)(2,1)} %fusion.18.own_ref), channel_id=1, source_target_pairs={{0,1},{1,0},{2,3},{3,2},{4,5},{5,4},{6,7},{7,6},{8,9},{9,8},{10,11... | collective-permute-start | bytes 3145736 | tf_op jit(solution)/shard_map/ppermute | solution.py:29
  556.2 42.4 %copy-start.14 = (bf16[256,2048]{1,0:T(8,128)(2,1)}, bf16[256,2048]{1,0:T(8,128)(2,1)S(1)}, u32[]{:S(2)}) copy-start(bf16[256,2048]{1,0:T(8,128)(2,1)S(1)} %fusion.14.own_ref) | copy-start | bytes 3145732
  556.3 45.4 %collective-permute-start.10 = (bf16[256,2048]{1,0:T(8,128)(2,1)S(1)}, bf16[256,2048]{1,0:T(8,128)(2,1)}, u32[]{:S(2)}, u32[]{:S(2)}) collective-permute-start(bf16[256,2048]{1,0:T(8,128)(2,1)S(1)} %fusion.14.own_ref), channel_id=1, source_target_pairs={{0,1},{1,0},{2,3},{3,2},{4,5},{5,4},{6,7},{7,6},{8,9},{9,8},{10,11... | collective-permute-start | bytes 3145736 | tf_op jit(solution)/shard_map/ppermute | solution.py:29
  558.1 49.9 %copy-start.16 = (bf16[256,1536]{1,0:T(8,128)(2,1)}, bf16[256,1536]{1,0:T(8,128)(2,1)S(1)}, u32[]{:S(2)}) copy-start(bf16[256,1536]{1,0:T(8,128)(2,1)S(1)} %get-tuple-element.92.kept_ref) | copy-start | bytes 2359300
  558.1 44.1 %collective-permute-start.15 = (bf16[256,1536]{1,0:T(8,128)(2,1)S(1)}, bf16[256,1536]{1,0:T(8,128)(2,1)}, u32[]{:S(2)}, u32[]{:S(2)}) collective-permute-start(bf16[256,1536]{1,0:T(8,128)(2,1)S(1)} %get-tuple-element.91), channel_id=1, source_target_pairs={{0,4},{4,0},{8,12},{12,8},{16,20},{20,16},{24,28},{28,24},{1,5},{5... | collective-permute-start | bytes 2359304 | tf_op jit(solution)/shard_map/ppermute | solution.py:38
  559.1 39.6 %collective-permute-start.11 = (f32[34,128]{1,0:T(8,128)S(1)}, f32[34,128]{1,0:T(8,128)S(1)}, u32[]{:S(2)}, u32[]{:S(2)}) collective-permute-start(f32[34,128]{1,0:T(8,128)S(1)} %maximum_bitcast_fusion), channel_id=1, source_target_pairs={{0,2},{2,0},{1,3},{3,1},{4,6},{6,4},{5,7},{7,5},{8,10},{10,8},{9,1... | collective-permute-start | bytes 52232 | tf_op jit(solution)/shard_map/ppermute | solution.py:33
  562.1 67.6 %copy-start.21 = (bf16[256,768]{1,0:T(8,128)(2,1)}, bf16[256,768]{1,0:T(8,128)(2,1)S(1)}, u32[]{:S(2)}) copy-start(bf16[256,768]{1,0:T(8,128)(2,1)S(1)} %get-tuple-element.96.kept_ref) | copy-start | bytes 1179652
  562.1 45.9 %collective-permute-start.12 = (bf16[256,768]{1,0:T(8,128)(2,1)}, bf16[256,768]{1,0:T(8,128)(2,1)}, u32[]{:S(2)}, u32[]{:S(2)}) collective-permute-start(bf16[256,768]{1,0:T(8,128)(2,1)} %get-tuple-element.95), channel_id=1, source_target_pairs={{0,4},{4,0},{8,12},{12,8},{16,20},{20,16},{24,28},{28,24},{1,5},{5... | collective-permute-start | bytes 1179656 | tf_op jit(solution)/shard_map/ppermute | solution.py:38
  598.7 12.2 %collective-permute-start.13 = (bf16[256,768]{1,0:T(8,128)(2,1)S(1)}, bf16[256,768]{1,0:T(8,128)(2,1)}, u32[]{:S(2)}, u32[]{:S(2)}) collective-permute-start(bf16[256,768]{1,0:T(8,128)(2,1)S(1)} %get-tuple-element.96.kept_ref), channel_id=1, source_target_pairs={{0,2},{2,0},{1,3},{3,1},{4,6},{6,4},{5,7},{7,5},{8,10},{10,8},{9,1... | collective-permute-start | bytes 1179656 | tf_op jit(solution)/shard_map/ppermute | solution.py:33
  600.2 12.1 %collective-permute-start.18 = (bf16[256,768]{1,0:T(8,128)(2,1)}, bf16[256,768]{1,0:T(8,128)(2,1)}, u32[]{:S(2)}, u32[]{:S(2)}) collective-permute-start(bf16[256,768]{1,0:T(8,128)(2,1)} %get-tuple-element.93), channel_id=1, source_target_pairs={{0,4},{4,0},{8,12},{12,8},{16,20},{20,16},{24,28},{28,24},{1,5},{5... | collective-permute-start | bytes 1179656 | tf_op jit(solution)/shard_map/ppermute | solution.py:38
  601.7 71.2 %collective-permute-start.16 = (bf16[256,1536]{1,0:T(8,128)(2,1)S(1)}, bf16[256,1536]{1,0:T(8,128)(2,1)S(1)}, u32[]{:S(2)}, u32[]{:S(2)}) collective-permute-start(bf16[256,1536]{1,0:T(8,128)(2,1)S(1)} %get-tuple-element.92.kept_ref), channel_id=1, source_target_pairs={{0,2},{2,0},{1,3},{3,1},{4,6},{6,4},{5,7},{7,5},{8,10},{10,8},{9,1... | collective-permute-start | bytes 2359304 | tf_op jit(solution)/shard_map/ppermute | solution.py:33
  602.2 70.7 %collective-permute-start.17 = (bf16[256,1536]{1,0:T(8,128)(2,1)}, bf16[256,1536]{1,0:T(8,128)(2,1)S(1)}, u32[]{:S(2)}, u32[]{:S(2)}) collective-permute-start(bf16[256,1536]{1,0:T(8,128)(2,1)} %collective-permute-done.15.x_ref), channel_id=1, source_target_pairs={{0,2},{2,0},{1,3},{3,1},{4,6},{6,4},{5,7},{7,5},{8,10},{10,8},{9,1... | collective-permute-start | bytes 2359304 | tf_op jit(solution)/shard_map/ppermute | solution.py:33
  608.0 58.0 %collective-permute-start.19 = (bf16[256,768]{1,0:T(8,128)(2,1)S(1)}, bf16[256,768]{1,0:T(8,128)(2,1)}, u32[]{:S(2)}, u32[]{:S(2)}) collective-permute-start(bf16[256,768]{1,0:T(8,128)(2,1)S(1)} %get-tuple-element.94.kept_ref), channel_id=1, source_target_pairs={{0,2},{2,0},{1,3},{3,1},{4,6},{6,4},{5,7},{7,5},{8,10},{10,8},{9,1... | collective-permute-start | bytes 1179656 | tf_op jit(solution)/shard_map/ppermute | solution.py:33
  610.8 50.6 %collective-permute-start.14 = (bf16[256,768]{1,0:T(8,128)(2,1)}, bf16[256,768]{1,0:T(8,128)(2,1)}, u32[]{:S(2)}, u32[]{:S(2)}) collective-permute-start(bf16[256,768]{1,0:T(8,128)(2,1)} %collective-permute-done.12.x_ref), channel_id=1, source_target_pairs={{0,2},{2,0},{1,3},{3,1},{4,6},{6,4},{5,7},{7,5},{8,10},{10,8},{9,1... | collective-permute-start | bytes 1179656 | tf_op jit(solution)/shard_map/ppermute | solution.py:33
  612.3 56.0 %collective-permute-start.20 = (bf16[256,768]{1,0:T(8,128)(2,1)}, bf16[256,768]{1,0:T(8,128)(2,1)}, u32[]{:S(2)}, u32[]{:S(2)}) collective-permute-start(bf16[256,768]{1,0:T(8,128)(2,1)} %collective-permute-done.18.x_ref), channel_id=1, source_target_pairs={{0,2},{2,0},{1,3},{3,1},{4,6},{6,4},{5,7},{7,5},{8,10},{10,8},{9,1... | collective-permute-start | bytes 1179656 | tf_op jit(solution)/shard_map/ppermute | solution.py:33
  (31 other events, 316.8 us)
Sparse Core Ops, SparseCore 0:
  24.2 73.5 all-gather.3
  99.4 113.8 all-gather.5
  214.9 61.6 all-gather.7
  359.4 111.1 reduce-scatter.5
  473.3 60.9 reduce-scatter.3
  536.4 60.3 reduce-scatter.7

commit v8 on v7

--- a/solution.py
+++ b/solution.py
@@ -657,24 +657,19 @@
     return outs if filler else outs[0]
 
 
-def shard_kernel(plan, outs, *refs):
-    ins, out_refs = refs[: len(plan)], refs[len(plan) : len(plan) + outs]
-    stage = refs[len(plan) + outs : 2 * len(plan) + outs]
-    send_sem, recv_sem, load_sem, store_sem = refs[2 * len(plan) + outs :]
+def shard_copies(plan, ins, out_refs, stage, sems):
+    send_sem, recv_sem, load_sem, store_sem = sems
     x_peer, _, _ = neighbours()
     odd = lax.rem(lax.axis_index("fsdp"), 2)
     column = 2 * lax.axis_index("ctx") + odd
     other = 2 * lax.axis_index("ctx") + 1 - odd
-    greet((x_peer,))
     remote, loads, stores = [], [], []
-    for number, (which, start, size, cut) in enumerate(plan):
+    for number, (which, start, size) in enumerate(plan):
         rows = ins[number].shape[0]
         place = pl.ds(pl.multiple_of(odd * rows, rows), rows)
         target = out_refs[which].at[place, pl.ds(start, size)]
 
-        def source(index, ref=ins[number], size=size, cut=cut):
-            if not cut:
-                return ref
+        def source(index, ref=ins[number], size=size):
             return ref.at[:, pl.ds(pl.multiple_of(index * size, HEAD), size)]
 
         remote.append(
@@ -689,78 +684,210 @@
         )
         loads.append(pltpu.make_async_copy(source(column), stage[number], load_sem.at[number]))
         stores.append(pltpu.make_async_copy(stage[number], target, store_sem.at[number]))
-    for copy in remote:
-        copy.start()
-    for copy in loads:
-        copy.start()
-    for load, store in zip(loads, stores):
-        load.wait()
-        store.start()
-    for copy in stores:
-        copy.wait()
-    for copy in remote:
-        copy.wait()
-
-
-def shards(groups, number):
+    return remote, loads, stores
+
+
+def shard_plan(groups):
     plan, arrays, shapes = [], [], []
     for which, group in enumerate(groups):
         start = 0
-        for array, cut in group:
-            size = array.shape[1] // 4 if cut else array.shape[1]
-            plan.append((which, start, size, cut))
+        for array in group:
+            size = array.shape[1] // 4
+            plan.append((which, start, size))
             arrays.append(array)
             start += size
-        shapes.append((2 * group[0][0].shape[0], start))
-    hbm = pl.BlockSpec(memory_space=pl.ANY)
-    return pl.pallas_call(
-        functools.partial(shard_kernel, tuple(plan), len(groups)),
-        out_shape=[jax.ShapeDtypeStruct(shape, BF16) for shape in shapes],
-        in_specs=[hbm] * len(arrays),
-        out_specs=[hbm] * len(groups),
-        scratch_shapes=[
-            pltpu.VMEM((array.shape[0], size), BF16)
-            for array, (_, _, size, _) in zip(arrays, plan)
-        ]
-        + [pltpu.SemaphoreType.DMA((len(plan),))] * 4,
-        compiler_params=remote_params(number),
-        name="shards",
-    )(*arrays)
-
-
-def total_kernel(stages, part_ref, out_ref, inbox, outbox, send_sem, recv_sem):
-    peers = []
-    for axis, bit in stages:
-        mine = lax.axis_index(axis)
-        peers.append({axis: mine + bit * (1 - 2 * lax.rem(mine // bit, 2))})
-    greet(peers)
-    value = part_ref[...]
+        shapes.append(jax.ShapeDtypeStruct((2 * group[0].shape[0], start), BF16))
+    return tuple(plan), arrays, shapes
+
+
+def shard_scratch(plan, arrays):
+    return [
+        pltpu.VMEM((array.shape[0], size), BF16) for array, (_, _, size) in zip(arrays, plan)
+    ] + [pltpu.SemaphoreType.DMA((len(plan),))] * 4
+
+
+def bit_peer(axis, bit):
+    mine = lax.axis_index(axis)
+    return {axis: mine + bit * (1 - 2 * lax.rem(mine // bit, 2))}
+
+
+def sum_over(stages, value, inbox, outbox, send_sem, recv_sem):
     copies = []
-    for index, peer in enumerate(peers):
+    for index, (axis, bit) in enumerate(stages):
         outbox[index] = value
         copy = pltpu.make_async_remote_copy(
             src_ref=outbox.at[index],
             dst_ref=inbox.at[index],
             send_sem=send_sem.at[index],
             recv_sem=recv_sem.at[index],
-            device_id=peer,
+            device_id=bit_peer(axis, bit),
             device_id_type=MESH,
         )
         copy.start()
         copies.append(copy)
         copy.wait_recv()
         value = value + inbox[index]
-    out_ref[...] = value
-    for copy in copies:
-        copy.wait_send()
-
-
-def total(part):
+    return value, copies
+
+
+def fsdp_stages():
     stages, bit = [], 2
     while bit < lax.axis_size("fsdp"):
         stages.append(("fsdp", bit))
         bit *= 2
-    stages += [("tp", 1), ("fsdp", 1)]
+    return stages
+
+
+def first_kernel(plan, stages, *refs):
+    count = len(plan)
+    ins, row_ref, out_ref, gain_ref = refs[:count], refs[count], refs[count + 1], refs[count + 2]
+    stage, sems = refs[count + 3 : 2 * count + 3], refs[2 * count + 3 : 2 * count + 7]
+    inbox, outbox, gain_send, gain_recv = refs[2 * count + 7 :]
+    remote, loads, stores = shard_copies(plan, ins, [out_ref], stage, sems)
+    for copy in loads:
+        copy.start()
+    greet([bit_peer(axis, bit) for axis, bit in stages])
+    for copy in remote:
+        copy.start()
+    for load, store in zip(loads, stores):
+        load.wait()
+        store.start()
+    member = lax.broadcasted_iota(jnp.int32, gain_ref.shape, 0)
+    value = jnp.where(
+        member == lax.axis_index("fsdp"), jnp.broadcast_to(row_ref[...], gain_ref.shape), 0.0
+    )
+    value, copies = sum_over(stages, value, inbox, outbox, gain_send, gain_recv)
+    gain_ref[...] = value
+    for copy in copies:
+        copy.wait_send()
+    for copy in stores + remote:
+        copy.wait()
+
+
+def first_shards(arrays, row, count):
+    plan, arrays, shapes = shard_plan([arrays])
+    stages = fsdp_stages() + [("fsdp", 1)]
+    hbm = pl.BlockSpec(memory_space=pl.ANY)
+    vmem = pl.BlockSpec(memory_space=pltpu.VMEM)
+    gains = jax.ShapeDtypeStruct((count, row.shape[1]), F32)
+    box = pltpu.VMEM((len(stages),) + gains.shape, F32)
+    sem = pltpu.SemaphoreType.DMA((len(stages),))
+    return pl.pallas_call(
+        functools.partial(first_kernel, plan, tuple(stages)),
+        out_shape=shapes + [gains],
+        in_specs=[hbm] * len(arrays) + [vmem],
+        out_specs=[hbm, vmem],
+        scratch_shapes=shard_scratch(plan, arrays) + [box, box, sem, sem],
+        compiler_params=remote_params(3),
+        name="first_shards",
+    )(*arrays, row)
+
+
+def second_kernel(plan, outs, rows, *refs):
+    count = len(plan)
+    ins, token_ref, out_ref = refs[:count], refs[count], refs[count + 1]
+    pair_refs, refs = refs[count + 2 : count + 2 + outs], refs[count + 2 + outs :]
+    stage, sems = refs[:count], refs[count : count + 4]
+    own, own_sem, send_sem, recv_sem, local_sem = refs[count + 4 :]
+    x_peer, y_peer, c_peer = neighbours()
+    core = lax.axis_index("tp")
+    load_own = pltpu.make_async_copy(
+        token_ref.at[pl.ds(pl.multiple_of(core * 2 * rows, 2 * rows), 2 * rows)], own, own_sem
+    )
+    load_own.start()
+    remote, loads, stores = shard_copies(plan, ins, pair_refs, stage, sems)
+    for copy in loads:
+        copy.start()
+    load_own.wait()
+    greet((x_peer, y_peer, c_peer))
+
+    def slot(away_t, half, outer, inner):
+        return out_ref.at[pl.ds((away_t * 8 + half * 4 + outer * 2 + inner) * rows, rows)]
+
+    number = iter(range(14))
+
+    def send(source, target, peer):
+        index = next(number)
+        copy = pltpu.make_async_remote_copy(
+            src_ref=source,
+            dst_ref=target,
+            send_sem=send_sem.at[index],
+            recv_sem=recv_sem.at[index],
+            device_id=peer,
+            device_id_type=MESH,
+        )
+        copy.start()
+        return copy
+
+    first, second = own.at[pl.ds(0, rows)], own.at[pl.ds(rows, rows)]
+    x1 = send(first, slot(0, 0, 0, 1), x_peer)
+    y1 = send(second, slot(0, 1, 0, 1), y_peer)
+    x2 = send(second, slot(0, 1, 1, 0), x_peer)
+    y2 = send(first, slot(0, 0, 1, 0), y_peer)
+    rest = [send(first, slot(1, 0, 0, 0), c_peer), send(second, slot(1, 1, 0, 0), c_peer)]
+    kept = [
+        pltpu.make_async_copy(first, slot(0, 0, 0, 0), local_sem.at[0]),
+        pltpu.make_async_copy(second, slot(0, 1, 0, 0), local_sem.at[1]),
+    ]
+    for copy in kept:
+        copy.start()
+    for load, store in zip(loads, stores):
+        load.wait()
+        store.start()
+    x1.wait_recv()
+    y3 = send(slot(0, 0, 0, 1), slot(0, 0, 1, 1), y_peer)
+    y1.wait_recv()
+    x3 = send(slot(0, 1, 0, 1), slot(0, 1, 1, 1), x_peer)
+    for copy in remote:
+        copy.start()
+    rest.append(send(slot(0, 0, 0, 1), slot(1, 0, 0, 1), c_peer))
+    rest.append(send(slot(0, 1, 0, 1), slot(1, 1, 0, 1), c_peer))
+    x2.wait_recv()
+    rest.append(send(slot(0, 1, 1, 0), slot(1, 1, 1, 0), c_peer))
+    y2.wait_recv()
+    rest.append(send(slot(0, 0, 1, 0), slot(1, 0, 1, 0), c_peer))
+    y3.wait_recv()
+    rest.append(send(slot(0, 0, 1, 1), slot(1, 0, 1, 1), c_peer))
+    x3.wait_recv()
+    rest.append(send(slot(0, 1, 1, 1), slot(1, 1, 1, 1), c_peer))
+    for copy in (x1, y1, x2, y2, y3, x3):
+        copy.wait_send()
+    for copy in rest + kept + stores + remote:
+        copy.wait()
+
+
+def second_shards(groups, tokens):
+    plan, arrays, shapes = shard_plan(groups)
+    rows, width = tokens.shape[0] // 4, tokens.shape[1]
+    hbm = pl.BlockSpec(memory_space=pl.ANY)
+    return pl.pallas_call(
+        functools.partial(second_kernel, plan, len(groups), rows),
+        out_shape=[jax.ShapeDtypeStruct((16 * rows, width), tokens.dtype)] + shapes,
+        in_specs=[hbm] * (len(arrays) + 1),
+        out_specs=[hbm] * (len(groups) + 1),
+        scratch_shapes=shard_scratch(plan, arrays)
+        + [
+            pltpu.VMEM((2 * rows, width), tokens.dtype),
+            pltpu.SemaphoreType.DMA,
+            pltpu.SemaphoreType.DMA((14,)),
+            pltpu.SemaphoreType.DMA((14,)),
+            pltpu.SemaphoreType.DMA((2,)),
+        ],
+        compiler_params=remote_params(4),
+        name="second_shards",
+    )(*arrays, tokens)
+
+
+def total_kernel(stages, part_ref, out_ref, inbox, outbox, send_sem, recv_sem):
+    greet([bit_peer(axis, bit) for axis, bit in stages])
+    value, copies = sum_over(stages, part_ref[...], inbox, outbox, send_sem, recv_sem)
+    out_ref[...] = value
+    for copy in copies:
+        copy.wait_send()
+
+
+def total(part):
+    stages = fsdp_stages() + [("tp", 1), ("fsdp", 1)]
     return pl.pallas_call(
         functools.partial(total_kernel, tuple(stages)),
         out_shape=jax.ShapeDtypeStruct(part.shape, F32),
@@ -1120,42 +1247,18 @@
     core = lax.axis_index("tp")
 
     small = query_gain.shape[0]
-    lanes = jnp.arange(HEAD)[None, :]
-
-    def pad_rows(vector):
-        return jnp.concatenate([vector, jnp.zeros((block - small,), BF16)])
-
-    gains = jnp.where(
-        lanes == 0,
-        norm_gain[:, None],
-        jnp.where(
-            lanes == 1,
-            mlp_gain[:, None],
-            jnp.where(
-                lanes == 2, pad_rows(query_gain)[:, None], pad_rows(key_gain)[:, None]
-            ),
-        ),
-    )
+    members = [norm_gain, mlp_gain, query_gain, key_gain]
+    used = sum(member.shape[0] for member in members)
+    lanes = -(-used // HEAD) * HEAD
+    row = jnp.concatenate(members + [jnp.zeros((lanes - used,), BF16)]).astype(F32)[None]
     far_segments = swap_x(segment_ids)
-    (first_pair,) = shards(
-        [
-            [
-                (query_weight, True),
-                (key_matrix, True),
-                (value_matrix, True),
-                (output_weight, True),
-                (gains, False),
-            ]
-        ],
-        3,
+    first_pair, all_gains = first_shards(
+        [query_weight, key_matrix, value_matrix, output_weight], row, count
     )
     first = gather_line(first_pair)
-    gate_up_pair, down_pair = shards(
-        [
-            [(after(gate_weight, first_pair), True), (up_weight, True)],
-            [(down_weight, True)],
-        ],
-        4,
+    tok, gate_up_pair, down_pair = second_shards(
+        [[after(gate_weight, first_pair), up_weight], [down_weight]],
+        tokens.reshape(local, width),
     )
     gate_up_w = gather_line(gate_up_pair)
     down_w = gather_line(down_pair)
@@ -1164,7 +1267,6 @@
         return lax.dynamic_slice_in_dim(value.reshape(local, width), core * quarter, quarter, 0)
 
     own_tok, own_cot = own_quarter(tokens), own_quarter(cotangent)
-    tok = gather8(after(own_tok, gate_up_pair))
     segments = jnp.concatenate([segment_ids, far_segments])
     seg_cols, seg_rows = segments[:, :, None], segments[:, None, :]
     cosine, sine = rope_tables(jnp.arange(length).astype(F32))
@@ -1174,9 +1276,10 @@
     cols = (heads_q + 2) * HEAD
     qkv_w = first[:, :cols]
     out_w = first[:, cols : cols + heads_q * HEAD]
-    gain_cols = first[:, cols + heads_q * HEAD :].astype(F32)
-    in_gain, mid_gain = gain_cols[:, 0][None], gain_cols[:, 1][None]
-    head_gains = gain_cols.reshape(count, block, HEAD)[:, :small, 2:4].reshape(HEAD, 2).T
+    in_gain = all_gains[:, :block].reshape(1, width)
+    mid_gain = all_gains[:, block : 2 * block].reshape(1, width)
+    head_gains = all_gains[:, 2 * block : 2 * block + 2 * small].reshape(count, 2, small)
+    head_gains = jnp.moveaxis(head_gains, 0, 1).reshape(2, HEAD)
 
     in_f = tok.astype(F32)
     cot_from = after(own_cot, tok)

time: 697 us -> 687 us (0.986)
    pallas_call x2 -> x1, Pallas kernels: 81.5 us -> 40.9 us  [gather8(): pl.pallas_call(functools.partial(gather8_kernel, rows, bool(also)), out_s...]
    pallas_call x2, Pallas kernels: 41.6 us -> 79.6 us  [the longest x1 63 us: second_shards(): pl.pallas_call(functools.partial(second_kernel, plan, len(groups), rows),...]
where the time goes in v8:
time: 687 us; the launch traced here: 679 us
  Pallas kernels  372 us (54%)
  waiting for transfers between devices  124 us (18%)
  matrix products  86.1 us (13%)
  other arithmetic  34.1 us (5%)
  local copies, waits for them, and re-layouts  26.6 us (4%)
  starting transfers between devices  20.9 us (3%)
  between operations  14.9 us (2%)
    pallas_call x2, Pallas kernels, product_reduce8(): pl.pallas_call(functools.partial(product_reduce8_kernel, rows, groups, fi...  89.7 us
    dot_general x9, matrix products, mm(): lax.dot_general(left, right, (((left_dim,), (right_dim,)), ((), ())), pre...  86.1 us
    ppermute x11, waiting for transfers between devices, swap_ctx(): return lax.ppermute(value, 'ctx', [(0, 1), (1, 0)])  79.4 us
    pallas_call x1, Pallas kernels, second_shards(): pl.pallas_call(functools.partial(second_kernel, plan, len(groups), rows),...  63 us
    pallas_call x1, Pallas kernels, gather8_product(): pl.pallas_call(functools.partial(gather8_product_kernel, rows), out_shape...  41.5 us
    pallas_call x1, Pallas kernels, gather8(): pl.pallas_call(functools.partial(gather8_kernel, rows, bool(also)), out_s...  40.9 us
    pallas_call x1, Pallas kernels, reduce8(): pl.pallas_call(functools.partial(reduce8_kernel, rows), out_shape=jax.Sha...  40.8 us
    reduce_scatter x3, waiting for transfers between devices, scatter_line(): lax.psum_scatter(value, 'fsdp', scatter_dimension=0, tiled=True, axis_ind...  31.3 us
  transfers between devices with their start and end apart: 27, of which 11 were waited for; matrix products, arithmetic and copies ran while one was open for 17% of the time, Pallas kernels for 45%

profile of v8, /device:TPU:0, one launch (start us, length us, event | category | flops | bytes accessed | tf_op | source)
XLA Modules:
  0.0 678.5 jit_solution(2586863731480963657)
XLA Ops:
  9.9 16.6 %first_shards.1 = (bf16[512,768]{1,0:T(8,128)(2,1)}, f32[8,640]{1,0:T(8,128)}) custom-call(bf16[256,1024]{1,0:T(8,128)(2,1)} %refs_0_.1, bf16[256,512]{1,0:T(8,128)(2,1)} %refs_1_.2, bf16[256,512]{1,0:T(8,128)(2,1)} %refs_2_.2, bf16[256,1024]{1,0:T(8,128)(2,1)} %refs_3_.1, f32[1,640]{1,0:T(1,128)} %convert_element_type.91.refs_4_), custom_call_target="tpu_custom_call" | custom-call | tf_op jit(solution)/shard_map/first_shards/pallas_call | solution.py:775
  26.5 63.0 %second_shards.1 = (bf16[2048,2048]{1,0:T(8,128)(2,1)}, bf16[512,1536]{1,0:T(8,128)(2,1)}, bf16[512,768]{1,0:T(8,128)(2,1)}) custom-call(bf16[256,3072]{1,0:T(8,128)(2,1)} %refs_0_.2, bf16[256,3072]{1,0:T(8,128)(2,1)} %refs_1_.3, bf16[256,3072]{1,0:T(8,128)(2,1)} %refs_2_.3, bf16[512,2048]{1,0:T(8,128)(2,1)} %bitcast.49), custom_call_target="tpu_custom_call" | custom-call | tf_op jit(solution)/shard_map/second_shards/pallas_call | solution.py:863
  93.5 5.4 fusion
  103.6 9.9 %collective-permute-done = s32[1,1024]{1,0:T(1,128)S(1)} collective-permute-done((s32[1,1024]{1,0:T(1,128)S(1)}, s32[1,1024]{1,0:T(1,128)S(1)}, u32[]{:S(2)}, u32[]{:S(2)}) %collective-permute-start) | collective-permute-done | bytes 4128 | tf_op jit(solution)/shard_map/ppermute | solution.py:38
  115.4 10.6 %fusion.8.qkv_ref = f32[2048,512]{1,0:T(8,128)} fusion(bf16[2048,2048]{1,0:T(8,128)(2,1)} %get-tuple-element.49, f32[2048]{0:T(1024)S(1)} %bitcast.56, f32[2048]{0:T(1024)S(1)} %add_rsqrt_fusion, bf16[2048,768]{1,0:T(8,128)(2,1)} %all-gather.4.cloned.1.call-done.refs_1_), kind=kOutput, calls=%fused_computation.22 | convolution fusion | flops 4311744512 | bytes 14696448 | tf_op jit(solution)/shard_map/dot_general | solution.py:23
  126.0 16.2 %attend.1 = bf16[2048,256]{1,0:T(8,128)(2,1)} custom-call(s32[2]{0:T(128)} %pad_add_fusion.1.meta_ref.spot_ref, f32[2048,512]{1,0:T(8,128)} %fusion.8.qkv_ref, s32[2,1024,1]{2,1,0:T(8,128)} %copy.28.segc_ref, s32[2,1,1024]{2,1,0:T(1,128)} %broadcast_in_dim.8.segr_ref, f32[1024,128]{1,0:T(8,128)} %get-tuple-element.109.cos_ref, ...), custom_call_target="tpu_custom_call" | custom-call | flops 1073741824 | bytes 5242880 | tf_op jit(solution)/shard_map/attend/pallas_call | solution.py:1166
  142.2 4.8 convolution_convert_fusion.far_ref
  147.0 6.2 fusion.21.near_ref
  153.2 40.8 %reduce8.1 = f32[256,2048]{1,0:T(8,128)S(1)} custom-call(f32[1024,2048]{1,0:T(8,128)} %fusion.21.near_ref, bf16[1024,2048]{1,0:T(8,128)(2,1)} %convolution_convert_fusion.far_ref), custom_call_target="tpu_custom_call" | custom-call | tf_op jit(solution)/shard_map/reduce8/pallas_call | solution.py:441
  198.6 11.3 %collective-permute-done.3.refs_4_ = bf16[128,2048]{1,0:T(8,128)(2,1)S(1)} collective-permute-done((bf16[128,2048]{1,0:T(8,128)(2,1)S(1)}, bf16[128,2048]{1,0:T(8,128)(2,1)S(1)}, u32[]{:S(2)}, u32[]{:S(2)}) %collective-permute-start.3) | collective-permute-done | bytes 524320 | tf_op jit(solution)/shard_map/ppermute | solution.py:33
  211.5 40.9 %gather8_also.1 = (bf16[2048,2048]{1,0:T(8,128)(2,1)}, bf16[2048,2048]{1,0:T(8,128)(2,1)}) custom-call(bf16[256,2048]{1,0:T(8,128)(2,1)} %multiply_convert_fusion.3.refs_0_, bf16[256,2048]{1,0:T(8,128)(2,1)} %copy-done.14, bf16[256,2048]{1,0:T(8,128)(2,1)} %copy-done.17, bf16[256,2048]{1,0:T(8,128)(2,1)} %copy-done.18, bf16[128,2048]{1,0:T(8,128)(2,1)} %copy-done.23, ...), custom_call_target="tpu_custom_call" | custom-call | tf_op jit(solution)/shard_map/gather8_also/pallas_call | solution.py:348
  252.5 17.6 %fusion.31 = f32[2048,1536]{1,0:T(8,128)S(1)} fusion(bf16[2048,2048]{1,0:T(8,128)(2,1)} %get-tuple-element.57.refs_3_, bf16[2048,1536]{1,0:T(8,128)(2,1)} %all-gather.6.cloned.1.call-done.refs_2_), kind=kOutput, calls=%fused_computation.81 | convolution fusion | flops 12884901888 | bytes 27262976 | tf_op jit(solution)/shard_map/dot_general | solution.py:23
  272.2 4.3 copy-done.6
  279.2 8.5 %convolution_convert_fusion.1 = bf16[2048,768]{1,0:T(8,128)(2,1)} fusion(bf16[2048,2048]{1,0:T(8,128)(2,1)S(1)} %copy-done.33, bf16[2048,768]{1,0:T(8,128)(2,1)S(1)} %multiply_convert_fusion.2.acts_ref), kind=kOutput, calls=%fused_computation.11 | convolution fusion | flops 6444023808 | bytes 14680064 | tf_op jit(solution)/shard_map/dot_general | solution.py:23
  287.7 16.4 %multiply_convert_fusion = (bf16[2048,768]{1,0:T(8,128)(2,1)}, bf16[2048,768]{1,0:T(8,128)(2,1)}) fusion(f32[2048,1536]{1,0:T(8,128)} %copy-done.6, bf16[2048,2048]{1,0:T(8,128)(2,1)} %get-tuple-element.59, bf16[2048,768]{1,0:T(8,128)(2,1)} %all-gather.8.cloned.1.call-done.weight_ref), kind=kOutput, calls=%fused_computation.5 | convolution fusion | flops 6462898176 | bytes 30408704 | tf_op jit(solution)/shard_map/dot_general | solution.py:23
  304.1 47.6 %product_reduce8.2 = (f32[256,2048]{1,0:T(8,128)}, bf16[2048,1536]{1,0:T(8,128)(2,1)}) custom-call(bf16[2048,768]{1,0:T(8,128)(2,1)} %get-tuple-element.88.refs_0_, bf16[2048,768]{1,0:T(8,128)(2,1)} %get-tuple-element.87.refs_1_, bf16[2048,1536]{1,0:T(8,128)(2,1)} %all-gather.6.cloned.1.call-done.refs_2_, bf16[2048,2048]{1,0:T(8,128)(2,1)} %get-tuple-element.57.refs_3_), custom_call_target="tpu_custom_call" | custom-call | flops 25769803776 | bytes 25165824 | tf_op jit(solution)/shard_map/product_reduce8/pallas_call | solution.py:645
  356.5 41.5 %gather8_product.1 = (bf16[2048,2048]{1,0:T(8,128)(2,1)}, f32[512,2048]{1,0:T(8,128)}, bf16[256,2048]{1,0:T(8,128)(2,1)S(1)}, bf16[256,2048]{1,0:T(8,128)(2,1)S(1)}) custom-call(bf16[256,2048]{1,0:T(8,128)(2,1)S(1)} %fusion.28.own_ref, bf16[2048,768]{1,0:T(8,128)(2,1)} %copy-done.16, bf16[2048,768]{1,0:T(8,128)(2,1)} %all-gather.8.cloned.1.call-done.weight_ref), custom_call_target="tpu_custom_call" | custom-call | flops 6442450944 | bytes 8388608 | tf_op jit(solution)/shard_map/gather8_product/pallas_call | solution.py:307
  398.0 7.1 %convolution_convert_fusion.4.grad_ref = bf16[2048,256]{1,0:T(8,128)(2,1)} fusion(bf16[2048,2048]{1,0:T(8,128)(2,1)} %get-tuple-element.64, bf16[2048,768]{1,0:T(8,128)(2,1)} %all-gather.4.cloned.1.call-done.refs_1_), kind=kOutput, calls=%fused_computation.21 | convolution fusion | flops 2148007936 | bytes 10485760 | tf_op jit(solution)/shard_map/dot_general | solution.py:23
  405.0 28.8 %attend_back.1 = (bf16[2048,512]{1,0:T(8,128)(2,1)}, f32[2,128]{1,0:T(2,128)}) custom-call(s32[2]{0:T(128)} %pad_add_fusion.1.meta_ref.spot_ref, f32[2048,512]{1,0:T(8,128)} %fusion.8.qkv_ref, bf16[2048,256]{1,0:T(8,128)(2,1)} %convolution_convert_fusion.4.grad_ref, s32[2,1024,1]{2,1,0:T(8,128)} %copy.28.segc_ref, s32[2,1,1024]{2,1,0:T(1,128)} %broadcast_in_dim.8.segr_ref, ...), custom_call_target="tpu_custom_call" | custom-call | flops 2684354560 | bytes 8388608 | tf_op jit(solution)/shard_map/attend_back/pallas_call | solution.py:1194
  433.9 6.2 convolution_convert_fusion.3
  440.1 8.7 %convolution_convert_fusion.2 = bf16[2048,512]{1,0:T(8,128)(2,1)S(1)} fusion(bf16[2048,512]{1,0:T(8,128)(2,1)S(1)} %copy-done.34, bf16[2048,2048]{1,0:T(8,128)(2,1)} %get-tuple-element.49, f32[2048]{0:T(1024)S(1)} %bitcast.57, f32[2048]{0:T(1024)S(1)} %copy-done.29), kind=kOutput, calls=%fused_computation.16 | convolution fusion | flops 4312793088 | bytes 12599296 | tf_op jit(solution)/shard_map/dot_general | solution.py:23
  453.1 23.7 %collective-permute-done.5 = bf16[256,2048]{1,0:T(8,128)(2,1)S(1)} collective-permute-done((bf16[256,2048]{1,0:T(8,128)(2,1)S(1)}, bf16[256,2048]{1,0:T(8,128)(2,1)S(1)}, u32[]{:S(2)}, u32[]{:S(2)}) %collective-permute-start.5) | collective-permute-done | bytes 1048608 | tf_op jit(solution)/shard_map/ppermute | solution.py:33
  484.0 10.8 %collective-permute-done.8 = bf16[128,2048]{1,0:T(8,128)(2,1)S(1)} collective-permute-done((bf16[128,2048]{1,0:T(8,128)(2,1)}, bf16[128,2048]{1,0:T(8,128)(2,1)S(1)}, u32[]{:S(2)}, u32[]{:S(2)}) %collective-permute-start.8) | collective-permute-done | bytes 524320 | tf_op jit(solution)/shard_map/ppermute | solution.py:33
  500.5 42.0 %product_reduce8.3 = f32[256,2048]{1,0:T(8,128)} custom-call(bf16[2048,512]{1,0:T(8,128)(2,1)} %get-tuple-element.71.refs_0_, bf16[2048,768]{1,0:T(8,128)(2,1)} %all-gather.4.cloned.1.call-done.refs_1_), custom_call_target="tpu_custom_call" | custom-call | flops 4294967296 | bytes 8388608 | tf_op jit(solution)/shard_map/product_reduce8/pallas_call | solution.py:645
  545.3 4.0 fusion.14.own_ref
  556.4 31.3 %reduce-scatter.8.cloned.1.call-done = bf16[512,768]{1,0:T(8,128)(2,1)} async-done(((bf16[2048,768]{1,0:T(8,128)(2,1)}), bf16[512,768]{1,0:T(8,128)(2,1)}) %reduce-scatter.8.cloned.1.call-update) | async-done | bytes 786448 | tf_op jit(solution)/shard_map/reduce_scatter | solution.py:51
  604.4 12.6 %total.1 = f32[34,128]{1,0:T(8,128)} custom-call(f32[34,128]{1,0:T(8,128)} %fusion.26.part_ref), custom_call_target="tpu_custom_call" | custom-call | tf_op jit(solution)/shard_map/total/pallas_call | solution.py:891
  617.0 3.6 stack.23
  623.3 29.0 %collective-permute-done.14.both_ref = bf16[256,768]{1,0:T(8,128)(2,1)} collective-permute-done((bf16[256,768]{1,0:T(8,128)(2,1)}, bf16[256,768]{1,0:T(8,128)(2,1)}, u32[]{:S(2)}, u32[]{:S(2)}) %collective-permute-start.14) | collective-permute-done | bytes 393248 | tf_op jit(solution)/shard_map/ppermute | solution.py:33
  652.3 4.6 join.3
  659.2 4.6 join.5
  665.7 5.8 join.4
  (173 shorter events, 79.1 us)
Async XLA Ops:
  7.2 108.2 %all-gather.4.cloned.1.call-start = ((), (), s32[]{:S(2)}) async-start(), calls=%async_computation.3 | async-start | bytes 3932160 | tf_op jit(solution)/shard_map/all_gather | solution.py:47
  26.5 226.0 %all-gather.6.cloned.1.call-start = ((), (), s32[]{:S(2)}) async-start(), calls=%async_computation.4 | async-start | bytes 7864320 | tf_op jit(solution)/shard_map/all_gather | solution.py:47
  26.5 63.1 %copy-start.11 = (bf16[1,512,2048]{2,1,0:T(8,128)(2,1)S(1)}, bf16[1,512,2048]{2,1,0:T(8,128)(2,1)}, u32[]{:S(2)}) copy-start(bf16[1,512,2048]{2,1,0:T(8,128)(2,1)} %param.27) | copy-start | bytes 6291460
  89.6 198.1 %all-gather.8.cloned.1.call-start = ((), (), s32[]{:S(2)}) async-start(), calls=%async_computation.5 | async-start | bytes 3932160 | tf_op jit(solution)/shard_map/all_gather | solution.py:47
  89.8 57.2 %collective-permute-start.1 = (bf16[256,2048]{1,0:T(8,128)(2,1)S(1)}, bf16[256,2048]{1,0:T(8,128)(2,1)S(1)}, u32[]{:S(2)}, u32[]{:S(2)}) collective-permute-start(bf16[256,2048]{1,0:T(8,128)(2,1)S(1)} %dynamic-slice_bitcast_fusion.refs_1_), channel_id=1, source_target_pairs={{0,4},{4,0},{8,12},{12,8},{16,20},{20,16},{24,28},{28,24},{1,5},{5... | collective-permute-start | bytes 3145736 | tf_op jit(solution)/shard_map/ppermute | solution.py:38
  91.3 103.8 %collective-permute-start.2 = (bf16[256,2048]{1,0:T(8,128)(2,1)S(1)}, bf16[256,2048]{1,0:T(8,128)(2,1)S(1)}, u32[]{:S(2)}, u32[]{:S(2)}) collective-permute-start(bf16[256,2048]{1,0:T(8,128)(2,1)S(1)} %dynamic-slice_bitcast_fusion.refs_1_), channel_id=1, source_target_pairs={{0,2},{2,0},{1,3},{3,1},{4,6},{6,4},{5,7},{7,5},{8,10},{10,8},{9,1... | collective-permute-start | bytes 3145736 | tf_op jit(solution)/shard_map/ppermute | solution.py:33
  92.9 20.6 %collective-permute-start = (s32[1,1024]{1,0:T(1,128)S(1)}, s32[1,1024]{1,0:T(1,128)S(1)}, u32[]{:S(2)}, u32[]{:S(2)}) collective-permute-start(s32[1,1024]{1,0:T(1,128)S(1)} %copy-done.32), channel_id=1, source_target_pairs={{0,4},{4,0},{8,12},{12,8},{16,20},{20,16},{24,28},{28,24},{1,5},{5... | collective-permute-start | bytes 12296 | tf_op jit(solution)/shard_map/ppermute | solution.py:38
  93.4 456.0 %reduce-scatter.6.cloned.1.call-start = ((), (), s32[]{:S(2)}) async-start(), calls=%async_computation.7 | async-start | bytes 7864320 | tf_op jit(solution)/shard_map/reduce_scatter | solution.py:51
  147.0 48.1 %copy-start.17 = (bf16[256,2048]{1,0:T(8,128)(2,1)}, bf16[256,2048]{1,0:T(8,128)(2,1)S(1)}, u32[]{:S(2)}) copy-start(bf16[256,2048]{1,0:T(8,128)(2,1)S(1)} %collective-permute-done.1.refs_2_) | copy-start | bytes 3145732
  153.2 40.8 %copy-start.5 = (bf16[1,512,2048]{2,1,0:T(8,128)(2,1)S(1)}, bf16[1,512,2048]{2,1,0:T(8,128)(2,1)}, u32[]{:S(2)}) copy-start(bf16[1,512,2048]{2,1,0:T(8,128)(2,1)} %param.14) | copy-start | bytes 6291460
  195.2 14.7 %collective-permute-start.3 = (bf16[128,2048]{1,0:T(8,128)(2,1)S(1)}, bf16[128,2048]{1,0:T(8,128)(2,1)S(1)}, u32[]{:S(2)}, u32[]{:S(2)}) collective-permute-start(bf16[128,2048]{1,0:T(8,128)(2,1)S(1)} %slice.60), channel_id=1, source_target_pairs={{0,2},{2,0},{1,3},{3,1},{4,6},{6,4},{5,7},{7,5},{8,10},{10,8},{9,1... | collective-permute-start | bytes 1572872 | tf_op jit(solution)/shard_map/ppermute | solution.py:33
  196.8 13.4 %collective-permute-start.4 = (bf16[128,2048]{1,0:T(8,128)(2,1)S(1)}, bf16[128,2048]{1,0:T(8,128)(2,1)S(1)}, u32[]{:S(2)}, u32[]{:S(2)}) collective-permute-start(bf16[128,2048]{1,0:T(8,128)(2,1)S(1)} %slice.61), channel_id=1, source_target_pairs={{0,4},{4,0},{8,12},{12,8},{16,20},{20,16},{24,28},{28,24},{1,5},{5... | collective-permute-start | bytes 1572872 | tf_op jit(solution)/shard_map/ppermute | solution.py:38
  351.8 201.7 %reduce-scatter.4.cloned.1.call-start = ((), (), s32[]{:S(2)}) async-start(), calls=%async_computation.6 | async-start | bytes 3932160 | tf_op jit(solution)/shard_map/reduce_scatter | solution.py:51
  450.7 137.0 %reduce-scatter.8.cloned.1.call-start = ((), (), s32[]{:S(2)}) async-start(), calls=%async_computation.8 | async-start | bytes 3932160 | tf_op jit(solution)/shard_map/reduce_scatter | solution.py:51
  451.3 25.6 %collective-permute-start.5 = (bf16[256,2048]{1,0:T(8,128)(2,1)S(1)}, bf16[256,2048]{1,0:T(8,128)(2,1)S(1)}, u32[]{:S(2)}, u32[]{:S(2)}) collective-permute-start(bf16[256,2048]{1,0:T(8,128)(2,1)S(1)} %get-tuple-element.63), channel_id=1, source_target_pairs={{0,2},{2,0},{1,3},{3,1},{4,6},{6,4},{5,7},{7,5},{8,10},{10,8},{9,1... | collective-permute-start | bytes 3145736 | tf_op jit(solution)/shard_map/ppermute | solution.py:33
  451.9 25.3 %collective-permute-start.7 = (bf16[256,2048]{1,0:T(8,128)(2,1)S(1)}, bf16[256,2048]{1,0:T(8,128)(2,1)S(1)}, u32[]{:S(2)}, u32[]{:S(2)}) collective-permute-start(bf16[256,2048]{1,0:T(8,128)(2,1)S(1)} %get-tuple-element.68), channel_id=1, source_target_pairs={{0,4},{4,0},{8,12},{12,8},{16,20},{20,16},{24,28},{28,24},{1,5},{5... | collective-permute-start | bytes 3145736 | tf_op jit(solution)/shard_map/ppermute | solution.py:38
  481.2 13.6 %collective-permute-start.8 = (bf16[128,2048]{1,0:T(8,128)(2,1)}, bf16[128,2048]{1,0:T(8,128)(2,1)S(1)}, u32[]{:S(2)}, u32[]{:S(2)}) collective-permute-start(bf16[128,2048]{1,0:T(8,128)(2,1)} %slice.108), channel_id=1, source_target_pairs={{0,2},{2,0},{1,3},{3,1},{4,6},{6,4},{5,7},{7,5},{8,10},{10,8},{9,1... | collective-permute-start | bytes 1572872 | tf_op jit(solution)/shard_map/ppermute | solution.py:33
  483.3 13.2 %collective-permute-start.6 = (bf16[128,2048]{1,0:T(8,128)(2,1)}, bf16[128,2048]{1,0:T(8,128)(2,1)S(1)}, u32[]{:S(2)}, u32[]{:S(2)}) collective-permute-start(bf16[128,2048]{1,0:T(8,128)(2,1)} %slice.109), channel_id=1, source_target_pairs={{0,4},{4,0},{8,12},{12,8},{16,20},{20,16},{24,28},{28,24},{1,5},{5... | collective-permute-start | bytes 1572872 | tf_op jit(solution)/shard_map/ppermute | solution.py:38
  500.5 90.6 %collective-permute-start.9 = (bf16[256,2048]{1,0:T(8,128)(2,1)}, bf16[256,2048]{1,0:T(8,128)(2,1)}, u32[]{:S(2)}, u32[]{:S(2)}) collective-permute-start(bf16[256,2048]{1,0:T(8,128)(2,1)} %fusion.18.own_ref), channel_id=1, source_target_pairs={{0,1},{1,0},{2,3},{3,2},{4,5},{5,4},{6,7},{7,6},{8,9},{9,8},{10,11... | collective-permute-start | bytes 3145736 | tf_op jit(solution)/shard_map/ppermute | solution.py:29
  549.3 43.3 %collective-permute-start.10 = (bf16[256,2048]{1,0:T(8,128)(2,1)S(1)}, bf16[256,2048]{1,0:T(8,128)(2,1)}, u32[]{:S(2)}, u32[]{:S(2)}) collective-permute-start(bf16[256,2048]{1,0:T(8,128)(2,1)S(1)} %fusion.14.own_ref), channel_id=1, source_target_pairs={{0,1},{1,0},{2,3},{3,2},{4,5},{5,4},{6,7},{7,6},{8,9},{9,8},{10,11... | collective-permute-start | bytes 3145736 | tf_op jit(solution)/shard_map/ppermute | solution.py:29
  551.2 47.7 %copy-start.15 = (bf16[256,1536]{1,0:T(8,128)(2,1)}, bf16[256,1536]{1,0:T(8,128)(2,1)S(1)}, u32[]{:S(2)}) copy-start(bf16[256,1536]{1,0:T(8,128)(2,1)S(1)} %get-tuple-element.93.kept_ref) | copy-start | bytes 2359300
  551.2 42.0 %collective-permute-start.15 = (bf16[256,1536]{1,0:T(8,128)(2,1)S(1)}, bf16[256,1536]{1,0:T(8,128)(2,1)}, u32[]{:S(2)}, u32[]{:S(2)}) collective-permute-start(bf16[256,1536]{1,0:T(8,128)(2,1)S(1)} %get-tuple-element.92), channel_id=1, source_target_pairs={{0,4},{4,0},{8,12},{12,8},{16,20},{20,16},{24,28},{28,24},{1,5},{5... | collective-permute-start | bytes 2359304 | tf_op jit(solution)/shard_map/ppermute | solution.py:38
  552.6 37.0 %collective-permute-start.11 = (f32[34,128]{1,0:T(8,128)S(1)}, f32[34,128]{1,0:T(8,128)S(1)}, u32[]{:S(2)}, u32[]{:S(2)}) collective-permute-start(f32[34,128]{1,0:T(8,128)S(1)} %maximum_bitcast_fusion), channel_id=1, source_target_pairs={{0,2},{2,0},{1,3},{3,1},{4,6},{6,4},{5,7},{7,5},{8,10},{10,8},{9,1... | collective-permute-start | bytes 52232 | tf_op jit(solution)/shard_map/ppermute | solution.py:33
  555.4 65.3 %copy-start.20 = (bf16[256,768]{1,0:T(8,128)(2,1)}, bf16[256,768]{1,0:T(8,128)(2,1)S(1)}, u32[]{:S(2)}) copy-start(bf16[256,768]{1,0:T(8,128)(2,1)S(1)} %get-tuple-element.97.kept_ref) | copy-start | bytes 1179652
  555.4 43.5 %collective-permute-start.12 = (bf16[256,768]{1,0:T(8,128)(2,1)}, bf16[256,768]{1,0:T(8,128)(2,1)}, u32[]{:S(2)}, u32[]{:S(2)}) collective-permute-start(bf16[256,768]{1,0:T(8,128)(2,1)} %get-tuple-element.96), channel_id=1, source_target_pairs={{0,4},{4,0},{8,12},{12,8},{16,20},{20,16},{24,28},{28,24},{1,5},{5... | collective-permute-start | bytes 1179656 | tf_op jit(solution)/shard_map/ppermute | solution.py:38
  589.6 12.2 %collective-permute-start.13 = (bf16[256,768]{1,0:T(8,128)(2,1)S(1)}, bf16[256,768]{1,0:T(8,128)(2,1)}, u32[]{:S(2)}, u32[]{:S(2)}) collective-permute-start(bf16[256,768]{1,0:T(8,128)(2,1)S(1)} %get-tuple-element.97.kept_ref), channel_id=1, source_target_pairs={{0,2},{2,0},{1,3},{3,1},{4,6},{6,4},{5,7},{7,5},{8,10},{10,8},{9,1... | collective-permute-start | bytes 1179656 | tf_op jit(solution)/shard_map/ppermute | solution.py:33
  591.2 12.1 %collective-permute-start.18 = (bf16[256,768]{1,0:T(8,128)(2,1)}, bf16[256,768]{1,0:T(8,128)(2,1)}, u32[]{:S(2)}, u32[]{:S(2)}) collective-permute-start(bf16[256,768]{1,0:T(8,128)(2,1)} %get-tuple-element.94), channel_id=1, source_target_pairs={{0,4},{4,0},{8,12},{12,8},{16,20},{20,16},{24,28},{28,24},{1,5},{5... | collective-permute-start | bytes 1179656 | tf_op jit(solution)/shard_map/ppermute | solution.py:38
  592.6 71.3 %collective-permute-start.16 = (bf16[256,1536]{1,0:T(8,128)(2,1)S(1)}, bf16[256,1536]{1,0:T(8,128)(2,1)S(1)}, u32[]{:S(2)}, u32[]{:S(2)}) collective-permute-start(bf16[256,1536]{1,0:T(8,128)(2,1)S(1)} %get-tuple-element.93.kept_ref), channel_id=1, source_target_pairs={{0,2},{2,0},{1,3},{3,1},{4,6},{6,4},{5,7},{7,5},{8,10},{10,8},{9,1... | collective-permute-start | bytes 2359304 | tf_op jit(solution)/shard_map/ppermute | solution.py:33
  593.2 70.7 %collective-permute-start.17 = (bf16[256,1536]{1,0:T(8,128)(2,1)}, bf16[256,1536]{1,0:T(8,128)(2,1)S(1)}, u32[]{:S(2)}, u32[]{:S(2)}) collective-permute-start(bf16[256,1536]{1,0:T(8,128)(2,1)} %collective-permute-done.15.x_ref), channel_id=1, source_target_pairs={{0,2},{2,0},{1,3},{3,1},{4,6},{6,4},{5,7},{7,5},{8,10},{10,8},{9,1... | collective-permute-start | bytes 2359304 | tf_op jit(solution)/shard_map/ppermute | solution.py:33
  598.9 58.1 %collective-permute-start.19 = (bf16[256,768]{1,0:T(8,128)(2,1)S(1)}, bf16[256,768]{1,0:T(8,128)(2,1)}, u32[]{:S(2)}, u32[]{:S(2)}) collective-permute-start(bf16[256,768]{1,0:T(8,128)(2,1)S(1)} %get-tuple-element.95.kept_ref), channel_id=1, source_target_pairs={{0,2},{2,0},{1,3},{3,1},{4,6},{6,4},{5,7},{7,5},{8,10},{10,8},{9,1... | collective-permute-start | bytes 1179656 | tf_op jit(solution)/shard_map/ppermute | solution.py:33
  601.8 50.6 %collective-permute-start.14 = (bf16[256,768]{1,0:T(8,128)(2,1)}, bf16[256,768]{1,0:T(8,128)(2,1)}, u32[]{:S(2)}, u32[]{:S(2)}) collective-permute-start(bf16[256,768]{1,0:T(8,128)(2,1)} %collective-permute-done.12.x_ref), channel_id=1, source_target_pairs={{0,2},{2,0},{1,3},{3,1},{4,6},{6,4},{5,7},{7,5},{8,10},{10,8},{9,1... | collective-permute-start | bytes 1179656 | tf_op jit(solution)/shard_map/ppermute | solution.py:33
  603.3 56.0 %collective-permute-start.20 = (bf16[256,768]{1,0:T(8,128)(2,1)}, bf16[256,768]{1,0:T(8,128)(2,1)}, u32[]{:S(2)}, u32[]{:S(2)}) collective-permute-start(bf16[256,768]{1,0:T(8,128)(2,1)} %collective-permute-done.18.x_ref), channel_id=1, source_target_pairs={{0,2},{2,0},{1,3},{3,1},{4,6},{6,4},{5,7},{7,5},{8,10},{10,8},{9,1... | collective-permute-start | bytes 1179656 | tf_op jit(solution)/shard_map/ppermute | solution.py:33
  (30 other events, 273.9 us)
Sparse Core Ops, SparseCore 0:
  26.6 62.6 all-gather.3
  90.8 113.9 all-gather.5
  206.4 61.6 all-gather.7
  351.9 109.6 reduce-scatter.5
  464.3 60.8 reduce-scatter.3
  527.3 60.2 reduce-scatter.7

commit v9 on v8

--- a/solution.py
+++ b/solution.py
@@ -711,7 +711,7 @@
     return {axis: mine + bit * (1 - 2 * lax.rem(mine // bit, 2))}
 
 
-def sum_over(stages, value, inbox, outbox, send_sem, recv_sem):
+def sum_over(stages, value, inbox, outbox, send_sem, recv_sem, behind=()):
     copies = []
     for index, (axis, bit) in enumerate(stages):
         outbox[index] = value
@@ -725,6 +725,9 @@
         )
         copy.start()
         copies.append(copy)
+        if index == 0:
+            for later in behind:
+                later.start()
         copy.wait_recv()
         value = value + inbox[index]
     return value, copies
@@ -747,8 +750,6 @@
     for copy in loads:
         copy.start()
     greet([bit_peer(axis, bit) for axis, bit in stages])
-    for copy in remote:
-        copy.start()
     for load, store in zip(loads, stores):
         load.wait()
         store.start()
@@ -756,7 +757,7 @@
     value = jnp.where(
         member == lax.axis_index("fsdp"), jnp.broadcast_to(row_ref[...], gain_ref.shape), 0.0
     )
-    value, copies = sum_over(stages, value, inbox, outbox, gain_send, gain_recv)
+    value, copies = sum_over(stages, value, inbox, outbox, gain_send, gain_recv, remote)
     gain_ref[...] = value
     for copy in copies:
         copy.wait_send()
@@ -766,7 +767,7 @@
 
 def first_shards(arrays, row, count):
     plan, arrays, shapes = shard_plan([arrays])
-    stages = fsdp_stages() + [("fsdp", 1)]
+    stages = [("fsdp", 1)] + fsdp_stages()
     hbm = pl.BlockSpec(memory_space=pl.ANY)
     vmem = pl.BlockSpec(memory_space=pltpu.VMEM)
     gains = jax.ShapeDtypeStruct((count, row.shape[1]), F32)
@@ -878,55 +879,57 @@
     )(*arrays, tokens)
 
 
-def total_kernel(stages, part_ref, out_ref, inbox, outbox, send_sem, recv_sem):
+def total_kernel(stages, part_ref, *refs):
+    row_refs, (out_ref, first_ref, second_ref), refs = refs[:4], refs[4:7], refs[7:]
+    inbox, outbox, send_sem, recv_sem, stage, load_sem, store_sem = refs
+    core = lax.axis_index("tp")
+    rows = stage.shape[1]
+    loads, stores = [], []
+    for index, row_ref in enumerate(row_refs):
+        side = core if index % 2 == 0 else 1 - core
+        place = pl.ds(pl.multiple_of(side * rows, rows), rows)
+        target = (first_ref, second_ref)[index // 2]
+        loads.append(pltpu.make_async_copy(row_ref, stage.at[index], load_sem.at[index]))
+        stores.append(
+            pltpu.make_async_copy(stage.at[index], target.at[place], store_sem.at[index])
+        )
+    for copy in loads:
+        copy.start()
     greet([bit_peer(axis, bit) for axis, bit in stages])
+    for load, store in zip(loads, stores):
+        load.wait()
+        store.start()
     value, copies = sum_over(stages, part_ref[...], inbox, outbox, send_sem, recv_sem)
     out_ref[...] = value
     for copy in copies:
         copy.wait_send()
-
-
-def total(part):
+    for copy in stores:
+        copy.wait()
+
+
+def total(part, first, second):
     stages = fsdp_stages() + [("tp", 1), ("fsdp", 1)]
+    rows, width = first[0].shape
+    hbm = pl.BlockSpec(memory_space=pl.ANY)
+    vmem = pl.BlockSpec(memory_space=pltpu.VMEM)
+    both = jax.ShapeDtypeStruct((2 * rows, width), BF16)
     return pl.pallas_call(
         functools.partial(total_kernel, tuple(stages)),
-        out_shape=jax.ShapeDtypeStruct(part.shape, F32),
-        in_specs=[pl.BlockSpec(memory_space=pltpu.VMEM)],
-        out_specs=pl.BlockSpec(memory_space=pltpu.VMEM),
+        out_shape=[jax.ShapeDtypeStruct(part.shape, F32), both, both],
+        in_specs=[vmem] + [hbm] * 4,
+        out_specs=[vmem, hbm, hbm],
         scratch_shapes=[
             pltpu.VMEM((len(stages),) + part.shape, F32),
             pltpu.VMEM((len(stages),) + part.shape, F32),
             pltpu.SemaphoreType.DMA((len(stages),)),
             pltpu.SemaphoreType.DMA((len(stages),)),
+            pltpu.VMEM((4, rows, width), BF16),
+            pltpu.SemaphoreType.DMA((4,)),
+            pltpu.SemaphoreType.DMA((4,)),
         ],
         compiler_params=remote_params(5),
         name="total",
-    )(part)
-
-
-def stack_kernel(spot_ref, own_ref, other_ref, out_ref):
-    @pl.when(pl.program_id(0) == 0)
-    def _():
-        out_ref[...] = own_ref[...]
-
-    @pl.when(pl.program_id(0) == 1)
-    def _():
-        out_ref[...] = other_ref[...]
-
-
-def stack_rows(spot, own, other):
-    block = pl.BlockSpec(own.shape, lambda i, spot: (0, 0))
-    return pl.pallas_call(
-        stack_kernel,
-        out_shape=jax.ShapeDtypeStruct((2 * own.shape[0], own.shape[1]), own.dtype),
-        grid_spec=pltpu.PrefetchScalarGridSpec(
-            num_scalar_prefetch=1,
-            grid=(2,),
-            in_specs=[block, block],
-            out_specs=pl.BlockSpec(own.shape, lambda i, spot: (lax.rem(spot[1] + i, 2), 0)),
-        ),
-        name="stack",
-    )(spot, own, other)
+    )(part, *first, *second)
 
 
 def join_kernel(sizes, spot_ref, kept_ref, x_ref, y_ref, both_ref, *out_refs):
@@ -1308,9 +1311,6 @@
     hidden = (active * up_value).astype(BF16)
     down_grad = mm(cot, hidden, 0, 0).astype(BF16)
 
-    def finish_rows(own):
-        return stack_rows(meta, own, swap_core(own)).reshape(tokens.shape)
-
     grad_hidden = mm(after(cot, down_grad), down_w, 1, 0)
     grad_up = (grad_hidden * active).astype(BF16)
     grad_gate = (grad_hidden * up_value * (sig * (1.0 + gate * (1.0 - sig)))).astype(BF16)
@@ -1334,7 +1334,7 @@
     mlp_first = mlp_first + after(mlp_came1, first_grad).astype(F32)
     mlp_second = mlp_second + after(mlp_came2, first_grad).astype(F32)
     mlp_sum = (middle + jnp.concatenate([mlp_first, mlp_second])).astype(BF16)
-    layer_out = finish_rows(mlp_sum)
+    far_sum = swap_core(mlp_sum)
     in_grad = product_reduce8((after(raw_grads, first_grad, mlp_sum),), first, 8)
 
     spot = jnp.stack([place, odd]).astype(jnp.int32)
@@ -1359,12 +1359,18 @@
     scaled_in = own_in * inverse_in
     norm_gain_part = jnp.sum(in_grad * scaled_in, axis=0)
     own_token_grad = (grad_middle + norm_back(in_grad, scaled_in, inverse_in, in_gain)).astype(BF16)
-    token_grad = finish_rows(own_token_grad)
+    far_token_grad = swap_core(own_token_grad)
 
     parts = jnp.concatenate([norm_gain_part, mlp_gain_part, head_gain_parts.reshape(-1)])
     parts = parts.reshape(-1, HEAD)
     far_parts = swap_ctx(parts)
-    sums = total(parts + after(far_parts, token_grad)).reshape(-1)
+    sums, layer_out, token_grad = total(
+        parts + after(far_parts, far_token_grad),
+        (mlp_sum, far_sum),
+        (own_token_grad, far_token_grad),
+    )
+    sums = sums.reshape(-1)
+    layer_out, token_grad = layer_out.reshape(tokens.shape), token_grad.reshape(tokens.shape)
     norm_gain_grad = lax.dynamic_slice_in_dim(sums, mine * block, block, 0)
     mlp_gain_grad = lax.dynamic_slice_in_dim(sums, width + mine * block, block, 0)
     query_gain_grad = lax.dynamic_slice_in_dim(sums, 2 * width + mine * small, small, 0)

time: 687 us -> 690 us (level)
  waiting for transfers between devices: 124 us -> 133 us
  Pallas kernels: 372 us -> 365 us
    pallas_call x2 -> x0, Pallas kernels: 7.25 us -> none  [stack_rows(): pl.pallas_call(stack_kernel, out_shape=jax.ShapeDtypeStruct((2 * own.shap...]
    unnamed x73 -> x77, local copies, waits for them, and re-layouts: 11.7 us -> 15.9 us
  transfers between devices with their start and end apart: 27 -> 27, of which waited for: 11 -> 11; matrix products, arithmetic and copies ran while one was open for 17% -> 17% of each run, Pallas kernels for 45% -> 43%
where the time goes in v9:
time: 690 us; the launch traced here: 682 us
  Pallas kernels  365 us (53%)
  waiting for transfers between devices  133 us (19%)
  matrix products  86.1 us (12%)
  other arithmetic  31.6 us (5%)
  local copies, waits for them, and re-layouts  30 us (4%)
  starting transfers between devices  21.5 us (3%)
  between operations  14.9 us (2%)
    pallas_call x2, Pallas kernels, product_reduce8(): pl.pallas_call(functools.partial(product_reduce8_kernel, rows, groups, fi...  88.7 us
    dot_general x9, matrix products, mm(): lax.dot_general(left, right, (((left_dim,), (right_dim,)), ((), ())), pre...  86.1 us
    ppermute x11, waiting for transfers between devices, swap_ctx(): return lax.ppermute(value, 'ctx', [(0, 1), (1, 0)])  86 us
    pallas_call x1, Pallas kernels, second_shards(): pl.pallas_call(functools.partial(second_kernel, plan, len(groups), rows),...  63 us
    pallas_call x1, Pallas kernels, gather8_product(): pl.pallas_call(functools.partial(gather8_product_kernel, rows), out_shape...  41.5 us
    pallas_call x1, Pallas kernels, gather8(): pl.pallas_call(functools.partial(gather8_kernel, rows, bool(also)), out_s...  40.9 us
    pallas_call x1, Pallas kernels, reduce8(): pl.pallas_call(functools.partial(reduce8_kernel, rows), out_shape=jax.Sha...  40.8 us
    reduce_scatter x3, waiting for transfers between devices, scatter_line(): lax.psum_scatter(value, 'fsdp', scatter_dimension=0, tiled=True, axis_ind...  35.1 us
  transfers between devices with their start and end apart: 27, of which 11 were waited for; matrix products, arithmetic and copies ran while one was open for 17% of the time, Pallas kernels for 43%

profile of v9, /device:TPU:0, one launch (start us, length us, event | category | flops | bytes accessed | tf_op | source)
XLA Modules:
  0.0 682.1 jit_solution(15126318019087252447)
XLA Ops:
  9.9 16.4 %first_shards.1 = (bf16[512,768]{1,0:T(8,128)(2,1)}, f32[8,640]{1,0:T(8,128)}) custom-call(bf16[256,1024]{1,0:T(8,128)(2,1)} %refs_0_.1, bf16[256,512]{1,0:T(8,128)(2,1)} %refs_1_.2, bf16[256,512]{1,0:T(8,128)(2,1)} %refs_2_.2, bf16[256,1024]{1,0:T(8,128)(2,1)} %refs_3_.1, f32[1,640]{1,0:T(1,128)} %convert_element_type.89.refs_4_), custom_call_target="tpu_custom_call" | custom-call | tf_op jit(solution)/shard_map/first_shards/pallas_call | solution.py:776
  26.4 63.0 %second_shards.1 = (bf16[2048,2048]{1,0:T(8,128)(2,1)}, bf16[512,1536]{1,0:T(8,128)(2,1)}, bf16[512,768]{1,0:T(8,128)(2,1)}) custom-call(bf16[256,3072]{1,0:T(8,128)(2,1)} %refs_0_.2, bf16[256,3072]{1,0:T(8,128)(2,1)} %refs_1_.3, bf16[256,3072]{1,0:T(8,128)(2,1)} %refs_2_.3, bf16[512,2048]{1,0:T(8,128)(2,1)} %bitcast.49), custom_call_target="tpu_custom_call" | custom-call | tf_op jit(solution)/shard_map/second_shards/pallas_call | solution.py:864
  93.4 5.4 fusion
  103.4 9.9 %collective-permute-done = s32[1,1024]{1,0:T(1,128)S(1)} collective-permute-done((s32[1,1024]{1,0:T(1,128)S(1)}, s32[1,1024]{1,0:T(1,128)S(1)}, u32[]{:S(2)}, u32[]{:S(2)}) %collective-permute-start) | collective-permute-done | bytes 4128 | tf_op jit(solution)/shard_map/ppermute | solution.py:38
  115.3 10.6 %fusion.8.qkv_ref = f32[2048,512]{1,0:T(8,128)} fusion(bf16[2048,2048]{1,0:T(8,128)(2,1)} %get-tuple-element.52, f32[2048]{0:T(1024)S(1)} %bitcast.56, f32[2048]{0:T(1024)S(1)} %add_rsqrt_fusion, bf16[2048,768]{1,0:T(8,128)(2,1)} %all-gather.4.cloned.1.call-done.refs_1_), kind=kOutput, calls=%fused_computation.22 | convolution fusion | flops 4311744512 | bytes 14696448 | tf_op jit(solution)/shard_map/dot_general | solution.py:23
  125.9 16.2 %attend.1 = bf16[2048,256]{1,0:T(8,128)(2,1)} custom-call(s32[2]{0:T(128)} %pad_add_fusion.1.meta_ref, f32[2048,512]{1,0:T(8,128)} %fusion.8.qkv_ref, s32[2,1024,1]{2,1,0:T(8,128)} %copy.28.segc_ref, s32[2,1,1024]{2,1,0:T(1,128)} %broadcast_in_dim.8.segr_ref, f32[1024,128]{1,0:T(8,128)} %get-tuple-element.115.cos_ref, ...), custom_call_target="tpu_custom_call" | custom-call | flops 1073741824 | bytes 5242880 | tf_op jit(solution)/shard_map/attend/pallas_call | solution.py:1169
  142.1 4.8 convolution_convert_fusion.far_ref
  146.9 6.2 fusion.21.near_ref
  153.1 40.8 %reduce8.1 = f32[256,2048]{1,0:T(8,128)S(1)} custom-call(f32[1024,2048]{1,0:T(8,128)} %fusion.21.near_ref, bf16[1024,2048]{1,0:T(8,128)(2,1)} %convolution_convert_fusion.far_ref), custom_call_target="tpu_custom_call" | custom-call | tf_op jit(solution)/shard_map/reduce8/pallas_call | solution.py:441
  198.5 11.3 %collective-permute-done.3.refs_4_ = bf16[128,2048]{1,0:T(8,128)(2,1)S(1)} collective-permute-done((bf16[128,2048]{1,0:T(8,128)(2,1)S(1)}, bf16[128,2048]{1,0:T(8,128)(2,1)S(1)}, u32[]{:S(2)}, u32[]{:S(2)}) %collective-permute-start.3) | collective-permute-done | bytes 524320 | tf_op jit(solution)/shard_map/ppermute | solution.py:33
  211.4 40.9 %gather8_also.1 = (bf16[2048,2048]{1,0:T(8,128)(2,1)}, bf16[2048,2048]{1,0:T(8,128)(2,1)}) custom-call(bf16[256,2048]{1,0:T(8,128)(2,1)} %multiply_convert_fusion.3.refs_0_, bf16[256,2048]{1,0:T(8,128)(2,1)} %copy-done.13, bf16[256,2048]{1,0:T(8,128)(2,1)} %copy-done.16, bf16[256,2048]{1,0:T(8,128)(2,1)} %copy-done.17, bf16[128,2048]{1,0:T(8,128)(2,1)} %copy-done.20, ...), custom_call_target="tpu_custom_call" | custom-call | tf_op jit(solution)/shard_map/gather8_also/pallas_call | solution.py:348
  252.4 17.6 %fusion.31 = f32[2048,1536]{1,0:T(8,128)S(1)} fusion(bf16[2048,2048]{1,0:T(8,128)(2,1)} %get-tuple-element.60.refs_3_, bf16[2048,1536]{1,0:T(8,128)(2,1)} %all-gather.6.cloned.1.call-done.refs_2_), kind=kOutput, calls=%fused_computation.81 | convolution fusion | flops 12884901888 | bytes 27262976 | tf_op jit(solution)/shard_map/dot_general | solution.py:23
  272.1 4.3 copy-done.6
  279.1 8.5 %convolution_convert_fusion.1 = bf16[2048,768]{1,0:T(8,128)(2,1)} fusion(bf16[2048,2048]{1,0:T(8,128)(2,1)S(1)} %copy-done.34, bf16[2048,768]{1,0:T(8,128)(2,1)S(1)} %multiply_convert_fusion.2.acts_ref), kind=kOutput, calls=%fused_computation.11 | convolution fusion | flops 6444023808 | bytes 14680064 | tf_op jit(solution)/shard_map/dot_general | solution.py:23
  287.5 16.4 %multiply_convert_fusion = (bf16[2048,768]{1,0:T(8,128)(2,1)}, bf16[2048,768]{1,0:T(8,128)(2,1)}) fusion(f32[2048,1536]{1,0:T(8,128)} %copy-done.6, bf16[2048,2048]{1,0:T(8,128)(2,1)} %get-tuple-element.62, bf16[2048,768]{1,0:T(8,128)(2,1)} %all-gather.8.cloned.1.call-done.weight_ref), kind=kOutput, calls=%fused_computation.5 | convolution fusion | flops 6462898176 | bytes 30408704 | tf_op jit(solution)/shard_map/dot_general | solution.py:23
  303.9 47.6 %product_reduce8.2 = (f32[256,2048]{1,0:T(8,128)}, bf16[2048,1536]{1,0:T(8,128)(2,1)}) custom-call(bf16[2048,768]{1,0:T(8,128)(2,1)} %get-tuple-element.94.refs_0_, bf16[2048,768]{1,0:T(8,128)(2,1)} %get-tuple-element.93.refs_1_, bf16[2048,1536]{1,0:T(8,128)(2,1)} %all-gather.6.cloned.1.call-done.refs_2_, bf16[2048,2048]{1,0:T(8,128)(2,1)} %get-tuple-element.60.refs_3_), custom_call_target="tpu_custom_call" | custom-call | flops 25769803776 | bytes 25165824 | tf_op jit(solution)/shard_map/product_reduce8/pallas_call | solution.py:645
  356.3 41.5 %gather8_product.1 = (bf16[2048,2048]{1,0:T(8,128)(2,1)}, f32[512,2048]{1,0:T(8,128)}, bf16[256,2048]{1,0:T(8,128)(2,1)S(1)}, bf16[256,2048]{1,0:T(8,128)(2,1)S(1)}) custom-call(bf16[256,2048]{1,0:T(8,128)(2,1)S(1)} %fusion.28.own_ref, bf16[2048,768]{1,0:T(8,128)(2,1)} %copy-done.15, bf16[2048,768]{1,0:T(8,128)(2,1)} %all-gather.8.cloned.1.call-done.weight_ref), custom_call_target="tpu_custom_call" | custom-call | flops 6442450944 | bytes 8388608 | tf_op jit(solution)/shard_map/gather8_product/pallas_call | solution.py:307
  397.8 7.1 %convolution_convert_fusion.4.grad_ref = bf16[2048,256]{1,0:T(8,128)(2,1)} fusion(bf16[2048,2048]{1,0:T(8,128)(2,1)} %get-tuple-element.65, bf16[2048,768]{1,0:T(8,128)(2,1)} %all-gather.4.cloned.1.call-done.refs_1_), kind=kOutput, calls=%fused_computation.21 | convolution fusion | flops 2148007936 | bytes 10485760 | tf_op jit(solution)/shard_map/dot_general | solution.py:23
  404.9 28.8 %attend_back.1 = (bf16[2048,512]{1,0:T(8,128)(2,1)}, f32[2,128]{1,0:T(2,128)}) custom-call(s32[2]{0:T(128)} %pad_add_fusion.1.meta_ref, f32[2048,512]{1,0:T(8,128)} %fusion.8.qkv_ref, bf16[2048,256]{1,0:T(8,128)(2,1)} %convolution_convert_fusion.4.grad_ref, s32[2,1024,1]{2,1,0:T(8,128)} %copy.28.segc_ref, s32[2,1,1024]{2,1,0:T(1,128)} %broadcast_in_dim.8.segr_ref, ...), custom_call_target="tpu_custom_call" | custom-call | flops 2684354560 | bytes 8388608 | tf_op jit(solution)/shard_map/attend_back/pallas_call | solution.py:1197
  433.7 6.2 convolution_convert_fusion.3
  440.0 8.7 %convolution_convert_fusion.2 = bf16[2048,512]{1,0:T(8,128)(2,1)S(1)} fusion(bf16[2048,512]{1,0:T(8,128)(2,1)S(1)} %copy-done.35, bf16[2048,2048]{1,0:T(8,128)(2,1)} %get-tuple-element.52, f32[2048]{0:T(1024)S(1)} %bitcast.57, f32[2048]{0:T(1024)S(1)} %copy-done.30), kind=kOutput, calls=%fused_computation.16 | convolution fusion | flops 4312793088 | bytes 12599296 | tf_op jit(solution)/shard_map/dot_general | solution.py:23
  453.0 23.7 %collective-permute-done.5 = bf16[256,2048]{1,0:T(8,128)(2,1)S(1)} collective-permute-done((bf16[256,2048]{1,0:T(8,128)(2,1)S(1)}, bf16[256,2048]{1,0:T(8,128)(2,1)S(1)}, u32[]{:S(2)}, u32[]{:S(2)}) %collective-permute-start.5) | collective-permute-done | bytes 1048608 | tf_op jit(solution)/shard_map/ppermute | solution.py:33
  482.3 11.2 %collective-permute-done.8 = bf16[128,2048]{1,0:T(8,128)(2,1)S(1)} collective-permute-done((bf16[128,2048]{1,0:T(8,128)(2,1)S(1)}, bf16[128,2048]{1,0:T(8,128)(2,1)S(1)}, u32[]{:S(2)}, u32[]{:S(2)}) %collective-permute-start.8) | collective-permute-done | bytes 524320 | tf_op jit(solution)/shard_map/ppermute | solution.py:33
  496.1 41.1 %product_reduce8.3 = f32[256,2048]{1,0:T(8,128)} custom-call(bf16[2048,512]{1,0:T(8,128)(2,1)} %get-tuple-element.74.refs_0_, bf16[2048,768]{1,0:T(8,128)(2,1)} %all-gather.4.cloned.1.call-done.refs_1_), custom_call_target="tpu_custom_call" | custom-call | flops 4294967296 | bytes 8388608 | tf_op jit(solution)/shard_map/product_reduce8/pallas_call | solution.py:645
  539.9 4.2 fusion.15.refs_2_
  552.4 35.1 %reduce-scatter.8.cloned.1.call-done = bf16[512,768]{1,0:T(8,128)(2,1)} async-done(((bf16[2048,768]{1,0:T(8,128)(2,1)}), bf16[512,768]{1,0:T(8,128)(2,1)}) %reduce-scatter.8.cloned.1.call-update) | async-done | bytes 786448 | tf_op jit(solution)/shard_map/reduce_scatter | solution.py:51
  595.6 6.2 collective-permute-done.13.y_ref
  604.5 13.1 %total.1 = (f32[34,128]{1,0:T(8,128)}, bf16[512,2048]{1,0:T(8,128)(2,1)}, bf16[512,2048]{1,0:T(8,128)(2,1)}) custom-call(f32[34,128]{1,0:T(8,128)} %fusion.26.part_ref, bf16[256,2048]{1,0:T(8,128)(2,1)} %fusion.18.refs_0_, bf16[256,2048]{1,0:T(8,128)(2,1)} %collective-permute-done.11.refs_1_, bf16[256,2048]{1,0:T(8,128)(2,1)} %copy-done.12, ...), custom_call_target="tpu_custom_call" | custom-call | tf_op jit(solution)/shard_map/total/pallas_call | solution.py:916
  620.2 32.1 %collective-permute-done.14.both_ref = bf16[256,768]{1,0:T(8,128)(2,1)S(1)} collective-permute-done((bf16[256,768]{1,0:T(8,128)(2,1)}, bf16[256,768]{1,0:T(8,128)(2,1)S(1)}, u32[]{:S(2)}, u32[]{:S(2)}) %collective-permute-start.14) | collective-permute-done | bytes 393248 | tf_op jit(solution)/shard_map/ppermute | solution.py:33
  653.0 4.6 join.3
  659.9 4.6 join.5
  664.6 5.9 join.4
  (175 shorter events, 73.1 us)
Async XLA Ops:
  7.2 108.1 %all-gather.4.cloned.1.call-start = ((), (), s32[]{:S(2)}) async-start(), calls=%async_computation.3 | async-start | bytes 3932160 | tf_op jit(solution)/shard_map/all_gather | solution.py:47
  26.4 226.0 %all-gather.6.cloned.1.call-start = ((), (), s32[]{:S(2)}) async-start(), calls=%async_computation.4 | async-start | bytes 7864320 | tf_op jit(solution)/shard_map/all_gather | solution.py:47
  26.4 63.1 %copy-start.9 = (bf16[1,512,2048]{2,1,0:T(8,128)(2,1)S(1)}, bf16[1,512,2048]{2,1,0:T(8,128)(2,1)}, u32[]{:S(2)}) copy-start(bf16[1,512,2048]{2,1,0:T(8,128)(2,1)} %param.27) | copy-start | bytes 6291460
  89.5 198.1 %all-gather.8.cloned.1.call-start = ((), (), s32[]{:S(2)}) async-start(), calls=%async_computation.5 | async-start | bytes 3932160 | tf_op jit(solution)/shard_map/all_gather | solution.py:47
  89.7 57.2 %collective-permute-start.1 = (bf16[256,2048]{1,0:T(8,128)(2,1)S(1)}, bf16[256,2048]{1,0:T(8,128)(2,1)S(1)}, u32[]{:S(2)}, u32[]{:S(2)}) collective-permute-start(bf16[256,2048]{1,0:T(8,128)(2,1)S(1)} %dynamic-slice_bitcast_fusion.refs_1_), channel_id=1, source_target_pairs={{0,4},{4,0},{8,12},{12,8},{16,20},{20,16},{24,28},{28,24},{1,5},{5... | collective-permute-start | bytes 3145736 | tf_op jit(solution)/shard_map/ppermute | solution.py:38
  91.2 103.8 %collective-permute-start.2 = (bf16[256,2048]{1,0:T(8,128)(2,1)S(1)}, bf16[256,2048]{1,0:T(8,128)(2,1)S(1)}, u32[]{:S(2)}, u32[]{:S(2)}) collective-permute-start(bf16[256,2048]{1,0:T(8,128)(2,1)S(1)} %dynamic-slice_bitcast_fusion.refs_1_), channel_id=1, source_target_pairs={{0,2},{2,0},{1,3},{3,1},{4,6},{6,4},{5,7},{7,5},{8,10},{10,8},{9,1... | collective-permute-start | bytes 3145736 | tf_op jit(solution)/shard_map/ppermute | solution.py:33
  92.7 20.6 %collective-permute-start = (s32[1,1024]{1,0:T(1,128)S(1)}, s32[1,1024]{1,0:T(1,128)S(1)}, u32[]{:S(2)}, u32[]{:S(2)}) collective-permute-start(s32[1,1024]{1,0:T(1,128)S(1)} %copy-done.33), channel_id=1, source_target_pairs={{0,4},{4,0},{8,12},{12,8},{16,20},{20,16},{24,28},{28,24},{1,5},{5... | collective-permute-start | bytes 12296 | tf_op jit(solution)/shard_map/ppermute | solution.py:38
  93.3 451.4 %reduce-scatter.6.cloned.1.call-start = ((), (), s32[]{:S(2)}) async-start(), calls=%async_computation.7 | async-start | bytes 7864320 | tf_op jit(solution)/shard_map/reduce_scatter | solution.py:51
  146.9 48.1 %copy-start.16 = (bf16[256,2048]{1,0:T(8,128)(2,1)}, bf16[256,2048]{1,0:T(8,128)(2,1)S(1)}, u32[]{:S(2)}) copy-start(bf16[256,2048]{1,0:T(8,128)(2,1)S(1)} %collective-permute-done.1.refs_2_) | copy-start | bytes 3145732
  195.1 14.7 %collective-permute-start.3 = (bf16[128,2048]{1,0:T(8,128)(2,1)S(1)}, bf16[128,2048]{1,0:T(8,128)(2,1)S(1)}, u32[]{:S(2)}, u32[]{:S(2)}) collective-permute-start(bf16[128,2048]{1,0:T(8,128)(2,1)S(1)} %slice.60), channel_id=1, source_target_pairs={{0,2},{2,0},{1,3},{3,1},{4,6},{6,4},{5,7},{7,5},{8,10},{10,8},{9,1... | collective-permute-start | bytes 1572872 | tf_op jit(solution)/shard_map/ppermute | solution.py:33
  196.7 13.4 %collective-permute-start.4 = (bf16[128,2048]{1,0:T(8,128)(2,1)S(1)}, bf16[128,2048]{1,0:T(8,128)(2,1)S(1)}, u32[]{:S(2)}, u32[]{:S(2)}) collective-permute-start(bf16[128,2048]{1,0:T(8,128)(2,1)S(1)} %slice.61), channel_id=1, source_target_pairs={{0,4},{4,0},{8,12},{12,8},{16,20},{20,16},{24,28},{28,24},{1,5},{5... | collective-permute-start | bytes 1572872 | tf_op jit(solution)/shard_map/ppermute | solution.py:38
  351.6 197.5 %reduce-scatter.4.cloned.1.call-start = ((), (), s32[]{:S(2)}) async-start(), calls=%async_computation.6 | async-start | bytes 3932160 | tf_op jit(solution)/shard_map/reduce_scatter | solution.py:51
  450.6 137.0 %reduce-scatter.8.cloned.1.call-start = ((), (), s32[]{:S(2)}) async-start(), calls=%async_computation.8 | async-start | bytes 3932160 | tf_op jit(solution)/shard_map/reduce_scatter | solution.py:51
  451.2 25.5 %collective-permute-start.5 = (bf16[256,2048]{1,0:T(8,128)(2,1)S(1)}, bf16[256,2048]{1,0:T(8,128)(2,1)S(1)}, u32[]{:S(2)}, u32[]{:S(2)}) collective-permute-start(bf16[256,2048]{1,0:T(8,128)(2,1)S(1)} %get-tuple-element.68), channel_id=1, source_target_pairs={{0,2},{2,0},{1,3},{3,1},{4,6},{6,4},{5,7},{7,5},{8,10},{10,8},{9,1... | collective-permute-start | bytes 3145736 | tf_op jit(solution)/shard_map/ppermute | solution.py:33
  451.8 25.3 %collective-permute-start.7 = (bf16[256,2048]{1,0:T(8,128)(2,1)S(1)}, bf16[256,2048]{1,0:T(8,128)(2,1)S(1)}, u32[]{:S(2)}, u32[]{:S(2)}) collective-permute-start(bf16[256,2048]{1,0:T(8,128)(2,1)S(1)} %get-tuple-element.71), channel_id=1, source_target_pairs={{0,4},{4,0},{8,12},{12,8},{16,20},{20,16},{24,28},{28,24},{1,5},{5... | collective-permute-start | bytes 3145736 | tf_op jit(solution)/shard_map/ppermute | solution.py:38
  480.1 13.4 %collective-permute-start.8 = (bf16[128,2048]{1,0:T(8,128)(2,1)S(1)}, bf16[128,2048]{1,0:T(8,128)(2,1)S(1)}, u32[]{:S(2)}, u32[]{:S(2)}) collective-permute-start(bf16[128,2048]{1,0:T(8,128)(2,1)S(1)} %slice.108), channel_id=1, source_target_pairs={{0,2},{2,0},{1,3},{3,1},{4,6},{6,4},{5,7},{7,5},{8,10},{10,8},{9,1... | collective-permute-start | bytes 1572872 | tf_op jit(solution)/shard_map/ppermute | solution.py:33
  481.6 13.0 %collective-permute-start.6 = (bf16[128,2048]{1,0:T(8,128)(2,1)S(1)}, bf16[128,2048]{1,0:T(8,128)(2,1)S(1)}, u32[]{:S(2)}, u32[]{:S(2)}) collective-permute-start(bf16[128,2048]{1,0:T(8,128)(2,1)S(1)} %slice.109), channel_id=1, source_target_pairs={{0,4},{4,0},{8,12},{12,8},{16,20},{20,16},{24,28},{28,24},{1,5},{5... | collective-permute-start | bytes 1572872 | tf_op jit(solution)/shard_map/ppermute | solution.py:38
  544.2 46.8 %collective-permute-start.10 = (bf16[256,2048]{1,0:T(8,128)(2,1)S(1)}, bf16[256,2048]{1,0:T(8,128)(2,1)}, u32[]{:S(2)}, u32[]{:S(2)}) collective-permute-start(bf16[256,2048]{1,0:T(8,128)(2,1)S(1)} %fusion.15.refs_2_), channel_id=1, source_target_pairs={{0,1},{1,0},{2,3},{3,2},{4,5},{5,4},{6,7},{7,6},{8,9},{9,8},{10,11... | collective-permute-start | bytes 3145736 | tf_op jit(solution)/shard_map/ppermute | solution.py:29
  544.4 48.0 %collective-permute-start.11 = (bf16[256,2048]{1,0:T(8,128)(2,1)S(1)}, bf16[256,2048]{1,0:T(8,128)(2,1)}, u32[]{:S(2)}, u32[]{:S(2)}) collective-permute-start(bf16[256,2048]{1,0:T(8,128)(2,1)S(1)} %copy-done.11), channel_id=1, source_target_pairs={{0,1},{1,0},{2,3},{3,2},{4,5},{5,4},{6,7},{7,6},{8,9},{9,8},{10,11... | collective-permute-start | bytes 3145736 | tf_op jit(solution)/shard_map/ppermute | solution.py:29
  547.1 70.4 %copy-start.14 = (bf16[256,1536]{1,0:T(8,128)(2,1)}, bf16[256,1536]{1,0:T(8,128)(2,1)S(1)}, u32[]{:S(2)}) copy-start(bf16[256,1536]{1,0:T(8,128)(2,1)S(1)} %get-tuple-element.99.kept_ref) | copy-start | bytes 2359300
  547.1 45.9 %collective-permute-start.15 = (bf16[256,1536]{1,0:T(8,128)(2,1)}, bf16[256,1536]{1,0:T(8,128)(2,1)}, u32[]{:S(2)}, u32[]{:S(2)}) collective-permute-start(bf16[256,1536]{1,0:T(8,128)(2,1)} %get-tuple-element.98), channel_id=1, source_target_pairs={{0,4},{4,0},{8,12},{12,8},{16,20},{20,16},{24,28},{28,24},{1,5},{5... | collective-permute-start | bytes 2359304 | tf_op jit(solution)/shard_map/ppermute | solution.py:38
  548.4 41.1 %collective-permute-start.9 = (f32[34,128]{1,0:T(8,128)S(1)}, f32[34,128]{1,0:T(8,128)S(1)}, u32[]{:S(2)}, u32[]{:S(2)}) collective-permute-start(f32[34,128]{1,0:T(8,128)S(1)} %maximum_bitcast_fusion), channel_id=1, source_target_pairs={{0,2},{2,0},{1,3},{3,1},{4,6},{6,4},{5,7},{7,5},{8,10},{10,8},{9,1... | collective-permute-start | bytes 52232 | tf_op jit(solution)/shard_map/ppermute | solution.py:33
  551.2 43.9 %collective-permute-start.12 = (bf16[256,768]{1,0:T(8,128)(2,1)}, bf16[256,768]{1,0:T(8,128)(2,1)}, u32[]{:S(2)}, u32[]{:S(2)}) collective-permute-start(bf16[256,768]{1,0:T(8,128)(2,1)} %get-tuple-element.102), channel_id=1, source_target_pairs={{0,4},{4,0},{8,12},{12,8},{16,20},{20,16},{24,28},{28,24},{1,5},{5... | collective-permute-start | bytes 1179656 | tf_op jit(solution)/shard_map/ppermute | solution.py:38
  589.4 69.7 %copy-start.19 = (bf16[256,768]{1,0:T(8,128)(2,1)}, bf16[256,768]{1,0:T(8,128)(2,1)S(1)}, u32[]{:S(2)}) copy-start(bf16[256,768]{1,0:T(8,128)(2,1)S(1)} %get-tuple-element.101.kept_ref) | copy-start | bytes 1179652
  589.5 12.4 %collective-permute-start.13 = (bf16[256,768]{1,0:T(8,128)(2,1)}, bf16[256,768]{1,0:T(8,128)(2,1)}, u32[]{:S(2)}, u32[]{:S(2)}) collective-permute-start(bf16[256,768]{1,0:T(8,128)(2,1)} %get-tuple-element.103.kept_ref), channel_id=1, source_target_pairs={{0,2},{2,0},{1,3},{3,1},{4,6},{6,4},{5,7},{7,5},{8,10},{10,8},{9,1... | collective-permute-start | bytes 1179656 | tf_op jit(solution)/shard_map/ppermute | solution.py:33
  591.0 12.3 %collective-permute-start.18 = (bf16[256,768]{1,0:T(8,128)(2,1)}, bf16[256,768]{1,0:T(8,128)(2,1)S(1)}, u32[]{:S(2)}, u32[]{:S(2)}) collective-permute-start(bf16[256,768]{1,0:T(8,128)(2,1)} %get-tuple-element.100), channel_id=1, source_target_pairs={{0,4},{4,0},{8,12},{12,8},{16,20},{20,16},{24,28},{28,24},{1,5},{5... | collective-permute-start | bytes 1179656 | tf_op jit(solution)/shard_map/ppermute | solution.py:38
  592.5 72.1 %collective-permute-start.16 = (bf16[256,1536]{1,0:T(8,128)(2,1)S(1)}, bf16[256,1536]{1,0:T(8,128)(2,1)}, u32[]{:S(2)}, u32[]{:S(2)}) collective-permute-start(bf16[256,1536]{1,0:T(8,128)(2,1)S(1)} %get-tuple-element.99.kept_ref), channel_id=1, source_target_pairs={{0,2},{2,0},{1,3},{3,1},{4,6},{6,4},{5,7},{7,5},{8,10},{10,8},{9,1... | collective-permute-start | bytes 2359304 | tf_op jit(solution)/shard_map/ppermute | solution.py:33
  593.0 71.6 %collective-permute-start.17 = (bf16[256,1536]{1,0:T(8,128)(2,1)}, bf16[256,1536]{1,0:T(8,128)(2,1)}, u32[]{:S(2)}, u32[]{:S(2)}) collective-permute-start(bf16[256,1536]{1,0:T(8,128)(2,1)} %collective-permute-done.15.x_ref), channel_id=1, source_target_pairs={{0,2},{2,0},{1,3},{3,1},{4,6},{6,4},{5,7},{7,5},{8,10},{10,8},{9,1... | collective-permute-start | bytes 2359304 | tf_op jit(solution)/shard_map/ppermute | solution.py:33
  595.1 62.6 %collective-permute-start.19 = (bf16[256,768]{1,0:T(8,128)(2,1)S(1)}, bf16[256,768]{1,0:T(8,128)(2,1)S(1)}, u32[]{:S(2)}, u32[]{:S(2)}) collective-permute-start(bf16[256,768]{1,0:T(8,128)(2,1)S(1)} %get-tuple-element.101.kept_ref), channel_id=1, source_target_pairs={{0,2},{2,0},{1,3},{3,1},{4,6},{6,4},{5,7},{7,5},{8,10},{10,8},{9,1... | collective-permute-start | bytes 1179656 | tf_op jit(solution)/shard_map/ppermute | solution.py:33
  601.8 50.5 %collective-permute-start.14 = (bf16[256,768]{1,0:T(8,128)(2,1)}, bf16[256,768]{1,0:T(8,128)(2,1)S(1)}, u32[]{:S(2)}, u32[]{:S(2)}) collective-permute-start(bf16[256,768]{1,0:T(8,128)(2,1)} %collective-permute-done.12.x_ref), channel_id=1, source_target_pairs={{0,2},{2,0},{1,3},{3,1},{4,6},{6,4},{5,7},{7,5},{8,10},{10,8},{9,1... | collective-permute-start | bytes 1179656 | tf_op jit(solution)/shard_map/ppermute | solution.py:33
  603.3 55.9 %copy-start.22 = (bf16[256,768]{1,0:T(8,128)(2,1)}, bf16[256,768]{1,0:T(8,128)(2,1)S(1)}, u32[]{:S(2)}) copy-start(bf16[256,768]{1,0:T(8,128)(2,1)S(1)} %collective-permute-done.18.x_ref) | copy-start | bytes 1179652
  603.3 55.9 %collective-permute-start.20 = (bf16[256,768]{1,0:T(8,128)(2,1)S(1)}, bf16[256,768]{1,0:T(8,128)(2,1)S(1)}, u32[]{:S(2)}, u32[]{:S(2)}) collective-permute-start(bf16[256,768]{1,0:T(8,128)(2,1)S(1)} %collective-permute-done.18.x_ref), channel_id=1, source_target_pairs={{0,2},{2,0},{1,3},{3,1},{4,6},{6,4},{5,7},{7,5},{8,10},{10,8},{9,1... | collective-permute-start | bytes 1179656 | tf_op jit(solution)/shard_map/ppermute | solution.py:33
  (31 other events, 294.3 us)
Sparse Core Ops, SparseCore 0:
  26.5 62.6 all-gather.3
  90.7 114.1 all-gather.5
  206.5 61.6 all-gather.7
  351.7 109.6 reduce-scatter.5
  464.1 60.8 reduce-scatter.3
  527.2 60.3 reduce-scatter.7
